TPU v7x, 32 devices: a whole 2x2x4 slice. The times are simulated.
32 devices in a mesh: fsdp: 8 (over z, y), dp: 4 (over x, core).
Axes of the slice: x: 2, y: 2, z: 4, core: 2. Of those that a mesh axis runs over, the one named last changes fastest.
Arguments:
- tokens: bfloat16 [32, 128, 3584], P(('fsdp', 'dp')), may hold values from -6 to 6
- lengths: int32 [32], P(('fsdp', 'dp')), may hold values from 32 to 128
- partner: int32 [32], replicated, may hold values from 0 to 31, as said below
- pair_weight: float32 [32], P(('fsdp', 'dp')), may hold values from 0.25 to 27
- norm_gain: float32 [3584], replicated, may hold values from 0.5 to 1.5
- qkv_weight: bfloat16 [3584, 4608], P('fsdp'), may hold values from -0.09375 to 0.09375
- qkv_bias: float32 [4608], replicated, may hold values from -40 to 40
- out_weight: bfloat16 [3584, 3584], P(None, 'fsdp'), may hold values from -0.09375 to 0.09375
- final_gain: float32 [3584], replicated, may hold values from 0.5 to 1.5
- value_head: float32 [3584], replicated, may hold values from -0.09375 to 0.09375
Outputs:
- hidden: bfloat16 [32, 128, 3584], P(('fsdp', 'dp'))
- margins: float32 [32], P(('fsdp', 'dp'))
- loss: float32 [], replicated
Inputs may be any that keep to these rules, and one draw needn't show every extreme that they name: partner[partner[i]] = i and partner[i] != i.
All inputs are finite; a program needn't handle non-finite values.
Results may differ from a plain program's by a relative error of at most 0.013.
The roundings to bfloat16 on the way count: a program that leaves them out, or rounds other values in their place, can miss the bound.
Values may be sent and summed in bfloat16 or wider, within the bound.
No kernel may reach another device: no remote copies, remote signals or barrier semaphores. Data moves between devices by JAX's collectives and lax.ppermute only.
A program may use at most 128 MiB of HBM per device.

v0:
```python
import jax
import jax.numpy as jnp
from jax import lax
from jax.experimental import pallas as pl
from jax.experimental.pallas import tpu as pltpu
from jax.sharding import PartitionSpec as P


QUERY_HEADS = 28
KEY_VALUE_HEADS = 4
HEAD_SIZE = 128
QUERY_FEATURES = 3584
KEY_FEATURES = 512
AXES = ("fsdp", "dp")


def rms_scale(value_rows, gain):
    return (
        value_rows
        * lax.rsqrt(jnp.mean(value_rows * value_rows, axis=-1, keepdims=True) + 1e-06)
        * gain
    )


def rotary_tables(length_rows):
    half = HEAD_SIZE // 2
    positions = jnp.arange(length_rows, dtype=jnp.float32)
    freqs = jnp.exp(
        -(2.0 * jnp.arange(half, dtype=jnp.float32) / HEAD_SIZE) * jnp.log(jnp.float32(1000000.0))
    )
    angles = positions[:, None] * freqs[None, :]
    cosine = jnp.cos(angles)
    sine = jnp.sin(angles)
    return (
        jnp.concatenate([cosine, cosine], axis=-1),
        jnp.concatenate([-sine, sine], axis=-1),
    )


def attention_kernel(
    query_heads, lengths_ref, acc_ref, bias_ref, cos_ref, sin_ref, out_ref
):
    length = lengths_ref[pl.program_id(0)]
    rows = acc_ref.shape[0]
    cosine = cos_ref[...]
    sine = sin_ref[...]

    def head(index):
        cols = pl.ds(index * HEAD_SIZE, HEAD_SIZE)
        return acc_ref[:, cols] + bias_ref[:, cols]

    def rotate(values):
        return (
            values * cosine + pltpu.roll(values, HEAD_SIZE // 2, 1) * sine
        ).astype(jnp.bfloat16)

    key_rows = rotate(head(query_heads))
    value_rows = head(query_heads + 1).astype(jnp.bfloat16)
    row = lax.broadcasted_iota(jnp.int32, (rows, rows), 0)
    col = lax.broadcasted_iota(jnp.int32, (rows, rows), 1)
    allowed = (col <= row) & (col < length)
    scale = 1.0 / jnp.sqrt(jnp.float32(HEAD_SIZE))
    for index in range(query_heads):
        scores = (
            lax.dot_general(
                rotate(head(index)),
                key_rows,
                (((1,), (1,)), ((), ())),
                preferred_element_type=jnp.float32,
            )
            * scale
        )
        scores = jnp.where(allowed, scores, jnp.float32(-1e30))
        expd = jnp.exp(scores - jnp.max(scores, axis=-1, keepdims=True))
        inverse = 1.0 / jnp.sum(expd, axis=-1, keepdims=True)
        probs = (expd * inverse).astype(jnp.bfloat16)
        mixed = jnp.dot(probs, value_rows, preferred_element_type=jnp.float32)
        out_ref[:, pl.ds(index * HEAD_SIZE, HEAD_SIZE)] = mixed.astype(jnp.bfloat16)


def attend(acc, bias_cols, tables, group_lengths, query_heads, length_rows):
    total_rows, width = acc.shape
    seq_count = total_rows // length_rows
    query_cols = query_heads * HEAD_SIZE

    def kernel(*refs):
        attention_kernel(query_heads, *refs)

    return pl.pallas_call(
        kernel,
        name="attention",
        out_shape=jax.ShapeDtypeStruct((total_rows, query_cols), jnp.bfloat16),
        grid_spec=pltpu.PrefetchScalarGridSpec(
            num_scalar_prefetch=1,
            grid=(seq_count,),
            in_specs=[
                pl.BlockSpec((length_rows, width), lambda i, lengths: (i, 0)),
                pl.BlockSpec((1, width), lambda i, lengths: (0, 0)),
                pl.BlockSpec((length_rows, HEAD_SIZE), lambda i, lengths: (0, 0)),
                pl.BlockSpec((length_rows, HEAD_SIZE), lambda i, lengths: (0, 0)),
            ],
            out_specs=pl.BlockSpec((length_rows, query_cols), lambda i, lengths: (i, 0)),
        ),
        cost_estimate=pl.CostEstimate(
            flops=32 * seq_count * query_heads * length_rows * length_rows * HEAD_SIZE,
            bytes_accessed=acc.size * 4 + total_rows * query_cols * 2,
            transcendentals=seq_count * query_heads * length_rows * length_rows,
        ),
    )(group_lengths, acc, bias_cols.reshape(1, width), *tables)


def norm_kernel(own_ref, by_y_ref, by_x_ref, far_a_ref, far_b_ref, gain_ref, out_ref):
    shards, _, shard_rows = out_ref.shape
    step = 16
    base = 0
    for source in (own_ref, by_y_ref, by_x_ref, far_a_ref, far_b_ref):

        def body(i, carry, source=source, base=base):
            start = pl.multiple_of(i * step, step)
            values = source[pl.ds(start, step), :].astype(jnp.float32)
            normed = rms_scale(values, gain_ref[...]).astype(jnp.bfloat16)
            target = pl.ds(pl.multiple_of(base + i * step, step), step)
            for s in range(shards):
                out_ref[s, target, :] = normed[:, s * shard_rows : (s + 1) * shard_rows]
            return carry

        lax.fori_loop(0, source.shape[0] // step, body, 0)
        base += source.shape[0]


def normalise(parts, gain, shards):
    rows = sum(part.shape[0] for part in parts)
    width = gain.shape[0]
    return pl.pallas_call(
        norm_kernel,
        name="normalise",
        out_shape=jax.ShapeDtypeStruct((shards, rows, width // shards), jnp.bfloat16),
        cost_estimate=pl.CostEstimate(
            flops=8 * rows * width, bytes_accessed=4 * rows * width, transcendentals=rows
        ),
    )(*parts, gain.reshape(1, width))


def finish_kernel(groups, place_ref, tokens_ref, gain_ref, head_ref, *refs):
    pieces, hidden_ref, score_ref = refs[:-2], refs[-2], refs[-1]
    length = place_ref[0]
    rows, width = tokens_ref.shape
    planes = place_ref.shape[0] - 1
    wide = width // planes
    square = jnp.zeros((1, 1), jnp.float32)
    dotted = jnp.zeros((1, 1), jnp.float32)
    picked = lax.broadcasted_iota(jnp.int32, (rows, 1), 0) == length - 1
    gained = gain_ref[...] * head_ref[...]
    for plane in range(planes):
        slot = place_ref[1 + plane]
        cols = slice(plane * wide, (plane + 1) * wide)
        total = tokens_ref[:, cols].astype(jnp.float32)
        for first in range(0, len(pieces), groups):
            value = None
            base = 0
            for ref in pieces[first : first + groups]:
                count = ref.shape[0]
                part = ref[jnp.clip(slot - base, 0, count - 1)]
                value = part if value is None else jnp.where(slot >= base, part, value)
                base += count
            total += value.astype(jnp.float32)
        hidden = total.astype(jnp.bfloat16)
        hidden_ref[:, cols] = hidden
        last = jnp.sum(jnp.where(picked, hidden.astype(jnp.float32), 0.0), axis=0, keepdims=True)
        square += jnp.sum(last * last, axis=1, keepdims=True)
        dotted += jnp.sum(last * gained[:, cols], axis=1, keepdims=True)
    score_ref[...] = jnp.broadcast_to(
        dotted * lax.rsqrt(square / width + 1e-06), score_ref.shape
    )


def finish(place, tokens, gain, head, pieces, groups):
    rows, width = tokens.shape

    def kernel(*refs):
        finish_kernel(groups, *refs)

    return pl.pallas_call(
        kernel,
        name="finish",
        out_shape=(
            jax.ShapeDtypeStruct((rows, width), jnp.bfloat16),
            jax.ShapeDtypeStruct((1, 128), jnp.float32),
        ),
        in_specs=[pl.BlockSpec(memory_space=pltpu.SMEM)]
        + [pl.BlockSpec(memory_space=pltpu.VMEM)] * (3 + len(pieces)),
        cost_estimate=pl.CostEstimate(
            flops=8 * rows * width, bytes_accessed=6 * rows * width, transcendentals=1
        ),
    )(place, tokens, gain.reshape(1, width), head.reshape(1, width), *pieces)


def solution(mesh):
    fsdp_size = mesh.shape["fsdp"]
    dp_size = mesh.shape["dp"]
    planes = fsdp_size // 2
    ranks = dp_size
    query_heads = QUERY_HEADS // ranks
    key_value_heads = KEY_VALUE_HEADS // ranks
    query_cols = query_heads * HEAD_SIZE
    key_cols = key_value_heads * HEAD_SIZE

    def route(move):
        pairs = []
        for f in range(fsdp_size):
            for d in range(dp_size):
                target = move(f // 2, f % 2, d // 2, d % 2)
                if target is not None:
                    z, y, x, c = target
                    pairs.append((f * dp_size + d, (z * 2 + y) * dp_size + x * 2 + c))
        return pairs

    def send(array, move):
        return lax.ppermute(array, AXES, route(move))

    def to_y(z, y, x, c):
        return (z, 1 - y, x, c)

    def to_x(z, y, x, c):
        return (z, y, x ^ 1, c)

    def to_xy(z, y, x, c):
        return (z, 1 - y, x ^ 1, c)

    def to_core(z, y, x, c):
        return (z, y, x, 1 - c)

    def hop_y(z, y, x, c):
        return (z, 1 - y, x, 1 - c) if c != y else None

    def along(shift, holds):
        def move(z, y, x, c):
            return (z + shift, y, x, c) if holds(z) and 0 <= z + shift < planes else None

        return move

    def outward(step):
        def move(z, y, x, c):
            if z >= step - 1:
                return (z + 1, y, x, c) if z + 1 < planes else None
            if z + step <= planes:
                return (z - 1, y, x, c) if z >= 1 else None
            return None

        return move

    def whole(
        tokens,
        lengths,
        partner,
        pair_weight,
        norm_gain,
        qkv_weight,
        qkv_bias,
        out_weight,
        final_gain,
        value_head,
    ):
        f = lax.axis_index("fsdp")
        d = lax.axis_index("dp")
        z, y, x, c = f // 2, f % 2, d // 2, d % 2
        g = x * 2 + y
        sequence = tokens[0]
        length = lengths[0]
        length_rows, _ = sequence.shape

        def group_slices(array, group, dim):
            return jnp.concatenate(
                [
                    lax.dynamic_slice_in_dim(array, group * query_cols, query_cols, dim),
                    lax.dynamic_slice_in_dim(
                        array, QUERY_FEATURES + group * key_cols, key_cols, dim
                    ),
                    lax.dynamic_slice_in_dim(
                        array, QUERY_FEATURES + KEY_FEATURES + group * key_cols, key_cols, dim
                    ),
                ],
                axis=dim,
            )

        def spread(own, gate=None):
            found = [(z, own, 0)]
            up = down = merged = own
            for step in range(1, planes):
                low, high = z >= step, z + step < planes
                below = jnp.where(low, z - step, -1)
                above = jnp.where(high, z + step, -1)
                if 2 * step <= planes:
                    go_up = along(1, lambda p, step=step: p >= step - 1)
                    go_down = along(-1, lambda p, step=step: p + step <= planes)
                    up = send(up, go_up)
                    down = send(down, go_down)
                    if step == 1 and gate is not None:
                        up, down, _ = lax.optimization_barrier((up, down, gate))
                    if 2 * step < planes:
                        found += [(below, up, step), (above, down, step)]
                        continue
                    merged = jnp.where(low, up, down)
                else:
                    merged = send(merged, outward(step))
                found.append((jnp.where(low, below, above), merged, step))
            return found

        near = c == y

        def with_hop(cut):
            return jnp.where(near, cut, send(cut, hop_y))

        block = with_hop(group_slices(qkv_weight, jnp.where(near, g, g ^ 1), 1))
        qkv_blocks = spread(block)
        others = [send(own, to_core) for _, own, _ in qkv_blocks]

        half = length_rows // 2
        by_y = send(sequence, to_y)
        by_x = send(sequence, to_x)
        halves = by_x[:half], by_y[half:]
        far = [send(halves[0], to_y), send(halves[1], to_x)]
        normed = normalise([sequence, by_y, by_x, *far], norm_gain, fsdp_size)
        near_lengths = [send(lengths, to_y), send(lengths, to_x), send(lengths, to_xy)]
        normed, *near_lengths = lax.optimization_barrier((normed, *near_lengths))
        group_lengths = jnp.stack([lengths, *near_lengths])[:, 0]
        acc = None
        for (plane, own, _), other in zip(qkv_blocks, others):
            for core, weights in ((c, own), (1 - c, other)):
                part = jnp.dot(
                    lax.dynamic_index_in_dim(
                        normed, jnp.maximum(plane, 0) * 2 + core, 0, False
                    ),
                    weights,
                    preferred_element_type=jnp.float32,
                )
                acc = part if acc is None else acc + part

        attn = attend(
            acc,
            group_slices(qkv_bias, g, 0),
            rotary_tables(length_rows),
            group_lengths,
            query_heads,
            length_rows,
        )

        cut = lax.dynamic_slice_in_dim(
            out_weight.T, jnp.where(near, g, g ^ 1) * query_cols, query_cols, 1
        )
        out_blocks = spread(with_hop(cut), attn)
        groups = [[], [], []]
        for index, (_, own, step) in enumerate(out_blocks):
            other = send(own, to_core)
            weights = jnp.where(
                c == 0,
                jnp.concatenate([own, other], axis=0),
                jnp.concatenate([other, own], axis=0),
            )
            part = lax.dot_general(
                attn, weights, (((1,), (1,)), ((), ())), preferred_element_type=jnp.float32
            ).astype(jnp.bfloat16)
            at = 0 if 2 * step < planes else 1
            groups[2 if index == len(out_blocks) - 1 else at].append(part)
        groups = [group for group in groups if group]
        pieces = []
        for j, move in enumerate((None, to_y, to_x, to_xy)):
            for group in groups:
                rows = slice(j * length_rows, (j + 1) * length_rows)
                piece = jnp.stack([part[rows] for part in group])
                pieces.append(piece if move is None else send(piece, move))
        counted = []
        for group in (0, 1, 2):
            for index, (plane, _, step) in enumerate(out_blocks):
                at = 0 if 2 * step < planes else 1
                if group == (2 if index == len(out_blocks) - 1 else at):
                    counted.append(plane)
        slots = [
            sum(b * (plane == p).astype(jnp.int32) for b, plane in enumerate(counted))
            for p in range(planes)
        ]
        place = jnp.stack([length, *slots]).astype(jnp.int32)
        hidden, scored = finish(place, sequence, final_gain, value_head, pieces, len(groups))
        score = scored[0, 0]

        total_seqs = fsdp_size * dp_size
        index_all = jnp.arange(total_seqs, dtype=jnp.int32)
        mine = f * dp_size + d
        lane = lax.broadcasted_iota(jnp.int32, (total_seqs, 1, 128), 2)
        both = jnp.where(lane == 0, score, pair_weight[0])
        gathered = lax.all_to_all(both, AXES, 0, 0, tiled=True)
        everyone = gathered[:, 0, 0]
        weights_all = gathered[:, 0, 1]
        matches = partner[:, None] == index_all[None, :]
        others_all = jnp.sum(jnp.where(matches, everyone[None, :], jnp.float32(0.0)), axis=1)
        margins_all = jnp.where(index_all < partner, everyone - others_all, others_all - everyone)
        margin = jnp.sum(jnp.where(index_all == mine, margins_all, 0.0))
        loss = jnp.sum(weights_all * jax.nn.softplus(-margins_all)) / total_seqs
        return (hidden[None], margin.reshape(1), loss)


    return jax.shard_map(
        whole,
        mesh=mesh,
        in_specs=(
            P(("fsdp", "dp"), None, None),
            P(("fsdp", "dp")),
            P(),
            P(("fsdp", "dp")),
            P(),
            P("fsdp", None),
            P(),
            P(None, "fsdp"),
            P(),
            P(),
        ),
        out_specs=(P(("fsdp", "dp"), None, None), P(("fsdp", "dp")), P()),
        check_vma=False,
    )
```

profile of v0, /device:TPU:0, one launch (start us, length us, event | category | flops | bytes accessed | tf_op | source)
XLA Modules:
  0.0 272.3 jit_solution(13756173289180487052)
XLA Ops:
  0.7 1.3 constant_dynamic-slice_fusion.2
  3.1 1.7 collective-permute-start.7
  4.7 3.0 %collective-permute-start.1 = (bf16[128,3584]{1,0:T(8,128)(2,1)S(1)}, bf16[128,3584]{1,0:T(8,128)(2,1)}, u32[]{:S(2)}, u32[]{:S(2)}) collective-permute-start(bf16[128,3584]{1,0:T(8,128)(2,1)S(1)} %bitcast.109), channel_id=1, source_target_pairs={{0,2},{1,3},{2,0},{3,1},{4,6},{5,7},{6,4},{7,5},{8,10},{9,11},{10,... | collective-permute-start | bytes 2752520 | tf_op jit(solution)/shard_map/ppermute | solution.py:219
  7.7 1.9 collective-permute-start
  9.6 2.1 dynamic-slice_bitcast_fusion
  11.7 1.6 collective-permute-start.18
  13.5 4.5 %collective-permute-start.9 = (bf16[448,1152]{1,0:T(8,128)(2,1)S(1)}, bf16[448,1152]{1,0:T(8,128)(2,1)}, u32[]{:S(2)}, u32[]{:S(2)}) collective-permute-start(bf16[448,1152]{1,0:T(8,128)(2,1)S(1)} %broadcast_select_fusion.1), channel_id=1, source_target_pairs={{0,8},{1,9},{2,10},{3,11},{4,12},{5,13},{6,14},{7,15},{8,16},{9,17... | collective-permute-start | bytes 3096584 | tf_op jit(solution)/shard_map/ppermute | solution.py:219
  17.9 1.3 collective-permute-start.11
  19.5 8.0 %collective-permute-done.1.by_x_ref = bf16[128,3584]{1,0:T(8,128)(2,1)} collective-permute-done((bf16[128,3584]{1,0:T(8,128)(2,1)S(1)}, bf16[128,3584]{1,0:T(8,128)(2,1)}, u32[]{:S(2)}, u32[]{:S(2)}) %collective-permute-start.1) | collective-permute-done | bytes 917536 | tf_op jit(solution)/shard_map/ppermute | solution.py:219
  27.5 9.2 %collective-permute-start.8 = (bf16[448,1152]{1,0:T(8,128)(2,1)S(1)}, bf16[448,1152]{1,0:T(8,128)(2,1)}, u32[]{:S(2)}, u32[]{:S(2)}) collective-permute-start(bf16[448,1152]{1,0:T(8,128)(2,1)S(1)} %broadcast_select_fusion.1), channel_id=1, source_target_pairs={{0,1},{1,0},{2,3},{3,2},{4,5},{5,4},{6,7},{7,6},{8,9},{9,8},{10,11... | collective-permute-start | bytes 3096584 | tf_op jit(solution)/shard_map/ppermute | solution.py:219
  40.3 1.6 collective-permute-start.2
  43.0 2.5 collective-permute-start.3
  47.6 1.3 broadcast_select_fusion.3
  48.9 9.8 %collective-permute-done.2.far_a_ref = bf16[64,3584]{1,0:T(8,128)(2,1)S(1)} collective-permute-done((bf16[64,3584]{1,0:T(8,128)(2,1)S(1)}, bf16[64,3584]{1,0:T(8,128)(2,1)S(1)}, u32[]{:S(2)}, u32[]{:S(2)}) %collective-permute-start.2) | collective-permute-done | bytes 458784 | tf_op jit(solution)/shard_map/ppermute | solution.py:219
  59.4 1.5 collective-permute-start.5
  60.9 10.7 %normalise.1 = bf16[8,512,448]{2,1,0:T(8,128)(2,1)} custom-call(bf16[128,3584]{1,0:T(8,128)(2,1)} %bitcast.107, bf16[128,3584]{1,0:T(8,128)(2,1)} %collective-permute-done.by_y_ref, bf16[128,3584]{1,0:T(8,128)(2,1)} %collective-permute-done.1.by_x_ref, bf16[64,3584]{1,0:T(8,128)(2,1)} %copy-done.5, bf16[64,3584]{1,0:T(8,128)(2,1)} %collective-permute-done.3.far_b_ref, ...), custom_call_target="tpu_custom_call" | custom-call | flops 14680064 | bytes 7340032 | tf_op jit(solution)/shard_map/normalise/pallas_call | solution.py:134
  71.6 4.3 %collective-permute-start.6 = (s32[1]{0:T(128)}, s32[1]{0:T(128)}, u32[]{:S(2)}, u32[]{:S(2)}) collective-permute-start(s32[1]{0:T(128)} %param.11), channel_id=1, source_target_pairs={{0,6},{1,7},{2,4},{3,5},{4,2},{5,3},{6,0},{7,1},{8,14},{9,15},{10,... | collective-permute-start | bytes 20 | tf_op jit(solution)/shard_map/ppermute | solution.py:219
  75.9 1.6 collective-permute-done.6
  77.6 2.5 collective-permute-start.20
  80.0 2.4 add_bitcast_fusion.refs_0_
  83.1 1.3 collective-permute-start.14
  84.4 2.4 fusion.56
  86.9 2.2 fusion.58
  90.0 21.0 %collective-permute-done.14 = bf16[448,1152]{1,0:T(8,128)(2,1)S(1)} collective-permute-done((bf16[448,1152]{1,0:T(8,128)(2,1)}, bf16[448,1152]{1,0:T(8,128)(2,1)S(1)}, u32[]{:S(2)}, u32[]{:S(2)}) %collective-permute-start.14) | collective-permute-done | bytes 1032224 | tf_op jit(solution)/shard_map/ppermute | solution.py:219
  111.2 1.3 collective-permute-start.16
  112.5 2.1 fusion.53
  117.0 26.3 %collective-permute-done.16 = bf16[448,1152]{1,0:T(8,128)(2,1)S(1)} collective-permute-done((bf16[448,1152]{1,0:T(8,128)(2,1)S(1)}, bf16[448,1152]{1,0:T(8,128)(2,1)S(1)}, u32[]{:S(2)}, u32[]{:S(2)}) %collective-permute-start.16) | collective-permute-done | bytes 1032224 | tf_op jit(solution)/shard_map/ppermute | solution.py:219
  144.2 1.3 collective-permute-start.21
  147.3 2.3 convolution_add_fusion.refs_1_
  149.6 12.6 %attention.1 = bf16[512,896]{1,0:T(8,128)(2,1)} custom-call(s32[4]{0:T(128)} %add_bitcast_fusion.refs_0_, f32[512,1152]{1,0:T(8,128)} %convolution_add_fusion.refs_1_, f32[1,1152]{1,0:T(1,128)} %reshape.38.refs_2_, f32[128,128]{1,0:T(8,128)} %get-tuple-element.50.refs_3_, f32[128,128]{1,0:T(8,128)} %get-tuple-element.51.refs_4_), custom_call_target="tpu_custom_call" | custom-call | flops 1879048192 | bytes 3276800 | tf_op jit(solution)/shard_map/attention/pallas_call | solution.py:89
  162.2 4.3 %collective-permute-done.21 = bf16[448,896]{1,0:T(8,128)(2,1)} collective-permute-done((bf16[448,896]{1,0:T(8,128)(2,1)S(1)}, bf16[448,896]{1,0:T(8,128)(2,1)}, u32[]{:S(2)}, u32[]{:S(2)}) %collective-permute-start.21) | collective-permute-done | bytes 802848 | tf_op jit(solution)/shard_map/ppermute | solution.py:219
  167.4 1.3 collective-permute-start.25
  169.3 3.0 %fusion.44 = bf16[512,896]{1,0:T(8,128)(2,1)S(1)} fusion(bf16[512,896]{1,0:T(8,128)(2,1)} %attention.1, bf16[448,896]{1,0:T(8,128)(2,1)} %collective-permute-done.19, bf16[448,896]{1,0:T(8,128)(2,1)S(1)} %broadcast_select_fusion.3, pred[]{:T(512)S(6)} %eq.104), kind=kOutput, calls=%fused_computation.53 | convolution fusion | flops 829767680 | bytes 3440641 | tf_op jit(solution)/shard_map/dot_general | solution.py:360
  172.4 19.3 %collective-permute-done.25 = bf16[448,896]{1,0:T(8,128)(2,1)S(1)} collective-permute-done((bf16[448,896]{1,0:T(8,128)(2,1)}, bf16[448,896]{1,0:T(8,128)(2,1)S(1)}, u32[]{:S(2)}, u32[]{:S(2)}) %collective-permute-start.25) | collective-permute-done | bytes 802848 | tf_op jit(solution)/shard_map/ppermute | solution.py:219
  191.8 1.3 collective-permute-start.27
  193.2 1.3 fusion.43
  194.4 2.6 fusion.42
  197.4 15.0 %collective-permute-done.27 = bf16[448,896]{1,0:T(8,128)(2,1)S(1)} collective-permute-done((bf16[448,896]{1,0:T(8,128)(2,1)S(1)}, bf16[448,896]{1,0:T(8,128)(2,1)S(1)}, u32[]{:S(2)}, u32[]{:S(2)}) %collective-permute-start.27) | collective-permute-done | bytes 802848 | tf_op jit(solution)/shard_map/ppermute | solution.py:219
  212.5 1.9 collective-permute-start.32
  214.6 1.2 fusion.41
  216.5 2.0 collective-permute-start.30
  220.9 1.3 collective-permute-start.36
  222.2 8.6 %collective-permute-done.32.refs_10_ = bf16[3,128,896]{2,1,0:T(8,128)(2,1)S(1)} collective-permute-done((bf16[3,128,896]{2,1,0:T(8,128)(2,1)S(1)}, bf16[3,128,896]{2,1,0:T(8,128)(2,1)S(1)}, u32[]{:S(2)}, u32[]{:S(2)}) %collective-permute-start.32) | collective-permute-done | bytes 688160 | tf_op jit(solution)/shard_map/ppermute | solution.py:219
  233.8 8.9 %collective-permute-done.30.refs_8_ = bf16[1,128,896]{2,1,0:T(8,128)(2,1)S(1)} collective-permute-done((bf16[1,128,896]{2,1,0:T(8,128)(2,1)S(1)}, bf16[1,128,896]{2,1,0:T(8,128)(2,1)S(1)}, u32[]{:S(2)}, u32[]{:S(2)}) %collective-permute-start.30) | collective-permute-done | bytes 229408 | tf_op jit(solution)/shard_map/ppermute | solution.py:219
  246.9 5.0 %collective-permute-done.31.refs_9_ = bf16[1,128,896]{2,1,0:T(8,128)(2,1)} collective-permute-done((bf16[1,128,896]{2,1,0:T(8,128)(2,1)}, bf16[1,128,896]{2,1,0:T(8,128)(2,1)}, u32[]{:S(2)}, u32[]{:S(2)}) %collective-permute-start.31) | collective-permute-done | bytes 229408 | tf_op jit(solution)/shard_map/ppermute | solution.py:219
  251.9 5.6 %finish.1 = (bf16[128,3584]{1,0:T(8,128)(2,1)}, f32[1,128]{1,0:T(1,128)}) custom-call(s32[5]{0:T(128)} %stack.106.refs_0_, bf16[128,3584]{1,0:T(8,128)(2,1)} %bitcast.108, f32[1,3584]{1,0:T(1,128)} %reshape.35.refs_2_, f32[1,3584]{1,0:T(1,128)} %reshape.36.refs_3_, bf16[3,128,896]{2,1,0:T(8,128)(2,1)} %pad_maximum_fusion.1.refs_4_, ...), custom_call_target="tpu_custom_call" | custom-call | flops 3670016 | bytes 2752512 | tf_op jit(solution)/shard_map/finish/pallas_call | solution.py:183
  258.8 3.2 %all-to-all-start = ((f32[32,1,128]{2,1,0:T(1,128)}), f32[32,1,128]{2,1,0:T(1,128)S(1)}, u32[]{:S(2)}, u32[]{:S(2)}) async-start(f32[32,1,128]{2,1,0:T(1,128)} %iota.33), calls=%async_computation | async-start | bytes 32768 | tf_op jit(solution)/shard_map/all_to_all | solution.py:391
  261.9 7.2 %all-to-all-done = f32[32,1,128]{2,1,0:T(1,128)S(1)} async-done(((f32[32,1,128]{2,1,0:T(1,128)}), f32[32,1,128]{2,1,0:T(1,128)S(1)}, u32[]{:S(2)}, u32[]{:S(2)}) %all-to-all-start) | async-done | bytes 16416 | tf_op jit(solution)/shard_map/all_to_all | solution.py:391
  (108 shorter events, 29.6 us)
Async XLA Ops:
  3.1 10.2 %collective-permute-start.7 = (bf16[448,1152]{1,0:T(8,128)(2,1)S(1)}, bf16[448,1152]{1,0:T(8,128)(2,1)}, u32[]{:S(2)}, u32[]{:S(2)}) collective-permute-start(bf16[448,1152]{1,0:T(8,128)(2,1)S(1)} %pad_maximum_fusion), channel_id=1, source_target_pairs={{1,4},{3,6},{4,1},{6,3},{9,12},{11,14},{12,9},{14,11},{17,20},{19,... | collective-permute-start | bytes 3096584 | tf_op jit(solution)/shard_map/ppermute | solution.py:219
  4.7 22.8 %collective-permute-start.1 = (bf16[128,3584]{1,0:T(8,128)(2,1)S(1)}, bf16[128,3584]{1,0:T(8,128)(2,1)}, u32[]{:S(2)}, u32[]{:S(2)}) collective-permute-start(bf16[128,3584]{1,0:T(8,128)(2,1)S(1)} %bitcast.109), channel_id=1, source_target_pairs={{0,2},{1,3},{2,0},{3,1},{4,6},{5,7},{6,4},{7,5},{8,10},{9,11},{10,... | collective-permute-start | bytes 2752520 | tf_op jit(solution)/shard_map/ppermute | solution.py:219
  7.7 32.6 %collective-permute-start = (bf16[128,3584]{1,0:T(8,128)(2,1)S(1)}, bf16[128,3584]{1,0:T(8,128)(2,1)}, u32[]{:S(2)}, u32[]{:S(2)}) collective-permute-start(bf16[128,3584]{1,0:T(8,128)(2,1)S(1)} %bitcast.110), channel_id=1, source_target_pairs={{0,4},{1,5},{2,6},{3,7},{4,0},{5,1},{6,2},{7,3},{8,12},{9,13},{10,... | collective-permute-start | bytes 2752520 | tf_op jit(solution)/shard_map/ppermute | solution.py:219
  9.6 27.1 %copy-start.7 = (f32[3584]{0:T(1024)S(1)}, f32[3584]{0:T(1024)}, u32[]{:S(2)}) copy-start(f32[3584]{0:T(1024)} %param.14) | copy-start | bytes 43012
  11.7 31.3 %collective-permute-start.18 = (bf16[448,896]{1,0:T(8,128)(2,1)}, bf16[448,896]{1,0:T(8,128)(2,1)}, u32[]{:S(2)}, u32[]{:S(2)}) collective-permute-start(bf16[448,896]{1,0:T(8,128)(2,1)} %dynamic-slice_bitcast_fusion), channel_id=1, source_target_pairs={{1,4},{3,6},{4,1},{6,3},{9,12},{11,14},{12,9},{14,11},{17,20},{19,... | collective-permute-start | bytes 2408456 | tf_op jit(solution)/shard_map/ppermute | solution.py:219
  13.5 68.9 %collective-permute-start.9 = (bf16[448,1152]{1,0:T(8,128)(2,1)S(1)}, bf16[448,1152]{1,0:T(8,128)(2,1)}, u32[]{:S(2)}, u32[]{:S(2)}) collective-permute-start(bf16[448,1152]{1,0:T(8,128)(2,1)S(1)} %broadcast_select_fusion.1), channel_id=1, source_target_pairs={{0,8},{1,9},{2,10},{3,11},{4,12},{5,13},{6,14},{7,15},{8,16},{9,17... | collective-permute-start | bytes 3096584 | tf_op jit(solution)/shard_map/ppermute | solution.py:219
  17.9 65.2 %collective-permute-start.11 = (bf16[448,1152]{1,0:T(8,128)(2,1)S(1)}, bf16[448,1152]{1,0:T(8,128)(2,1)}, u32[]{:S(2)}, u32[]{:S(2)}) collective-permute-start(bf16[448,1152]{1,0:T(8,128)(2,1)S(1)} %broadcast_select_fusion.1), channel_id=1, source_target_pairs={{8,0},{9,1},{10,2},{11,3},{12,4},{13,5},{14,6},{15,7},{16,8},{17,9... | collective-permute-start | bytes 3096584 | tf_op jit(solution)/shard_map/ppermute | solution.py:219
  27.5 59.3 %collective-permute-start.8 = (bf16[448,1152]{1,0:T(8,128)(2,1)S(1)}, bf16[448,1152]{1,0:T(8,128)(2,1)}, u32[]{:S(2)}, u32[]{:S(2)}) collective-permute-start(bf16[448,1152]{1,0:T(8,128)(2,1)S(1)} %broadcast_select_fusion.1), channel_id=1, source_target_pairs={{0,1},{1,0},{2,3},{3,2},{4,5},{5,4},{6,7},{7,6},{8,9},{9,8},{10,11... | collective-permute-start | bytes 3096584 | tf_op jit(solution)/shard_map/ppermute | solution.py:219
  40.3 18.3 %collective-permute-start.2 = (bf16[64,3584]{1,0:T(8,128)(2,1)S(1)}, bf16[64,3584]{1,0:T(8,128)(2,1)S(1)}, u32[]{:S(2)}, u32[]{:S(2)}) collective-permute-start(bf16[64,3584]{1,0:T(8,128)(2,1)S(1)} %slice.100), channel_id=1, source_target_pairs={{0,4},{1,5},{2,6},{3,7},{4,0},{5,1},{6,2},{7,3},{8,12},{9,13},{10,... | collective-permute-start | bytes 1376264 | tf_op jit(solution)/shard_map/ppermute | solution.py:219
  43.0 16.4 %collective-permute-start.3 = (bf16[64,3584]{1,0:T(8,128)(2,1)S(1)}, bf16[64,3584]{1,0:T(8,128)(2,1)}, u32[]{:S(2)}, u32[]{:S(2)}) collective-permute-start(bf16[64,3584]{1,0:T(8,128)(2,1)S(1)} %slice.101), channel_id=1, source_target_pairs={{0,2},{1,3},{2,0},{3,1},{4,6},{5,7},{6,4},{7,5},{8,10},{9,11},{10,... | collective-permute-start | bytes 1376264 | tf_op jit(solution)/shard_map/ppermute | solution.py:219
  58.7 13.0 %collective-permute-start.4 = (s32[1]{0:T(128)}, s32[1]{0:T(128)}, u32[]{:S(2)}, u32[]{:S(2)}) collective-permute-start(s32[1]{0:T(128)} %param.11), channel_id=1, source_target_pairs={{0,4},{1,5},{2,6},{3,7},{4,0},{5,1},{6,2},{7,3},{8,12},{9,13},{10,... | collective-permute-start | bytes 20 | tf_op jit(solution)/shard_map/ppermute | solution.py:219
  59.4 16.5 %collective-permute-start.5 = (s32[1]{0:T(128)}, s32[1]{0:T(128)}, u32[]{:S(2)}, u32[]{:S(2)}) collective-permute-start(s32[1]{0:T(128)} %param.11), channel_id=1, source_target_pairs={{0,2},{1,3},{2,0},{3,1},{4,6},{5,7},{6,4},{7,5},{8,10},{9,11},{10,... | collective-permute-start | bytes 20 | tf_op jit(solution)/shard_map/ppermute | solution.py:219
  71.6 5.9 %collective-permute-start.6 = (s32[1]{0:T(128)}, s32[1]{0:T(128)}, u32[]{:S(2)}, u32[]{:S(2)}) collective-permute-start(s32[1]{0:T(128)} %param.11), channel_id=1, source_target_pairs={{0,6},{1,7},{2,4},{3,5},{4,2},{5,3},{6,0},{7,1},{8,14},{9,15},{10,... | collective-permute-start | bytes 20 | tf_op jit(solution)/shard_map/ppermute | solution.py:219
  75.9 93.3 %collective-permute-start.19 = (bf16[448,896]{1,0:T(8,128)(2,1)S(1)}, bf16[448,896]{1,0:T(8,128)(2,1)}, u32[]{:S(2)}, u32[]{:S(2)}) collective-permute-start(bf16[448,896]{1,0:T(8,128)(2,1)S(1)} %broadcast_select_fusion.3), channel_id=1, source_target_pairs={{0,1},{1,0},{2,3},{3,2},{4,5},{5,4},{6,7},{7,6},{8,9},{9,8},{10,11... | collective-permute-start | bytes 2408456 | tf_op jit(solution)/shard_map/ppermute | solution.py:219
  77.6 84.6 %collective-permute-start.20 = (bf16[448,896]{1,0:T(8,128)(2,1)S(1)}, bf16[448,896]{1,0:T(8,128)(2,1)S(1)}, u32[]{:S(2)}, u32[]{:S(2)}) collective-permute-start(bf16[448,896]{1,0:T(8,128)(2,1)S(1)} %broadcast_select_fusion.3), channel_id=1, source_target_pairs={{0,8},{1,9},{2,10},{3,11},{4,12},{5,13},{6,14},{7,15},{8,16},{9,17... | collective-permute-start | bytes 2408456 | tf_op jit(solution)/shard_map/ppermute | solution.py:219
  82.4 7.6 %collective-permute-start.13 = (bf16[448,1152]{1,0:T(8,128)(2,1)}, bf16[448,1152]{1,0:T(8,128)(2,1)S(1)}, u32[]{:S(2)}, u32[]{:S(2)}) collective-permute-start(bf16[448,1152]{1,0:T(8,128)(2,1)} %collective-permute-done.9), channel_id=1, source_target_pairs={{8,16},{9,17},{10,18},{11,19},{12,20},{13,21},{14,22},{15,23},{16,... | collective-permute-start | bytes 3096584 | tf_op jit(solution)/shard_map/ppermute | solution.py:219
  83.1 27.9 %collective-permute-start.14 = (bf16[448,1152]{1,0:T(8,128)(2,1)}, bf16[448,1152]{1,0:T(8,128)(2,1)S(1)}, u32[]{:S(2)}, u32[]{:S(2)}) collective-permute-start(bf16[448,1152]{1,0:T(8,128)(2,1)} %collective-permute-done.11), channel_id=1, source_target_pairs={{8,0},{9,1},{10,2},{11,3},{12,4},{13,5},{14,6},{15,7},{16,8},{17,9... | collective-permute-start | bytes 3096584 | tf_op jit(solution)/shard_map/ppermute | solution.py:219
  84.4 4.7 %copy-start = (bf16[8,512,448]{2,1,0:T(8,128)(2,1)S(1)}, bf16[8,512,448]{2,1,0:T(8,128)(2,1)}, u32[]{:S(2)}) copy-start(bf16[8,512,448]{2,1,0:T(8,128)(2,1)} %normalise.1) | copy-start | bytes 11010052
  86.8 28.7 %collective-permute-start.10 = (bf16[448,1152]{1,0:T(8,128)(2,1)}, bf16[448,1152]{1,0:T(8,128)(2,1)S(1)}, u32[]{:S(2)}, u32[]{:S(2)}) collective-permute-start(bf16[448,1152]{1,0:T(8,128)(2,1)} %collective-permute-done.9), channel_id=1, source_target_pairs={{0,1},{1,0},{2,3},{3,2},{4,5},{5,4},{6,7},{7,6},{8,9},{9,8},{10,11... | collective-permute-start | bytes 3096584 | tf_op jit(solution)/shard_map/ppermute | solution.py:219
  111.2 32.1 %collective-permute-start.16 = (bf16[448,1152]{1,0:T(8,128)(2,1)S(1)}, bf16[448,1152]{1,0:T(8,128)(2,1)S(1)}, u32[]{:S(2)}, u32[]{:S(2)}) collective-permute-start(bf16[448,1152]{1,0:T(8,128)(2,1)S(1)} %broadcast_select_fusion), channel_id=1, source_target_pairs={{8,0},{9,1},{10,2},{11,3},{12,4},{13,5},{14,6},{15,7},{16,24},{17,... | collective-permute-start | bytes 3096584 | tf_op jit(solution)/shard_map/ppermute | solution.py:219
  114.6 29.6 %collective-permute-start.15 = (bf16[448,1152]{1,0:T(8,128)(2,1)S(1)}, bf16[448,1152]{1,0:T(8,128)(2,1)S(1)}, u32[]{:S(2)}, u32[]{:S(2)}) collective-permute-start(bf16[448,1152]{1,0:T(8,128)(2,1)S(1)} %broadcast_select_fusion), channel_id=1, source_target_pairs={{0,1},{1,0},{2,3},{3,2},{4,5},{5,4},{6,7},{7,6},{8,9},{9,8},{10,11... | collective-permute-start | bytes 3096584 | tf_op jit(solution)/shard_map/ppermute | solution.py:219
  115.5 30.8 %collective-permute-start.12 = (bf16[448,1152]{1,0:T(8,128)(2,1)}, bf16[448,1152]{1,0:T(8,128)(2,1)S(1)}, u32[]{:S(2)}, u32[]{:S(2)}) collective-permute-start(bf16[448,1152]{1,0:T(8,128)(2,1)} %collective-permute-done.11), channel_id=1, source_target_pairs={{0,1},{1,0},{2,3},{3,2},{4,5},{5,4},{6,7},{7,6},{8,9},{9,8},{10,11... | collective-permute-start | bytes 3096584 | tf_op jit(solution)/shard_map/ppermute | solution.py:219
  143.3 4.0 %collective-permute-start.17 = (bf16[448,1152]{1,0:T(8,128)(2,1)S(1)}, bf16[448,1152]{1,0:T(8,128)(2,1)S(1)}, u32[]{:S(2)}, u32[]{:S(2)}) collective-permute-start(bf16[448,1152]{1,0:T(8,128)(2,1)S(1)} %collective-permute-done.16), channel_id=1, source_target_pairs={{0,1},{1,0},{2,3},{3,2},{4,5},{5,4},{6,7},{7,6},{8,9},{9,8},{10,11... | collective-permute-start | bytes 3096584 | tf_op jit(solution)/shard_map/ppermute | solution.py:219
  144.2 22.3 %collective-permute-start.21 = (bf16[448,896]{1,0:T(8,128)(2,1)S(1)}, bf16[448,896]{1,0:T(8,128)(2,1)}, u32[]{:S(2)}, u32[]{:S(2)}) collective-permute-start(bf16[448,896]{1,0:T(8,128)(2,1)S(1)} %broadcast_select_fusion.3), channel_id=1, source_target_pairs={{8,0},{9,1},{10,2},{11,3},{12,4},{13,5},{14,6},{15,7},{16,8},{17,9... | collective-permute-start | bytes 2408456 | tf_op jit(solution)/shard_map/ppermute | solution.py:219
  166.5 5.9 %collective-permute-start.24 = (bf16[448,896]{1,0:T(8,128)(2,1)S(1)}, bf16[448,896]{1,0:T(8,128)(2,1)S(1)}, u32[]{:S(2)}, u32[]{:S(2)}) collective-permute-start(bf16[448,896]{1,0:T(8,128)(2,1)S(1)} %collective-permute-done.20), channel_id=1, source_target_pairs={{8,16},{9,17},{10,18},{11,19},{12,20},{13,21},{14,22},{15,23},{16,... | collective-permute-start | bytes 2408456 | tf_op jit(solution)/shard_map/ppermute | solution.py:219
  167.4 24.3 %collective-permute-start.25 = (bf16[448,896]{1,0:T(8,128)(2,1)}, bf16[448,896]{1,0:T(8,128)(2,1)S(1)}, u32[]{:S(2)}, u32[]{:S(2)}) collective-permute-start(bf16[448,896]{1,0:T(8,128)(2,1)} %collective-permute-done.21), channel_id=1, source_target_pairs={{8,0},{9,1},{10,2},{11,3},{12,4},{13,5},{14,6},{15,7},{16,8},{17,9... | collective-permute-start | bytes 2408456 | tf_op jit(solution)/shard_map/ppermute | solution.py:219
  168.7 24.5 %collective-permute-start.22 = (bf16[448,896]{1,0:T(8,128)(2,1)S(1)}, bf16[448,896]{1,0:T(8,128)(2,1)S(1)}, u32[]{:S(2)}, u32[]{:S(2)}) collective-permute-start(bf16[448,896]{1,0:T(8,128)(2,1)S(1)} %collective-permute-done.20), channel_id=1, source_target_pairs={{0,1},{1,0},{2,3},{3,2},{4,5},{5,4},{6,7},{7,6},{8,9},{9,8},{10,11... | collective-permute-start | bytes 2408456 | tf_op jit(solution)/shard_map/ppermute | solution.py:219
  168.8 25.7 %collective-permute-start.23 = (bf16[448,896]{1,0:T(8,128)(2,1)}, bf16[448,896]{1,0:T(8,128)(2,1)S(1)}, u32[]{:S(2)}, u32[]{:S(2)}) collective-permute-start(bf16[448,896]{1,0:T(8,128)(2,1)} %collective-permute-done.21), channel_id=1, source_target_pairs={{0,1},{1,0},{2,3},{3,2},{4,5},{5,4},{6,7},{7,6},{8,9},{9,8},{10,11... | collective-permute-start | bytes 2408456 | tf_op jit(solution)/shard_map/ppermute | solution.py:219
  172.3 20.9 %copy-start.11 = (bf16[512,896]{1,0:T(8,128)(2,1)S(1)}, bf16[512,896]{1,0:T(8,128)(2,1)}, u32[]{:S(2)}) copy-start(bf16[512,896]{1,0:T(8,128)(2,1)} %attention.1) | copy-start | bytes 2752516
  191.8 20.6 %collective-permute-start.27 = (bf16[448,896]{1,0:T(8,128)(2,1)S(1)}, bf16[448,896]{1,0:T(8,128)(2,1)S(1)}, u32[]{:S(2)}, u32[]{:S(2)}) collective-permute-start(bf16[448,896]{1,0:T(8,128)(2,1)S(1)} %broadcast_select_fusion.2), channel_id=1, source_target_pairs={{8,0},{9,1},{10,2},{11,3},{12,4},{13,5},{14,6},{15,7},{16,24},{17,... | collective-permute-start | bytes 2408456 | tf_op jit(solution)/shard_map/ppermute | solution.py:219
  193.1 21.5 %collective-permute-start.26 = (bf16[448,896]{1,0:T(8,128)(2,1)S(1)}, bf16[448,896]{1,0:T(8,128)(2,1)S(1)}, u32[]{:S(2)}, u32[]{:S(2)}) collective-permute-start(bf16[448,896]{1,0:T(8,128)(2,1)S(1)} %broadcast_select_fusion.2), channel_id=1, source_target_pairs={{0,1},{1,0},{2,3},{3,2},{4,5},{5,4},{6,7},{7,6},{8,9},{9,8},{10,11... | collective-permute-start | bytes 2408456 | tf_op jit(solution)/shard_map/ppermute | solution.py:219
  197.3 23.5 %collective-permute-start.35 = (bf16[3,128,896]{2,1,0:T(8,128)(2,1)S(1)}, bf16[3,128,896]{2,1,0:T(8,128)(2,1)S(1)}, u32[]{:S(2)}, u32[]{:S(2)}) collective-permute-start(bf16[3,128,896]{2,1,0:T(8,128)(2,1)S(1)} %pad_maximum_fusion.4), channel_id=1, source_target_pairs={{0,6},{1,7},{2,4},{3,5},{4,2},{5,3},{6,0},{7,1},{8,14},{9,15},{10,... | collective-permute-start | bytes 2064392 | tf_op jit(solution)/shard_map/ppermute | solution.py:219
  212.4 6.2 %collective-permute-start.28 = (bf16[448,896]{1,0:T(8,128)(2,1)S(1)}, bf16[448,896]{1,0:T(8,128)(2,1)S(1)}, u32[]{:S(2)}, u32[]{:S(2)}) collective-permute-start(bf16[448,896]{1,0:T(8,128)(2,1)S(1)} %collective-permute-done.27), channel_id=1, source_target_pairs={{0,1},{1,0},{2,3},{3,2},{4,5},{5,4},{6,7},{7,6},{8,9},{9,8},{10,11... | collective-permute-start | bytes 2408456 | tf_op jit(solution)/shard_map/ppermute | solution.py:219
  212.5 18.4 %collective-permute-start.32 = (bf16[3,128,896]{2,1,0:T(8,128)(2,1)S(1)}, bf16[3,128,896]{2,1,0:T(8,128)(2,1)S(1)}, u32[]{:S(2)}, u32[]{:S(2)}) collective-permute-start(bf16[3,128,896]{2,1,0:T(8,128)(2,1)S(1)} %pad_maximum_fusion.3), channel_id=1, source_target_pairs={{0,2},{1,3},{2,0},{3,1},{4,6},{5,7},{6,4},{7,5},{8,10},{9,11},{10,... | collective-permute-start | bytes 2064392 | tf_op jit(solution)/shard_map/ppermute | solution.py:219
  214.5 18.4 %collective-permute-start.29 = (bf16[3,128,896]{2,1,0:T(8,128)(2,1)S(1)}, bf16[3,128,896]{2,1,0:T(8,128)(2,1)S(1)}, u32[]{:S(2)}, u32[]{:S(2)}) collective-permute-start(bf16[3,128,896]{2,1,0:T(8,128)(2,1)S(1)} %pad_maximum_fusion.2), channel_id=1, source_target_pairs={{0,4},{1,5},{2,6},{3,7},{4,0},{5,1},{6,2},{7,3},{8,12},{9,13},{10,... | collective-permute-start | bytes 2064392 | tf_op jit(solution)/shard_map/ppermute | solution.py:219
  216.5 26.1 %collective-permute-start.30 = (bf16[1,128,896]{2,1,0:T(8,128)(2,1)S(1)}, bf16[1,128,896]{2,1,0:T(8,128)(2,1)S(1)}, u32[]{:S(2)}, u32[]{:S(2)}) collective-permute-start(bf16[1,128,896]{2,1,0:T(8,128)(2,1)S(1)} %get-tuple-element.31), channel_id=1, source_target_pairs={{0,4},{1,5},{2,6},{3,7},{4,0},{5,1},{6,2},{7,3},{8,12},{9,13},{10,... | collective-permute-start | bytes 688136 | tf_op jit(solution)/shard_map/ppermute | solution.py:219
  218.6 24.8 %copy-start.8 = (f32[3584]{0:T(1024)S(1)}, f32[3584]{0:T(1024)}, u32[]{:S(2)}) copy-start(f32[3584]{0:T(1024)} %param.18) | copy-start | bytes 43012
  218.6 25.4 %copy-start.9 = (f32[3584]{0:T(1024)S(1)}, f32[3584]{0:T(1024)}, u32[]{:S(2)}) copy-start(f32[3584]{0:T(1024)} %param.19) | copy-start | bytes 43012
  218.6 28.3 %collective-permute-start.33 = (bf16[1,128,896]{2,1,0:T(8,128)(2,1)S(1)}, bf16[1,128,896]{2,1,0:T(8,128)(2,1)}, u32[]{:S(2)}, u32[]{:S(2)}) collective-permute-start(bf16[1,128,896]{2,1,0:T(8,128)(2,1)S(1)} %get-tuple-element.30), channel_id=1, source_target_pairs={{0,2},{1,3},{2,0},{3,1},{4,6},{5,7},{6,4},{7,5},{8,10},{9,11},{10,... | collective-permute-start | bytes 688136 | tf_op jit(solution)/shard_map/ppermute | solution.py:219
  220.9 31.0 %copy-start.2 = (bf16[3,128,896]{2,1,0:T(8,128)(2,1)}, bf16[3,128,896]{2,1,0:T(8,128)(2,1)S(1)}, u32[]{:S(2)}) copy-start(bf16[3,128,896]{2,1,0:T(8,128)(2,1)S(1)} %collective-permute-done.35.refs_13_) | copy-start | bytes 2064388
  220.9 26.0 %collective-permute-start.36 = (bf16[1,128,896]{2,1,0:T(8,128)(2,1)S(1)}, bf16[1,128,896]{2,1,0:T(8,128)(2,1)}, u32[]{:S(2)}, u32[]{:S(2)}) collective-permute-start(bf16[1,128,896]{2,1,0:T(8,128)(2,1)S(1)} %get-tuple-element.29), channel_id=1, source_target_pairs={{0,6},{1,7},{2,4},{3,5},{4,2},{5,3},{6,0},{7,1},{8,14},{9,15},{10,... | collective-permute-start | bytes 688136 | tf_op jit(solution)/shard_map/ppermute | solution.py:219
  230.8 21.0 %copy-start.3 = (bf16[3,128,896]{2,1,0:T(8,128)(2,1)}, bf16[3,128,896]{2,1,0:T(8,128)(2,1)S(1)}, u32[]{:S(2)}) copy-start(bf16[3,128,896]{2,1,0:T(8,128)(2,1)S(1)} %collective-permute-done.32.refs_10_) | copy-start | bytes 2064388
  230.8 21.0 %collective-permute-start.31 = (bf16[1,128,896]{2,1,0:T(8,128)(2,1)}, bf16[1,128,896]{2,1,0:T(8,128)(2,1)}, u32[]{:S(2)}, u32[]{:S(2)}) collective-permute-start(bf16[1,128,896]{2,1,0:T(8,128)(2,1)} %get-tuple-element.27), channel_id=1, source_target_pairs={{0,4},{1,5},{2,6},{3,7},{4,0},{5,1},{6,2},{7,3},{8,12},{9,13},{10,... | collective-permute-start | bytes 688136 | tf_op jit(solution)/shard_map/ppermute | solution.py:219
  232.8 19.1 %copy-start.4 = (bf16[3,128,896]{2,1,0:T(8,128)(2,1)}, bf16[3,128,896]{2,1,0:T(8,128)(2,1)S(1)}, u32[]{:S(2)}) copy-start(bf16[3,128,896]{2,1,0:T(8,128)(2,1)S(1)} %collective-permute-done.29.refs_7_) | copy-start | bytes 2064388
  232.8 19.0 %collective-permute-start.34 = (bf16[1,128,896]{2,1,0:T(8,128)(2,1)}, bf16[1,128,896]{2,1,0:T(8,128)(2,1)}, u32[]{:S(2)}, u32[]{:S(2)}) collective-permute-start(bf16[1,128,896]{2,1,0:T(8,128)(2,1)} %get-tuple-element.26), channel_id=1, source_target_pairs={{0,2},{1,3},{2,0},{3,1},{4,6},{5,7},{6,4},{7,5},{8,10},{9,11},{10,... | collective-permute-start | bytes 688136 | tf_op jit(solution)/shard_map/ppermute | solution.py:219
  243.4 8.5 %collective-permute-start.37 = (bf16[1,128,896]{2,1,0:T(8,128)(2,1)S(1)}, bf16[1,128,896]{2,1,0:T(8,128)(2,1)}, u32[]{:S(2)}, u32[]{:S(2)}) collective-permute-start(bf16[1,128,896]{2,1,0:T(8,128)(2,1)S(1)} %get-tuple-element.25), channel_id=1, source_target_pairs={{0,6},{1,7},{2,4},{3,5},{4,2},{5,3},{6,0},{7,1},{8,14},{9,15},{10,... | collective-permute-start | bytes 688136 | tf_op jit(solution)/shard_map/ppermute | solution.py:219
  251.9 17.8 %copy-start.10 = (s32[32]{0:T(128)S(1)}, s32[32]{0:T(128)}, u32[]{:S(2)}) copy-start(s32[32]{0:T(128)} %param.12) | copy-start | bytes 388
  258.8 10.4 %all-to-all-start = ((f32[32,1,128]{2,1,0:T(1,128)}), f32[32,1,128]{2,1,0:T(1,128)S(1)}, u32[]{:S(2)}, u32[]{:S(2)}) async-start(f32[32,1,128]{2,1,0:T(1,128)} %iota.33), calls=%async_computation | async-start | bytes 32768 | tf_op jit(solution)/shard_map/all_to_all | solution.py:391
  (3 other events, 7.0 us)
where the time goes:
time: 273 us; the launch traced here: 272 us
  waiting for transfers between devices  136 us (50%)
  starting transfers between devices  56.2 us (21%)
  Pallas kernels  28.9 us (11%)
  matrix products  23.6 us (9%)
  local copies, waits for them, and re-layouts  14.8 us (5%)
  other arithmetic  7.97 us (3%)
  between operations  4.4 us (2%)
    ppermute x38, waiting for transfers between devices, send(): return lax.ppermute(array, AXES, route(move))  129 us
    ppermute x38, starting transfers between devices, send(): return lax.ppermute(array, AXES, route(move))  53 us
    dot_general x10, matrix products, whole(): jnp.dot(lax.dynamic_index_in_dim(normed, jnp.maximum(plane, 0) * 2 + core...  14.2 us
    pallas_call x1, Pallas kernels, attend(): pl.pallas_call(kernel, name='attention', out_shape=jax.ShapeDtypeStruct((...  12.6 us
    pallas_call x1, Pallas kernels, normalise(): pl.pallas_call(norm_kernel, name='normalise', out_shape=jax.ShapeDtypeStr...  10.7 us
    dot_general x5, matrix products, whole(): lax.dot_general(attn, weights, (((1,), (1,)), ((), ())), preferred_elemen...  9.37 us
    all_to_all x1, waiting for transfers between devices, whole(): gathered = lax.all_to_all(both, AXES, 0, 0, tiled=True)  7.17 us
    pallas_call x1, Pallas kernels, finish(): pl.pallas_call(kernel, name='finish', out_shape=(jax.ShapeDtypeStruct((ro...  5.59 us
  transfers between devices with their start and end apart: 39, of which 14 were waited for; matrix products, arithmetic and copies ran while one was open for 15% of the time, Pallas kernels for 9%

commit v1 on v0

--- a/solution.py
+++ b/solution.py
@@ -60,21 +60,22 @@
     col = lax.broadcasted_iota(jnp.int32, (rows, rows), 1)
     allowed = (col <= row) & (col < length)
     scale = 1.0 / jnp.sqrt(jnp.float32(HEAD_SIZE))
+    scores = []
     for index in range(query_heads):
-        scores = (
-            lax.dot_general(
-                rotate(head(index)),
-                key_rows,
-                (((1,), (1,)), ((), ())),
-                preferred_element_type=jnp.float32,
-            )
-            * scale
+        raw = lax.dot_general(
+            rotate(head(index)),
+            key_rows,
+            (((1,), (1,)), ((), ())),
+            preferred_element_type=jnp.float32,
         )
-        scores = jnp.where(allowed, scores, jnp.float32(-1e30))
-        expd = jnp.exp(scores - jnp.max(scores, axis=-1, keepdims=True))
+        scores.append(jnp.where(allowed, raw * scale, jnp.float32(-1e30)))
+    probs = []
+    for score in scores:
+        expd = jnp.exp(score - jnp.max(score, axis=-1, keepdims=True))
         inverse = 1.0 / jnp.sum(expd, axis=-1, keepdims=True)
-        probs = (expd * inverse).astype(jnp.bfloat16)
-        mixed = jnp.dot(probs, value_rows, preferred_element_type=jnp.float32)
+        probs.append((expd * inverse).astype(jnp.bfloat16))
+    for index, prob in enumerate(probs):
+        mixed = jnp.dot(prob, value_rows, preferred_element_type=jnp.float32)
         out_ref[:, pl.ds(index * HEAD_SIZE, HEAD_SIZE)] = mixed.astype(jnp.bfloat16)
 
 
@@ -111,7 +112,7 @@
 
 def norm_kernel(own_ref, by_y_ref, by_x_ref, far_a_ref, far_b_ref, gain_ref, out_ref):
     shards, _, shard_rows = out_ref.shape
-    step = 16
+    step = far_a_ref.shape[0]
     base = 0
     for source in (own_ref, by_y_ref, by_x_ref, far_a_ref, far_b_ref):
 

time: 273 us -> 269 us (0.985)
  Pallas kernels: 28.9 us -> 17.6 us
  waiting for transfers between devices: 136 us -> 143 us
    pallas_call x1, Pallas kernels: 12.6 us -> 5.72 us  [attend(): pl.pallas_call(kernel, name='attention', out_shape=jax.ShapeDtypeStruct((...]
    ppermute x38, waiting for transfers between devices: 129 us -> 136 us  [send(): return lax.ppermute(array, AXES, route(move))]
    pallas_call x1, Pallas kernels: 10.7 us -> 6.26 us  [normalise(): pl.pallas_call(norm_kernel, name='normalise', out_shape=jax.ShapeDtypeStr...]
  transfers between devices with their start and end apart: 39 -> 39, of which waited for: 14 -> 14; matrix products, arithmetic and copies ran while one was open for 15% -> 15% of each run, Pallas kernels for 9% -> 4%
where the time goes in v1:
time: 269 us; the launch traced here: 268 us
  waiting for transfers between devices  143 us (53%)
  starting transfers between devices  56.2 us (21%)
  matrix products  23.6 us (9%)
  Pallas kernels  17.6 us (7%)
  local copies, waits for them, and re-layouts  14.8 us (6%)
  other arithmetic  7.97 us (3%)
  between operations  4.41 us (2%)
    ppermute x38, waiting for transfers between devices, send(): return lax.ppermute(array, AXES, route(move))  136 us
    ppermute x38, starting transfers between devices, send(): return lax.ppermute(array, AXES, route(move))  53.1 us
    dot_general x10, matrix products, whole(): jnp.dot(lax.dynamic_index_in_dim(normed, jnp.maximum(plane, 0) * 2 + core...  14.2 us
    dot_general x5, matrix products, whole(): lax.dot_general(attn, weights, (((1,), (1,)), ((), ())), preferred_elemen...  9.37 us
    all_to_all x1, waiting for transfers between devices, whole(): gathered = lax.all_to_all(both, AXES, 0, 0, tiled=True)  7.17 us
    pallas_call x1, Pallas kernels, normalise(): pl.pallas_call(norm_kernel, name='normalise', out_shape=jax.ShapeDtypeStr...  6.26 us
    pallas_call x1, Pallas kernels, attend(): pl.pallas_call(kernel, name='attention', out_shape=jax.ShapeDtypeStruct((...  5.72 us
    pallas_call x1, Pallas kernels, finish(): pl.pallas_call(kernel, name='finish', out_shape=(jax.ShapeDtypeStruct((ro...  5.59 us
  transfers between devices with their start and end apart: 39, of which 14 were waited for; matrix products, arithmetic and copies ran while one was open for 15% of the time, Pallas kernels for 4%

profile of v1, /device:TPU:0, one launch (start us, length us, event | category | flops | bytes accessed | tf_op | source)
XLA Modules:
  0.0 267.6 jit_solution(7563199275949787779)
XLA Ops:
  0.7 1.3 constant_dynamic-slice_fusion.2
  3.1 1.7 collective-permute-start.7
  4.7 3.0 %collective-permute-start.1 = (bf16[128,3584]{1,0:T(8,128)(2,1)S(1)}, bf16[128,3584]{1,0:T(8,128)(2,1)}, u32[]{:S(2)}, u32[]{:S(2)}) collective-permute-start(bf16[128,3584]{1,0:T(8,128)(2,1)S(1)} %bitcast.109), channel_id=1, source_target_pairs={{0,2},{1,3},{2,0},{3,1},{4,6},{5,7},{6,4},{7,5},{8,10},{9,11},{10,... | collective-permute-start | bytes 2752520 | tf_op jit(solution)/shard_map/ppermute | solution.py:220
  7.7 1.9 collective-permute-start
  9.6 2.1 dynamic-slice_bitcast_fusion
  11.7 1.6 collective-permute-start.18
  13.5 4.5 %collective-permute-start.9 = (bf16[448,1152]{1,0:T(8,128)(2,1)S(1)}, bf16[448,1152]{1,0:T(8,128)(2,1)}, u32[]{:S(2)}, u32[]{:S(2)}) collective-permute-start(bf16[448,1152]{1,0:T(8,128)(2,1)S(1)} %broadcast_select_fusion.1), channel_id=1, source_target_pairs={{0,8},{1,9},{2,10},{3,11},{4,12},{5,13},{6,14},{7,15},{8,16},{9,17... | collective-permute-start | bytes 3096584 | tf_op jit(solution)/shard_map/ppermute | solution.py:220
  17.9 1.3 collective-permute-start.11
  19.5 8.0 %collective-permute-done.1.by_x_ref = bf16[128,3584]{1,0:T(8,128)(2,1)} collective-permute-done((bf16[128,3584]{1,0:T(8,128)(2,1)S(1)}, bf16[128,3584]{1,0:T(8,128)(2,1)}, u32[]{:S(2)}, u32[]{:S(2)}) %collective-permute-start.1) | collective-permute-done | bytes 917536 | tf_op jit(solution)/shard_map/ppermute | solution.py:220
  27.5 9.2 %collective-permute-start.8 = (bf16[448,1152]{1,0:T(8,128)(2,1)S(1)}, bf16[448,1152]{1,0:T(8,128)(2,1)}, u32[]{:S(2)}, u32[]{:S(2)}) collective-permute-start(bf16[448,1152]{1,0:T(8,128)(2,1)S(1)} %broadcast_select_fusion.1), channel_id=1, source_target_pairs={{0,1},{1,0},{2,3},{3,2},{4,5},{5,4},{6,7},{7,6},{8,9},{9,8},{10,11... | collective-permute-start | bytes 3096584 | tf_op jit(solution)/shard_map/ppermute | solution.py:220
  40.3 1.6 collective-permute-start.2
  43.0 2.5 collective-permute-start.3
  47.6 1.3 broadcast_select_fusion.3
  48.9 9.8 %collective-permute-done.2.far_a_ref = bf16[64,3584]{1,0:T(8,128)(2,1)S(1)} collective-permute-done((bf16[64,3584]{1,0:T(8,128)(2,1)S(1)}, bf16[64,3584]{1,0:T(8,128)(2,1)S(1)}, u32[]{:S(2)}, u32[]{:S(2)}) %collective-permute-start.2) | collective-permute-done | bytes 458784 | tf_op jit(solution)/shard_map/ppermute | solution.py:220
  59.4 1.5 collective-permute-start.5
  60.9 6.3 %normalise.1 = bf16[8,512,448]{2,1,0:T(8,128)(2,1)} custom-call(bf16[128,3584]{1,0:T(8,128)(2,1)} %bitcast.107, bf16[128,3584]{1,0:T(8,128)(2,1)} %collective-permute-done.by_y_ref, bf16[128,3584]{1,0:T(8,128)(2,1)} %collective-permute-done.1.by_x_ref, bf16[64,3584]{1,0:T(8,128)(2,1)} %copy-done.5, bf16[64,3584]{1,0:T(8,128)(2,1)} %collective-permute-done.3.far_b_ref, ...), custom_call_target="tpu_custom_call" | custom-call | flops 14680064 | bytes 7340032 | tf_op jit(solution)/shard_map/normalise/pallas_call | solution.py:135
  67.2 4.3 %collective-permute-start.6 = (s32[1]{0:T(128)}, s32[1]{0:T(128)}, u32[]{:S(2)}, u32[]{:S(2)}) collective-permute-start(s32[1]{0:T(128)} %param.11), channel_id=1, source_target_pairs={{0,6},{1,7},{2,4},{3,5},{4,2},{5,3},{6,0},{7,1},{8,14},{9,15},{10,... | collective-permute-start | bytes 20 | tf_op jit(solution)/shard_map/ppermute | solution.py:220
  71.5 1.6 collective-permute-done.6
  73.1 2.5 collective-permute-start.20
  75.5 2.4 add_bitcast_fusion.refs_0_
  78.7 1.3 collective-permute-start.14
  80.0 2.4 fusion.56
  82.4 2.2 fusion.58
  85.6 21.0 %collective-permute-done.14 = bf16[448,1152]{1,0:T(8,128)(2,1)S(1)} collective-permute-done((bf16[448,1152]{1,0:T(8,128)(2,1)}, bf16[448,1152]{1,0:T(8,128)(2,1)S(1)}, u32[]{:S(2)}, u32[]{:S(2)}) %collective-permute-start.14) | collective-permute-done | bytes 1032224 | tf_op jit(solution)/shard_map/ppermute | solution.py:220
  106.7 1.3 collective-permute-start.16
  108.0 2.1 fusion.53
  112.5 26.3 %collective-permute-done.16 = bf16[448,1152]{1,0:T(8,128)(2,1)S(1)} collective-permute-done((bf16[448,1152]{1,0:T(8,128)(2,1)S(1)}, bf16[448,1152]{1,0:T(8,128)(2,1)S(1)}, u32[]{:S(2)}, u32[]{:S(2)}) %collective-permute-start.16) | collective-permute-done | bytes 1032224 | tf_op jit(solution)/shard_map/ppermute | solution.py:220
  139.7 1.5 collective-permute-start.21
  143.0 2.3 convolution_add_fusion.refs_1_
  145.3 5.7 %attention.1 = bf16[512,896]{1,0:T(8,128)(2,1)} custom-call(s32[4]{0:T(128)} %add_bitcast_fusion.refs_0_, f32[512,1152]{1,0:T(8,128)} %convolution_add_fusion.refs_1_, f32[1,1152]{1,0:T(1,128)} %reshape.38.refs_2_, f32[128,128]{1,0:T(8,128)} %get-tuple-element.50.refs_3_, f32[128,128]{1,0:T(8,128)} %get-tuple-element.51.refs_4_), custom_call_target="tpu_custom_call" | custom-call | flops 1879048192 | bytes 3276800 | tf_op jit(solution)/shard_map/attention/pallas_call | solution.py:90
  151.0 11.0 %collective-permute-done.21 = bf16[448,896]{1,0:T(8,128)(2,1)} collective-permute-done((bf16[448,896]{1,0:T(8,128)(2,1)S(1)}, bf16[448,896]{1,0:T(8,128)(2,1)}, u32[]{:S(2)}, u32[]{:S(2)}) %collective-permute-start.21) | collective-permute-done | bytes 802848 | tf_op jit(solution)/shard_map/ppermute | solution.py:220
  162.7 1.3 collective-permute-start.25
  164.6 3.0 %fusion.44 = bf16[512,896]{1,0:T(8,128)(2,1)S(1)} fusion(bf16[512,896]{1,0:T(8,128)(2,1)} %attention.1, bf16[448,896]{1,0:T(8,128)(2,1)} %collective-permute-done.19, bf16[448,896]{1,0:T(8,128)(2,1)S(1)} %broadcast_select_fusion.3, pred[]{:T(512)S(6)} %eq.104), kind=kOutput, calls=%fused_computation.53 | convolution fusion | flops 829767680 | bytes 3440641 | tf_op jit(solution)/shard_map/dot_general | solution.py:361
  167.7 19.3 %collective-permute-done.25 = bf16[448,896]{1,0:T(8,128)(2,1)S(1)} collective-permute-done((bf16[448,896]{1,0:T(8,128)(2,1)}, bf16[448,896]{1,0:T(8,128)(2,1)S(1)}, u32[]{:S(2)}, u32[]{:S(2)}) %collective-permute-start.25) | collective-permute-done | bytes 802848 | tf_op jit(solution)/shard_map/ppermute | solution.py:220
  187.1 1.3 collective-permute-start.27
  188.5 1.3 fusion.43
  189.8 2.6 fusion.42
  192.8 14.9 %collective-permute-done.27 = bf16[448,896]{1,0:T(8,128)(2,1)S(1)} collective-permute-done((bf16[448,896]{1,0:T(8,128)(2,1)S(1)}, bf16[448,896]{1,0:T(8,128)(2,1)S(1)}, u32[]{:S(2)}, u32[]{:S(2)}) %collective-permute-start.27) | collective-permute-done | bytes 802848 | tf_op jit(solution)/shard_map/ppermute | solution.py:220
  207.8 1.9 collective-permute-start.32
  209.9 1.2 fusion.41
  211.9 2.0 collective-permute-start.30
  216.2 1.4 collective-permute-start.36
  217.6 8.6 %collective-permute-done.32.refs_10_ = bf16[3,128,896]{2,1,0:T(8,128)(2,1)S(1)} collective-permute-done((bf16[3,128,896]{2,1,0:T(8,128)(2,1)S(1)}, bf16[3,128,896]{2,1,0:T(8,128)(2,1)S(1)}, u32[]{:S(2)}, u32[]{:S(2)}) %collective-permute-start.32) | collective-permute-done | bytes 688160 | tf_op jit(solution)/shard_map/ppermute | solution.py:220
  229.1 8.9 %collective-permute-done.30.refs_8_ = bf16[1,128,896]{2,1,0:T(8,128)(2,1)S(1)} collective-permute-done((bf16[1,128,896]{2,1,0:T(8,128)(2,1)S(1)}, bf16[1,128,896]{2,1,0:T(8,128)(2,1)S(1)}, u32[]{:S(2)}, u32[]{:S(2)}) %collective-permute-start.30) | collective-permute-done | bytes 229408 | tf_op jit(solution)/shard_map/ppermute | solution.py:220
  242.2 5.0 %collective-permute-done.31.refs_9_ = bf16[1,128,896]{2,1,0:T(8,128)(2,1)} collective-permute-done((bf16[1,128,896]{2,1,0:T(8,128)(2,1)}, bf16[1,128,896]{2,1,0:T(8,128)(2,1)}, u32[]{:S(2)}, u32[]{:S(2)}) %collective-permute-start.31) | collective-permute-done | bytes 229408 | tf_op jit(solution)/shard_map/ppermute | solution.py:220
  247.2 5.6 %finish.1 = (bf16[128,3584]{1,0:T(8,128)(2,1)}, f32[1,128]{1,0:T(1,128)}) custom-call(s32[5]{0:T(128)} %stack.106.refs_0_, bf16[128,3584]{1,0:T(8,128)(2,1)} %bitcast.108, f32[1,3584]{1,0:T(1,128)} %reshape.35.refs_2_, f32[1,3584]{1,0:T(1,128)} %reshape.36.refs_3_, bf16[3,128,896]{2,1,0:T(8,128)(2,1)} %pad_maximum_fusion.1.refs_4_, ...), custom_call_target="tpu_custom_call" | custom-call | flops 3670016 | bytes 2752512 | tf_op jit(solution)/shard_map/finish/pallas_call | solution.py:184
  254.1 3.2 %all-to-all-start = ((f32[32,1,128]{2,1,0:T(1,128)}), f32[32,1,128]{2,1,0:T(1,128)S(1)}, u32[]{:S(2)}, u32[]{:S(2)}) async-start(f32[32,1,128]{2,1,0:T(1,128)} %iota.33), calls=%async_computation | async-start | bytes 32768 | tf_op jit(solution)/shard_map/all_to_all | solution.py:392
  257.3 7.2 %all-to-all-done = f32[32,1,128]{2,1,0:T(1,128)S(1)} async-done(((f32[32,1,128]{2,1,0:T(1,128)}), f32[32,1,128]{2,1,0:T(1,128)S(1)}, u32[]{:S(2)}, u32[]{:S(2)}) %all-to-all-start) | async-done | bytes 16416 | tf_op jit(solution)/shard_map/all_to_all | solution.py:392
  (108 shorter events, 29.5 us)
Async XLA Ops:
  3.1 10.2 %collective-permute-start.7 = (bf16[448,1152]{1,0:T(8,128)(2,1)S(1)}, bf16[448,1152]{1,0:T(8,128)(2,1)}, u32[]{:S(2)}, u32[]{:S(2)}) collective-permute-start(bf16[448,1152]{1,0:T(8,128)(2,1)S(1)} %pad_maximum_fusion), channel_id=1, source_target_pairs={{1,4},{3,6},{4,1},{6,3},{9,12},{11,14},{12,9},{14,11},{17,20},{19,... | collective-permute-start | bytes 3096584 | tf_op jit(solution)/shard_map/ppermute | solution.py:220
  4.7 22.8 %collective-permute-start.1 = (bf16[128,3584]{1,0:T(8,128)(2,1)S(1)}, bf16[128,3584]{1,0:T(8,128)(2,1)}, u32[]{:S(2)}, u32[]{:S(2)}) collective-permute-start(bf16[128,3584]{1,0:T(8,128)(2,1)S(1)} %bitcast.109), channel_id=1, source_target_pairs={{0,2},{1,3},{2,0},{3,1},{4,6},{5,7},{6,4},{7,5},{8,10},{9,11},{10,... | collective-permute-start | bytes 2752520 | tf_op jit(solution)/shard_map/ppermute | solution.py:220
  7.7 32.6 %collective-permute-start = (bf16[128,3584]{1,0:T(8,128)(2,1)S(1)}, bf16[128,3584]{1,0:T(8,128)(2,1)}, u32[]{:S(2)}, u32[]{:S(2)}) collective-permute-start(bf16[128,3584]{1,0:T(8,128)(2,1)S(1)} %bitcast.110), channel_id=1, source_target_pairs={{0,4},{1,5},{2,6},{3,7},{4,0},{5,1},{6,2},{7,3},{8,12},{9,13},{10,... | collective-permute-start | bytes 2752520 | tf_op jit(solution)/shard_map/ppermute | solution.py:220
  9.6 27.1 %copy-start.7 = (f32[3584]{0:T(1024)S(1)}, f32[3584]{0:T(1024)}, u32[]{:S(2)}) copy-start(f32[3584]{0:T(1024)} %param.14) | copy-start | bytes 43012
  11.7 31.3 %collective-permute-start.18 = (bf16[448,896]{1,0:T(8,128)(2,1)}, bf16[448,896]{1,0:T(8,128)(2,1)}, u32[]{:S(2)}, u32[]{:S(2)}) collective-permute-start(bf16[448,896]{1,0:T(8,128)(2,1)} %dynamic-slice_bitcast_fusion), channel_id=1, source_target_pairs={{1,4},{3,6},{4,1},{6,3},{9,12},{11,14},{12,9},{14,11},{17,20},{19,... | collective-permute-start | bytes 2408456 | tf_op jit(solution)/shard_map/ppermute | solution.py:220
  13.5 64.4 %collective-permute-start.9 = (bf16[448,1152]{1,0:T(8,128)(2,1)S(1)}, bf16[448,1152]{1,0:T(8,128)(2,1)}, u32[]{:S(2)}, u32[]{:S(2)}) collective-permute-start(bf16[448,1152]{1,0:T(8,128)(2,1)S(1)} %broadcast_select_fusion.1), channel_id=1, source_target_pairs={{0,8},{1,9},{2,10},{3,11},{4,12},{5,13},{6,14},{7,15},{8,16},{9,17... | collective-permute-start | bytes 3096584 | tf_op jit(solution)/shard_map/ppermute | solution.py:220
  17.9 60.7 %collective-permute-start.11 = (bf16[448,1152]{1,0:T(8,128)(2,1)S(1)}, bf16[448,1152]{1,0:T(8,128)(2,1)}, u32[]{:S(2)}, u32[]{:S(2)}) collective-permute-start(bf16[448,1152]{1,0:T(8,128)(2,1)S(1)} %broadcast_select_fusion.1), channel_id=1, source_target_pairs={{8,0},{9,1},{10,2},{11,3},{12,4},{13,5},{14,6},{15,7},{16,8},{17,9... | collective-permute-start | bytes 3096584 | tf_op jit(solution)/shard_map/ppermute | solution.py:220
  27.5 54.9 %collective-permute-start.8 = (bf16[448,1152]{1,0:T(8,128)(2,1)S(1)}, bf16[448,1152]{1,0:T(8,128)(2,1)}, u32[]{:S(2)}, u32[]{:S(2)}) collective-permute-start(bf16[448,1152]{1,0:T(8,128)(2,1)S(1)} %broadcast_select_fusion.1), channel_id=1, source_target_pairs={{0,1},{1,0},{2,3},{3,2},{4,5},{5,4},{6,7},{7,6},{8,9},{9,8},{10,11... | collective-permute-start | bytes 3096584 | tf_op jit(solution)/shard_map/ppermute | solution.py:220
  40.3 18.3 %collective-permute-start.2 = (bf16[64,3584]{1,0:T(8,128)(2,1)S(1)}, bf16[64,3584]{1,0:T(8,128)(2,1)S(1)}, u32[]{:S(2)}, u32[]{:S(2)}) collective-permute-start(bf16[64,3584]{1,0:T(8,128)(2,1)S(1)} %slice.100), channel_id=1, source_target_pairs={{0,4},{1,5},{2,6},{3,7},{4,0},{5,1},{6,2},{7,3},{8,12},{9,13},{10,... | collective-permute-start | bytes 1376264 | tf_op jit(solution)/shard_map/ppermute | solution.py:220
  43.0 16.4 %collective-permute-start.3 = (bf16[64,3584]{1,0:T(8,128)(2,1)S(1)}, bf16[64,3584]{1,0:T(8,128)(2,1)}, u32[]{:S(2)}, u32[]{:S(2)}) collective-permute-start(bf16[64,3584]{1,0:T(8,128)(2,1)S(1)} %slice.101), channel_id=1, source_target_pairs={{0,2},{1,3},{2,0},{3,1},{4,6},{5,7},{6,4},{7,5},{8,10},{9,11},{10,... | collective-permute-start | bytes 1376264 | tf_op jit(solution)/shard_map/ppermute | solution.py:220
  58.7 8.5 %collective-permute-start.4 = (s32[1]{0:T(128)}, s32[1]{0:T(128)}, u32[]{:S(2)}, u32[]{:S(2)}) collective-permute-start(s32[1]{0:T(128)} %param.11), channel_id=1, source_target_pairs={{0,4},{1,5},{2,6},{3,7},{4,0},{5,1},{6,2},{7,3},{8,12},{9,13},{10,... | collective-permute-start | bytes 20 | tf_op jit(solution)/shard_map/ppermute | solution.py:220
  59.4 12.1 %collective-permute-start.5 = (s32[1]{0:T(128)}, s32[1]{0:T(128)}, u32[]{:S(2)}, u32[]{:S(2)}) collective-permute-start(s32[1]{0:T(128)} %param.11), channel_id=1, source_target_pairs={{0,2},{1,3},{2,0},{3,1},{4,6},{5,7},{6,4},{7,5},{8,10},{9,11},{10,... | collective-permute-start | bytes 20 | tf_op jit(solution)/shard_map/ppermute | solution.py:220
  67.2 5.9 %collective-permute-start.6 = (s32[1]{0:T(128)}, s32[1]{0:T(128)}, u32[]{:S(2)}, u32[]{:S(2)}) collective-permute-start(s32[1]{0:T(128)} %param.11), channel_id=1, source_target_pairs={{0,6},{1,7},{2,4},{3,5},{4,2},{5,3},{6,0},{7,1},{8,14},{9,15},{10,... | collective-permute-start | bytes 20 | tf_op jit(solution)/shard_map/ppermute | solution.py:220
  71.5 93.1 %collective-permute-start.19 = (bf16[448,896]{1,0:T(8,128)(2,1)S(1)}, bf16[448,896]{1,0:T(8,128)(2,1)}, u32[]{:S(2)}, u32[]{:S(2)}) collective-permute-start(bf16[448,896]{1,0:T(8,128)(2,1)S(1)} %broadcast_select_fusion.3), channel_id=1, source_target_pairs={{0,1},{1,0},{2,3},{3,2},{4,5},{5,4},{6,7},{7,6},{8,9},{9,8},{10,11... | collective-permute-start | bytes 2408456 | tf_op jit(solution)/shard_map/ppermute | solution.py:220
  73.1 77.9 %collective-permute-start.20 = (bf16[448,896]{1,0:T(8,128)(2,1)S(1)}, bf16[448,896]{1,0:T(8,128)(2,1)S(1)}, u32[]{:S(2)}, u32[]{:S(2)}) collective-permute-start(bf16[448,896]{1,0:T(8,128)(2,1)S(1)} %broadcast_select_fusion.3), channel_id=1, source_target_pairs={{0,8},{1,9},{2,10},{3,11},{4,12},{5,13},{6,14},{7,15},{8,16},{9,17... | collective-permute-start | bytes 2408456 | tf_op jit(solution)/shard_map/ppermute | solution.py:220
  77.9 7.6 %collective-permute-start.13 = (bf16[448,1152]{1,0:T(8,128)(2,1)}, bf16[448,1152]{1,0:T(8,128)(2,1)S(1)}, u32[]{:S(2)}, u32[]{:S(2)}) collective-permute-start(bf16[448,1152]{1,0:T(8,128)(2,1)} %collective-permute-done.9), channel_id=1, source_target_pairs={{8,16},{9,17},{10,18},{11,19},{12,20},{13,21},{14,22},{15,23},{16,... | collective-permute-start | bytes 3096584 | tf_op jit(solution)/shard_map/ppermute | solution.py:220
  78.7 27.9 %collective-permute-start.14 = (bf16[448,1152]{1,0:T(8,128)(2,1)}, bf16[448,1152]{1,0:T(8,128)(2,1)S(1)}, u32[]{:S(2)}, u32[]{:S(2)}) collective-permute-start(bf16[448,1152]{1,0:T(8,128)(2,1)} %collective-permute-done.11), channel_id=1, source_target_pairs={{8,0},{9,1},{10,2},{11,3},{12,4},{13,5},{14,6},{15,7},{16,8},{17,9... | collective-permute-start | bytes 3096584 | tf_op jit(solution)/shard_map/ppermute | solution.py:220
  80.0 4.7 %copy-start = (bf16[8,512,448]{2,1,0:T(8,128)(2,1)S(1)}, bf16[8,512,448]{2,1,0:T(8,128)(2,1)}, u32[]{:S(2)}) copy-start(bf16[8,512,448]{2,1,0:T(8,128)(2,1)} %normalise.1) | copy-start | bytes 11010052
  82.4 28.7 %collective-permute-start.10 = (bf16[448,1152]{1,0:T(8,128)(2,1)}, bf16[448,1152]{1,0:T(8,128)(2,1)S(1)}, u32[]{:S(2)}, u32[]{:S(2)}) collective-permute-start(bf16[448,1152]{1,0:T(8,128)(2,1)} %collective-permute-done.9), channel_id=1, source_target_pairs={{0,1},{1,0},{2,3},{3,2},{4,5},{5,4},{6,7},{7,6},{8,9},{9,8},{10,11... | collective-permute-start | bytes 3096584 | tf_op jit(solution)/shard_map/ppermute | solution.py:220
  106.7 32.1 %collective-permute-start.16 = (bf16[448,1152]{1,0:T(8,128)(2,1)S(1)}, bf16[448,1152]{1,0:T(8,128)(2,1)S(1)}, u32[]{:S(2)}, u32[]{:S(2)}) collective-permute-start(bf16[448,1152]{1,0:T(8,128)(2,1)S(1)} %broadcast_select_fusion), channel_id=1, source_target_pairs={{8,0},{9,1},{10,2},{11,3},{12,4},{13,5},{14,6},{15,7},{16,24},{17,... | collective-permute-start | bytes 3096584 | tf_op jit(solution)/shard_map/ppermute | solution.py:220
  110.1 29.6 %collective-permute-start.15 = (bf16[448,1152]{1,0:T(8,128)(2,1)S(1)}, bf16[448,1152]{1,0:T(8,128)(2,1)S(1)}, u32[]{:S(2)}, u32[]{:S(2)}) collective-permute-start(bf16[448,1152]{1,0:T(8,128)(2,1)S(1)} %broadcast_select_fusion), channel_id=1, source_target_pairs={{0,1},{1,0},{2,3},{3,2},{4,5},{5,4},{6,7},{7,6},{8,9},{9,8},{10,11... | collective-permute-start | bytes 3096584 | tf_op jit(solution)/shard_map/ppermute | solution.py:220
  111.0 31.0 %collective-permute-start.12 = (bf16[448,1152]{1,0:T(8,128)(2,1)}, bf16[448,1152]{1,0:T(8,128)(2,1)S(1)}, u32[]{:S(2)}, u32[]{:S(2)}) collective-permute-start(bf16[448,1152]{1,0:T(8,128)(2,1)} %collective-permute-done.11), channel_id=1, source_target_pairs={{0,1},{1,0},{2,3},{3,2},{4,5},{5,4},{6,7},{7,6},{8,9},{9,8},{10,11... | collective-permute-start | bytes 3096584 | tf_op jit(solution)/shard_map/ppermute | solution.py:220
  138.8 4.2 %collective-permute-start.17 = (bf16[448,1152]{1,0:T(8,128)(2,1)S(1)}, bf16[448,1152]{1,0:T(8,128)(2,1)S(1)}, u32[]{:S(2)}, u32[]{:S(2)}) collective-permute-start(bf16[448,1152]{1,0:T(8,128)(2,1)S(1)} %collective-permute-done.16), channel_id=1, source_target_pairs={{0,1},{1,0},{2,3},{3,2},{4,5},{5,4},{6,7},{7,6},{8,9},{9,8},{10,11... | collective-permute-start | bytes 3096584 | tf_op jit(solution)/shard_map/ppermute | solution.py:220
  139.7 22.3 %collective-permute-start.21 = (bf16[448,896]{1,0:T(8,128)(2,1)S(1)}, bf16[448,896]{1,0:T(8,128)(2,1)}, u32[]{:S(2)}, u32[]{:S(2)}) collective-permute-start(bf16[448,896]{1,0:T(8,128)(2,1)S(1)} %broadcast_select_fusion.3), channel_id=1, source_target_pairs={{8,0},{9,1},{10,2},{11,3},{12,4},{13,5},{14,6},{15,7},{16,8},{17,9... | collective-permute-start | bytes 2408456 | tf_op jit(solution)/shard_map/ppermute | solution.py:220
  162.0 5.7 %collective-permute-start.24 = (bf16[448,896]{1,0:T(8,128)(2,1)S(1)}, bf16[448,896]{1,0:T(8,128)(2,1)S(1)}, u32[]{:S(2)}, u32[]{:S(2)}) collective-permute-start(bf16[448,896]{1,0:T(8,128)(2,1)S(1)} %collective-permute-done.20), channel_id=1, source_target_pairs={{8,16},{9,17},{10,18},{11,19},{12,20},{13,21},{14,22},{15,23},{16,... | collective-permute-start | bytes 2408456 | tf_op jit(solution)/shard_map/ppermute | solution.py:220
  162.7 24.3 %collective-permute-start.25 = (bf16[448,896]{1,0:T(8,128)(2,1)}, bf16[448,896]{1,0:T(8,128)(2,1)S(1)}, u32[]{:S(2)}, u32[]{:S(2)}) collective-permute-start(bf16[448,896]{1,0:T(8,128)(2,1)} %collective-permute-done.21), channel_id=1, source_target_pairs={{8,0},{9,1},{10,2},{11,3},{12,4},{13,5},{14,6},{15,7},{16,8},{17,9... | collective-permute-start | bytes 2408456 | tf_op jit(solution)/shard_map/ppermute | solution.py:220
  164.0 24.5 %collective-permute-start.22 = (bf16[448,896]{1,0:T(8,128)(2,1)S(1)}, bf16[448,896]{1,0:T(8,128)(2,1)S(1)}, u32[]{:S(2)}, u32[]{:S(2)}) collective-permute-start(bf16[448,896]{1,0:T(8,128)(2,1)S(1)} %collective-permute-done.20), channel_id=1, source_target_pairs={{0,1},{1,0},{2,3},{3,2},{4,5},{5,4},{6,7},{7,6},{8,9},{9,8},{10,11... | collective-permute-start | bytes 2408456 | tf_op jit(solution)/shard_map/ppermute | solution.py:220
  164.1 25.7 %collective-permute-start.23 = (bf16[448,896]{1,0:T(8,128)(2,1)}, bf16[448,896]{1,0:T(8,128)(2,1)S(1)}, u32[]{:S(2)}, u32[]{:S(2)}) collective-permute-start(bf16[448,896]{1,0:T(8,128)(2,1)} %collective-permute-done.21), channel_id=1, source_target_pairs={{0,1},{1,0},{2,3},{3,2},{4,5},{5,4},{6,7},{7,6},{8,9},{9,8},{10,11... | collective-permute-start | bytes 2408456 | tf_op jit(solution)/shard_map/ppermute | solution.py:220
  167.6 20.9 %copy-start.11 = (bf16[512,896]{1,0:T(8,128)(2,1)S(1)}, bf16[512,896]{1,0:T(8,128)(2,1)}, u32[]{:S(2)}) copy-start(bf16[512,896]{1,0:T(8,128)(2,1)} %attention.1) | copy-start | bytes 2752516
  187.1 20.6 %collective-permute-start.27 = (bf16[448,896]{1,0:T(8,128)(2,1)S(1)}, bf16[448,896]{1,0:T(8,128)(2,1)S(1)}, u32[]{:S(2)}, u32[]{:S(2)}) collective-permute-start(bf16[448,896]{1,0:T(8,128)(2,1)S(1)} %broadcast_select_fusion.2), channel_id=1, source_target_pairs={{8,0},{9,1},{10,2},{11,3},{12,4},{13,5},{14,6},{15,7},{16,24},{17,... | collective-permute-start | bytes 2408456 | tf_op jit(solution)/shard_map/ppermute | solution.py:220
  188.4 21.5 %collective-permute-start.26 = (bf16[448,896]{1,0:T(8,128)(2,1)S(1)}, bf16[448,896]{1,0:T(8,128)(2,1)S(1)}, u32[]{:S(2)}, u32[]{:S(2)}) collective-permute-start(bf16[448,896]{1,0:T(8,128)(2,1)S(1)} %broadcast_select_fusion.2), channel_id=1, source_target_pairs={{0,1},{1,0},{2,3},{3,2},{4,5},{5,4},{6,7},{7,6},{8,9},{9,8},{10,11... | collective-permute-start | bytes 2408456 | tf_op jit(solution)/shard_map/ppermute | solution.py:220
  192.7 23.5 %collective-permute-start.35 = (bf16[3,128,896]{2,1,0:T(8,128)(2,1)S(1)}, bf16[3,128,896]{2,1,0:T(8,128)(2,1)S(1)}, u32[]{:S(2)}, u32[]{:S(2)}) collective-permute-start(bf16[3,128,896]{2,1,0:T(8,128)(2,1)S(1)} %pad_maximum_fusion.4), channel_id=1, source_target_pairs={{0,6},{1,7},{2,4},{3,5},{4,2},{5,3},{6,0},{7,1},{8,14},{9,15},{10,... | collective-permute-start | bytes 2064392 | tf_op jit(solution)/shard_map/ppermute | solution.py:220
  207.7 6.2 %collective-permute-start.28 = (bf16[448,896]{1,0:T(8,128)(2,1)S(1)}, bf16[448,896]{1,0:T(8,128)(2,1)S(1)}, u32[]{:S(2)}, u32[]{:S(2)}) collective-permute-start(bf16[448,896]{1,0:T(8,128)(2,1)S(1)} %collective-permute-done.27), channel_id=1, source_target_pairs={{0,1},{1,0},{2,3},{3,2},{4,5},{5,4},{6,7},{7,6},{8,9},{9,8},{10,11... | collective-permute-start | bytes 2408456 | tf_op jit(solution)/shard_map/ppermute | solution.py:220
  207.8 18.4 %collective-permute-start.32 = (bf16[3,128,896]{2,1,0:T(8,128)(2,1)S(1)}, bf16[3,128,896]{2,1,0:T(8,128)(2,1)S(1)}, u32[]{:S(2)}, u32[]{:S(2)}) collective-permute-start(bf16[3,128,896]{2,1,0:T(8,128)(2,1)S(1)} %pad_maximum_fusion.3), channel_id=1, source_target_pairs={{0,2},{1,3},{2,0},{3,1},{4,6},{5,7},{6,4},{7,5},{8,10},{9,11},{10,... | collective-permute-start | bytes 2064392 | tf_op jit(solution)/shard_map/ppermute | solution.py:220
  209.8 18.4 %collective-permute-start.29 = (bf16[3,128,896]{2,1,0:T(8,128)(2,1)S(1)}, bf16[3,128,896]{2,1,0:T(8,128)(2,1)S(1)}, u32[]{:S(2)}, u32[]{:S(2)}) collective-permute-start(bf16[3,128,896]{2,1,0:T(8,128)(2,1)S(1)} %pad_maximum_fusion.2), channel_id=1, source_target_pairs={{0,4},{1,5},{2,6},{3,7},{4,0},{5,1},{6,2},{7,3},{8,12},{9,13},{10,... | collective-permute-start | bytes 2064392 | tf_op jit(solution)/shard_map/ppermute | solution.py:220
  211.9 26.1 %collective-permute-start.30 = (bf16[1,128,896]{2,1,0:T(8,128)(2,1)S(1)}, bf16[1,128,896]{2,1,0:T(8,128)(2,1)S(1)}, u32[]{:S(2)}, u32[]{:S(2)}) collective-permute-start(bf16[1,128,896]{2,1,0:T(8,128)(2,1)S(1)} %get-tuple-element.31), channel_id=1, source_target_pairs={{0,4},{1,5},{2,6},{3,7},{4,0},{5,1},{6,2},{7,3},{8,12},{9,13},{10,... | collective-permute-start | bytes 688136 | tf_op jit(solution)/shard_map/ppermute | solution.py:220
  213.9 24.8 %copy-start.8 = (f32[3584]{0:T(1024)S(1)}, f32[3584]{0:T(1024)}, u32[]{:S(2)}) copy-start(f32[3584]{0:T(1024)} %param.18) | copy-start | bytes 43012
  213.9 25.4 %copy-start.9 = (f32[3584]{0:T(1024)S(1)}, f32[3584]{0:T(1024)}, u32[]{:S(2)}) copy-start(f32[3584]{0:T(1024)} %param.19) | copy-start | bytes 43012
  213.9 28.3 %collective-permute-start.33 = (bf16[1,128,896]{2,1,0:T(8,128)(2,1)S(1)}, bf16[1,128,896]{2,1,0:T(8,128)(2,1)}, u32[]{:S(2)}, u32[]{:S(2)}) collective-permute-start(bf16[1,128,896]{2,1,0:T(8,128)(2,1)S(1)} %get-tuple-element.30), channel_id=1, source_target_pairs={{0,2},{1,3},{2,0},{3,1},{4,6},{5,7},{6,4},{7,5},{8,10},{9,11},{10,... | collective-permute-start | bytes 688136 | tf_op jit(solution)/shard_map/ppermute | solution.py:220
  216.2 31.0 %copy-start.2 = (bf16[3,128,896]{2,1,0:T(8,128)(2,1)}, bf16[3,128,896]{2,1,0:T(8,128)(2,1)S(1)}, u32[]{:S(2)}) copy-start(bf16[3,128,896]{2,1,0:T(8,128)(2,1)S(1)} %collective-permute-done.35.refs_13_) | copy-start | bytes 2064388
  216.2 26.0 %collective-permute-start.36 = (bf16[1,128,896]{2,1,0:T(8,128)(2,1)S(1)}, bf16[1,128,896]{2,1,0:T(8,128)(2,1)}, u32[]{:S(2)}, u32[]{:S(2)}) collective-permute-start(bf16[1,128,896]{2,1,0:T(8,128)(2,1)S(1)} %get-tuple-element.29), channel_id=1, source_target_pairs={{0,6},{1,7},{2,4},{3,5},{4,2},{5,3},{6,0},{7,1},{8,14},{9,15},{10,... | collective-permute-start | bytes 688136 | tf_op jit(solution)/shard_map/ppermute | solution.py:220
  226.2 21.0 %copy-start.3 = (bf16[3,128,896]{2,1,0:T(8,128)(2,1)}, bf16[3,128,896]{2,1,0:T(8,128)(2,1)S(1)}, u32[]{:S(2)}) copy-start(bf16[3,128,896]{2,1,0:T(8,128)(2,1)S(1)} %collective-permute-done.32.refs_10_) | copy-start | bytes 2064388
  226.2 21.0 %collective-permute-start.31 = (bf16[1,128,896]{2,1,0:T(8,128)(2,1)}, bf16[1,128,896]{2,1,0:T(8,128)(2,1)}, u32[]{:S(2)}, u32[]{:S(2)}) collective-permute-start(bf16[1,128,896]{2,1,0:T(8,128)(2,1)} %get-tuple-element.27), channel_id=1, source_target_pairs={{0,4},{1,5},{2,6},{3,7},{4,0},{5,1},{6,2},{7,3},{8,12},{9,13},{10,... | collective-permute-start | bytes 688136 | tf_op jit(solution)/shard_map/ppermute | solution.py:220
  228.2 19.1 %copy-start.4 = (bf16[3,128,896]{2,1,0:T(8,128)(2,1)}, bf16[3,128,896]{2,1,0:T(8,128)(2,1)S(1)}, u32[]{:S(2)}) copy-start(bf16[3,128,896]{2,1,0:T(8,128)(2,1)S(1)} %collective-permute-done.29.refs_7_) | copy-start | bytes 2064388
  228.2 19.0 %collective-permute-start.34 = (bf16[1,128,896]{2,1,0:T(8,128)(2,1)}, bf16[1,128,896]{2,1,0:T(8,128)(2,1)}, u32[]{:S(2)}, u32[]{:S(2)}) collective-permute-start(bf16[1,128,896]{2,1,0:T(8,128)(2,1)} %get-tuple-element.26), channel_id=1, source_target_pairs={{0,2},{1,3},{2,0},{3,1},{4,6},{5,7},{6,4},{7,5},{8,10},{9,11},{10,... | collective-permute-start | bytes 688136 | tf_op jit(solution)/shard_map/ppermute | solution.py:220
  238.7 8.5 %collective-permute-start.37 = (bf16[1,128,896]{2,1,0:T(8,128)(2,1)S(1)}, bf16[1,128,896]{2,1,0:T(8,128)(2,1)}, u32[]{:S(2)}, u32[]{:S(2)}) collective-permute-start(bf16[1,128,896]{2,1,0:T(8,128)(2,1)S(1)} %get-tuple-element.25), channel_id=1, source_target_pairs={{0,6},{1,7},{2,4},{3,5},{4,2},{5,3},{6,0},{7,1},{8,14},{9,15},{10,... | collective-permute-start | bytes 688136 | tf_op jit(solution)/shard_map/ppermute | solution.py:220
  247.2 17.8 %copy-start.10 = (s32[32]{0:T(128)S(1)}, s32[32]{0:T(128)}, u32[]{:S(2)}) copy-start(s32[32]{0:T(128)} %param.12) | copy-start | bytes 388
  254.1 10.4 %all-to-all-start = ((f32[32,1,128]{2,1,0:T(1,128)}), f32[32,1,128]{2,1,0:T(1,128)S(1)}, u32[]{:S(2)}, u32[]{:S(2)}) async-start(f32[32,1,128]{2,1,0:T(1,128)} %iota.33), calls=%async_computation | async-start | bytes 32768 | tf_op jit(solution)/shard_map/all_to_all | solution.py:392
  (3 other events, 7.0 us)

commit v2 on v1

--- a/solution.py
+++ b/solution.py
@@ -142,58 +142,92 @@
     )(*parts, gain.reshape(1, width))
 
 
-def finish_kernel(groups, place_ref, tokens_ref, gain_ref, head_ref, *refs):
-    pieces, hidden_ref, score_ref = refs[:-2], refs[-2], refs[-1]
+def finish_kernel(
+    groups, width, place_ref, tokens_ref, gained_ref, *refs
+):
+    pieces, hidden_ref, score_ref, sums_ref = refs[:-3], refs[-3], refs[-2], refs[-1]
+    plane = pl.program_id(0)
     length = place_ref[0]
-    rows, width = tokens_ref.shape
-    planes = place_ref.shape[0] - 1
+    slot = place_ref[1 + plane]
+    rows = tokens_ref.shape[0]
+    total = tokens_ref[...].astype(jnp.float32)
+    for first in range(0, len(pieces), len(groups)):
+        value = None
+        for ref, base in zip(pieces[first : first + len(groups)], groups):
+            part = ref[0]
+            value = part if value is None else jnp.where(slot >= base, part, value)
+        total += value.astype(jnp.float32)
+    hidden = total.astype(jnp.bfloat16)
+    hidden_ref[...] = hidden
+    picked = lax.broadcasted_iota(jnp.int32, (rows, 1), 0) == length - 1
+    last = jnp.sum(jnp.where(picked, hidden.astype(jnp.float32), 0.0), axis=0, keepdims=True)
+    square = jnp.sum(last * last, axis=1, keepdims=True)
+    dotted = jnp.sum(last * gained_ref[...], axis=1, keepdims=True)
+
+    @pl.when(plane == 0)
+    def _():
+        sums_ref[...] = jnp.zeros_like(sums_ref)
+
+    sums_ref[0] += jnp.broadcast_to(square, sums_ref.shape[1:])
+    sums_ref[1] += jnp.broadcast_to(dotted, sums_ref.shape[1:])
+
+    @pl.when(plane == pl.num_programs(0) - 1)
+    def _():
+        score_ref[...] = sums_ref[1] * lax.rsqrt(sums_ref[0] / width + 1e-06)
+
+
+def finish(place, tokens, gain, head, pieces, counts):
+    rows, width = tokens.shape
+    planes = place.shape[0] - 1
     wide = width // planes
-    square = jnp.zeros((1, 1), jnp.float32)
-    dotted = jnp.zeros((1, 1), jnp.float32)
-    picked = lax.broadcasted_iota(jnp.int32, (rows, 1), 0) == length - 1
-    gained = gain_ref[...] * head_ref[...]
-    for plane in range(planes):
-        slot = place_ref[1 + plane]
-        cols = slice(plane * wide, (plane + 1) * wide)
-        total = tokens_ref[:, cols].astype(jnp.float32)
-        for first in range(0, len(pieces), groups):
-            value = None
-            base = 0
-            for ref in pieces[first : first + groups]:
-                count = ref.shape[0]
-                part = ref[jnp.clip(slot - base, 0, count - 1)]
-                value = part if value is None else jnp.where(slot >= base, part, value)
-                base += count
-            total += value.astype(jnp.float32)
-        hidden = total.astype(jnp.bfloat16)
-        hidden_ref[:, cols] = hidden
-        last = jnp.sum(jnp.where(picked, hidden.astype(jnp.float32), 0.0), axis=0, keepdims=True)
-        square += jnp.sum(last * last, axis=1, keepdims=True)
-        dotted += jnp.sum(last * gained[:, cols], axis=1, keepdims=True)
-    score_ref[...] = jnp.broadcast_to(
-        dotted * lax.rsqrt(square / width + 1e-06), score_ref.shape
-    )
-
-
-def finish(place, tokens, gain, head, pieces, groups):
-    rows, width = tokens.shape
+    groups = [sum(counts[:index]) for index in range(len(counts))]
+    gained = jnp.broadcast_to((gain * head).reshape(1, width), (8, width))
 
     def kernel(*refs):
-        finish_kernel(groups, *refs)
-
-    return pl.pallas_call(
+        finish_kernel(groups, width, *refs)
+
+    def cols(i, place):
+        return (0, i)
+
+    def picked(base, count):
+        return lambda i, place: (jnp.clip(place[1 + i] - base, 0, count - 1), 0, 0)
+
+    if wide % 128:
+        tokens = tokens.reshape(rows, planes, wide).transpose(1, 0, 2)
+        gained = gained.reshape(8, planes, wide).transpose(1, 0, 2)
+        plane_spec = pl.BlockSpec((None, rows, wide), lambda i, place: (i, 0, 0))
+        row_spec = pl.BlockSpec((None, 8, wide), lambda i, place: (i, 0, 0))
+        shape = (planes, rows, wide)
+    else:
+        plane_spec = pl.BlockSpec((rows, wide), cols)
+        row_spec = pl.BlockSpec((8, wide), cols)
+        shape = (rows, width)
+    hidden, score = pl.pallas_call(
         kernel,
         name="finish",
         out_shape=(
-            jax.ShapeDtypeStruct((rows, width), jnp.bfloat16),
-            jax.ShapeDtypeStruct((1, 128), jnp.float32),
-        ),
-        in_specs=[pl.BlockSpec(memory_space=pltpu.SMEM)]
-        + [pl.BlockSpec(memory_space=pltpu.VMEM)] * (3 + len(pieces)),
+            jax.ShapeDtypeStruct(shape, jnp.bfloat16),
+            jax.ShapeDtypeStruct((8, 128), jnp.float32),
+        ),
+        grid_spec=pltpu.PrefetchScalarGridSpec(
+            num_scalar_prefetch=1,
+            grid=(planes,),
+            in_specs=[plane_spec, row_spec]
+            + [
+                pl.BlockSpec((1, rows, wide), picked(base, count))
+                for _ in range(len(pieces) // len(counts))
+                for base, count in zip(groups, counts)
+            ],
+            out_specs=(plane_spec, pl.BlockSpec((8, 128), lambda i, place: (0, 0))),
+            scratch_shapes=[pltpu.VMEM((2, 8, 128), jnp.float32)],
+        ),
         cost_estimate=pl.CostEstimate(
             flops=8 * rows * width, bytes_accessed=6 * rows * width, transcendentals=1
         ),
-    )(place, tokens, gain.reshape(1, width), head.reshape(1, width), *pieces)
+    )(place, tokens, gained, *pieces)
+    if wide % 128:
+        hidden = hidden.transpose(1, 0, 2).reshape(rows, width)
+    return hidden, score
 
 
 def solution(mesh):
@@ -329,9 +363,7 @@
         for (plane, own, _), other in zip(qkv_blocks, others):
             for core, weights in ((c, own), (1 - c, other)):
                 part = jnp.dot(
-                    lax.dynamic_index_in_dim(
-                        normed, jnp.maximum(plane, 0) * 2 + core, 0, False
-                    ),
+                    lax.dynamic_index_in_dim(normed, jnp.maximum(plane, 0) * 2 + core, 0, False),
                     weights,
                     preferred_element_type=jnp.float32,
                 )
@@ -381,7 +413,9 @@
             for p in range(planes)
         ]
         place = jnp.stack([length, *slots]).astype(jnp.int32)
-        hidden, scored = finish(place, sequence, final_gain, value_head, pieces, len(groups))
+        hidden, scored = finish(
+            place, sequence, final_gain, value_head, pieces, [len(group) for group in groups]
+        )
         score = scored[0, 0]
 
         total_seqs = fsdp_size * dp_size

time: 269 us -> 272 us (1.011)
  no operation moved by 1% of the time
where the time goes in v2:
time: 272 us; the launch traced here: 270 us
  waiting for transfers between devices  144 us (53%)
  starting transfers between devices  56.6 us (21%)
  matrix products  23.6 us (9%)
  Pallas kernels  18.2 us (7%)
  local copies, waits for them, and re-layouts  15.4 us (6%)
  other arithmetic  7.97 us (3%)
  between operations  4.36 us (2%)
    ppermute x38, waiting for transfers between devices, send(): return lax.ppermute(array, AXES, route(move))  137 us
    ppermute x38, starting transfers between devices, send(): return lax.ppermute(array, AXES, route(move))  53.1 us
    dot_general x10, matrix products, whole(): jnp.dot(lax.dynamic_index_in_dim(normed, jnp.maximum(plane, 0) * 2 + core...  14.2 us
    dot_general x5, matrix products, whole(): lax.dot_general(attn, weights, (((1,), (1,)), ((), ())), preferred_elemen...  9.37 us
    all_to_all x1, waiting for transfers between devices, whole(): gathered = lax.all_to_all(both, AXES, 0, 0, tiled=True)  7.17 us
    pallas_call x1, Pallas kernels, normalise(): pl.pallas_call(norm_kernel, name='normalise', out_shape=jax.ShapeDtypeStr...  6.26 us
    pallas_call x1, Pallas kernels, finish(): pl.pallas_call(kernel, name='finish', out_shape=(jax.ShapeDtypeStruct(sha...  6.23 us
    pallas_call x1, Pallas kernels, attend(): pl.pallas_call(kernel, name='attention', out_shape=jax.ShapeDtypeStruct((...  5.72 us
  transfers between devices with their start and end apart: 39, of which 14 were waited for; matrix products, arithmetic and copies ran while one was open for 15% of the time, Pallas kernels for 4%

profile of v2, /device:TPU:0, one launch (start us, length us, event | category | flops | bytes accessed | tf_op | source)
XLA Modules:
  0.0 270.4 jit_solution(14736976295515121778)
XLA Ops:
  0.7 1.3 constant_dynamic-slice_fusion.2
  3.1 1.7 collective-permute-start.7
  4.7 3.0 %collective-permute-start.1 = (bf16[128,3584]{1,0:T(8,128)(2,1)S(1)}, bf16[128,3584]{1,0:T(8,128)(2,1)}, u32[]{:S(2)}, u32[]{:S(2)}) collective-permute-start(bf16[128,3584]{1,0:T(8,128)(2,1)S(1)} %bitcast.108), channel_id=1, source_target_pairs={{0,2},{1,3},{2,0},{3,1},{4,6},{5,7},{6,4},{7,5},{8,10},{9,11},{10,... | collective-permute-start | bytes 2752520 | tf_op jit(solution)/shard_map/ppermute | solution.py:254
  7.7 1.9 collective-permute-start
  9.6 2.1 dynamic-slice_bitcast_fusion
  11.7 1.6 collective-permute-start.18
  13.5 4.5 %collective-permute-start.9 = (bf16[448,1152]{1,0:T(8,128)(2,1)S(1)}, bf16[448,1152]{1,0:T(8,128)(2,1)}, u32[]{:S(2)}, u32[]{:S(2)}) collective-permute-start(bf16[448,1152]{1,0:T(8,128)(2,1)S(1)} %broadcast_select_fusion.1), channel_id=1, source_target_pairs={{0,8},{1,9},{2,10},{3,11},{4,12},{5,13},{6,14},{7,15},{8,16},{9,17... | collective-permute-start | bytes 3096584 | tf_op jit(solution)/shard_map/ppermute | solution.py:254
  17.9 1.3 collective-permute-start.11
  19.5 8.0 %collective-permute-done.1.by_x_ref = bf16[128,3584]{1,0:T(8,128)(2,1)} collective-permute-done((bf16[128,3584]{1,0:T(8,128)(2,1)S(1)}, bf16[128,3584]{1,0:T(8,128)(2,1)}, u32[]{:S(2)}, u32[]{:S(2)}) %collective-permute-start.1) | collective-permute-done | bytes 917536 | tf_op jit(solution)/shard_map/ppermute | solution.py:254
  27.5 9.2 %collective-permute-start.8 = (bf16[448,1152]{1,0:T(8,128)(2,1)S(1)}, bf16[448,1152]{1,0:T(8,128)(2,1)}, u32[]{:S(2)}, u32[]{:S(2)}) collective-permute-start(bf16[448,1152]{1,0:T(8,128)(2,1)S(1)} %broadcast_select_fusion.1), channel_id=1, source_target_pairs={{0,1},{1,0},{2,3},{3,2},{4,5},{5,4},{6,7},{7,6},{8,9},{9,8},{10,11... | collective-permute-start | bytes 3096584 | tf_op jit(solution)/shard_map/ppermute | solution.py:254
  40.3 1.6 collective-permute-start.2
  43.0 2.5 collective-permute-start.3
  47.6 1.3 broadcast_select_fusion.3
  48.9 9.8 %collective-permute-done.2.far_a_ref = bf16[64,3584]{1,0:T(8,128)(2,1)S(1)} collective-permute-done((bf16[64,3584]{1,0:T(8,128)(2,1)S(1)}, bf16[64,3584]{1,0:T(8,128)(2,1)S(1)}, u32[]{:S(2)}, u32[]{:S(2)}) %collective-permute-start.2) | collective-permute-done | bytes 458784 | tf_op jit(solution)/shard_map/ppermute | solution.py:254
  59.4 1.5 collective-permute-start.5
  60.9 6.3 %normalise.1 = bf16[8,512,448]{2,1,0:T(8,128)(2,1)} custom-call(bf16[128,3584]{1,0:T(8,128)(2,1)} %bitcast.106, bf16[128,3584]{1,0:T(8,128)(2,1)} %collective-permute-done.by_y_ref, bf16[128,3584]{1,0:T(8,128)(2,1)} %collective-permute-done.1.by_x_ref, bf16[64,3584]{1,0:T(8,128)(2,1)} %copy-done.5, bf16[64,3584]{1,0:T(8,128)(2,1)} %collective-permute-done.3.far_b_ref, ...), custom_call_target="tpu_custom_call" | custom-call | flops 14680064 | bytes 7340032 | tf_op jit(solution)/shard_map/normalise/pallas_call | solution.py:135
  67.2 4.3 %collective-permute-start.6 = (s32[1]{0:T(128)}, s32[1]{0:T(128)}, u32[]{:S(2)}, u32[]{:S(2)}) collective-permute-start(s32[1]{0:T(128)} %param.11), channel_id=1, source_target_pairs={{0,6},{1,7},{2,4},{3,5},{4,2},{5,3},{6,0},{7,1},{8,14},{9,15},{10,... | collective-permute-start | bytes 20 | tf_op jit(solution)/shard_map/ppermute | solution.py:254
  71.5 1.6 collective-permute-done.6
  73.1 2.5 collective-permute-start.20
  75.5 2.4 add_bitcast_fusion.refs_0_
  78.7 1.3 collective-permute-start.14
  80.0 2.4 fusion.56
  82.4 2.2 fusion.58
  85.6 21.0 %collective-permute-done.14 = bf16[448,1152]{1,0:T(8,128)(2,1)S(1)} collective-permute-done((bf16[448,1152]{1,0:T(8,128)(2,1)}, bf16[448,1152]{1,0:T(8,128)(2,1)S(1)}, u32[]{:S(2)}, u32[]{:S(2)}) %collective-permute-start.14) | collective-permute-done | bytes 1032224 | tf_op jit(solution)/shard_map/ppermute | solution.py:254
  106.7 1.3 collective-permute-start.16
  108.0 2.1 fusion.53
  112.5 26.3 %collective-permute-done.16 = bf16[448,1152]{1,0:T(8,128)(2,1)S(1)} collective-permute-done((bf16[448,1152]{1,0:T(8,128)(2,1)S(1)}, bf16[448,1152]{1,0:T(8,128)(2,1)S(1)}, u32[]{:S(2)}, u32[]{:S(2)}) %collective-permute-start.16) | collective-permute-done | bytes 1032224 | tf_op jit(solution)/shard_map/ppermute | solution.py:254
  139.7 1.5 collective-permute-start.21
  143.0 2.3 convolution_add_fusion.refs_1_
  145.3 5.7 %attention.1 = bf16[512,896]{1,0:T(8,128)(2,1)} custom-call(s32[4]{0:T(128)} %add_bitcast_fusion.refs_0_, f32[512,1152]{1,0:T(8,128)} %convolution_add_fusion.refs_1_, f32[1,1152]{1,0:T(1,128)} %reshape.32.refs_2_, f32[128,128]{1,0:T(8,128)} %get-tuple-element.50.refs_3_, f32[128,128]{1,0:T(8,128)} %get-tuple-element.51.refs_4_), custom_call_target="tpu_custom_call" | custom-call | flops 1879048192 | bytes 3276800 | tf_op jit(solution)/shard_map/attention/pallas_call | solution.py:90
  151.0 11.0 %collective-permute-done.21 = bf16[448,896]{1,0:T(8,128)(2,1)} collective-permute-done((bf16[448,896]{1,0:T(8,128)(2,1)S(1)}, bf16[448,896]{1,0:T(8,128)(2,1)}, u32[]{:S(2)}, u32[]{:S(2)}) %collective-permute-start.21) | collective-permute-done | bytes 802848 | tf_op jit(solution)/shard_map/ppermute | solution.py:254
  162.7 1.3 collective-permute-start.25
  164.6 3.0 %fusion.44 = bf16[512,896]{1,0:T(8,128)(2,1)S(1)} fusion(bf16[512,896]{1,0:T(8,128)(2,1)} %attention.1, bf16[448,896]{1,0:T(8,128)(2,1)} %collective-permute-done.19, bf16[448,896]{1,0:T(8,128)(2,1)S(1)} %broadcast_select_fusion.3, pred[]{:T(512)S(6)} %eq.104), kind=kOutput, calls=%fused_computation.53 | convolution fusion | flops 829767680 | bytes 3440641 | tf_op jit(solution)/shard_map/dot_general | solution.py:393
  167.7 19.3 %collective-permute-done.25 = bf16[448,896]{1,0:T(8,128)(2,1)S(1)} collective-permute-done((bf16[448,896]{1,0:T(8,128)(2,1)}, bf16[448,896]{1,0:T(8,128)(2,1)S(1)}, u32[]{:S(2)}, u32[]{:S(2)}) %collective-permute-start.25) | collective-permute-done | bytes 802848 | tf_op jit(solution)/shard_map/ppermute | solution.py:254
  187.1 1.3 collective-permute-start.27
  188.5 1.3 fusion.43
  189.8 2.6 fusion.42
  192.8 14.9 %collective-permute-done.27 = bf16[448,896]{1,0:T(8,128)(2,1)S(1)} collective-permute-done((bf16[448,896]{1,0:T(8,128)(2,1)S(1)}, bf16[448,896]{1,0:T(8,128)(2,1)S(1)}, u32[]{:S(2)}, u32[]{:S(2)}) %collective-permute-start.27) | collective-permute-done | bytes 802848 | tf_op jit(solution)/shard_map/ppermute | solution.py:254
  207.8 1.9 collective-permute-start.32
  209.9 1.2 fusion.41
  211.9 2.0 collective-permute-start.30
  216.2 1.4 collective-permute-start.36
  217.6 8.6 %collective-permute-done.32.refs_9_ = bf16[3,128,896]{2,1,0:T(8,128)(2,1)S(1)} collective-permute-done((bf16[3,128,896]{2,1,0:T(8,128)(2,1)S(1)}, bf16[3,128,896]{2,1,0:T(8,128)(2,1)S(1)}, u32[]{:S(2)}, u32[]{:S(2)}) %collective-permute-start.32) | collective-permute-done | bytes 688160 | tf_op jit(solution)/shard_map/ppermute | solution.py:254
  229.1 8.9 %collective-permute-done.30.refs_7_ = bf16[1,128,896]{2,1,0:T(8,128)(2,1)S(1)} collective-permute-done((bf16[1,128,896]{2,1,0:T(8,128)(2,1)S(1)}, bf16[1,128,896]{2,1,0:T(8,128)(2,1)S(1)}, u32[]{:S(2)}, u32[]{:S(2)}) %collective-permute-start.30) | collective-permute-done | bytes 229408 | tf_op jit(solution)/shard_map/ppermute | solution.py:254
  240.9 6.3 %collective-permute-done.31.refs_8_ = bf16[1,128,896]{2,1,0:T(8,128)(2,1)} collective-permute-done((bf16[1,128,896]{2,1,0:T(8,128)(2,1)}, bf16[1,128,896]{2,1,0:T(8,128)(2,1)}, u32[]{:S(2)}, u32[]{:S(2)}) %collective-permute-start.31) | collective-permute-done | bytes 229408 | tf_op jit(solution)/shard_map/ppermute | solution.py:254
  247.9 6.2 %finish.1 = (bf16[128,3584]{1,0:T(8,128)(2,1)}, f32[8,128]{1,0:T(8,128)}) custom-call(s32[5]{0:T(128)} %stack.106.refs_0_, bf16[128,3584]{1,0:T(8,128)(2,1)} %bitcast.107, f32[8,3584]{1,0:T(8,128)} %broadcast_in_dim.36.refs_2_, bf16[3,128,896]{2,1,0:T(8,128)(2,1)} %pad_maximum_fusion.1.refs_3_, bf16[1,128,896]{2,1,0:T(8,128)(2,1)} %get-tuple-element.32.refs_4_, ...), custom_call_target="tpu_custom_call" | custom-call | flops 3670016 | bytes 2752512 | tf_op jit(solution)/shard_map/finish/pallas_call | solution.py:205
  256.5 3.5 %all-to-all-start = ((f32[32,1,128]{2,1,0:T(1,128)}), f32[32,1,128]{2,1,0:T(1,128)S(1)}, u32[]{:S(2)}, u32[]{:S(2)}) async-start(f32[32,1,128]{2,1,0:T(1,128)} %iota.33), calls=%async_computation | async-start | bytes 32768 | tf_op jit(solution)/shard_map/all_to_all | solution.py:426
  260.1 7.2 %all-to-all-done = f32[32,1,128]{2,1,0:T(1,128)S(1)} async-done(((f32[32,1,128]{2,1,0:T(1,128)}), f32[32,1,128]{2,1,0:T(1,128)S(1)}, u32[]{:S(2)}, u32[]{:S(2)}) %all-to-all-start) | async-done | bytes 16416 | tf_op jit(solution)/shard_map/all_to_all | solution.py:426
  (109 shorter events, 30.1 us)
Async XLA Ops:
  3.1 10.2 %collective-permute-start.7 = (bf16[448,1152]{1,0:T(8,128)(2,1)S(1)}, bf16[448,1152]{1,0:T(8,128)(2,1)}, u32[]{:S(2)}, u32[]{:S(2)}) collective-permute-start(bf16[448,1152]{1,0:T(8,128)(2,1)S(1)} %pad_maximum_fusion), channel_id=1, source_target_pairs={{1,4},{3,6},{4,1},{6,3},{9,12},{11,14},{12,9},{14,11},{17,20},{19,... | collective-permute-start | bytes 3096584 | tf_op jit(solution)/shard_map/ppermute | solution.py:254
  4.7 22.8 %collective-permute-start.1 = (bf16[128,3584]{1,0:T(8,128)(2,1)S(1)}, bf16[128,3584]{1,0:T(8,128)(2,1)}, u32[]{:S(2)}, u32[]{:S(2)}) collective-permute-start(bf16[128,3584]{1,0:T(8,128)(2,1)S(1)} %bitcast.108), channel_id=1, source_target_pairs={{0,2},{1,3},{2,0},{3,1},{4,6},{5,7},{6,4},{7,5},{8,10},{9,11},{10,... | collective-permute-start | bytes 2752520 | tf_op jit(solution)/shard_map/ppermute | solution.py:254
  7.7 32.6 %collective-permute-start = (bf16[128,3584]{1,0:T(8,128)(2,1)S(1)}, bf16[128,3584]{1,0:T(8,128)(2,1)}, u32[]{:S(2)}, u32[]{:S(2)}) collective-permute-start(bf16[128,3584]{1,0:T(8,128)(2,1)S(1)} %bitcast.109), channel_id=1, source_target_pairs={{0,4},{1,5},{2,6},{3,7},{4,0},{5,1},{6,2},{7,3},{8,12},{9,13},{10,... | collective-permute-start | bytes 2752520 | tf_op jit(solution)/shard_map/ppermute | solution.py:254
  9.6 27.1 %copy-start.9 = (f32[3584]{0:T(1024)S(1)}, f32[3584]{0:T(1024)}, u32[]{:S(2)}) copy-start(f32[3584]{0:T(1024)} %param.14) | copy-start | bytes 43012
  11.7 31.3 %collective-permute-start.18 = (bf16[448,896]{1,0:T(8,128)(2,1)}, bf16[448,896]{1,0:T(8,128)(2,1)}, u32[]{:S(2)}, u32[]{:S(2)}) collective-permute-start(bf16[448,896]{1,0:T(8,128)(2,1)} %dynamic-slice_bitcast_fusion), channel_id=1, source_target_pairs={{1,4},{3,6},{4,1},{6,3},{9,12},{11,14},{12,9},{14,11},{17,20},{19,... | collective-permute-start | bytes 2408456 | tf_op jit(solution)/shard_map/ppermute | solution.py:254
  13.5 64.4 %collective-permute-start.9 = (bf16[448,1152]{1,0:T(8,128)(2,1)S(1)}, bf16[448,1152]{1,0:T(8,128)(2,1)}, u32[]{:S(2)}, u32[]{:S(2)}) collective-permute-start(bf16[448,1152]{1,0:T(8,128)(2,1)S(1)} %broadcast_select_fusion.1), channel_id=1, source_target_pairs={{0,8},{1,9},{2,10},{3,11},{4,12},{5,13},{6,14},{7,15},{8,16},{9,17... | collective-permute-start | bytes 3096584 | tf_op jit(solution)/shard_map/ppermute | solution.py:254
  17.9 60.7 %collective-permute-start.11 = (bf16[448,1152]{1,0:T(8,128)(2,1)S(1)}, bf16[448,1152]{1,0:T(8,128)(2,1)}, u32[]{:S(2)}, u32[]{:S(2)}) collective-permute-start(bf16[448,1152]{1,0:T(8,128)(2,1)S(1)} %broadcast_select_fusion.1), channel_id=1, source_target_pairs={{8,0},{9,1},{10,2},{11,3},{12,4},{13,5},{14,6},{15,7},{16,8},{17,9... | collective-permute-start | bytes 3096584 | tf_op jit(solution)/shard_map/ppermute | solution.py:254
  27.5 54.9 %collective-permute-start.8 = (bf16[448,1152]{1,0:T(8,128)(2,1)S(1)}, bf16[448,1152]{1,0:T(8,128)(2,1)}, u32[]{:S(2)}, u32[]{:S(2)}) collective-permute-start(bf16[448,1152]{1,0:T(8,128)(2,1)S(1)} %broadcast_select_fusion.1), channel_id=1, source_target_pairs={{0,1},{1,0},{2,3},{3,2},{4,5},{5,4},{6,7},{7,6},{8,9},{9,8},{10,11... | collective-permute-start | bytes 3096584 | tf_op jit(solution)/shard_map/ppermute | solution.py:254
  40.3 18.3 %collective-permute-start.2 = (bf16[64,3584]{1,0:T(8,128)(2,1)S(1)}, bf16[64,3584]{1,0:T(8,128)(2,1)S(1)}, u32[]{:S(2)}, u32[]{:S(2)}) collective-permute-start(bf16[64,3584]{1,0:T(8,128)(2,1)S(1)} %slice.100), channel_id=1, source_target_pairs={{0,4},{1,5},{2,6},{3,7},{4,0},{5,1},{6,2},{7,3},{8,12},{9,13},{10,... | collective-permute-start | bytes 1376264 | tf_op jit(solution)/shard_map/ppermute | solution.py:254
  43.0 16.4 %collective-permute-start.3 = (bf16[64,3584]{1,0:T(8,128)(2,1)S(1)}, bf16[64,3584]{1,0:T(8,128)(2,1)}, u32[]{:S(2)}, u32[]{:S(2)}) collective-permute-start(bf16[64,3584]{1,0:T(8,128)(2,1)S(1)} %slice.101), channel_id=1, source_target_pairs={{0,2},{1,3},{2,0},{3,1},{4,6},{5,7},{6,4},{7,5},{8,10},{9,11},{10,... | collective-permute-start | bytes 1376264 | tf_op jit(solution)/shard_map/ppermute | solution.py:254
  58.7 8.5 %collective-permute-start.4 = (s32[1]{0:T(128)}, s32[1]{0:T(128)}, u32[]{:S(2)}, u32[]{:S(2)}) collective-permute-start(s32[1]{0:T(128)} %param.11), channel_id=1, source_target_pairs={{0,4},{1,5},{2,6},{3,7},{4,0},{5,1},{6,2},{7,3},{8,12},{9,13},{10,... | collective-permute-start | bytes 20 | tf_op jit(solution)/shard_map/ppermute | solution.py:254
  59.4 12.1 %collective-permute-start.5 = (s32[1]{0:T(128)}, s32[1]{0:T(128)}, u32[]{:S(2)}, u32[]{:S(2)}) collective-permute-start(s32[1]{0:T(128)} %param.11), channel_id=1, source_target_pairs={{0,2},{1,3},{2,0},{3,1},{4,6},{5,7},{6,4},{7,5},{8,10},{9,11},{10,... | collective-permute-start | bytes 20 | tf_op jit(solution)/shard_map/ppermute | solution.py:254
  67.2 5.9 %collective-permute-start.6 = (s32[1]{0:T(128)}, s32[1]{0:T(128)}, u32[]{:S(2)}, u32[]{:S(2)}) collective-permute-start(s32[1]{0:T(128)} %param.11), channel_id=1, source_target_pairs={{0,6},{1,7},{2,4},{3,5},{4,2},{5,3},{6,0},{7,1},{8,14},{9,15},{10,... | collective-permute-start | bytes 20 | tf_op jit(solution)/shard_map/ppermute | solution.py:254
  71.5 93.1 %collective-permute-start.19 = (bf16[448,896]{1,0:T(8,128)(2,1)S(1)}, bf16[448,896]{1,0:T(8,128)(2,1)}, u32[]{:S(2)}, u32[]{:S(2)}) collective-permute-start(bf16[448,896]{1,0:T(8,128)(2,1)S(1)} %broadcast_select_fusion.3), channel_id=1, source_target_pairs={{0,1},{1,0},{2,3},{3,2},{4,5},{5,4},{6,7},{7,6},{8,9},{9,8},{10,11... | collective-permute-start | bytes 2408456 | tf_op jit(solution)/shard_map/ppermute | solution.py:254
  73.1 77.9 %collective-permute-start.20 = (bf16[448,896]{1,0:T(8,128)(2,1)S(1)}, bf16[448,896]{1,0:T(8,128)(2,1)S(1)}, u32[]{:S(2)}, u32[]{:S(2)}) collective-permute-start(bf16[448,896]{1,0:T(8,128)(2,1)S(1)} %broadcast_select_fusion.3), channel_id=1, source_target_pairs={{0,8},{1,9},{2,10},{3,11},{4,12},{5,13},{6,14},{7,15},{8,16},{9,17... | collective-permute-start | bytes 2408456 | tf_op jit(solution)/shard_map/ppermute | solution.py:254
  77.9 7.6 %collective-permute-start.13 = (bf16[448,1152]{1,0:T(8,128)(2,1)}, bf16[448,1152]{1,0:T(8,128)(2,1)S(1)}, u32[]{:S(2)}, u32[]{:S(2)}) collective-permute-start(bf16[448,1152]{1,0:T(8,128)(2,1)} %collective-permute-done.9), channel_id=1, source_target_pairs={{8,16},{9,17},{10,18},{11,19},{12,20},{13,21},{14,22},{15,23},{16,... | collective-permute-start | bytes 3096584 | tf_op jit(solution)/shard_map/ppermute | solution.py:254
  78.7 27.9 %collective-permute-start.14 = (bf16[448,1152]{1,0:T(8,128)(2,1)}, bf16[448,1152]{1,0:T(8,128)(2,1)S(1)}, u32[]{:S(2)}, u32[]{:S(2)}) collective-permute-start(bf16[448,1152]{1,0:T(8,128)(2,1)} %collective-permute-done.11), channel_id=1, source_target_pairs={{8,0},{9,1},{10,2},{11,3},{12,4},{13,5},{14,6},{15,7},{16,8},{17,9... | collective-permute-start | bytes 3096584 | tf_op jit(solution)/shard_map/ppermute | solution.py:254
  80.0 4.7 %copy-start = (bf16[8,512,448]{2,1,0:T(8,128)(2,1)S(1)}, bf16[8,512,448]{2,1,0:T(8,128)(2,1)}, u32[]{:S(2)}) copy-start(bf16[8,512,448]{2,1,0:T(8,128)(2,1)} %normalise.1) | copy-start | bytes 11010052
  82.4 28.7 %collective-permute-start.10 = (bf16[448,1152]{1,0:T(8,128)(2,1)}, bf16[448,1152]{1,0:T(8,128)(2,1)S(1)}, u32[]{:S(2)}, u32[]{:S(2)}) collective-permute-start(bf16[448,1152]{1,0:T(8,128)(2,1)} %collective-permute-done.9), channel_id=1, source_target_pairs={{0,1},{1,0},{2,3},{3,2},{4,5},{5,4},{6,7},{7,6},{8,9},{9,8},{10,11... | collective-permute-start | bytes 3096584 | tf_op jit(solution)/shard_map/ppermute | solution.py:254
  106.7 32.1 %collective-permute-start.16 = (bf16[448,1152]{1,0:T(8,128)(2,1)S(1)}, bf16[448,1152]{1,0:T(8,128)(2,1)S(1)}, u32[]{:S(2)}, u32[]{:S(2)}) collective-permute-start(bf16[448,1152]{1,0:T(8,128)(2,1)S(1)} %broadcast_select_fusion), channel_id=1, source_target_pairs={{8,0},{9,1},{10,2},{11,3},{12,4},{13,5},{14,6},{15,7},{16,24},{17,... | collective-permute-start | bytes 3096584 | tf_op jit(solution)/shard_map/ppermute | solution.py:254
  110.1 29.6 %collective-permute-start.15 = (bf16[448,1152]{1,0:T(8,128)(2,1)S(1)}, bf16[448,1152]{1,0:T(8,128)(2,1)S(1)}, u32[]{:S(2)}, u32[]{:S(2)}) collective-permute-start(bf16[448,1152]{1,0:T(8,128)(2,1)S(1)} %broadcast_select_fusion), channel_id=1, source_target_pairs={{0,1},{1,0},{2,3},{3,2},{4,5},{5,4},{6,7},{7,6},{8,9},{9,8},{10,11... | collective-permute-start | bytes 3096584 | tf_op jit(solution)/shard_map/ppermute | solution.py:254
  111.0 31.0 %collective-permute-start.12 = (bf16[448,1152]{1,0:T(8,128)(2,1)}, bf16[448,1152]{1,0:T(8,128)(2,1)S(1)}, u32[]{:S(2)}, u32[]{:S(2)}) collective-permute-start(bf16[448,1152]{1,0:T(8,128)(2,1)} %collective-permute-done.11), channel_id=1, source_target_pairs={{0,1},{1,0},{2,3},{3,2},{4,5},{5,4},{6,7},{7,6},{8,9},{9,8},{10,11... | collective-permute-start | bytes 3096584 | tf_op jit(solution)/shard_map/ppermute | solution.py:254
  138.8 4.2 %collective-permute-start.17 = (bf16[448,1152]{1,0:T(8,128)(2,1)S(1)}, bf16[448,1152]{1,0:T(8,128)(2,1)S(1)}, u32[]{:S(2)}, u32[]{:S(2)}) collective-permute-start(bf16[448,1152]{1,0:T(8,128)(2,1)S(1)} %collective-permute-done.16), channel_id=1, source_target_pairs={{0,1},{1,0},{2,3},{3,2},{4,5},{5,4},{6,7},{7,6},{8,9},{9,8},{10,11... | collective-permute-start | bytes 3096584 | tf_op jit(solution)/shard_map/ppermute | solution.py:254
  139.7 22.3 %collective-permute-start.21 = (bf16[448,896]{1,0:T(8,128)(2,1)S(1)}, bf16[448,896]{1,0:T(8,128)(2,1)}, u32[]{:S(2)}, u32[]{:S(2)}) collective-permute-start(bf16[448,896]{1,0:T(8,128)(2,1)S(1)} %broadcast_select_fusion.3), channel_id=1, source_target_pairs={{8,0},{9,1},{10,2},{11,3},{12,4},{13,5},{14,6},{15,7},{16,8},{17,9... | collective-permute-start | bytes 2408456 | tf_op jit(solution)/shard_map/ppermute | solution.py:254
  162.0 5.7 %collective-permute-start.24 = (bf16[448,896]{1,0:T(8,128)(2,1)S(1)}, bf16[448,896]{1,0:T(8,128)(2,1)S(1)}, u32[]{:S(2)}, u32[]{:S(2)}) collective-permute-start(bf16[448,896]{1,0:T(8,128)(2,1)S(1)} %collective-permute-done.20), channel_id=1, source_target_pairs={{8,16},{9,17},{10,18},{11,19},{12,20},{13,21},{14,22},{15,23},{16,... | collective-permute-start | bytes 2408456 | tf_op jit(solution)/shard_map/ppermute | solution.py:254
  162.7 24.3 %collective-permute-start.25 = (bf16[448,896]{1,0:T(8,128)(2,1)}, bf16[448,896]{1,0:T(8,128)(2,1)S(1)}, u32[]{:S(2)}, u32[]{:S(2)}) collective-permute-start(bf16[448,896]{1,0:T(8,128)(2,1)} %collective-permute-done.21), channel_id=1, source_target_pairs={{8,0},{9,1},{10,2},{11,3},{12,4},{13,5},{14,6},{15,7},{16,8},{17,9... | collective-permute-start | bytes 2408456 | tf_op jit(solution)/shard_map/ppermute | solution.py:254
  164.0 24.5 %collective-permute-start.22 = (bf16[448,896]{1,0:T(8,128)(2,1)S(1)}, bf16[448,896]{1,0:T(8,128)(2,1)S(1)}, u32[]{:S(2)}, u32[]{:S(2)}) collective-permute-start(bf16[448,896]{1,0:T(8,128)(2,1)S(1)} %collective-permute-done.20), channel_id=1, source_target_pairs={{0,1},{1,0},{2,3},{3,2},{4,5},{5,4},{6,7},{7,6},{8,9},{9,8},{10,11... | collective-permute-start | bytes 2408456 | tf_op jit(solution)/shard_map/ppermute | solution.py:254
  164.1 25.7 %collective-permute-start.23 = (bf16[448,896]{1,0:T(8,128)(2,1)}, bf16[448,896]{1,0:T(8,128)(2,1)S(1)}, u32[]{:S(2)}, u32[]{:S(2)}) collective-permute-start(bf16[448,896]{1,0:T(8,128)(2,1)} %collective-permute-done.21), channel_id=1, source_target_pairs={{0,1},{1,0},{2,3},{3,2},{4,5},{5,4},{6,7},{7,6},{8,9},{9,8},{10,11... | collective-permute-start | bytes 2408456 | tf_op jit(solution)/shard_map/ppermute | solution.py:254
  167.6 20.9 %copy-start.11 = (bf16[512,896]{1,0:T(8,128)(2,1)S(1)}, bf16[512,896]{1,0:T(8,128)(2,1)}, u32[]{:S(2)}) copy-start(bf16[512,896]{1,0:T(8,128)(2,1)} %attention.1) | copy-start | bytes 2752516
  187.1 20.6 %collective-permute-start.27 = (bf16[448,896]{1,0:T(8,128)(2,1)S(1)}, bf16[448,896]{1,0:T(8,128)(2,1)S(1)}, u32[]{:S(2)}, u32[]{:S(2)}) collective-permute-start(bf16[448,896]{1,0:T(8,128)(2,1)S(1)} %broadcast_select_fusion.2), channel_id=1, source_target_pairs={{8,0},{9,1},{10,2},{11,3},{12,4},{13,5},{14,6},{15,7},{16,24},{17,... | collective-permute-start | bytes 2408456 | tf_op jit(solution)/shard_map/ppermute | solution.py:254
  188.4 21.5 %collective-permute-start.26 = (bf16[448,896]{1,0:T(8,128)(2,1)S(1)}, bf16[448,896]{1,0:T(8,128)(2,1)S(1)}, u32[]{:S(2)}, u32[]{:S(2)}) collective-permute-start(bf16[448,896]{1,0:T(8,128)(2,1)S(1)} %broadcast_select_fusion.2), channel_id=1, source_target_pairs={{0,1},{1,0},{2,3},{3,2},{4,5},{5,4},{6,7},{7,6},{8,9},{9,8},{10,11... | collective-permute-start | bytes 2408456 | tf_op jit(solution)/shard_map/ppermute | solution.py:254
  192.7 23.5 %collective-permute-start.35 = (bf16[3,128,896]{2,1,0:T(8,128)(2,1)S(1)}, bf16[3,128,896]{2,1,0:T(8,128)(2,1)S(1)}, u32[]{:S(2)}, u32[]{:S(2)}) collective-permute-start(bf16[3,128,896]{2,1,0:T(8,128)(2,1)S(1)} %pad_maximum_fusion.4), channel_id=1, source_target_pairs={{0,6},{1,7},{2,4},{3,5},{4,2},{5,3},{6,0},{7,1},{8,14},{9,15},{10,... | collective-permute-start | bytes 2064392 | tf_op jit(solution)/shard_map/ppermute | solution.py:254
  207.7 6.2 %collective-permute-start.28 = (bf16[448,896]{1,0:T(8,128)(2,1)S(1)}, bf16[448,896]{1,0:T(8,128)(2,1)S(1)}, u32[]{:S(2)}, u32[]{:S(2)}) collective-permute-start(bf16[448,896]{1,0:T(8,128)(2,1)S(1)} %collective-permute-done.27), channel_id=1, source_target_pairs={{0,1},{1,0},{2,3},{3,2},{4,5},{5,4},{6,7},{7,6},{8,9},{9,8},{10,11... | collective-permute-start | bytes 2408456 | tf_op jit(solution)/shard_map/ppermute | solution.py:254
  207.8 18.4 %collective-permute-start.32 = (bf16[3,128,896]{2,1,0:T(8,128)(2,1)S(1)}, bf16[3,128,896]{2,1,0:T(8,128)(2,1)S(1)}, u32[]{:S(2)}, u32[]{:S(2)}) collective-permute-start(bf16[3,128,896]{2,1,0:T(8,128)(2,1)S(1)} %pad_maximum_fusion.3), channel_id=1, source_target_pairs={{0,2},{1,3},{2,0},{3,1},{4,6},{5,7},{6,4},{7,5},{8,10},{9,11},{10,... | collective-permute-start | bytes 2064392 | tf_op jit(solution)/shard_map/ppermute | solution.py:254
  209.8 18.4 %collective-permute-start.29 = (bf16[3,128,896]{2,1,0:T(8,128)(2,1)S(1)}, bf16[3,128,896]{2,1,0:T(8,128)(2,1)S(1)}, u32[]{:S(2)}, u32[]{:S(2)}) collective-permute-start(bf16[3,128,896]{2,1,0:T(8,128)(2,1)S(1)} %pad_maximum_fusion.2), channel_id=1, source_target_pairs={{0,4},{1,5},{2,6},{3,7},{4,0},{5,1},{6,2},{7,3},{8,12},{9,13},{10,... | collective-permute-start | bytes 2064392 | tf_op jit(solution)/shard_map/ppermute | solution.py:254
  211.9 26.1 %collective-permute-start.30 = (bf16[1,128,896]{2,1,0:T(8,128)(2,1)S(1)}, bf16[1,128,896]{2,1,0:T(8,128)(2,1)S(1)}, u32[]{:S(2)}, u32[]{:S(2)}) collective-permute-start(bf16[1,128,896]{2,1,0:T(8,128)(2,1)S(1)} %get-tuple-element.31), channel_id=1, source_target_pairs={{0,4},{1,5},{2,6},{3,7},{4,0},{5,1},{6,2},{7,3},{8,12},{9,13},{10,... | collective-permute-start | bytes 688136 | tf_op jit(solution)/shard_map/ppermute | solution.py:254
  213.9 25.5 %copy-start.7 = (f32[3584]{0:T(1024)S(1)}, f32[3584]{0:T(1024)}, u32[]{:S(2)}) copy-start(f32[3584]{0:T(1024)} %param.18) | copy-start | bytes 43012
  213.9 25.5 %copy-start.8 = (f32[3584]{0:T(1024)S(1)}, f32[3584]{0:T(1024)}, u32[]{:S(2)}) copy-start(f32[3584]{0:T(1024)} %param.19) | copy-start | bytes 43012
  213.9 27.0 %collective-permute-start.33 = (bf16[1,128,896]{2,1,0:T(8,128)(2,1)S(1)}, bf16[1,128,896]{2,1,0:T(8,128)(2,1)}, u32[]{:S(2)}, u32[]{:S(2)}) collective-permute-start(bf16[1,128,896]{2,1,0:T(8,128)(2,1)S(1)} %get-tuple-element.30), channel_id=1, source_target_pairs={{0,2},{1,3},{2,0},{3,1},{4,6},{5,7},{6,4},{7,5},{8,10},{9,11},{10,... | collective-permute-start | bytes 688136 | tf_op jit(solution)/shard_map/ppermute | solution.py:254
  216.2 31.7 %copy-start.2 = (bf16[3,128,896]{2,1,0:T(8,128)(2,1)}, bf16[3,128,896]{2,1,0:T(8,128)(2,1)S(1)}, u32[]{:S(2)}) copy-start(bf16[3,128,896]{2,1,0:T(8,128)(2,1)S(1)} %collective-permute-done.35.refs_12_) | copy-start | bytes 2064388
  216.2 24.7 %collective-permute-start.36 = (bf16[1,128,896]{2,1,0:T(8,128)(2,1)S(1)}, bf16[1,128,896]{2,1,0:T(8,128)(2,1)}, u32[]{:S(2)}, u32[]{:S(2)}) collective-permute-start(bf16[1,128,896]{2,1,0:T(8,128)(2,1)S(1)} %get-tuple-element.29), channel_id=1, source_target_pairs={{0,6},{1,7},{2,4},{3,5},{4,2},{5,3},{6,0},{7,1},{8,14},{9,15},{10,... | collective-permute-start | bytes 688136 | tf_op jit(solution)/shard_map/ppermute | solution.py:254
  226.2 21.7 %copy-start.3 = (bf16[3,128,896]{2,1,0:T(8,128)(2,1)}, bf16[3,128,896]{2,1,0:T(8,128)(2,1)S(1)}, u32[]{:S(2)}) copy-start(bf16[3,128,896]{2,1,0:T(8,128)(2,1)S(1)} %collective-permute-done.32.refs_9_) | copy-start | bytes 2064388
  226.2 21.0 %collective-permute-start.31 = (bf16[1,128,896]{2,1,0:T(8,128)(2,1)}, bf16[1,128,896]{2,1,0:T(8,128)(2,1)}, u32[]{:S(2)}, u32[]{:S(2)}) collective-permute-start(bf16[1,128,896]{2,1,0:T(8,128)(2,1)} %get-tuple-element.27), channel_id=1, source_target_pairs={{0,4},{1,5},{2,6},{3,7},{4,0},{5,1},{6,2},{7,3},{8,12},{9,13},{10,... | collective-permute-start | bytes 688136 | tf_op jit(solution)/shard_map/ppermute | solution.py:254
  228.2 19.7 %copy-start.4 = (bf16[3,128,896]{2,1,0:T(8,128)(2,1)}, bf16[3,128,896]{2,1,0:T(8,128)(2,1)S(1)}, u32[]{:S(2)}) copy-start(bf16[3,128,896]{2,1,0:T(8,128)(2,1)S(1)} %collective-permute-done.29.refs_6_) | copy-start | bytes 2064388
  228.2 19.0 %collective-permute-start.34 = (bf16[1,128,896]{2,1,0:T(8,128)(2,1)}, bf16[1,128,896]{2,1,0:T(8,128)(2,1)}, u32[]{:S(2)}, u32[]{:S(2)}) collective-permute-start(bf16[1,128,896]{2,1,0:T(8,128)(2,1)} %get-tuple-element.26), channel_id=1, source_target_pairs={{0,2},{1,3},{2,0},{3,1},{4,6},{5,7},{6,4},{7,5},{8,10},{9,11},{10,... | collective-permute-start | bytes 688136 | tf_op jit(solution)/shard_map/ppermute | solution.py:254
  238.7 8.5 %collective-permute-start.37 = (bf16[1,128,896]{2,1,0:T(8,128)(2,1)S(1)}, bf16[1,128,896]{2,1,0:T(8,128)(2,1)}, u32[]{:S(2)}, u32[]{:S(2)}) collective-permute-start(bf16[1,128,896]{2,1,0:T(8,128)(2,1)S(1)} %get-tuple-element.25), channel_id=1, source_target_pairs={{0,6},{1,7},{2,4},{3,5},{4,2},{5,3},{6,0},{7,1},{8,14},{9,15},{10,... | collective-permute-start | bytes 688136 | tf_op jit(solution)/shard_map/ppermute | solution.py:254
  247.9 20.0 %copy-start.10 = (s32[32]{0:T(128)S(1)}, s32[32]{0:T(128)}, u32[]{:S(2)}) copy-start(s32[32]{0:T(128)} %param.12) | copy-start | bytes 388
  256.5 10.7 %all-to-all-start = ((f32[32,1,128]{2,1,0:T(1,128)}), f32[32,1,128]{2,1,0:T(1,128)S(1)}, u32[]{:S(2)}, u32[]{:S(2)}) async-start(f32[32,1,128]{2,1,0:T(1,128)} %iota.33), calls=%async_computation | async-start | bytes 32768 | tf_op jit(solution)/shard_map/all_to_all | solution.py:426
  (3 other events, 7.0 us)

commit v3 on v1

--- a/solution.py
+++ b/solution.py
@@ -110,11 +110,11 @@
     )(group_lengths, acc, bias_cols.reshape(1, width), *tables)
 
 
-def norm_kernel(own_ref, by_y_ref, by_x_ref, far_a_ref, far_b_ref, gain_ref, out_ref):
+def norm_kernel(own_ref, by_y_ref, by_x_ref, far_ref, gain_ref, out_ref):
     shards, _, shard_rows = out_ref.shape
-    step = far_a_ref.shape[0]
+    step = own_ref.shape[0] // 2
     base = 0
-    for source in (own_ref, by_y_ref, by_x_ref, far_a_ref, far_b_ref):
+    for source in (own_ref, by_y_ref, by_x_ref, far_ref):
 
         def body(i, carry, source=source, base=base):
             start = pl.multiple_of(i * step, step)
@@ -232,7 +232,7 @@
         return (z, y, x, 1 - c)
 
     def hop_y(z, y, x, c):
-        return (z, 1 - y, x, 1 - c) if c != y else None
+        return (z, 1 - y, x, 1 - c) if c != y else (z, y, x, c)
 
     def along(shift, holds):
         def move(z, y, x, c):
@@ -309,29 +309,25 @@
 
         near = c == y
 
-        def with_hop(cut):
-            return jnp.where(near, cut, send(cut, hop_y))
-
-        block = with_hop(group_slices(qkv_weight, jnp.where(near, g, g ^ 1), 1))
-        qkv_blocks = spread(block)
-        others = [send(own, to_core) for _, own, _ in qkv_blocks]
-
-        half = length_rows // 2
+        cut = group_slices(qkv_weight, jnp.where(near, g, g ^ 1), 1)
+        qkv_blocks = [
+            (plane, send(block, hop_y))
+            for plane, block, _ in spread(cut)
+        ]
+        others = [send(own, to_core) for _, own in qkv_blocks]
+
         by_y = send(sequence, to_y)
         by_x = send(sequence, to_x)
-        halves = by_x[:half], by_y[half:]
-        far = [send(halves[0], to_y), send(halves[1], to_x)]
-        normed = normalise([sequence, by_y, by_x, *far], norm_gain, fsdp_size)
+        far = send(by_y, to_x)
+        normed = normalise([sequence, by_y, by_x, far], norm_gain, fsdp_size)
         near_lengths = [send(lengths, to_y), send(lengths, to_x), send(lengths, to_xy)]
         normed, *near_lengths = lax.optimization_barrier((normed, *near_lengths))
         group_lengths = jnp.stack([lengths, *near_lengths])[:, 0]
         acc = None
-        for (plane, own, _), other in zip(qkv_blocks, others):
+        for (plane, own), other in zip(qkv_blocks, others):
             for core, weights in ((c, own), (1 - c, other)):
                 part = jnp.dot(
-                    lax.dynamic_index_in_dim(
-                        normed, jnp.maximum(plane, 0) * 2 + core, 0, False
-                    ),
+                    lax.dynamic_index_in_dim(normed, jnp.maximum(plane, 0) * 2 + core, 0, False),
                     weights,
                     preferred_element_type=jnp.float32,
                 )
@@ -349,7 +345,7 @@
         cut = lax.dynamic_slice_in_dim(
             out_weight.T, jnp.where(near, g, g ^ 1) * query_cols, query_cols, 1
         )
-        out_blocks = spread(with_hop(cut), attn)
+        out_blocks = spread(send(cut, hop_y), attn)
         groups = [[], [], []]
         for index, (_, own, step) in enumerate(out_blocks):
             other = send(own, to_core)

time: 269 us -> 285 us (1.059)
  starting transfers between devices: 56.2 us -> 78.8 us
  local copies, waits for them, and re-layouts: 14.8 us -> 11.5 us
  waiting for transfers between devices: 143 us -> 140 us
    ppermute x38 -> x41, starting transfers between devices: 53.1 us -> 75.7 us  [send(): return lax.ppermute(array, AXES, route(move))]
    ppermute x38 -> x41, waiting for transfers between devices: 136 us -> 133 us  [send(): return lax.ppermute(array, AXES, route(move))]
  transfers between devices with their start and end apart: 39 -> 42, of which waited for: 14 -> 12; matrix products, arithmetic and copies ran while one was open for 15% -> 12% of each run, Pallas kernels for 4% -> 4%
where the time goes in v3:
time: 285 us; the launch traced here: 283 us
  waiting for transfers between devices  140 us (49%)
  starting transfers between devices  78.8 us (28%)
  matrix products  23.1 us (8%)
  Pallas kernels  17.9 us (6%)
  local copies, waits for them, and re-layouts  11.5 us (4%)
  other arithmetic  7.42 us (3%)
  between operations  4.43 us (2%)
    ppermute x41, waiting for transfers between devices, send(): return lax.ppermute(array, AXES, route(move))  133 us
    ppermute x41, starting transfers between devices, send(): return lax.ppermute(array, AXES, route(move))  75.7 us
    dot_general x10, matrix products, whole(): jnp.dot(lax.dynamic_index_in_dim(normed, jnp.maximum(plane, 0) * 2 + core...  13.7 us
    dot_general x5, matrix products, whole(): lax.dot_general(attn, weights, (((1,), (1,)), ((), ())), preferred_elemen...  9.35 us
    all_to_all x1, waiting for transfers between devices, whole(): gathered = lax.all_to_all(both, AXES, 0, 0, tiled=True)  7.17 us
    pallas_call x1, Pallas kernels, normalise(): pl.pallas_call(norm_kernel, name='normalise', out_shape=jax.ShapeDtypeStr...  6.5 us
    pallas_call x1, Pallas kernels, finish(): pl.pallas_call(kernel, name='finish', out_shape=(jax.ShapeDtypeStruct((ro...  5.73 us
    pallas_call x1, Pallas kernels, attend(): pl.pallas_call(kernel, name='attention', out_shape=jax.ShapeDtypeStruct((...  5.72 us
  transfers between devices with their start and end apart: 42, of which 12 were waited for; matrix products, arithmetic and copies ran while one was open for 12% of the time, Pallas kernels for 4%

profile of v3, /device:TPU:0, one launch (start us, length us, event | category | flops | bytes accessed | tf_op | source)
XLA Modules:
  0.0 283.0 jit_solution(15825469596487665586)
XLA Ops:
  0.7 1.4 constant_dynamic-slice_fusion.2
  4.1 5.9 %collective-permute-start.8 = (bf16[448,1152]{1,0:T(8,128)(2,1)}, bf16[448,1152]{1,0:T(8,128)(2,1)}, u32[]{:S(2)}, u32[]{:S(2)}) collective-permute-start(bf16[448,1152]{1,0:T(8,128)(2,1)} %pad_maximum_fusion), channel_id=1, source_target_pairs={{0,8},{1,9},{2,10},{3,11},{4,12},{5,13},{6,14},{7,15},{8,16},{9,17... | collective-permute-start | bytes 3096584 | tf_op jit(solution)/shard_map/ppermute | solution.py:220
  10.1 1.3 collective-permute-start.11
  11.4 1.6 collective-permute-start
  13.0 1.6 collective-permute-start.21
  14.7 1.3 collective-permute-start.3
  15.9 26.3 %collective-permute-done.3 = s32[1]{0:T(128)} collective-permute-done((s32[1]{0:T(128)}, s32[1]{0:T(128)}, u32[]{:S(2)}, u32[]{:S(2)}) %collective-permute-start.3) | collective-permute-done | bytes 36 | tf_op jit(solution)/shard_map/ppermute | solution.py:220
  42.2 1.5 collective-permute-start.4
  43.7 2.2 collective-permute-done.4
  46.2 4.3 %collective-permute-done.5 = s32[1]{0:T(128)} collective-permute-done((s32[1]{0:T(128)}, s32[1]{0:T(128)}, u32[]{:S(2)}, u32[]{:S(2)}) %collective-permute-start.5) | collective-permute-done | bytes 36 | tf_op jit(solution)/shard_map/ppermute | solution.py:220
  50.5 9.4 %collective-permute-start.6 = (bf16[448,1152]{1,0:T(8,128)(2,1)}, bf16[448,1152]{1,0:T(8,128)(2,1)}, u32[]{:S(2)}, u32[]{:S(2)}) collective-permute-start(bf16[448,1152]{1,0:T(8,128)(2,1)} %pad_maximum_fusion), channel_id=1, source_target_pairs={{0,0},{1,4},{2,2},{3,6},{4,1},{5,5},{6,3},{7,7},{8,8},{9,12},{10,1... | collective-permute-start | bytes 3096584 | tf_op jit(solution)/shard_map/ppermute | solution.py:220
  60.0 1.5 collective-permute-start.1
  62.7 1.3 collective-permute-start.15
  66.7 16.8 %collective-permute-done.1.by_x_ref = bf16[128,3584]{1,0:T(8,128)(2,1)} collective-permute-done((bf16[128,3584]{1,0:T(8,128)(2,1)}, bf16[128,3584]{1,0:T(8,128)(2,1)}, u32[]{:S(2)}, u32[]{:S(2)}) %collective-permute-start.1) | collective-permute-done | bytes 917536 | tf_op jit(solution)/shard_map/ppermute | solution.py:220
  83.5 1.9 collective-permute-start.9
  85.4 9.4 %collective-permute-start.12 = (bf16[448,1152]{1,0:T(8,128)(2,1)}, bf16[448,1152]{1,0:T(8,128)(2,1)}, u32[]{:S(2)}, u32[]{:S(2)}) collective-permute-start(bf16[448,1152]{1,0:T(8,128)(2,1)} %collective-permute-done.11), channel_id=1, source_target_pairs={{0,0},{1,4},{2,2},{3,6},{4,1},{5,5},{6,3},{7,7},{8,8},{9,12},{10,1... | collective-permute-start | bytes 3096584 | tf_op jit(solution)/shard_map/ppermute | solution.py:220
  96.9 6.5 %normalise.1 = bf16[8,512,448]{2,1,0:T(8,128)(2,1)} custom-call(bf16[128,3584]{1,0:T(8,128)(2,1)} %bitcast.4.own_ref.refs_1_, bf16[128,3584]{1,0:T(8,128)(2,1)} %collective-permute-done.by_y_ref, bf16[128,3584]{1,0:T(8,128)(2,1)} %collective-permute-done.1.by_x_ref, bf16[128,3584]{1,0:T(8,128)(2,1)} %collective-permute-done.2.far_ref, ...), custom_call_target="tpu_custom_call" | custom-call | flops 14680064 | bytes 7340032 | tf_op jit(solution)/shard_map/normalise/pallas_call | solution.py:135
  103.4 2.4 add_bitcast_fusion.refs_0_
  105.8 5.2 %collective-permute-start.23 = (bf16[448,896]{1,0:T(8,128)(2,1)}, bf16[448,896]{1,0:T(8,128)(2,1)}, u32[]{:S(2)}, u32[]{:S(2)}) collective-permute-start(bf16[448,896]{1,0:T(8,128)(2,1)} %collective-permute-done.21), channel_id=1, source_target_pairs={{0,8},{1,9},{2,10},{3,11},{4,12},{5,13},{6,14},{7,15},{8,16},{9,17... | collective-permute-start | bytes 2408456 | tf_op jit(solution)/shard_map/ppermute | solution.py:220
  111.1 1.6 collective-permute-start.18
  112.7 2.2 fusion.55
  115.6 2.2 collective-permute-start.10
  118.0 2.1 convolution_add_fusion.5
  120.9 17.2 %collective-permute-done.18 = bf16[448,1152]{1,0:T(8,128)(2,1)S(1)} collective-permute-done((bf16[448,1152]{1,0:T(8,128)(2,1)S(1)}, bf16[448,1152]{1,0:T(8,128)(2,1)S(1)}, u32[]{:S(2)}, u32[]{:S(2)}) %collective-permute-start.18) | collective-permute-done | bytes 1032224 | tf_op jit(solution)/shard_map/ppermute | solution.py:220
  138.8 2.1 fusion.50
  140.9 1.5 collective-permute-start.24
  142.4 1.9 collective-permute-start.17
  146.1 7.5 %collective-permute-start.20 = (bf16[448,1152]{1,0:T(8,128)(2,1)S(1)}, bf16[448,1152]{1,0:T(8,128)(2,1)S(1)}, u32[]{:S(2)}, u32[]{:S(2)}) collective-permute-start(bf16[448,1152]{1,0:T(8,128)(2,1)S(1)} %collective-permute-done.19), channel_id=1, source_target_pairs={{0,1},{1,0},{2,3},{3,2},{4,5},{5,4},{6,7},{7,6},{8,9},{9,8},{10,11... | collective-permute-start | bytes 3096584 | tf_op jit(solution)/shard_map/ppermute | solution.py:220
  156.1 2.3 convolution_add_fusion.refs_1_
  158.4 5.7 %attention.1 = bf16[512,896]{1,0:T(8,128)(2,1)} custom-call(s32[4]{0:T(128)} %add_bitcast_fusion.refs_0_, f32[512,1152]{1,0:T(8,128)} %convolution_add_fusion.refs_1_, f32[1,1152]{1,0:T(1,128)} %reshape.38.refs_2_, f32[128,128]{1,0:T(8,128)} %get-tuple-element.50.refs_3_, f32[128,128]{1,0:T(8,128)} %get-tuple-element.51.refs_4_), custom_call_target="tpu_custom_call" | custom-call | flops 1879048192 | bytes 3276800 | tf_op jit(solution)/shard_map/attention/pallas_call | solution.py:90
  164.9 1.3 collective-permute-start.28
  166.7 3.0 %fusion.42 = bf16[512,896]{1,0:T(8,128)(2,1)S(1)} fusion(bf16[512,896]{1,0:T(8,128)(2,1)} %attention.1, bf16[448,896]{1,0:T(8,128)(2,1)S(1)} %collective-permute-done.22, bf16[448,896]{1,0:T(8,128)(2,1)} %collective-permute-done.21, pred[]{:T(512)S(6)} %eq.104), kind=kOutput, calls=%fused_computation.53 | convolution fusion | flops 829767680 | bytes 3440641 | tf_op jit(solution)/shard_map/dot_general | solution.py:357
  169.8 31.4 %collective-permute-done.28 = bf16[448,896]{1,0:T(8,128)(2,1)S(1)} collective-permute-done((bf16[448,896]{1,0:T(8,128)(2,1)S(1)}, bf16[448,896]{1,0:T(8,128)(2,1)S(1)}, u32[]{:S(2)}, u32[]{:S(2)}) %collective-permute-start.28) | collective-permute-done | bytes 802848 | tf_op jit(solution)/shard_map/ppermute | solution.py:220
  201.3 1.5 collective-permute-start.30
  202.9 2.6 fusion.41
  207.1 1.6 collective-permute-start.38
  208.7 13.5 %collective-permute-done.30 = bf16[448,896]{1,0:T(8,128)(2,1)S(1)} collective-permute-done((bf16[448,896]{1,0:T(8,128)(2,1)S(1)}, bf16[448,896]{1,0:T(8,128)(2,1)S(1)}, u32[]{:S(2)}, u32[]{:S(2)}) %collective-permute-start.30) | collective-permute-done | bytes 802848 | tf_op jit(solution)/shard_map/ppermute | solution.py:220
  222.3 1.4 collective-permute-start.35
  225.0 1.3 fusion.39
  230.7 1.9 collective-permute-start.39
  232.6 8.2 %collective-permute-done.35.refs_10_ = bf16[3,128,896]{2,1,0:T(8,128)(2,1)} collective-permute-done((bf16[3,128,896]{2,1,0:T(8,128)(2,1)S(1)}, bf16[3,128,896]{2,1,0:T(8,128)(2,1)}, u32[]{:S(2)}, u32[]{:S(2)}) %collective-permute-start.35) | collective-permute-done | bytes 688160 | tf_op jit(solution)/shard_map/ppermute | solution.py:220
  240.8 1.5 collective-permute-start.34
  243.3 8.8 %collective-permute-done.33.refs_8_ = bf16[1,128,896]{2,1,0:T(8,128)(2,1)S(1)} collective-permute-done((bf16[1,128,896]{2,1,0:T(8,128)(2,1)S(1)}, bf16[1,128,896]{2,1,0:T(8,128)(2,1)S(1)}, u32[]{:S(2)}, u32[]{:S(2)}) %collective-permute-start.33) | collective-permute-done | bytes 229408 | tf_op jit(solution)/shard_map/ppermute | solution.py:220
  252.0 1.6 collective-permute-start.40
  257.2 4.0 %collective-permute-done.34.refs_9_ = bf16[1,128,896]{2,1,0:T(8,128)(2,1)S(1)} collective-permute-done((bf16[1,128,896]{2,1,0:T(8,128)(2,1)S(1)}, bf16[1,128,896]{2,1,0:T(8,128)(2,1)S(1)}, u32[]{:S(2)}, u32[]{:S(2)}) %collective-permute-start.34) | collective-permute-done | bytes 229408 | tf_op jit(solution)/shard_map/ppermute | solution.py:220
  262.6 5.7 %finish.1 = (bf16[128,3584]{1,0:T(8,128)(2,1)}, f32[1,128]{1,0:T(1,128)}) custom-call(s32[5]{0:T(128)} %stack.106.refs_0_, bf16[128,3584]{1,0:T(8,128)(2,1)} %bitcast.4.own_ref.refs_1_, f32[1,3584]{1,0:T(1,128)} %reshape.35.refs_2_, f32[1,3584]{1,0:T(1,128)} %reshape.36.refs_3_, bf16[3,128,896]{2,1,0:T(8,128)(2,1)} %pad_maximum_fusion.1.refs_4_, ...), custom_call_target="tpu_custom_call" | custom-call | flops 3670016 | bytes 2752512 | tf_op jit(solution)/shard_map/finish/pallas_call | solution.py:184
  269.6 3.1 %all-to-all-start = ((f32[32,1,128]{2,1,0:T(1,128)}), f32[32,1,128]{2,1,0:T(1,128)S(1)}, u32[]{:S(2)}, u32[]{:S(2)}) async-start(f32[32,1,128]{2,1,0:T(1,128)} %iota.33), calls=%async_computation | async-start | bytes 32768 | tf_op jit(solution)/shard_map/all_to_all | solution.py:388
  272.7 7.2 %all-to-all-done = f32[32,1,128]{2,1,0:T(1,128)S(1)} async-done(((f32[32,1,128]{2,1,0:T(1,128)}), f32[32,1,128]{2,1,0:T(1,128)S(1)}, u32[]{:S(2)}, u32[]{:S(2)}) %all-to-all-start) | async-done | bytes 16416 | tf_op jit(solution)/shard_map/all_to_all | solution.py:388
  (114 shorter events, 31.2 us)
Async XLA Ops:
  2.1 93.6 %copy-start.9 = (f32[3584]{0:T(1024)S(1)}, f32[3584]{0:T(1024)}, u32[]{:S(2)}) copy-start(f32[3584]{0:T(1024)} %param.14) | copy-start | bytes 43012
  4.1 57.9 %collective-permute-start.8 = (bf16[448,1152]{1,0:T(8,128)(2,1)}, bf16[448,1152]{1,0:T(8,128)(2,1)}, u32[]{:S(2)}, u32[]{:S(2)}) collective-permute-start(bf16[448,1152]{1,0:T(8,128)(2,1)} %pad_maximum_fusion), channel_id=1, source_target_pairs={{0,8},{1,9},{2,10},{3,11},{4,12},{5,13},{6,14},{7,15},{8,16},{9,17... | collective-permute-start | bytes 3096584 | tf_op jit(solution)/shard_map/ppermute | solution.py:220
  10.1 52.6 %collective-permute-start.11 = (bf16[448,1152]{1,0:T(8,128)(2,1)}, bf16[448,1152]{1,0:T(8,128)(2,1)}, u32[]{:S(2)}, u32[]{:S(2)}) collective-permute-start(bf16[448,1152]{1,0:T(8,128)(2,1)} %pad_maximum_fusion), channel_id=1, source_target_pairs={{8,0},{9,1},{10,2},{11,3},{12,4},{13,5},{14,6},{15,7},{16,8},{17,9... | collective-permute-start | bytes 3096584 | tf_op jit(solution)/shard_map/ppermute | solution.py:220
  11.4 50.1 %collective-permute-start = (bf16[128,3584]{1,0:T(8,128)(2,1)}, bf16[128,3584]{1,0:T(8,128)(2,1)}, u32[]{:S(2)}, u32[]{:S(2)}) collective-permute-start(bf16[128,3584]{1,0:T(8,128)(2,1)} %bitcast.4.own_ref.refs_1_), channel_id=1, source_target_pairs={{0,4},{1,5},{2,6},{3,7},{4,0},{5,1},{6,2},{7,3},{8,12},{9,13},{10,... | collective-permute-start | bytes 2752520 | tf_op jit(solution)/shard_map/ppermute | solution.py:220
  13.0 46.9 %collective-permute-start.21 = (bf16[448,896]{1,0:T(8,128)(2,1)S(1)}, bf16[448,896]{1,0:T(8,128)(2,1)}, u32[]{:S(2)}, u32[]{:S(2)}) collective-permute-start(bf16[448,896]{1,0:T(8,128)(2,1)S(1)} %dynamic-slice_bitcast_fusion), channel_id=1, source_target_pairs={{0,0},{1,4},{2,2},{3,6},{4,1},{5,5},{6,3},{7,7},{8,8},{9,12},{10,1... | collective-permute-start | bytes 2408456 | tf_op jit(solution)/shard_map/ppermute | solution.py:220
  14.7 27.5 %collective-permute-start.3 = (s32[1]{0:T(128)}, s32[1]{0:T(128)}, u32[]{:S(2)}, u32[]{:S(2)}) collective-permute-start(s32[1]{0:T(128)} %param.11), channel_id=1, source_target_pairs={{0,4},{1,5},{2,6},{3,7},{4,0},{5,1},{6,2},{7,3},{8,12},{9,13},{10,... | collective-permute-start | bytes 20 | tf_op jit(solution)/shard_map/ppermute | solution.py:220
  42.2 3.7 %collective-permute-start.4 = (s32[1]{0:T(128)}, s32[1]{0:T(128)}, u32[]{:S(2)}, u32[]{:S(2)}) collective-permute-start(s32[1]{0:T(128)} %param.11), channel_id=1, source_target_pairs={{0,2},{1,3},{2,0},{3,1},{4,6},{5,7},{6,4},{7,5},{8,10},{9,11},{10,... | collective-permute-start | bytes 20 | tf_op jit(solution)/shard_map/ppermute | solution.py:220
  45.8 4.7 %collective-permute-start.5 = (s32[1]{0:T(128)}, s32[1]{0:T(128)}, u32[]{:S(2)}, u32[]{:S(2)}) collective-permute-start(s32[1]{0:T(128)} %param.11), channel_id=1, source_target_pairs={{0,6},{1,7},{2,4},{3,5},{4,2},{5,3},{6,0},{7,1},{8,14},{9,15},{10,... | collective-permute-start | bytes 20 | tf_op jit(solution)/shard_map/ppermute | solution.py:220
  50.5 34.8 %collective-permute-start.6 = (bf16[448,1152]{1,0:T(8,128)(2,1)}, bf16[448,1152]{1,0:T(8,128)(2,1)}, u32[]{:S(2)}, u32[]{:S(2)}) collective-permute-start(bf16[448,1152]{1,0:T(8,128)(2,1)} %pad_maximum_fusion), channel_id=1, source_target_pairs={{0,0},{1,4},{2,2},{3,6},{4,1},{5,5},{6,3},{7,7},{8,8},{9,12},{10,1... | collective-permute-start | bytes 3096584 | tf_op jit(solution)/shard_map/ppermute | solution.py:220
  60.0 23.5 %collective-permute-start.1 = (bf16[128,3584]{1,0:T(8,128)(2,1)}, bf16[128,3584]{1,0:T(8,128)(2,1)}, u32[]{:S(2)}, u32[]{:S(2)}) collective-permute-start(bf16[128,3584]{1,0:T(8,128)(2,1)} %bitcast.4.own_ref.refs_1_), channel_id=1, source_target_pairs={{0,2},{1,3},{2,0},{3,1},{4,6},{5,7},{6,4},{7,5},{8,10},{9,11},{10,... | collective-permute-start | bytes 2752520 | tf_op jit(solution)/shard_map/ppermute | solution.py:220
  61.5 33.4 %collective-permute-start.2 = (bf16[128,3584]{1,0:T(8,128)(2,1)}, bf16[128,3584]{1,0:T(8,128)(2,1)}, u32[]{:S(2)}, u32[]{:S(2)}) collective-permute-start(bf16[128,3584]{1,0:T(8,128)(2,1)} %collective-permute-done.by_y_ref), channel_id=1, source_target_pairs={{0,2},{1,3},{2,0},{3,1},{4,6},{5,7},{6,4},{7,5},{8,10},{9,11},{10,... | collective-permute-start | bytes 2752520 | tf_op jit(solution)/shard_map/ppermute | solution.py:220
  62.0 43.8 %collective-permute-start.14 = (bf16[448,1152]{1,0:T(8,128)(2,1)}, bf16[448,1152]{1,0:T(8,128)(2,1)S(1)}, u32[]{:S(2)}, u32[]{:S(2)}) collective-permute-start(bf16[448,1152]{1,0:T(8,128)(2,1)} %collective-permute-done.8), channel_id=1, source_target_pairs={{8,16},{9,17},{10,18},{11,19},{12,20},{13,21},{14,22},{15,23},{16,... | collective-permute-start | bytes 3096584 | tf_op jit(solution)/shard_map/ppermute | solution.py:220
  62.7 48.2 %collective-permute-start.15 = (bf16[448,1152]{1,0:T(8,128)(2,1)}, bf16[448,1152]{1,0:T(8,128)(2,1)S(1)}, u32[]{:S(2)}, u32[]{:S(2)}) collective-permute-start(bf16[448,1152]{1,0:T(8,128)(2,1)} %collective-permute-done.11), channel_id=1, source_target_pairs={{8,0},{9,1},{10,2},{11,3},{12,4},{13,5},{14,6},{15,7},{16,8},{17,9... | collective-permute-start | bytes 3096584 | tf_op jit(solution)/shard_map/ppermute | solution.py:220
  83.5 32.1 %collective-permute-start.9 = (bf16[448,1152]{1,0:T(8,128)(2,1)}, bf16[448,1152]{1,0:T(8,128)(2,1)S(1)}, u32[]{:S(2)}, u32[]{:S(2)}) collective-permute-start(bf16[448,1152]{1,0:T(8,128)(2,1)} %collective-permute-done.8), channel_id=1, source_target_pairs={{0,0},{1,4},{2,2},{3,6},{4,1},{5,5},{6,3},{7,7},{8,8},{9,12},{10,1... | collective-permute-start | bytes 3096584 | tf_op jit(solution)/shard_map/ppermute | solution.py:220
  85.4 32.5 %collective-permute-start.12 = (bf16[448,1152]{1,0:T(8,128)(2,1)}, bf16[448,1152]{1,0:T(8,128)(2,1)}, u32[]{:S(2)}, u32[]{:S(2)}) collective-permute-start(bf16[448,1152]{1,0:T(8,128)(2,1)} %collective-permute-done.11), channel_id=1, source_target_pairs={{0,0},{1,4},{2,2},{3,6},{4,1},{5,5},{6,3},{7,7},{8,8},{9,12},{10,1... | collective-permute-start | bytes 3096584 | tf_op jit(solution)/shard_map/ppermute | solution.py:220
  94.9 20.0 %collective-permute-start.7 = (bf16[448,1152]{1,0:T(8,128)(2,1)}, bf16[448,1152]{1,0:T(8,128)(2,1)}, u32[]{:S(2)}, u32[]{:S(2)}) collective-permute-start(bf16[448,1152]{1,0:T(8,128)(2,1)} %collective-permute-done.6), channel_id=1, source_target_pairs={{0,1},{1,0},{2,3},{3,2},{4,5},{5,4},{6,7},{7,6},{8,9},{9,8},{10,11... | collective-permute-start | bytes 3096584 | tf_op jit(solution)/shard_map/ppermute | solution.py:220
  105.8 58.3 %collective-permute-start.23 = (bf16[448,896]{1,0:T(8,128)(2,1)}, bf16[448,896]{1,0:T(8,128)(2,1)}, u32[]{:S(2)}, u32[]{:S(2)}) collective-permute-start(bf16[448,896]{1,0:T(8,128)(2,1)} %collective-permute-done.21), channel_id=1, source_target_pairs={{0,8},{1,9},{2,10},{3,11},{4,12},{5,13},{6,14},{7,15},{8,16},{9,17... | collective-permute-start | bytes 2408456 | tf_op jit(solution)/shard_map/ppermute | solution.py:220
  111.1 27.0 %collective-permute-start.18 = (bf16[448,1152]{1,0:T(8,128)(2,1)S(1)}, bf16[448,1152]{1,0:T(8,128)(2,1)S(1)}, u32[]{:S(2)}, u32[]{:S(2)}) collective-permute-start(bf16[448,1152]{1,0:T(8,128)(2,1)S(1)} %broadcast_select_fusion), channel_id=1, source_target_pairs={{8,0},{9,1},{10,2},{11,3},{12,4},{13,5},{14,6},{15,7},{16,24},{17,... | collective-permute-start | bytes 3096584 | tf_op jit(solution)/shard_map/ppermute | solution.py:220
  114.9 27.5 %collective-permute-start.16 = (bf16[448,1152]{1,0:T(8,128)(2,1)S(1)}, bf16[448,1152]{1,0:T(8,128)(2,1)S(1)}, u32[]{:S(2)}, u32[]{:S(2)}) collective-permute-start(bf16[448,1152]{1,0:T(8,128)(2,1)S(1)} %broadcast_select_fusion), channel_id=1, source_target_pairs={{0,0},{1,4},{2,2},{3,6},{4,1},{5,5},{6,3},{7,7},{8,8},{9,12},{10,1... | collective-permute-start | bytes 3096584 | tf_op jit(solution)/shard_map/ppermute | solution.py:220
  115.6 25.2 %collective-permute-start.10 = (bf16[448,1152]{1,0:T(8,128)(2,1)S(1)}, bf16[448,1152]{1,0:T(8,128)(2,1)S(1)}, u32[]{:S(2)}, u32[]{:S(2)}) collective-permute-start(bf16[448,1152]{1,0:T(8,128)(2,1)S(1)} %collective-permute-done.9), channel_id=1, source_target_pairs={{0,1},{1,0},{2,3},{3,2},{4,5},{5,4},{6,7},{7,6},{8,9},{9,8},{10,11... | collective-permute-start | bytes 3096584 | tf_op jit(solution)/shard_map/ppermute | solution.py:220
  117.9 28.1 %collective-permute-start.13 = (bf16[448,1152]{1,0:T(8,128)(2,1)}, bf16[448,1152]{1,0:T(8,128)(2,1)S(1)}, u32[]{:S(2)}, u32[]{:S(2)}) collective-permute-start(bf16[448,1152]{1,0:T(8,128)(2,1)} %collective-permute-done.12), channel_id=1, source_target_pairs={{0,1},{1,0},{2,3},{3,2},{4,5},{5,4},{6,7},{7,6},{8,9},{9,8},{10,11... | collective-permute-start | bytes 3096584 | tf_op jit(solution)/shard_map/ppermute | solution.py:220
  138.1 8.0 %collective-permute-start.19 = (bf16[448,1152]{1,0:T(8,128)(2,1)S(1)}, bf16[448,1152]{1,0:T(8,128)(2,1)S(1)}, u32[]{:S(2)}, u32[]{:S(2)}) collective-permute-start(bf16[448,1152]{1,0:T(8,128)(2,1)S(1)} %collective-permute-done.18), channel_id=1, source_target_pairs={{0,0},{1,4},{2,2},{3,6},{4,1},{5,5},{6,3},{7,7},{8,8},{9,12},{10,1... | collective-permute-start | bytes 3096584 | tf_op jit(solution)/shard_map/ppermute | solution.py:220
  140.9 23.2 %collective-permute-start.24 = (bf16[448,896]{1,0:T(8,128)(2,1)}, bf16[448,896]{1,0:T(8,128)(2,1)S(1)}, u32[]{:S(2)}, u32[]{:S(2)}) collective-permute-start(bf16[448,896]{1,0:T(8,128)(2,1)} %collective-permute-done.21), channel_id=1, source_target_pairs={{8,0},{9,1},{10,2},{11,3},{12,4},{13,5},{14,6},{15,7},{16,8},{17,9... | collective-permute-start | bytes 2408456 | tf_op jit(solution)/shard_map/ppermute | solution.py:220
  142.4 12.9 %collective-permute-start.17 = (bf16[448,1152]{1,0:T(8,128)(2,1)S(1)}, bf16[448,1152]{1,0:T(8,128)(2,1)S(1)}, u32[]{:S(2)}, u32[]{:S(2)}) collective-permute-start(bf16[448,1152]{1,0:T(8,128)(2,1)S(1)} %collective-permute-done.16), channel_id=1, source_target_pairs={{0,1},{1,0},{2,3},{3,2},{4,5},{5,4},{6,7},{7,6},{8,9},{9,8},{10,11... | collective-permute-start | bytes 3096584 | tf_op jit(solution)/shard_map/ppermute | solution.py:220
  146.0 20.7 %collective-permute-start.22 = (bf16[448,896]{1,0:T(8,128)(2,1)}, bf16[448,896]{1,0:T(8,128)(2,1)S(1)}, u32[]{:S(2)}, u32[]{:S(2)}) collective-permute-start(bf16[448,896]{1,0:T(8,128)(2,1)} %collective-permute-done.21), channel_id=1, source_target_pairs={{0,1},{1,0},{2,3},{3,2},{4,5},{5,4},{6,7},{7,6},{8,9},{9,8},{10,11... | collective-permute-start | bytes 2408456 | tf_op jit(solution)/shard_map/ppermute | solution.py:220
  146.1 10.0 %collective-permute-start.20 = (bf16[448,1152]{1,0:T(8,128)(2,1)S(1)}, bf16[448,1152]{1,0:T(8,128)(2,1)S(1)}, u32[]{:S(2)}, u32[]{:S(2)}) collective-permute-start(bf16[448,1152]{1,0:T(8,128)(2,1)S(1)} %collective-permute-done.19), channel_id=1, source_target_pairs={{0,1},{1,0},{2,3},{3,2},{4,5},{5,4},{6,7},{7,6},{8,9},{9,8},{10,11... | collective-permute-start | bytes 3096584 | tf_op jit(solution)/shard_map/ppermute | solution.py:220
  164.1 5.7 %collective-permute-start.27 = (bf16[448,896]{1,0:T(8,128)(2,1)}, bf16[448,896]{1,0:T(8,128)(2,1)S(1)}, u32[]{:S(2)}, u32[]{:S(2)}) collective-permute-start(bf16[448,896]{1,0:T(8,128)(2,1)} %collective-permute-done.23), channel_id=1, source_target_pairs={{8,16},{9,17},{10,18},{11,19},{12,20},{13,21},{14,22},{15,23},{16,... | collective-permute-start | bytes 2408456 | tf_op jit(solution)/shard_map/ppermute | solution.py:220
  164.9 36.4 %collective-permute-start.28 = (bf16[448,896]{1,0:T(8,128)(2,1)S(1)}, bf16[448,896]{1,0:T(8,128)(2,1)S(1)}, u32[]{:S(2)}, u32[]{:S(2)}) collective-permute-start(bf16[448,896]{1,0:T(8,128)(2,1)S(1)} %collective-permute-done.24), channel_id=1, source_target_pairs={{8,0},{9,1},{10,2},{11,3},{12,4},{13,5},{14,6},{15,7},{16,8},{17,9... | collective-permute-start | bytes 2408456 | tf_op jit(solution)/shard_map/ppermute | solution.py:220
  166.2 36.7 %collective-permute-start.25 = (bf16[448,896]{1,0:T(8,128)(2,1)}, bf16[448,896]{1,0:T(8,128)(2,1)S(1)}, u32[]{:S(2)}, u32[]{:S(2)}) collective-permute-start(bf16[448,896]{1,0:T(8,128)(2,1)} %collective-permute-done.23), channel_id=1, source_target_pairs={{0,1},{1,0},{2,3},{3,2},{4,5},{5,4},{6,7},{7,6},{8,9},{9,8},{10,11... | collective-permute-start | bytes 2408456 | tf_op jit(solution)/shard_map/ppermute | solution.py:220
  166.3 39.3 %collective-permute-start.26 = (bf16[448,896]{1,0:T(8,128)(2,1)S(1)}, bf16[448,896]{1,0:T(8,128)(2,1)S(1)}, u32[]{:S(2)}, u32[]{:S(2)}) collective-permute-start(bf16[448,896]{1,0:T(8,128)(2,1)S(1)} %collective-permute-done.24), channel_id=1, source_target_pairs={{0,1},{1,0},{2,3},{3,2},{4,5},{5,4},{6,7},{7,6},{8,9},{9,8},{10,11... | collective-permute-start | bytes 2408456 | tf_op jit(solution)/shard_map/ppermute | solution.py:220
  169.7 33.2 %copy-start.13 = (bf16[512,896]{1,0:T(8,128)(2,1)S(1)}, bf16[512,896]{1,0:T(8,128)(2,1)}, u32[]{:S(2)}) copy-start(bf16[512,896]{1,0:T(8,128)(2,1)} %attention.1) | copy-start | bytes 2752516
  201.3 20.9 %collective-permute-start.30 = (bf16[448,896]{1,0:T(8,128)(2,1)S(1)}, bf16[448,896]{1,0:T(8,128)(2,1)S(1)}, u32[]{:S(2)}, u32[]{:S(2)}) collective-permute-start(bf16[448,896]{1,0:T(8,128)(2,1)S(1)} %broadcast_select_fusion.1), channel_id=1, source_target_pairs={{8,0},{9,1},{10,2},{11,3},{12,4},{13,5},{14,6},{15,7},{16,24},{17,... | collective-permute-start | bytes 2408456 | tf_op jit(solution)/shard_map/ppermute | solution.py:220
  202.8 22.2 %collective-permute-start.29 = (bf16[448,896]{1,0:T(8,128)(2,1)S(1)}, bf16[448,896]{1,0:T(8,128)(2,1)S(1)}, u32[]{:S(2)}, u32[]{:S(2)}) collective-permute-start(bf16[448,896]{1,0:T(8,128)(2,1)S(1)} %broadcast_select_fusion.1), channel_id=1, source_target_pairs={{0,1},{1,0},{2,3},{3,2},{4,5},{5,4},{6,7},{7,6},{8,9},{9,8},{10,11... | collective-permute-start | bytes 2408456 | tf_op jit(solution)/shard_map/ppermute | solution.py:220
  207.1 23.6 %collective-permute-start.38 = (bf16[3,128,896]{2,1,0:T(8,128)(2,1)S(1)}, bf16[3,128,896]{2,1,0:T(8,128)(2,1)}, u32[]{:S(2)}, u32[]{:S(2)}) collective-permute-start(bf16[3,128,896]{2,1,0:T(8,128)(2,1)S(1)} %pad_maximum_fusion.4), channel_id=1, source_target_pairs={{0,6},{1,7},{2,4},{3,5},{4,2},{5,3},{6,0},{7,1},{8,14},{9,15},{10,... | collective-permute-start | bytes 2064392 | tf_op jit(solution)/shard_map/ppermute | solution.py:220
  222.2 5.8 %collective-permute-start.31 = (bf16[448,896]{1,0:T(8,128)(2,1)S(1)}, bf16[448,896]{1,0:T(8,128)(2,1)S(1)}, u32[]{:S(2)}, u32[]{:S(2)}) collective-permute-start(bf16[448,896]{1,0:T(8,128)(2,1)S(1)} %collective-permute-done.30), channel_id=1, source_target_pairs={{0,1},{1,0},{2,3},{3,2},{4,5},{5,4},{6,7},{7,6},{8,9},{9,8},{10,11... | collective-permute-start | bytes 2408456 | tf_op jit(solution)/shard_map/ppermute | solution.py:220
  222.3 18.5 %collective-permute-start.35 = (bf16[3,128,896]{2,1,0:T(8,128)(2,1)S(1)}, bf16[3,128,896]{2,1,0:T(8,128)(2,1)}, u32[]{:S(2)}, u32[]{:S(2)}) collective-permute-start(bf16[3,128,896]{2,1,0:T(8,128)(2,1)S(1)} %pad_maximum_fusion.3), channel_id=1, source_target_pairs={{0,2},{1,3},{2,0},{3,1},{4,6},{5,7},{6,4},{7,5},{8,10},{9,11},{10,... | collective-permute-start | bytes 2064392 | tf_op jit(solution)/shard_map/ppermute | solution.py:220
  223.8 18.5 %collective-permute-start.32 = (bf16[3,128,896]{2,1,0:T(8,128)(2,1)S(1)}, bf16[3,128,896]{2,1,0:T(8,128)(2,1)}, u32[]{:S(2)}, u32[]{:S(2)}) collective-permute-start(bf16[3,128,896]{2,1,0:T(8,128)(2,1)S(1)} %pad_maximum_fusion.2), channel_id=1, source_target_pairs={{0,4},{1,5},{2,6},{3,7},{4,0},{5,1},{6,2},{7,3},{8,12},{9,13},{10,... | collective-permute-start | bytes 2064392 | tf_op jit(solution)/shard_map/ppermute | solution.py:220
  227.0 25.0 %collective-permute-start.33 = (bf16[1,128,896]{2,1,0:T(8,128)(2,1)S(1)}, bf16[1,128,896]{2,1,0:T(8,128)(2,1)S(1)}, u32[]{:S(2)}, u32[]{:S(2)}) collective-permute-start(bf16[1,128,896]{2,1,0:T(8,128)(2,1)S(1)} %get-tuple-element.31), channel_id=1, source_target_pairs={{0,4},{1,5},{2,6},{3,7},{4,0},{5,1},{6,2},{7,3},{8,12},{9,13},{10,... | collective-permute-start | bytes 688136 | tf_op jit(solution)/shard_map/ppermute | solution.py:220
  228.0 25.7 %copy-start.10 = (f32[3584]{0:T(1024)S(1)}, f32[3584]{0:T(1024)}, u32[]{:S(2)}) copy-start(f32[3584]{0:T(1024)} %param.18) | copy-start | bytes 43012
  228.0 26.3 %copy-start.11 = (f32[3584]{0:T(1024)S(1)}, f32[3584]{0:T(1024)}, u32[]{:S(2)}) copy-start(f32[3584]{0:T(1024)} %param.19) | copy-start | bytes 43012
  228.0 29.2 %collective-permute-start.36 = (bf16[1,128,896]{2,1,0:T(8,128)(2,1)S(1)}, bf16[1,128,896]{2,1,0:T(8,128)(2,1)S(1)}, u32[]{:S(2)}, u32[]{:S(2)}) collective-permute-start(bf16[1,128,896]{2,1,0:T(8,128)(2,1)S(1)} %get-tuple-element.30), channel_id=1, source_target_pairs={{0,2},{1,3},{2,0},{3,1},{4,6},{5,7},{6,4},{7,5},{8,10},{9,11},{10,... | collective-permute-start | bytes 688136 | tf_op jit(solution)/shard_map/ppermute | solution.py:220
  230.7 26.5 %collective-permute-start.39 = (bf16[1,128,896]{2,1,0:T(8,128)(2,1)S(1)}, bf16[1,128,896]{2,1,0:T(8,128)(2,1)S(1)}, u32[]{:S(2)}, u32[]{:S(2)}) collective-permute-start(bf16[1,128,896]{2,1,0:T(8,128)(2,1)S(1)} %get-tuple-element.29), channel_id=1, source_target_pairs={{0,6},{1,7},{2,4},{3,5},{4,2},{5,3},{6,0},{7,1},{8,14},{9,15},{10,... | collective-permute-start | bytes 688136 | tf_op jit(solution)/shard_map/ppermute | solution.py:220
  240.8 20.3 %collective-permute-start.34 = (bf16[1,128,896]{2,1,0:T(8,128)(2,1)S(1)}, bf16[1,128,896]{2,1,0:T(8,128)(2,1)S(1)}, u32[]{:S(2)}, u32[]{:S(2)}) collective-permute-start(bf16[1,128,896]{2,1,0:T(8,128)(2,1)S(1)} %get-tuple-element.27), channel_id=1, source_target_pairs={{0,4},{1,5},{2,6},{3,7},{4,0},{5,1},{6,2},{7,3},{8,12},{9,13},{10,... | collective-permute-start | bytes 688136 | tf_op jit(solution)/shard_map/ppermute | solution.py:220
  242.3 18.8 %collective-permute-start.37 = (bf16[1,128,896]{2,1,0:T(8,128)(2,1)S(1)}, bf16[1,128,896]{2,1,0:T(8,128)(2,1)S(1)}, u32[]{:S(2)}, u32[]{:S(2)}) collective-permute-start(bf16[1,128,896]{2,1,0:T(8,128)(2,1)S(1)} %get-tuple-element.26), channel_id=1, source_target_pairs={{0,2},{1,3},{2,0},{3,1},{4,6},{5,7},{6,4},{7,5},{8,10},{9,11},{10,... | collective-permute-start | bytes 688136 | tf_op jit(solution)/shard_map/ppermute | solution.py:220
  252.0 9.1 %collective-permute-start.40 = (bf16[1,128,896]{2,1,0:T(8,128)(2,1)S(1)}, bf16[1,128,896]{2,1,0:T(8,128)(2,1)S(1)}, u32[]{:S(2)}, u32[]{:S(2)}) collective-permute-start(bf16[1,128,896]{2,1,0:T(8,128)(2,1)S(1)} %get-tuple-element.25), channel_id=1, source_target_pairs={{0,6},{1,7},{2,4},{3,5},{4,2},{5,3},{6,0},{7,1},{8,14},{9,15},{10,... | collective-permute-start | bytes 688136 | tf_op jit(solution)/shard_map/ppermute | solution.py:220
  262.6 19.3 %copy-start.1 = (bf16[3584,448]{0,1:T(8,128)(2,1)S(1)}, bf16[3584,448]{0,1:T(8,128)(2,1)}, u32[]{:S(2)}) copy-start(bf16[3584,448]{0,1:T(8,128)(2,1)} %param.17) | copy-start | bytes 9633796
  262.6 17.8 %copy-start.12 = (s32[32]{0:T(128)S(1)}, s32[32]{0:T(128)}, u32[]{:S(2)}) copy-start(s32[32]{0:T(128)} %param.12) | copy-start | bytes 388
  269.6 10.2 %all-to-all-start = ((f32[32,1,128]{2,1,0:T(1,128)}), f32[32,1,128]{2,1,0:T(1,128)S(1)}, u32[]{:S(2)}, u32[]{:S(2)}) async-start(f32[32,1,128]{2,1,0:T(1,128)} %iota.33), calls=%async_computation | async-start | bytes 32768 | tf_op jit(solution)/shard_map/all_to_all | solution.py:388
  (8 other events, 40.1 us)

commit v4 on v3

--- a/solution.py
+++ b/solution.py
@@ -142,18 +142,13 @@
     )(*parts, gain.reshape(1, width))
 
 
-def finish_kernel(groups, place_ref, tokens_ref, gain_ref, head_ref, *refs):
-    pieces, hidden_ref, score_ref = refs[:-2], refs[-2], refs[-1]
-    length = place_ref[0]
-    rows, width = tokens_ref.shape
-    planes = place_ref.shape[0] - 1
+def finish_kernel(groups, place_ref, tokens_ref, *refs):
+    pieces, hidden_ref = refs[:-1], refs[-1]
+    width = tokens_ref.shape[1]
+    planes = place_ref.shape[0]
     wide = width // planes
-    square = jnp.zeros((1, 1), jnp.float32)
-    dotted = jnp.zeros((1, 1), jnp.float32)
-    picked = lax.broadcasted_iota(jnp.int32, (rows, 1), 0) == length - 1
-    gained = gain_ref[...] * head_ref[...]
     for plane in range(planes):
-        slot = place_ref[1 + plane]
+        slot = place_ref[plane]
         cols = slice(plane * wide, (plane + 1) * wide)
         total = tokens_ref[:, cols].astype(jnp.float32)
         for first in range(0, len(pieces), groups):
@@ -165,17 +160,10 @@
                 value = part if value is None else jnp.where(slot >= base, part, value)
                 base += count
             total += value.astype(jnp.float32)
-        hidden = total.astype(jnp.bfloat16)
-        hidden_ref[:, cols] = hidden
-        last = jnp.sum(jnp.where(picked, hidden.astype(jnp.float32), 0.0), axis=0, keepdims=True)
-        square += jnp.sum(last * last, axis=1, keepdims=True)
-        dotted += jnp.sum(last * gained[:, cols], axis=1, keepdims=True)
-    score_ref[...] = jnp.broadcast_to(
-        dotted * lax.rsqrt(square / width + 1e-06), score_ref.shape
-    )
-
-
-def finish(place, tokens, gain, head, pieces, groups):
+        hidden_ref[:, cols] = total.astype(jnp.bfloat16)
+
+
+def finish(place, tokens, pieces, groups):
     rows, width = tokens.shape
 
     def kernel(*refs):
@@ -184,16 +172,50 @@
     return pl.pallas_call(
         kernel,
         name="finish",
-        out_shape=(
-            jax.ShapeDtypeStruct((rows, width), jnp.bfloat16),
-            jax.ShapeDtypeStruct((1, 128), jnp.float32),
-        ),
+        out_shape=jax.ShapeDtypeStruct((rows, width), jnp.bfloat16),
         in_specs=[pl.BlockSpec(memory_space=pltpu.SMEM)]
-        + [pl.BlockSpec(memory_space=pltpu.VMEM)] * (3 + len(pieces)),
+        + [pl.BlockSpec(memory_space=pltpu.VMEM)] * (1 + len(pieces)),
         cost_estimate=pl.CostEstimate(
-            flops=8 * rows * width, bytes_accessed=6 * rows * width, transcendentals=1
-        ),
-    )(place, tokens, gain.reshape(1, width), head.reshape(1, width), *pieces)
+            flops=8 * rows * width, bytes_accessed=6 * rows * width, transcendentals=0
+        ),
+    )(place, tokens, *pieces)
+
+
+def score_kernel(slots_ref, weight_ref, last_ref, gained_ref, *refs):
+    rows, out_ref = refs[:-1], refs[-1]
+    planes = last_ref.shape[0]
+    count = rows[0].shape[0]
+    at = lax.broadcasted_iota(jnp.int32, (planes, count), 0)
+    slot = jnp.zeros((planes, count), jnp.int32)
+    for plane in range(planes):
+        slot = jnp.where(at == plane, slots_ref[plane], slot)
+    block = lax.broadcasted_iota(jnp.int32, (planes, count), 1)
+    chosen = jnp.where(slot == block, 1.0, 0.0).astype(jnp.bfloat16)
+    total = last_ref[...].astype(jnp.float32)
+    for ref in rows:
+        total += jnp.dot(chosen, ref[...], preferred_element_type=jnp.float32)
+    total = total.astype(jnp.bfloat16).astype(jnp.float32)
+
+    def summed(values):
+        return jnp.sum(jnp.sum(values, axis=1, keepdims=True), axis=0, keepdims=True)
+
+    width = last_ref.shape[0] * last_ref.shape[1]
+    score = summed(total * gained_ref[...]) * lax.rsqrt(summed(total * total) / width + 1e-06)
+    lane = lax.broadcasted_iota(jnp.int32, out_ref.shape, 1)
+    out_ref[...] = jnp.where(lane == 0, score, weight_ref[0])
+
+
+def score_rows(place, pair_weight, last, gained, ahead, total_seqs):
+    return pl.pallas_call(
+        score_kernel,
+        name="score",
+        out_shape=jax.ShapeDtypeStruct((total_seqs, 128), jnp.float32),
+        in_specs=[pl.BlockSpec(memory_space=pltpu.SMEM)] * 2
+        + [pl.BlockSpec(memory_space=pltpu.VMEM)] * (2 + len(ahead)),
+        cost_estimate=pl.CostEstimate(
+            flops=8 * gained.size, bytes_accessed=16 * gained.size, transcendentals=1
+        ),
+    )(place, pair_weight, last, gained, *ahead)
 
 
 def solution(mesh):
@@ -232,7 +254,10 @@
         return (z, y, x, 1 - c)
 
     def hop_y(z, y, x, c):
-        return (z, 1 - y, x, 1 - c) if c != y else (z, y, x, c)
+        return (z, 1 - y, x, 1 - c) if c != y else None
+
+    def hop_or_stay(z, y, x, c):
+        return hop_y(z, y, x, c) or (z, y, x, c)
 
     def along(shift, holds):
         def move(z, y, x, c):
@@ -310,9 +335,11 @@
         near = c == y
 
         cut = group_slices(qkv_weight, jnp.where(near, g, g ^ 1), 1)
-        qkv_blocks = [
-            (plane, send(block, hop_y))
-            for plane, block, _ in spread(cut)
+        chain = spread(cut)
+        qkv_blocks = [(z, jnp.where(near, cut, send(cut, hop_y)))] + [
+            (plane, send(block, hop_or_stay))
+            for index, (plane, block, _) in enumerate(chain)
+            if index > 0
         ]
         others = [send(own, to_core) for _, own in qkv_blocks]
 
@@ -345,7 +372,7 @@
         cut = lax.dynamic_slice_in_dim(
             out_weight.T, jnp.where(near, g, g ^ 1) * query_cols, query_cols, 1
         )
-        out_blocks = spread(send(cut, hop_y), attn)
+        out_blocks = spread(jnp.where(near, cut, send(cut, hop_y)), attn)
         groups = [[], [], []]
         for index, (_, own, step) in enumerate(out_blocks):
             other = send(own, to_core)
@@ -360,6 +387,14 @@
             at = 0 if 2 * step < planes else 1
             groups[2 if index == len(out_blocks) - 1 else at].append(part)
         groups = [group for group in groups if group]
+        parts = [part for group in groups for part in group]
+        ahead = []
+        for j, move in enumerate((None, to_y, to_x, to_xy)):
+            at = j * length_rows + group_lengths[j] - 1
+            chosen = jnp.concatenate(
+                [lax.dynamic_slice_in_dim(part, at, 1, 0) for part in parts], axis=0
+            )
+            ahead.append(chosen if move is None else send(chosen, move))
         pieces = []
         for j, move in enumerate((None, to_y, to_x, to_xy)):
             for group in groups:
@@ -376,18 +411,18 @@
             sum(b * (plane == p).astype(jnp.int32) for b, plane in enumerate(counted))
             for p in range(planes)
         ]
-        place = jnp.stack([length, *slots]).astype(jnp.int32)
-        hidden, scored = finish(place, sequence, final_gain, value_head, pieces, len(groups))
-        score = scored[0, 0]
-
+        place = jnp.stack(slots).astype(jnp.int32)
+        hidden = finish(place, sequence, pieces, len(groups))
+        last = lax.dynamic_slice_in_dim(sequence, length - 1, 1, 0).reshape(planes, -1)
+        gained = (final_gain * value_head).reshape(planes, -1)
         total_seqs = fsdp_size * dp_size
+        both = score_rows(place, pair_weight, last, gained, ahead, total_seqs)
+
         index_all = jnp.arange(total_seqs, dtype=jnp.int32)
         mine = f * dp_size + d
-        lane = lax.broadcasted_iota(jnp.int32, (total_seqs, 1, 128), 2)
-        both = jnp.where(lane == 0, score, pair_weight[0])
         gathered = lax.all_to_all(both, AXES, 0, 0, tiled=True)
-        everyone = gathered[:, 0, 0]
-        weights_all = gathered[:, 0, 1]
+        everyone = gathered[:, 0]
+        weights_all = gathered[:, 1]
         matches = partner[:, None] == index_all[None, :]
         others_all = jnp.sum(jnp.where(matches, everyone[None, :], jnp.float32(0.0)), axis=1)
         margins_all = jnp.where(index_all < partner, everyone - others_all, others_all - everyone)

time: 285 us -> 275 us (0.965)
  waiting for transfers between devices: 140 us -> 113 us
  starting transfers between devices: 78.8 us -> 84.8 us
  other arithmetic: 7.42 us -> 13.1 us
  between operations: 4.43 us -> 8.13 us
    ppermute x41 -> x44, waiting for transfers between devices: 133 us -> 113 us  [send(): return lax.ppermute(array, AXES, route(move))]
    all_to_all x1, waiting for transfers between devices: 7.17 us -> 0.3 us  [whole(): gathered = lax.all_to_all(both, AXES, 0, 0, tiled=True)]
    ppermute x41 -> x44, starting transfers between devices: 75.7 us -> 79.9 us  [send(): return lax.ppermute(array, AXES, route(move))]
    pallas_call x1 -> x2, Pallas kernels: 5.73 us -> 5.98 us  [the longest x1 4.3 us: finish(): pl.pallas_call(kernel, name='finish', out_shape=jax.ShapeDtypeStruct((row...]
  transfers between devices with their start and end apart: 42 -> 45, of which waited for: 12 -> 15; matrix products, arithmetic and copies ran while one was open for 12% -> 16% of each run, Pallas kernels for 4% -> 5%
where the time goes in v4:
time: 275 us; the launch traced here: 273 us
  waiting for transfers between devices  113 us (41%)
  starting transfers between devices  84.8 us (31%)
  matrix products  22.5 us (8%)
  Pallas kernels  18.2 us (7%)
  other arithmetic  13.1 us (5%)
  local copies, waits for them, and re-layouts  13 us (5%)
  between operations  8.13 us (3%)
    ppermute x44, waiting for transfers between devices, send(): return lax.ppermute(array, AXES, route(move))  113 us
    ppermute x44, starting transfers between devices, send(): return lax.ppermute(array, AXES, route(move))  79.9 us
    dot_general x10, matrix products, whole(): jnp.dot(lax.dynamic_index_in_dim(normed, jnp.maximum(plane, 0) * 2 + core...  13.7 us
    dot_general x5, matrix products, whole(): lax.dot_general(attn, weights, (((1,), (1,)), ((), ())), preferred_elemen...  8.77 us
    pallas_call x1, Pallas kernels, normalise(): pl.pallas_call(norm_kernel, name='normalise', out_shape=jax.ShapeDtypeStr...  6.51 us
    pallas_call x1, Pallas kernels, attend(): pl.pallas_call(kernel, name='attention', out_shape=jax.ShapeDtypeStruct((...  5.72 us
  transfers between devices with their start and end apart: 45, of which 15 were waited for; matrix products, arithmetic and copies ran while one was open for 16% of the time, Pallas kernels for 5%

profile of v4, /device:TPU:0, one launch (start us, length us, event | category | flops | bytes accessed | tf_op | source)
XLA Modules:
  0.0 272.9 jit_solution(3716451996523799722)
XLA Ops:
  4.9 4.3 %collective-permute-start = (bf16[128,3584]{1,0:T(8,128)(2,1)S(1)}, bf16[128,3584]{1,0:T(8,128)(2,1)}, u32[]{:S(2)}, u32[]{:S(2)}) collective-permute-start(bf16[128,3584]{1,0:T(8,128)(2,1)S(1)} %bitcast.118), channel_id=1, source_target_pairs={{0,4},{1,5},{2,6},{3,7},{4,0},{5,1},{6,2},{7,3},{8,12},{9,13},{10,... | collective-permute-start | bytes 2752520 | tf_op jit(solution)/shard_map/ppermute | solution.py:242
  9.1 4.5 %collective-permute-start.8 = (bf16[448,1152]{1,0:T(8,128)(2,1)}, bf16[448,1152]{1,0:T(8,128)(2,1)}, u32[]{:S(2)}, u32[]{:S(2)}) collective-permute-start(bf16[448,1152]{1,0:T(8,128)(2,1)} %pad_maximum_fusion), channel_id=1, source_target_pairs={{0,8},{1,9},{2,10},{3,11},{4,12},{5,13},{6,14},{7,15},{8,16},{9,17... | collective-permute-start | bytes 3096584 | tf_op jit(solution)/shard_map/ppermute | solution.py:242
  16.6 2.1 dynamic-slice_bitcast_fusion
  18.6 23.0 %collective-permute-done.3 = s32[1]{0:T(128)} collective-permute-done((s32[1]{0:T(128)}, s32[1]{0:T(128)}, u32[]{:S(2)}, u32[]{:S(2)}) %collective-permute-start.3) | collective-permute-done | bytes 36 | tf_op jit(solution)/shard_map/ppermute | solution.py:242
  41.7 1.5 collective-permute-start.4
  43.2 2.3 collective-permute-done.4
  45.8 4.4 %collective-permute-done.5 = s32[1]{0:T(128)} collective-permute-done((s32[1]{0:T(128)}, s32[1]{0:T(128)}, u32[]{:S(2)}, u32[]{:S(2)}) %collective-permute-start.5) | collective-permute-done | bytes 36 | tf_op jit(solution)/shard_map/ppermute | solution.py:242
  50.2 1.5 collective-permute-start.1
  52.3 1.6 collective-permute-start.21
  58.1 1.6 collective-permute-start.14
  61.3 3.4 %collective-permute-start.7 = (bf16[448,1152]{1,0:T(8,128)(2,1)S(1)}, bf16[448,1152]{1,0:T(8,128)(2,1)}, u32[]{:S(2)}, u32[]{:S(2)}) collective-permute-start(bf16[448,1152]{1,0:T(8,128)(2,1)S(1)} %broadcast_select_fusion.1), channel_id=1, source_target_pairs={{0,1},{1,0},{2,3},{3,2},{4,5},{5,4},{6,7},{7,6},{8,9},{9,8},{10,11... | collective-permute-start | bytes 3096584 | tf_op jit(solution)/shard_map/ppermute | solution.py:242
  64.8 8.8 %collective-permute-done.1.by_x_ref = bf16[128,3584]{1,0:T(8,128)(2,1)} collective-permute-done((bf16[128,3584]{1,0:T(8,128)(2,1)S(1)}, bf16[128,3584]{1,0:T(8,128)(2,1)}, u32[]{:S(2)}, u32[]{:S(2)}) %collective-permute-start.1) | collective-permute-done | bytes 917536 | tf_op jit(solution)/shard_map/ppermute | solution.py:242
  73.5 9.4 %collective-permute-start.9 = (bf16[448,1152]{1,0:T(8,128)(2,1)}, bf16[448,1152]{1,0:T(8,128)(2,1)}, u32[]{:S(2)}, u32[]{:S(2)}) collective-permute-start(bf16[448,1152]{1,0:T(8,128)(2,1)} %collective-permute-done.8), channel_id=1, source_target_pairs={{0,0},{1,4},{2,2},{3,6},{4,1},{5,5},{6,3},{7,7},{8,8},{9,12},{10,1... | collective-permute-start | bytes 3096584 | tf_op jit(solution)/shard_map/ppermute | solution.py:242
  82.9 6.1 %collective-permute-done.2.far_ref = bf16[128,3584]{1,0:T(8,128)(2,1)} collective-permute-done((bf16[128,3584]{1,0:T(8,128)(2,1)}, bf16[128,3584]{1,0:T(8,128)(2,1)}, u32[]{:S(2)}, u32[]{:S(2)}) %collective-permute-start.2) | collective-permute-done | bytes 917536 | tf_op jit(solution)/shard_map/ppermute | solution.py:242
  89.1 9.4 %collective-permute-start.12 = (bf16[448,1152]{1,0:T(8,128)(2,1)}, bf16[448,1152]{1,0:T(8,128)(2,1)}, u32[]{:S(2)}, u32[]{:S(2)}) collective-permute-start(bf16[448,1152]{1,0:T(8,128)(2,1)} %collective-permute-done.11), channel_id=1, source_target_pairs={{0,0},{1,4},{2,2},{3,6},{4,1},{5,5},{6,3},{7,7},{8,8},{9,12},{10,1... | collective-permute-start | bytes 3096584 | tf_op jit(solution)/shard_map/ppermute | solution.py:242
  99.3 1.3 broadcast_select_fusion.3
  100.6 6.5 %normalise.1 = bf16[8,512,448]{2,1,0:T(8,128)(2,1)} custom-call(bf16[128,3584]{1,0:T(8,128)(2,1)} %bitcast.116, bf16[128,3584]{1,0:T(8,128)(2,1)} %collective-permute-done.by_y_ref, bf16[128,3584]{1,0:T(8,128)(2,1)} %collective-permute-done.1.by_x_ref, bf16[128,3584]{1,0:T(8,128)(2,1)} %collective-permute-done.2.far_ref, f32[1,3584]{1,0:T(1,128)} %reshape.64.gain_ref), custom_call_target="tpu_custom_call" | custom-call | flops 14680064 | bytes 7340032 | tf_op jit(solution)/shard_map/normalise/pallas_call | solution.py:135
  107.1 2.4 add_bitcast_fusion.refs_0_
  109.5 3.5 %collective-permute-start.23 = (bf16[448,896]{1,0:T(8,128)(2,1)S(1)}, bf16[448,896]{1,0:T(8,128)(2,1)S(1)}, u32[]{:S(2)}, u32[]{:S(2)}) collective-permute-start(bf16[448,896]{1,0:T(8,128)(2,1)S(1)} %broadcast_select_fusion.3), channel_id=1, source_target_pairs={{0,8},{1,9},{2,10},{3,11},{4,12},{5,13},{6,14},{7,15},{8,16},{9,17... | collective-permute-start | bytes 2408456 | tf_op jit(solution)/shard_map/ppermute | solution.py:242
  113.1 1.5 broadcast_select_fusion
  115.5 1.3 collective-permute-start.18
  117.4 2.2 fusion.54
  120.5 2.1 convolution_add_fusion.4
  122.5 15.3 %collective-permute-done.18 = bf16[448,1152]{1,0:T(8,128)(2,1)S(1)} collective-permute-done((bf16[448,1152]{1,0:T(8,128)(2,1)S(1)}, bf16[448,1152]{1,0:T(8,128)(2,1)S(1)}, u32[]{:S(2)}, u32[]{:S(2)}) %collective-permute-start.18) | collective-permute-done | bytes 1032224 | tf_op jit(solution)/shard_map/ppermute | solution.py:242
  138.5 2.1 fusion.50
  140.6 1.5 collective-permute-start.24
  142.1 2.6 collective-permute-start.17
  146.5 7.2 %collective-permute-start.20 = (bf16[448,1152]{1,0:T(8,128)(2,1)S(1)}, bf16[448,1152]{1,0:T(8,128)(2,1)S(1)}, u32[]{:S(2)}, u32[]{:S(2)}) collective-permute-start(bf16[448,1152]{1,0:T(8,128)(2,1)S(1)} %collective-permute-done.19), channel_id=1, source_target_pairs={{0,1},{1,0},{2,3},{3,2},{4,5},{5,4},{6,7},{7,6},{8,9},{9,8},{10,11... | collective-permute-start | bytes 3096584 | tf_op jit(solution)/shard_map/ppermute | solution.py:242
  156.3 2.3 convolution_add_fusion.refs_1_
  158.6 5.7 %attention.1 = bf16[512,896]{1,0:T(8,128)(2,1)} custom-call(s32[4]{0:T(128)} %add_bitcast_fusion.refs_0_, f32[512,1152]{1,0:T(8,128)} %convolution_add_fusion.refs_1_, f32[1,1152]{1,0:T(1,128)} %reshape.65.refs_2_, f32[128,128]{1,0:T(8,128)} %get-tuple-element.66.refs_3_, f32[128,128]{1,0:T(8,128)} %get-tuple-element.67.refs_4_), custom_call_target="tpu_custom_call" | custom-call | flops 1879048192 | bytes 3276800 | tf_op jit(solution)/shard_map/attention/pallas_call | solution.py:90
  166.0 1.3 collective-permute-start.28
  172.0 2.4 fusion.42
  174.6 20.5 %collective-permute-done.28 = bf16[448,896]{1,0:T(8,128)(2,1)S(1)} collective-permute-done((bf16[448,896]{1,0:T(8,128)(2,1)}, bf16[448,896]{1,0:T(8,128)(2,1)S(1)}, u32[]{:S(2)}, u32[]{:S(2)}) %collective-permute-start.28) | collective-permute-done | bytes 802848 | tf_op jit(solution)/shard_map/ppermute | solution.py:242
  195.2 1.6 collective-permute-start.30
  197.0 2.6 fusion.40
  202.0 1.9 collective-permute-start.38
  206.1 10.2 %collective-permute-done.30 = bf16[448,896]{1,0:T(8,128)(2,1)S(1)} collective-permute-done((bf16[448,896]{1,0:T(8,128)(2,1)S(1)}, bf16[448,896]{1,0:T(8,128)(2,1)S(1)}, u32[]{:S(2)}, u32[]{:S(2)}) %collective-permute-start.30) | collective-permute-done | bytes 802848 | tf_op jit(solution)/shard_map/ppermute | solution.py:242
  217.2 2.0 collective-permute-start.32
  224.6 11.6 %collective-permute-done.43.refs_3_ = bf16[5,896]{1,0:T(8,128)(2,1)S(1)} collective-permute-done((bf16[5,896]{1,0:T(8,128)(2,1)S(1)}, bf16[5,896]{1,0:T(8,128)(2,1)S(1)}, u32[]{:S(2)}, u32[]{:S(2)}) %collective-permute-start.43) | collective-permute-done | bytes 8992 | tf_op jit(solution)/shard_map/ppermute | solution.py:242
  236.2 1.7 collective-permute-start.41
  240.7 1.7 score.1
  242.4 4.9 %all-to-all-start = ((f32[32,1,128]{2,1,0:T(1,128)}), f32[32,1,128]{2,1,0:T(1,128)S(1)}, u32[]{:S(2)}, u32[]{:S(2)}) async-start(f32[32,1,128]{2,1,0:T(1,128)} %bitcast.122), calls=%async_computation | async-start | bytes 32768 | tf_op jit(solution)/shard_map/all_to_all | solution.py:423
  248.1 2.7 collective-permute-start.39
  251.6 2.7 collective-permute-start.40
  256.3 1.4 collective-permute-done.39.refs_12_
  257.6 4.8 %collective-permute-done.34.refs_7_ = bf16[1,128,896]{2,1,0:T(8,128)(2,1)S(1)} collective-permute-done((bf16[1,128,896]{2,1,0:T(8,128)(2,1)S(1)}, bf16[1,128,896]{2,1,0:T(8,128)(2,1)S(1)}, u32[]{:S(2)}, u32[]{:S(2)}) %collective-permute-start.34) | collective-permute-done | bytes 229408 | tf_op jit(solution)/shard_map/ppermute | solution.py:242
  262.8 4.0 %collective-permute-done.40.refs_13_ = bf16[1,128,896]{2,1,0:T(8,128)(2,1)S(1)} collective-permute-done((bf16[1,128,896]{2,1,0:T(8,128)(2,1)S(1)}, bf16[1,128,896]{2,1,0:T(8,128)(2,1)S(1)}, u32[]{:S(2)}, u32[]{:S(2)}) %collective-permute-start.40) | collective-permute-done | bytes 229408 | tf_op jit(solution)/shard_map/ppermute | solution.py:242
  267.5 4.3 %finish.1 = bf16[128,3584]{1,0:T(8,128)(2,1)} custom-call(s32[4]{0:T(128)} %pad_add_fusion.refs_0_.slots_ref, bf16[128,3584]{1,0:T(8,128)(2,1)} %bitcast.117, bf16[3,128,896]{2,1,0:T(8,128)(2,1)} %pad_maximum_fusion.1.refs_2_, bf16[1,128,896]{2,1,0:T(8,128)(2,1)} %get-tuple-element.48.refs_3_, bf16[1,128,896]{2,1,0:T(8,128)(2,1)} %get-tuple-element.44.refs_4_, ...), custom_call_target="tpu_custom_call" | custom-call | flops 3670016 | bytes 2752512 | tf_op jit(solution)/shard_map/finish/pallas_call | solution.py:172
  (144 shorter events, 41.0 us)
Async XLA Ops:
  2.0 52.6 %copy-start.12 = (f32[3584]{0:T(1024)S(1)}, f32[3584]{0:T(1024)}, u32[]{:S(2)}) copy-start(f32[3584]{0:T(1024)} %param.14) | copy-start | bytes 43012
  2.0 54.5 %copy-start.10 = (f32[3584]{0:T(1024)S(1)}, f32[3584]{0:T(1024)}, u32[]{:S(2)}) copy-start(f32[3584]{0:T(1024)} %param.18) | copy-start | bytes 43012
  2.0 54.4 %copy-start.11 = (f32[3584]{0:T(1024)S(1)}, f32[3584]{0:T(1024)}, u32[]{:S(2)}) copy-start(f32[3584]{0:T(1024)} %param.19) | copy-start | bytes 43012
  4.1 48.1 %collective-permute-start.6 = (bf16[448,1152]{1,0:T(8,128)(2,1)}, bf16[448,1152]{1,0:T(8,128)(2,1)S(1)}, u32[]{:S(2)}, u32[]{:S(2)}) collective-permute-start(bf16[448,1152]{1,0:T(8,128)(2,1)} %pad_maximum_fusion), channel_id=1, source_target_pairs={{1,4},{3,6},{4,1},{6,3},{9,12},{11,14},{12,9},{14,11},{17,20},{19,... | collective-permute-start | bytes 3096584 | tf_op jit(solution)/shard_map/ppermute | solution.py:242
  4.9 46.8 %collective-permute-start = (bf16[128,3584]{1,0:T(8,128)(2,1)S(1)}, bf16[128,3584]{1,0:T(8,128)(2,1)}, u32[]{:S(2)}, u32[]{:S(2)}) collective-permute-start(bf16[128,3584]{1,0:T(8,128)(2,1)S(1)} %bitcast.118), channel_id=1, source_target_pairs={{0,4},{1,5},{2,6},{3,7},{4,0},{5,1},{6,2},{7,3},{8,12},{9,13},{10,... | collective-permute-start | bytes 2752520 | tf_op jit(solution)/shard_map/ppermute | solution.py:242
  9.1 49.0 %collective-permute-start.8 = (bf16[448,1152]{1,0:T(8,128)(2,1)}, bf16[448,1152]{1,0:T(8,128)(2,1)}, u32[]{:S(2)}, u32[]{:S(2)}) collective-permute-start(bf16[448,1152]{1,0:T(8,128)(2,1)} %pad_maximum_fusion), channel_id=1, source_target_pairs={{0,8},{1,9},{2,10},{3,11},{4,12},{5,13},{6,14},{7,15},{8,16},{9,17... | collective-permute-start | bytes 3096584 | tf_op jit(solution)/shard_map/ppermute | solution.py:242
  13.6 46.2 %collective-permute-start.11 = (bf16[448,1152]{1,0:T(8,128)(2,1)}, bf16[448,1152]{1,0:T(8,128)(2,1)}, u32[]{:S(2)}, u32[]{:S(2)}) collective-permute-start(bf16[448,1152]{1,0:T(8,128)(2,1)} %pad_maximum_fusion), channel_id=1, source_target_pairs={{8,0},{9,1},{10,2},{11,3},{12,4},{13,5},{14,6},{15,7},{16,8},{17,9... | collective-permute-start | bytes 3096584 | tf_op jit(solution)/shard_map/ppermute | solution.py:242
  14.9 26.8 %collective-permute-start.3 = (s32[1]{0:T(128)}, s32[1]{0:T(128)}, u32[]{:S(2)}, u32[]{:S(2)}) collective-permute-start(s32[1]{0:T(128)} %param.11), channel_id=1, source_target_pairs={{0,4},{1,5},{2,6},{3,7},{4,0},{5,1},{6,2},{7,3},{8,12},{9,13},{10,... | collective-permute-start | bytes 20 | tf_op jit(solution)/shard_map/ppermute | solution.py:242
  41.7 3.8 %collective-permute-start.4 = (s32[1]{0:T(128)}, s32[1]{0:T(128)}, u32[]{:S(2)}, u32[]{:S(2)}) collective-permute-start(s32[1]{0:T(128)} %param.11), channel_id=1, source_target_pairs={{0,2},{1,3},{2,0},{3,1},{4,6},{5,7},{6,4},{7,5},{8,10},{9,11},{10,... | collective-permute-start | bytes 20 | tf_op jit(solution)/shard_map/ppermute | solution.py:242
  45.5 4.7 %collective-permute-start.5 = (s32[1]{0:T(128)}, s32[1]{0:T(128)}, u32[]{:S(2)}, u32[]{:S(2)}) collective-permute-start(s32[1]{0:T(128)} %param.11), channel_id=1, source_target_pairs={{0,6},{1,7},{2,4},{3,5},{4,2},{5,3},{6,0},{7,1},{8,14},{9,15},{10,... | collective-permute-start | bytes 20 | tf_op jit(solution)/shard_map/ppermute | solution.py:242
  50.2 23.3 %collective-permute-start.1 = (bf16[128,3584]{1,0:T(8,128)(2,1)S(1)}, bf16[128,3584]{1,0:T(8,128)(2,1)}, u32[]{:S(2)}, u32[]{:S(2)}) collective-permute-start(bf16[128,3584]{1,0:T(8,128)(2,1)S(1)} %bitcast.119), channel_id=1, source_target_pairs={{0,2},{1,3},{2,0},{3,1},{4,6},{5,7},{6,4},{7,5},{8,10},{9,11},{10,... | collective-permute-start | bytes 2752520 | tf_op jit(solution)/shard_map/ppermute | solution.py:242
  51.7 37.4 %collective-permute-start.2 = (bf16[128,3584]{1,0:T(8,128)(2,1)}, bf16[128,3584]{1,0:T(8,128)(2,1)}, u32[]{:S(2)}, u32[]{:S(2)}) collective-permute-start(bf16[128,3584]{1,0:T(8,128)(2,1)} %collective-permute-done.by_y_ref), channel_id=1, source_target_pairs={{0,2},{1,3},{2,0},{3,1},{4,6},{5,7},{6,4},{7,5},{8,10},{9,11},{10,... | collective-permute-start | bytes 2752520 | tf_op jit(solution)/shard_map/ppermute | solution.py:242
  52.3 9.1 %collective-permute-start.21 = (bf16[448,896]{1,0:T(8,128)(2,1)}, bf16[448,896]{1,0:T(8,128)(2,1)}, u32[]{:S(2)}, u32[]{:S(2)}) collective-permute-start(bf16[448,896]{1,0:T(8,128)(2,1)} %dynamic-slice_bitcast_fusion), channel_id=1, source_target_pairs={{1,4},{3,6},{4,1},{6,3},{9,12},{11,14},{12,9},{14,11},{17,20},{19,... | collective-permute-start | bytes 2408456 | tf_op jit(solution)/shard_map/ppermute | solution.py:242
  58.1 51.4 %collective-permute-start.14 = (bf16[448,1152]{1,0:T(8,128)(2,1)}, bf16[448,1152]{1,0:T(8,128)(2,1)}, u32[]{:S(2)}, u32[]{:S(2)}) collective-permute-start(bf16[448,1152]{1,0:T(8,128)(2,1)} %collective-permute-done.8), channel_id=1, source_target_pairs={{8,16},{9,17},{10,18},{11,19},{12,20},{13,21},{14,22},{15,23},{16,... | collective-permute-start | bytes 3096584 | tf_op jit(solution)/shard_map/ppermute | solution.py:242
  59.8 53.3 %collective-permute-start.15 = (bf16[448,1152]{1,0:T(8,128)(2,1)}, bf16[448,1152]{1,0:T(8,128)(2,1)}, u32[]{:S(2)}, u32[]{:S(2)}) collective-permute-start(bf16[448,1152]{1,0:T(8,128)(2,1)} %collective-permute-done.11), channel_id=1, source_target_pairs={{8,0},{9,1},{10,2},{11,3},{12,4},{13,5},{14,6},{15,7},{16,8},{17,9... | collective-permute-start | bytes 3096584 | tf_op jit(solution)/shard_map/ppermute | solution.py:242
  61.3 54.1 %collective-permute-start.7 = (bf16[448,1152]{1,0:T(8,128)(2,1)S(1)}, bf16[448,1152]{1,0:T(8,128)(2,1)}, u32[]{:S(2)}, u32[]{:S(2)}) collective-permute-start(bf16[448,1152]{1,0:T(8,128)(2,1)S(1)} %broadcast_select_fusion.1), channel_id=1, source_target_pairs={{0,1},{1,0},{2,3},{3,2},{4,5},{5,4},{6,7},{7,6},{8,9},{9,8},{10,11... | collective-permute-start | bytes 3096584 | tf_op jit(solution)/shard_map/ppermute | solution.py:242
  73.5 43.2 %collective-permute-start.9 = (bf16[448,1152]{1,0:T(8,128)(2,1)}, bf16[448,1152]{1,0:T(8,128)(2,1)}, u32[]{:S(2)}, u32[]{:S(2)}) collective-permute-start(bf16[448,1152]{1,0:T(8,128)(2,1)} %collective-permute-done.8), channel_id=1, source_target_pairs={{0,0},{1,4},{2,2},{3,6},{4,1},{5,5},{6,3},{7,7},{8,8},{9,12},{10,1... | collective-permute-start | bytes 3096584 | tf_op jit(solution)/shard_map/ppermute | solution.py:242
  89.1 27.8 %collective-permute-start.12 = (bf16[448,1152]{1,0:T(8,128)(2,1)}, bf16[448,1152]{1,0:T(8,128)(2,1)}, u32[]{:S(2)}, u32[]{:S(2)}) collective-permute-start(bf16[448,1152]{1,0:T(8,128)(2,1)} %collective-permute-done.11), channel_id=1, source_target_pairs={{0,0},{1,4},{2,2},{3,6},{4,1},{5,5},{6,3},{7,7},{8,8},{9,12},{10,1... | collective-permute-start | bytes 3096584 | tf_op jit(solution)/shard_map/ppermute | solution.py:242
  109.5 54.8 %collective-permute-start.23 = (bf16[448,896]{1,0:T(8,128)(2,1)S(1)}, bf16[448,896]{1,0:T(8,128)(2,1)S(1)}, u32[]{:S(2)}, u32[]{:S(2)}) collective-permute-start(bf16[448,896]{1,0:T(8,128)(2,1)S(1)} %broadcast_select_fusion.3), channel_id=1, source_target_pairs={{0,8},{1,9},{2,10},{3,11},{4,12},{5,13},{6,14},{7,15},{8,16},{9,17... | collective-permute-start | bytes 2408456 | tf_op jit(solution)/shard_map/ppermute | solution.py:242
  114.6 27.5 %collective-permute-start.16 = (bf16[448,1152]{1,0:T(8,128)(2,1)S(1)}, bf16[448,1152]{1,0:T(8,128)(2,1)S(1)}, u32[]{:S(2)}, u32[]{:S(2)}) collective-permute-start(bf16[448,1152]{1,0:T(8,128)(2,1)S(1)} %broadcast_select_fusion), channel_id=1, source_target_pairs={{0,0},{1,4},{2,2},{3,6},{4,1},{5,5},{6,3},{7,7},{8,8},{9,12},{10,1... | collective-permute-start | bytes 3096584 | tf_op jit(solution)/shard_map/ppermute | solution.py:242
  115.5 22.3 %collective-permute-start.18 = (bf16[448,1152]{1,0:T(8,128)(2,1)S(1)}, bf16[448,1152]{1,0:T(8,128)(2,1)S(1)}, u32[]{:S(2)}, u32[]{:S(2)}) collective-permute-start(bf16[448,1152]{1,0:T(8,128)(2,1)S(1)} %broadcast_select_fusion), channel_id=1, source_target_pairs={{8,0},{9,1},{10,2},{11,3},{12,4},{13,5},{14,6},{15,7},{16,24},{17,... | collective-permute-start | bytes 3096584 | tf_op jit(solution)/shard_map/ppermute | solution.py:242
  116.8 23.8 %collective-permute-start.10 = (bf16[448,1152]{1,0:T(8,128)(2,1)}, bf16[448,1152]{1,0:T(8,128)(2,1)S(1)}, u32[]{:S(2)}, u32[]{:S(2)}) collective-permute-start(bf16[448,1152]{1,0:T(8,128)(2,1)} %collective-permute-done.9), channel_id=1, source_target_pairs={{0,1},{1,0},{2,3},{3,2},{4,5},{5,4},{6,7},{7,6},{8,9},{9,8},{10,11... | collective-permute-start | bytes 3096584 | tf_op jit(solution)/shard_map/ppermute | solution.py:242
  116.9 29.5 %collective-permute-start.13 = (bf16[448,1152]{1,0:T(8,128)(2,1)}, bf16[448,1152]{1,0:T(8,128)(2,1)S(1)}, u32[]{:S(2)}, u32[]{:S(2)}) collective-permute-start(bf16[448,1152]{1,0:T(8,128)(2,1)} %collective-permute-done.12), channel_id=1, source_target_pairs={{0,1},{1,0},{2,3},{3,2},{4,5},{5,4},{6,7},{7,6},{8,9},{9,8},{10,11... | collective-permute-start | bytes 3096584 | tf_op jit(solution)/shard_map/ppermute | solution.py:242
  137.8 8.7 %collective-permute-start.19 = (bf16[448,1152]{1,0:T(8,128)(2,1)S(1)}, bf16[448,1152]{1,0:T(8,128)(2,1)S(1)}, u32[]{:S(2)}, u32[]{:S(2)}) collective-permute-start(bf16[448,1152]{1,0:T(8,128)(2,1)S(1)} %collective-permute-done.18), channel_id=1, source_target_pairs={{0,0},{1,4},{2,2},{3,6},{4,1},{5,5},{6,3},{7,7},{8,8},{9,12},{10,1... | collective-permute-start | bytes 3096584 | tf_op jit(solution)/shard_map/ppermute | solution.py:242
  140.6 24.6 %collective-permute-start.24 = (bf16[448,896]{1,0:T(8,128)(2,1)S(1)}, bf16[448,896]{1,0:T(8,128)(2,1)}, u32[]{:S(2)}, u32[]{:S(2)}) collective-permute-start(bf16[448,896]{1,0:T(8,128)(2,1)S(1)} %broadcast_select_fusion.3), channel_id=1, source_target_pairs={{8,0},{9,1},{10,2},{11,3},{12,4},{13,5},{14,6},{15,7},{16,8},{17,9... | collective-permute-start | bytes 2408456 | tf_op jit(solution)/shard_map/ppermute | solution.py:242
  142.1 13.3 %collective-permute-start.17 = (bf16[448,1152]{1,0:T(8,128)(2,1)S(1)}, bf16[448,1152]{1,0:T(8,128)(2,1)S(1)}, u32[]{:S(2)}, u32[]{:S(2)}) collective-permute-start(bf16[448,1152]{1,0:T(8,128)(2,1)S(1)} %collective-permute-done.16), channel_id=1, source_target_pairs={{0,1},{1,0},{2,3},{3,2},{4,5},{5,4},{6,7},{7,6},{8,9},{9,8},{10,11... | collective-permute-start | bytes 3096584 | tf_op jit(solution)/shard_map/ppermute | solution.py:242
  146.4 25.6 %collective-permute-start.22 = (bf16[448,896]{1,0:T(8,128)(2,1)S(1)}, bf16[448,896]{1,0:T(8,128)(2,1)S(1)}, u32[]{:S(2)}, u32[]{:S(2)}) collective-permute-start(bf16[448,896]{1,0:T(8,128)(2,1)S(1)} %broadcast_select_fusion.3), channel_id=1, source_target_pairs={{0,1},{1,0},{2,3},{3,2},{4,5},{5,4},{6,7},{7,6},{8,9},{9,8},{10,11... | collective-permute-start | bytes 2408456 | tf_op jit(solution)/shard_map/ppermute | solution.py:242
  146.5 9.8 %collective-permute-start.20 = (bf16[448,1152]{1,0:T(8,128)(2,1)S(1)}, bf16[448,1152]{1,0:T(8,128)(2,1)S(1)}, u32[]{:S(2)}, u32[]{:S(2)}) collective-permute-start(bf16[448,1152]{1,0:T(8,128)(2,1)S(1)} %collective-permute-done.19), channel_id=1, source_target_pairs={{0,1},{1,0},{2,3},{3,2},{4,5},{5,4},{6,7},{7,6},{8,9},{9,8},{10,11... | collective-permute-start | bytes 3096584 | tf_op jit(solution)/shard_map/ppermute | solution.py:242
  165.2 9.4 %collective-permute-start.27 = (bf16[448,896]{1,0:T(8,128)(2,1)}, bf16[448,896]{1,0:T(8,128)(2,1)S(1)}, u32[]{:S(2)}, u32[]{:S(2)}) collective-permute-start(bf16[448,896]{1,0:T(8,128)(2,1)} %copy-done.17), channel_id=1, source_target_pairs={{8,16},{9,17},{10,18},{11,19},{12,20},{13,21},{14,22},{15,23},{16,... | collective-permute-start | bytes 2408456 | tf_op jit(solution)/shard_map/ppermute | solution.py:242
  166.0 29.2 %collective-permute-start.28 = (bf16[448,896]{1,0:T(8,128)(2,1)}, bf16[448,896]{1,0:T(8,128)(2,1)S(1)}, u32[]{:S(2)}, u32[]{:S(2)}) collective-permute-start(bf16[448,896]{1,0:T(8,128)(2,1)} %collective-permute-done.24), channel_id=1, source_target_pairs={{8,0},{9,1},{10,2},{11,3},{12,4},{13,5},{14,6},{15,7},{16,8},{17,9... | collective-permute-start | bytes 2408456 | tf_op jit(solution)/shard_map/ppermute | solution.py:242
  171.5 25.5 %collective-permute-start.26 = (bf16[448,896]{1,0:T(8,128)(2,1)}, bf16[448,896]{1,0:T(8,128)(2,1)S(1)}, u32[]{:S(2)}, u32[]{:S(2)}) collective-permute-start(bf16[448,896]{1,0:T(8,128)(2,1)} %collective-permute-done.24), channel_id=1, source_target_pairs={{0,1},{1,0},{2,3},{3,2},{4,5},{5,4},{6,7},{7,6},{8,9},{9,8},{10,11... | collective-permute-start | bytes 2408456 | tf_op jit(solution)/shard_map/ppermute | solution.py:242
  171.6 28.0 %collective-permute-start.25 = (bf16[448,896]{1,0:T(8,128)(2,1)}, bf16[448,896]{1,0:T(8,128)(2,1)S(1)}, u32[]{:S(2)}, u32[]{:S(2)}) collective-permute-start(bf16[448,896]{1,0:T(8,128)(2,1)} %copy-done.17), channel_id=1, source_target_pairs={{0,1},{1,0},{2,3},{3,2},{4,5},{5,4},{6,7},{7,6},{8,9},{9,8},{10,11... | collective-permute-start | bytes 2408456 | tf_op jit(solution)/shard_map/ppermute | solution.py:242
  195.2 21.0 %collective-permute-start.30 = (bf16[448,896]{1,0:T(8,128)(2,1)S(1)}, bf16[448,896]{1,0:T(8,128)(2,1)S(1)}, u32[]{:S(2)}, u32[]{:S(2)}) collective-permute-start(bf16[448,896]{1,0:T(8,128)(2,1)S(1)} %broadcast_select_fusion.2), channel_id=1, source_target_pairs={{8,0},{9,1},{10,2},{11,3},{12,4},{13,5},{14,6},{15,7},{16,24},{17,... | collective-permute-start | bytes 2408456 | tf_op jit(solution)/shard_map/ppermute | solution.py:242
  196.9 22.4 %collective-permute-start.29 = (bf16[448,896]{1,0:T(8,128)(2,1)S(1)}, bf16[448,896]{1,0:T(8,128)(2,1)S(1)}, u32[]{:S(2)}, u32[]{:S(2)}) collective-permute-start(bf16[448,896]{1,0:T(8,128)(2,1)S(1)} %broadcast_select_fusion.2), channel_id=1, source_target_pairs={{0,1},{1,0},{2,3},{3,2},{4,5},{5,4},{6,7},{7,6},{8,9},{9,8},{10,11... | collective-permute-start | bytes 2408456 | tf_op jit(solution)/shard_map/ppermute | solution.py:242
  202.0 46.1 %collective-permute-start.38 = (bf16[3,128,896]{2,1,0:T(8,128)(2,1)}, bf16[3,128,896]{2,1,0:T(8,128)(2,1)S(1)}, u32[]{:S(2)}, u32[]{:S(2)}) collective-permute-start(bf16[3,128,896]{2,1,0:T(8,128)(2,1)} %pad_maximum_fusion.4), channel_id=1, source_target_pairs={{0,6},{1,7},{2,4},{3,5},{4,2},{5,3},{6,0},{7,1},{8,14},{9,15},{10,... | collective-permute-start | bytes 2064392 | tf_op jit(solution)/shard_map/ppermute | solution.py:242
  204.9 45.9 %collective-permute-start.35 = (bf16[3,128,896]{2,1,0:T(8,128)(2,1)}, bf16[3,128,896]{2,1,0:T(8,128)(2,1)}, u32[]{:S(2)}, u32[]{:S(2)}) collective-permute-start(bf16[3,128,896]{2,1,0:T(8,128)(2,1)} %pad_maximum_fusion.3), channel_id=1, source_target_pairs={{0,2},{1,3},{2,0},{3,1},{4,6},{5,7},{6,4},{7,5},{8,10},{9,11},{10,... | collective-permute-start | bytes 2064392 | tf_op jit(solution)/shard_map/ppermute | solution.py:242
  216.2 4.4 %collective-permute-start.31 = (bf16[448,896]{1,0:T(8,128)(2,1)S(1)}, bf16[448,896]{1,0:T(8,128)(2,1)S(1)}, u32[]{:S(2)}, u32[]{:S(2)}) collective-permute-start(bf16[448,896]{1,0:T(8,128)(2,1)S(1)} %collective-permute-done.30), channel_id=1, source_target_pairs={{0,1},{1,0},{2,3},{3,2},{4,5},{5,4},{6,7},{7,6},{8,9},{9,8},{10,11... | collective-permute-start | bytes 2408456 | tf_op jit(solution)/shard_map/ppermute | solution.py:242
  217.2 34.2 %collective-permute-start.32 = (bf16[3,128,896]{2,1,0:T(8,128)(2,1)}, bf16[3,128,896]{2,1,0:T(8,128)(2,1)}, u32[]{:S(2)}, u32[]{:S(2)}) collective-permute-start(bf16[3,128,896]{2,1,0:T(8,128)(2,1)} %pad_maximum_fusion.2), channel_id=1, source_target_pairs={{0,4},{1,5},{2,6},{3,7},{4,0},{5,1},{6,2},{7,3},{8,12},{9,13},{10,... | collective-permute-start | bytes 2064392 | tf_op jit(solution)/shard_map/ppermute | solution.py:242
  221.9 14.2 %collective-permute-start.43 = (bf16[5,896]{1,0:T(8,128)(2,1)S(1)}, bf16[5,896]{1,0:T(8,128)(2,1)S(1)}, u32[]{:S(2)}, u32[]{:S(2)}) collective-permute-start(bf16[5,896]{1,0:T(8,128)(2,1)S(1)} %concatenate.71), channel_id=1, source_target_pairs={{0,6},{1,7},{2,4},{3,5},{4,2},{5,3},{6,0},{7,1},{8,14},{9,15},{10,... | collective-permute-start | bytes 26888 | tf_op jit(solution)/shard_map/ppermute | solution.py:242
  223.3 16.0 %collective-permute-start.42 = (bf16[5,896]{1,0:T(8,128)(2,1)S(1)}, bf16[5,896]{1,0:T(8,128)(2,1)S(1)}, u32[]{:S(2)}, u32[]{:S(2)}) collective-permute-start(bf16[5,896]{1,0:T(8,128)(2,1)S(1)} %concatenate.70), channel_id=1, source_target_pairs={{0,2},{1,3},{2,0},{3,1},{4,6},{5,7},{6,4},{7,5},{8,10},{9,11},{10,... | collective-permute-start | bytes 26888 | tf_op jit(solution)/shard_map/ppermute | solution.py:242
  236.2 3.7 %collective-permute-start.41 = (bf16[5,896]{1,0:T(8,128)(2,1)S(1)}, bf16[5,896]{1,0:T(8,128)(2,1)S(1)}, u32[]{:S(2)}, u32[]{:S(2)}) collective-permute-start(bf16[5,896]{1,0:T(8,128)(2,1)S(1)} %concatenate.69), channel_id=1, source_target_pairs={{0,4},{1,5},{2,6},{3,7},{4,0},{5,1},{6,2},{7,3},{8,12},{9,13},{10,... | collective-permute-start | bytes 26888 | tf_op jit(solution)/shard_map/ppermute | solution.py:242
  239.3 12.4 %collective-permute-start.33 = (bf16[1,128,896]{2,1,0:T(8,128)(2,1)S(1)}, bf16[1,128,896]{2,1,0:T(8,128)(2,1)S(1)}, u32[]{:S(2)}, u32[]{:S(2)}) collective-permute-start(bf16[1,128,896]{2,1,0:T(8,128)(2,1)S(1)} %get-tuple-element.47), channel_id=1, source_target_pairs={{0,4},{1,5},{2,6},{3,7},{4,0},{5,1},{6,2},{7,3},{8,12},{9,13},{10,... | collective-permute-start | bytes 688136 | tf_op jit(solution)/shard_map/ppermute | solution.py:242
  239.9 16.4 %collective-permute-start.36 = (bf16[1,128,896]{2,1,0:T(8,128)(2,1)S(1)}, bf16[1,128,896]{2,1,0:T(8,128)(2,1)S(1)}, u32[]{:S(2)}, u32[]{:S(2)}) collective-permute-start(bf16[1,128,896]{2,1,0:T(8,128)(2,1)S(1)} %get-tuple-element.46), channel_id=1, source_target_pairs={{0,2},{1,3},{2,0},{3,1},{4,6},{5,7},{6,4},{7,5},{8,10},{9,11},{10,... | collective-permute-start | bytes 688136 | tf_op jit(solution)/shard_map/ppermute | solution.py:242
  242.4 12.2 %all-to-all-start = ((f32[32,1,128]{2,1,0:T(1,128)}), f32[32,1,128]{2,1,0:T(1,128)S(1)}, u32[]{:S(2)}, u32[]{:S(2)}) async-start(f32[32,1,128]{2,1,0:T(1,128)} %bitcast.122), calls=%async_computation | async-start | bytes 32768 | tf_op jit(solution)/shard_map/all_to_all | solution.py:423
  248.1 9.5 %collective-permute-start.39 = (bf16[1,128,896]{2,1,0:T(8,128)(2,1)S(1)}, bf16[1,128,896]{2,1,0:T(8,128)(2,1)S(1)}, u32[]{:S(2)}, u32[]{:S(2)}) collective-permute-start(bf16[1,128,896]{2,1,0:T(8,128)(2,1)S(1)} %get-tuple-element.45), channel_id=1, source_target_pairs={{0,6},{1,7},{2,4},{3,5},{4,2},{5,3},{6,0},{7,1},{8,14},{9,15},{10,... | collective-permute-start | bytes 688136 | tf_op jit(solution)/shard_map/ppermute | solution.py:242
  250.8 11.7 %collective-permute-start.34 = (bf16[1,128,896]{2,1,0:T(8,128)(2,1)S(1)}, bf16[1,128,896]{2,1,0:T(8,128)(2,1)S(1)}, u32[]{:S(2)}, u32[]{:S(2)}) collective-permute-start(bf16[1,128,896]{2,1,0:T(8,128)(2,1)S(1)} %get-tuple-element.43), channel_id=1, source_target_pairs={{0,4},{1,5},{2,6},{3,7},{4,0},{5,1},{6,2},{7,3},{8,12},{9,13},{10,... | collective-permute-start | bytes 688136 | tf_op jit(solution)/shard_map/ppermute | solution.py:242
  251.4 11.4 %collective-permute-start.37 = (bf16[1,128,896]{2,1,0:T(8,128)(2,1)S(1)}, bf16[1,128,896]{2,1,0:T(8,128)(2,1)S(1)}, u32[]{:S(2)}, u32[]{:S(2)}) collective-permute-start(bf16[1,128,896]{2,1,0:T(8,128)(2,1)S(1)} %get-tuple-element.42), channel_id=1, source_target_pairs={{0,2},{1,3},{2,0},{3,1},{4,6},{5,7},{6,4},{7,5},{8,10},{9,11},{10,... | collective-permute-start | bytes 688136 | tf_op jit(solution)/shard_map/ppermute | solution.py:242
  251.6 15.2 %collective-permute-start.40 = (bf16[1,128,896]{2,1,0:T(8,128)(2,1)S(1)}, bf16[1,128,896]{2,1,0:T(8,128)(2,1)S(1)}, u32[]{:S(2)}, u32[]{:S(2)}) collective-permute-start(bf16[1,128,896]{2,1,0:T(8,128)(2,1)S(1)} %get-tuple-element.41), channel_id=1, source_target_pairs={{0,6},{1,7},{2,4},{3,5},{4,2},{5,3},{6,0},{7,1},{8,14},{9,15},{10,... | collective-permute-start | bytes 688136 | tf_op jit(solution)/shard_map/ppermute | solution.py:242
  (17 other events, 148.0 us)

commit v5 on v4

--- a/solution.py
+++ b/solution.py
@@ -256,9 +256,6 @@
     def hop_y(z, y, x, c):
         return (z, 1 - y, x, 1 - c) if c != y else None
 
-    def hop_or_stay(z, y, x, c):
-        return hop_y(z, y, x, c) or (z, y, x, c)
-
     def along(shift, holds):
         def move(z, y, x, c):
             return (z + shift, y, x, c) if holds(z) and 0 <= z + shift < planes else None
@@ -336,10 +333,9 @@
 
         cut = group_slices(qkv_weight, jnp.where(near, g, g ^ 1), 1)
         chain = spread(cut)
-        qkv_blocks = [(z, jnp.where(near, cut, send(cut, hop_y)))] + [
-            (plane, send(block, hop_or_stay))
-            for index, (plane, block, _) in enumerate(chain)
-            if index > 0
+        qkv_blocks = [
+            (plane, jnp.where(near, block, send(block, hop_y)))
+            for plane, block, _ in chain
         ]
         others = [send(own, to_core) for _, own in qkv_blocks]
 
@@ -372,7 +368,9 @@
         cut = lax.dynamic_slice_in_dim(
             out_weight.T, jnp.where(near, g, g ^ 1) * query_cols, query_cols, 1
         )
-        out_blocks = spread(jnp.where(near, cut, send(cut, hop_y)), attn)
+        hopped = send(cut, hop_y)
+        kept = jnp.where(near, cut, hopped)
+        out_blocks = spread(kept, attn)
         groups = [[], [], []]
         for index, (_, own, step) in enumerate(out_blocks):
             other = send(own, to_core)
@@ -391,9 +389,8 @@
         ahead = []
         for j, move in enumerate((None, to_y, to_x, to_xy)):
             at = j * length_rows + group_lengths[j] - 1
-            chosen = jnp.concatenate(
-                [lax.dynamic_slice_in_dim(part, at, 1, 0) for part in parts], axis=0
-            )
+            rows = [lax.dynamic_slice_in_dim(part, at, 1, 0) for part in parts]
+            chosen = jnp.concatenate(rows, axis=0)
             ahead.append(chosen if move is None else send(chosen, move))
         pieces = []
         for j, move in enumerate((None, to_y, to_x, to_xy)):

time: 275 us -> 255 us (0.927)
  waiting for transfers between devices: 113 us -> 65.8 us
  starting transfers between devices: 84.8 us -> 109 us
  other arithmetic: 13.1 us -> 17.3 us
    ppermute x44, waiting for transfers between devices: 113 us -> 65.5 us  [send(): return lax.ppermute(array, AXES, route(move))]
    ppermute x44, starting transfers between devices: 79.9 us -> 104 us  [send(): return lax.ppermute(array, AXES, route(move))]
    select_n x2 -> x6, other arithmetic: 1.59 us -> 5.86 us  [the longest x5 3.63 us: whole(): jnp.where(near, block, send(block, hop_y))]
    dot_general x10, matrix products: 13.7 us -> 10 us  [whole(): jnp.dot(lax.dynamic_index_in_dim(normed, jnp.maximum(plane, 0) * 2 + core...]
  transfers between devices with their start and end apart: 45 -> 45, of which waited for: 15 -> 13; matrix products, arithmetic and copies ran while one was open for 16% -> 18% of each run, Pallas kernels for 5% -> 5%
where the time goes in v5:
time: 255 us; the launch traced here: 254 us
  starting transfers between devices  109 us (43%)
  waiting for transfers between devices  65.8 us (26%)
  matrix products  20.2 us (8%)
  Pallas kernels  18.2 us (7%)
  other arithmetic  17.3 us (7%)
  local copies, waits for them, and re-layouts  14 us (5%)
  between operations  8.64 us (3%)
    ppermute x44, starting transfers between devices, send(): return lax.ppermute(array, AXES, route(move))  104 us
    ppermute x44, waiting for transfers between devices, send(): return lax.ppermute(array, AXES, route(move))  65.5 us
    dot_general x5, matrix products, whole(): lax.dot_general(attn, weights, (((1,), (1,)), ((), ())), preferred_elemen...  10.2 us
    dot_general x10, matrix products, whole(): jnp.dot(lax.dynamic_index_in_dim(normed, jnp.maximum(plane, 0) * 2 + core...  10 us
    pallas_call x1, Pallas kernels, normalise(): pl.pallas_call(norm_kernel, name='normalise', out_shape=jax.ShapeDtypeStr...  6.5 us
    pallas_call x1, Pallas kernels, attend(): pl.pallas_call(kernel, name='attention', out_shape=jax.ShapeDtypeStruct((...  5.72 us
  transfers between devices with their start and end apart: 45, of which 13 were waited for; matrix products, arithmetic and copies ran while one was open for 18% of the time, Pallas kernels for 5%

profile of v5, /device:TPU:0, one launch (start us, length us, event | category | flops | bytes accessed | tf_op | source)
XLA Modules:
  0.0 253.5 jit_solution(6861225637252530802)
XLA Ops:
  4.1 5.9 %collective-permute-start.8 = (bf16[448,1152]{1,0:T(8,128)(2,1)}, bf16[448,1152]{1,0:T(8,128)(2,1)}, u32[]{:S(2)}, u32[]{:S(2)}) collective-permute-start(bf16[448,1152]{1,0:T(8,128)(2,1)} %pad_maximum_fusion), channel_id=1, source_target_pairs={{0,8},{1,9},{2,10},{3,11},{4,12},{5,13},{6,14},{7,15},{8,16},{9,17... | collective-permute-start | bytes 3096584 | tf_op jit(solution)/shard_map/ppermute | solution.py:242
  11.4 1.6 collective-permute-start
  12.9 2.1 dynamic-slice_bitcast_fusion
  15.0 1.6 collective-permute-start.21
  23.3 1.6 collective-permute-start.1
  24.9 8.8 %collective-permute-done.by_y_ref = bf16[128,3584]{1,0:T(8,128)(2,1)} collective-permute-done((bf16[128,3584]{1,0:T(8,128)(2,1)S(1)}, bf16[128,3584]{1,0:T(8,128)(2,1)}, u32[]{:S(2)}, u32[]{:S(2)}) %collective-permute-start) | collective-permute-done | bytes 917536 | tf_op jit(solution)/shard_map/ppermute | solution.py:242
  33.7 1.5 collective-permute-start.2
  35.2 1.6 collective-permute-start.14
  36.8 1.3 collective-permute-start.15
  38.9 2.2 broadcast_select_fusion.7
  42.1 1.6 collective-permute-start.9
  45.0 15.2 %collective-permute-start.3 = (s32[1]{0:T(128)}, s32[1]{0:T(128)}, u32[]{:S(2)}, u32[]{:S(2)}) collective-permute-start(s32[1]{0:T(128)} %param.11), channel_id=1, source_target_pairs={{0,4},{1,5},{2,6},{3,7},{4,0},{5,1},{6,2},{7,3},{8,12},{9,13},{10,... | collective-permute-start | bytes 20 | tf_op jit(solution)/shard_map/ppermute | solution.py:242
  60.1 1.5 collective-permute-start.4
  61.6 6.5 %normalise.1 = bf16[8,512,448]{2,1,0:T(8,128)(2,1)} custom-call(bf16[128,3584]{1,0:T(8,128)(2,1)} %bitcast.116, bf16[128,3584]{1,0:T(8,128)(2,1)} %collective-permute-done.by_y_ref, bf16[128,3584]{1,0:T(8,128)(2,1)} %copy-done.3, bf16[128,3584]{1,0:T(8,128)(2,1)} %collective-permute-done.2.far_ref, f32[1,3584]{1,0:T(1,128)} %reshape.64.gain_ref), custom_call_target="tpu_custom_call" | custom-call | flops 14680064 | bytes 7340032 | tf_op jit(solution)/shard_map/normalise/pallas_call | solution.py:135
  68.1 2.5 collective-permute-done.3
  70.6 4.2 %collective-permute-start.5 = (s32[1]{0:T(128)}, s32[1]{0:T(128)}, u32[]{:S(2)}, u32[]{:S(2)}) collective-permute-start(s32[1]{0:T(128)} %param.11), channel_id=1, source_target_pairs={{0,6},{1,7},{2,4},{3,5},{4,2},{5,3},{6,0},{7,1},{8,14},{9,15},{10,... | collective-permute-start | bytes 20 | tf_op jit(solution)/shard_map/ppermute | solution.py:242
  74.8 5.2 %collective-permute-start.23 = (bf16[448,896]{1,0:T(8,128)(2,1)S(1)}, bf16[448,896]{1,0:T(8,128)(2,1)}, u32[]{:S(2)}, u32[]{:S(2)}) collective-permute-start(bf16[448,896]{1,0:T(8,128)(2,1)S(1)} %copy-done.4), channel_id=1, source_target_pairs={{0,8},{1,9},{2,10},{3,11},{4,12},{5,13},{6,14},{7,15},{8,16},{9,17... | collective-permute-start | bytes 2408456 | tf_op jit(solution)/shard_map/ppermute | solution.py:242
  81.2 2.6 %add_bitcast_fusion.refs_0_ = s32[4]{0:T(128)} fusion(s32[1,1]{0,1:T(1,128)} %bitcast.8, s32[1,1]{0,1:T(1,128)} %bitcast.7, s32[1,1]{0,1:T(1,128)} %bitcast.6, s32[1,1]{0,1:T(1,128)} %bitcast.115), kind=kLoop, calls=%fused_computation.165 | loop fusion | flops 12 | bytes 32 | tf_op jit(solution)/shard_map/squeeze | solution.py:348
  84.6 1.4 broadcast_select_fusion
  86.8 1.7 broadcast_select_fusion.4
  88.5 1.3 collective-permute-start.18
  89.8 1.4 broadcast_select_fusion.3
  91.3 11.2 %collective-permute-start.10 = (bf16[448,1152]{1,0:T(8,128)(2,1)S(1)}, bf16[448,1152]{1,0:T(8,128)(2,1)S(1)}, u32[]{:S(2)}, u32[]{:S(2)}) collective-permute-start(bf16[448,1152]{1,0:T(8,128)(2,1)S(1)} %broadcast_select_fusion.4), channel_id=1, source_target_pairs={{0,1},{1,0},{2,3},{3,2},{4,5},{5,4},{6,7},{7,6},{8,9},{9,8},{10,11... | collective-permute-start | bytes 3096584 | tf_op jit(solution)/shard_map/ppermute | solution.py:242
  104.2 7.7 %collective-permute-start.13 = (bf16[448,1152]{1,0:T(8,128)(2,1)S(1)}, bf16[448,1152]{1,0:T(8,128)(2,1)S(1)}, u32[]{:S(2)}, u32[]{:S(2)}) collective-permute-start(bf16[448,1152]{1,0:T(8,128)(2,1)S(1)} %broadcast_select_fusion.3), channel_id=1, source_target_pairs={{0,1},{1,0},{2,3},{3,2},{4,5},{5,4},{6,7},{7,6},{8,9},{9,8},{10,11... | collective-permute-start | bytes 3096584 | tf_op jit(solution)/shard_map/ppermute | solution.py:242
  112.1 7.7 %collective-permute-done.18 = bf16[448,1152]{1,0:T(8,128)(2,1)S(1)} collective-permute-done((bf16[448,1152]{1,0:T(8,128)(2,1)S(1)}, bf16[448,1152]{1,0:T(8,128)(2,1)S(1)}, u32[]{:S(2)}, u32[]{:S(2)}) %collective-permute-start.18) | collective-permute-done | bytes 1032224 | tf_op jit(solution)/shard_map/ppermute | solution.py:242
  123.2 16.2 %collective-permute-start.22 = (bf16[448,896]{1,0:T(8,128)(2,1)S(1)}, bf16[448,896]{1,0:T(8,128)(2,1)S(1)}, u32[]{:S(2)}, u32[]{:S(2)}) collective-permute-start(bf16[448,896]{1,0:T(8,128)(2,1)S(1)} %copy-done.4), channel_id=1, source_target_pairs={{0,1},{1,0},{2,3},{3,2},{4,5},{5,4},{6,7},{7,6},{8,9},{9,8},{10,11... | collective-permute-start | bytes 2408456 | tf_op jit(solution)/shard_map/ppermute | solution.py:242
  143.6 2.3 fusion.3.refs_1_
  145.9 5.7 %attention.1 = bf16[512,896]{1,0:T(8,128)(2,1)} custom-call(s32[4]{0:T(128)} %add_bitcast_fusion.refs_0_, f32[512,1152]{1,0:T(8,128)} %fusion.3.refs_1_, f32[1,1152]{1,0:T(1,128)} %reshape.65.refs_2_, f32[128,128]{1,0:T(8,128)} %get-tuple-element.66.refs_3_, f32[128,128]{1,0:T(8,128)} %get-tuple-element.67.refs_4_), custom_call_target="tpu_custom_call" | custom-call | flops 1879048192 | bytes 3276800 | tf_op jit(solution)/shard_map/attention/pallas_call | solution.py:90
  152.3 1.3 collective-permute-start.28
  158.8 2.4 fusion.44
  161.3 13.3 %collective-permute-done.28 = bf16[448,896]{1,0:T(8,128)(2,1)S(1)} collective-permute-done((bf16[448,896]{1,0:T(8,128)(2,1)}, bf16[448,896]{1,0:T(8,128)(2,1)S(1)}, u32[]{:S(2)}, u32[]{:S(2)}) %collective-permute-start.28) | collective-permute-done | bytes 802848 | tf_op jit(solution)/shard_map/ppermute | solution.py:242
  174.7 1.5 collective-permute-start.30
  176.3 2.6 %fusion.42 = bf16[512,896]{1,0:T(8,128)(2,1)S(1)} fusion(bf16[512,896]{1,0:T(8,128)(2,1)S(1)} %copy-done.19, bf16[448,896]{1,0:T(8,128)(2,1)S(1)} %collective-permute-done.26, bf16[448,896]{1,0:T(8,128)(2,1)} %collective-permute-done.24, pred[]{:T(512)S(6)} %eq.97), kind=kOutput, calls=%fused_computation.51 | convolution fusion | flops 829767680 | bytes 3440641 | tf_op jit(solution)/shard_map/dot_general | solution.py:382
  179.0 2.7 %fusion.43 = bf16[512,896]{1,0:T(8,128)(2,1)S(1)} fusion(bf16[512,896]{1,0:T(8,128)(2,1)S(1)} %copy-done.19, bf16[448,896]{1,0:T(8,128)(2,1)S(1)} %collective-permute-done.25, bf16[448,896]{1,0:T(8,128)(2,1)} %collective-permute-done.23, pred[]{:T(512)S(6)} %eq.97), kind=kOutput, calls=%fused_computation.52 | convolution fusion | flops 829767680 | bytes 3440641 | tf_op jit(solution)/shard_map/dot_general | solution.py:382
  182.8 1.4 collective-permute-start.38
  185.2 1.5 collective-permute-start.35
  186.6 9.3 %collective-permute-done.30 = bf16[448,896]{1,0:T(8,128)(2,1)S(1)} collective-permute-done((bf16[448,896]{1,0:T(8,128)(2,1)S(1)}, bf16[448,896]{1,0:T(8,128)(2,1)S(1)}, u32[]{:S(2)}, u32[]{:S(2)}) %collective-permute-start.30) | collective-permute-done | bytes 802848 | tf_op jit(solution)/shard_map/ppermute | solution.py:242
  202.7 1.5 collective-permute-start.42
  204.3 12.6 %collective-permute-done.43.refs_3_ = bf16[5,896]{1,0:T(8,128)(2,1)S(1)} collective-permute-done((bf16[5,896]{1,0:T(8,128)(2,1)S(1)}, bf16[5,896]{1,0:T(8,128)(2,1)S(1)}, u32[]{:S(2)}, u32[]{:S(2)}) %collective-permute-start.43) | collective-permute-done | bytes 8992 | tf_op jit(solution)/shard_map/ppermute | solution.py:242
  216.9 1.5 collective-permute-start.41
  221.2 1.7 score.1
  222.9 5.0 %all-to-all-start = ((f32[32,1,128]{2,1,0:T(1,128)}), f32[32,1,128]{2,1,0:T(1,128)S(1)}, u32[]{:S(2)}, u32[]{:S(2)}) async-start(f32[32,1,128]{2,1,0:T(1,128)} %bitcast.122), calls=%async_computation | async-start | bytes 32768 | tf_op jit(solution)/shard_map/all_to_all | solution.py:420
  228.7 2.7 %collective-permute-start.39 = (bf16[1,128,896]{2,1,0:T(8,128)(2,1)S(1)}, bf16[1,128,896]{2,1,0:T(8,128)(2,1)S(1)}, u32[]{:S(2)}, u32[]{:S(2)}) collective-permute-start(bf16[1,128,896]{2,1,0:T(8,128)(2,1)S(1)} %get-tuple-element.45), channel_id=1, source_target_pairs={{0,6},{1,7},{2,4},{3,5},{4,2},{5,3},{6,0},{7,1},{8,14},{9,15},{10,... | collective-permute-start | bytes 688136 | tf_op jit(solution)/shard_map/ppermute | solution.py:242
  232.2 2.7 %collective-permute-start.40 = (bf16[1,128,896]{2,1,0:T(8,128)(2,1)S(1)}, bf16[1,128,896]{2,1,0:T(8,128)(2,1)S(1)}, u32[]{:S(2)}, u32[]{:S(2)}) collective-permute-start(bf16[1,128,896]{2,1,0:T(8,128)(2,1)S(1)} %get-tuple-element.41), channel_id=1, source_target_pairs={{0,6},{1,7},{2,4},{3,5},{4,2},{5,3},{6,0},{7,1},{8,14},{9,15},{10,... | collective-permute-start | bytes 688136 | tf_op jit(solution)/shard_map/ppermute | solution.py:242
  236.9 1.4 collective-permute-done.39.refs_12_
  238.2 4.8 %collective-permute-done.34.refs_7_ = bf16[1,128,896]{2,1,0:T(8,128)(2,1)S(1)} collective-permute-done((bf16[1,128,896]{2,1,0:T(8,128)(2,1)S(1)}, bf16[1,128,896]{2,1,0:T(8,128)(2,1)S(1)}, u32[]{:S(2)}, u32[]{:S(2)}) %collective-permute-start.34) | collective-permute-done | bytes 229408 | tf_op jit(solution)/shard_map/ppermute | solution.py:242
  243.4 4.0 %collective-permute-done.40.refs_13_ = bf16[1,128,896]{2,1,0:T(8,128)(2,1)S(1)} collective-permute-done((bf16[1,128,896]{2,1,0:T(8,128)(2,1)S(1)}, bf16[1,128,896]{2,1,0:T(8,128)(2,1)S(1)}, u32[]{:S(2)}, u32[]{:S(2)}) %collective-permute-start.40) | collective-permute-done | bytes 229408 | tf_op jit(solution)/shard_map/ppermute | solution.py:242
  248.1 4.3 %finish.1 = bf16[128,3584]{1,0:T(8,128)(2,1)} custom-call(s32[4]{0:T(128)} %pad_add_fusion.refs_0_.slots_ref, bf16[128,3584]{1,0:T(8,128)(2,1)} %bitcast.117, bf16[3,128,896]{2,1,0:T(8,128)(2,1)} %pad_maximum_fusion.1.refs_2_, bf16[1,128,896]{2,1,0:T(8,128)(2,1)} %get-tuple-element.48.refs_3_, bf16[1,128,896]{2,1,0:T(8,128)(2,1)} %get-tuple-element.44.refs_4_, ...), custom_call_target="tpu_custom_call" | custom-call | flops 3670016 | bytes 2752512 | tf_op jit(solution)/shard_map/finish/pallas_call | solution.py:172
  (148 shorter events, 42.9 us)
Async XLA Ops:
  2.0 19.6 %copy-start.12 = (f32[3584]{0:T(1024)S(1)}, f32[3584]{0:T(1024)}, u32[]{:S(2)}) copy-start(f32[3584]{0:T(1024)} %param.18) | copy-start | bytes 43012
  4.1 31.1 %collective-permute-start.8 = (bf16[448,1152]{1,0:T(8,128)(2,1)}, bf16[448,1152]{1,0:T(8,128)(2,1)}, u32[]{:S(2)}, u32[]{:S(2)}) collective-permute-start(bf16[448,1152]{1,0:T(8,128)(2,1)} %pad_maximum_fusion), channel_id=1, source_target_pairs={{0,8},{1,9},{2,10},{3,11},{4,12},{5,13},{6,14},{7,15},{8,16},{9,17... | collective-permute-start | bytes 3096584 | tf_op jit(solution)/shard_map/ppermute | solution.py:242
  10.1 26.8 %collective-permute-start.11 = (bf16[448,1152]{1,0:T(8,128)(2,1)}, bf16[448,1152]{1,0:T(8,128)(2,1)}, u32[]{:S(2)}, u32[]{:S(2)}) collective-permute-start(bf16[448,1152]{1,0:T(8,128)(2,1)} %pad_maximum_fusion), channel_id=1, source_target_pairs={{8,0},{9,1},{10,2},{11,3},{12,4},{13,5},{14,6},{15,7},{16,8},{17,9... | collective-permute-start | bytes 3096584 | tf_op jit(solution)/shard_map/ppermute | solution.py:242
  11.4 22.3 %collective-permute-start = (bf16[128,3584]{1,0:T(8,128)(2,1)S(1)}, bf16[128,3584]{1,0:T(8,128)(2,1)}, u32[]{:S(2)}, u32[]{:S(2)}) collective-permute-start(bf16[128,3584]{1,0:T(8,128)(2,1)S(1)} %bitcast.118), channel_id=1, source_target_pairs={{0,4},{1,5},{2,6},{3,7},{4,0},{5,1},{6,2},{7,3},{8,12},{9,13},{10,... | collective-permute-start | bytes 2752520 | tf_op jit(solution)/shard_map/ppermute | solution.py:242
  15.0 8.3 %collective-permute-start.21 = (bf16[448,896]{1,0:T(8,128)(2,1)}, bf16[448,896]{1,0:T(8,128)(2,1)}, u32[]{:S(2)}, u32[]{:S(2)}) collective-permute-start(bf16[448,896]{1,0:T(8,128)(2,1)} %dynamic-slice_bitcast_fusion), channel_id=1, source_target_pairs={{1,4},{3,6},{4,1},{6,3},{9,12},{11,14},{12,9},{14,11},{17,20},{19,... | collective-permute-start | bytes 2408456 | tf_op jit(solution)/shard_map/ppermute | solution.py:242
  16.6 24.5 %collective-permute-start.6 = (bf16[448,1152]{1,0:T(8,128)(2,1)}, bf16[448,1152]{1,0:T(8,128)(2,1)S(1)}, u32[]{:S(2)}, u32[]{:S(2)}) collective-permute-start(bf16[448,1152]{1,0:T(8,128)(2,1)} %pad_maximum_fusion), channel_id=1, source_target_pairs={{1,4},{3,6},{4,1},{6,3},{9,12},{11,14},{12,9},{14,11},{17,20},{19,... | collective-permute-start | bytes 3096584 | tf_op jit(solution)/shard_map/ppermute | solution.py:242
  23.3 20.7 %collective-permute-start.1 = (bf16[128,3584]{1,0:T(8,128)(2,1)S(1)}, bf16[128,3584]{1,0:T(8,128)(2,1)S(1)}, u32[]{:S(2)}, u32[]{:S(2)}) collective-permute-start(bf16[128,3584]{1,0:T(8,128)(2,1)S(1)} %bitcast.119), channel_id=1, source_target_pairs={{0,2},{1,3},{2,0},{3,1},{4,6},{5,7},{6,4},{7,5},{8,10},{9,11},{10,... | collective-permute-start | bytes 2752520 | tf_op jit(solution)/shard_map/ppermute | solution.py:242
  33.7 26.4 %collective-permute-start.2 = (bf16[128,3584]{1,0:T(8,128)(2,1)}, bf16[128,3584]{1,0:T(8,128)(2,1)}, u32[]{:S(2)}, u32[]{:S(2)}) collective-permute-start(bf16[128,3584]{1,0:T(8,128)(2,1)} %collective-permute-done.by_y_ref), channel_id=1, source_target_pairs={{0,2},{1,3},{2,0},{3,1},{4,6},{5,7},{6,4},{7,5},{8,10},{9,11},{10,... | collective-permute-start | bytes 2752520 | tf_op jit(solution)/shard_map/ppermute | solution.py:242
  35.2 48.6 %collective-permute-start.14 = (bf16[448,1152]{1,0:T(8,128)(2,1)}, bf16[448,1152]{1,0:T(8,128)(2,1)}, u32[]{:S(2)}, u32[]{:S(2)}) collective-permute-start(bf16[448,1152]{1,0:T(8,128)(2,1)} %collective-permute-done.8), channel_id=1, source_target_pairs={{8,16},{9,17},{10,18},{11,19},{12,20},{13,21},{14,22},{15,23},{16,... | collective-permute-start | bytes 3096584 | tf_op jit(solution)/shard_map/ppermute | solution.py:242
  36.8 47.0 %collective-permute-start.15 = (bf16[448,1152]{1,0:T(8,128)(2,1)}, bf16[448,1152]{1,0:T(8,128)(2,1)}, u32[]{:S(2)}, u32[]{:S(2)}) collective-permute-start(bf16[448,1152]{1,0:T(8,128)(2,1)} %collective-permute-done.11), channel_id=1, source_target_pairs={{8,0},{9,1},{10,2},{11,3},{12,4},{13,5},{14,6},{15,7},{16,8},{17,9... | collective-permute-start | bytes 3096584 | tf_op jit(solution)/shard_map/ppermute | solution.py:242
  42.1 43.8 %collective-permute-start.9 = (bf16[448,1152]{1,0:T(8,128)(2,1)}, bf16[448,1152]{1,0:T(8,128)(2,1)}, u32[]{:S(2)}, u32[]{:S(2)}) collective-permute-start(bf16[448,1152]{1,0:T(8,128)(2,1)} %collective-permute-done.8), channel_id=1, source_target_pairs={{1,4},{3,6},{4,1},{6,3},{9,12},{11,14},{12,9},{14,11},{17,20},{19,... | collective-permute-start | bytes 3096584 | tf_op jit(solution)/shard_map/ppermute | solution.py:242
  44.0 30.8 %copy-start.4 = (bf16[448,896]{1,0:T(8,128)(2,1)S(1)}, bf16[448,896]{1,0:T(8,128)(2,1)}, u32[]{:S(2)}) copy-start(bf16[448,896]{1,0:T(8,128)(2,1)} %broadcast_select_fusion.7) | copy-start | bytes 2408452
  45.0 25.6 %collective-permute-start.3 = (s32[1]{0:T(128)}, s32[1]{0:T(128)}, u32[]{:S(2)}, u32[]{:S(2)}) collective-permute-start(s32[1]{0:T(128)} %param.11), channel_id=1, source_target_pairs={{0,4},{1,5},{2,6},{3,7},{4,0},{5,1},{6,2},{7,3},{8,12},{9,13},{10,... | collective-permute-start | bytes 20 | tf_op jit(solution)/shard_map/ppermute | solution.py:242
  60.1 14.7 %collective-permute-start.4 = (s32[1]{0:T(128)}, s32[1]{0:T(128)}, u32[]{:S(2)}, u32[]{:S(2)}) collective-permute-start(s32[1]{0:T(128)} %param.11), channel_id=1, source_target_pairs={{0,2},{1,3},{2,0},{3,1},{4,6},{5,7},{6,4},{7,5},{8,10},{9,11},{10,... | collective-permute-start | bytes 20 | tf_op jit(solution)/shard_map/ppermute | solution.py:242
  70.6 9.4 %collective-permute-start.5 = (s32[1]{0:T(128)}, s32[1]{0:T(128)}, u32[]{:S(2)}, u32[]{:S(2)}) collective-permute-start(s32[1]{0:T(128)} %param.11), channel_id=1, source_target_pairs={{0,6},{1,7},{2,4},{3,5},{4,2},{5,3},{6,0},{7,1},{8,14},{9,15},{10,... | collective-permute-start | bytes 20 | tf_op jit(solution)/shard_map/ppermute | solution.py:242
  74.8 76.8 %collective-permute-start.23 = (bf16[448,896]{1,0:T(8,128)(2,1)S(1)}, bf16[448,896]{1,0:T(8,128)(2,1)}, u32[]{:S(2)}, u32[]{:S(2)}) collective-permute-start(bf16[448,896]{1,0:T(8,128)(2,1)S(1)} %copy-done.4), channel_id=1, source_target_pairs={{0,8},{1,9},{2,10},{3,11},{4,12},{5,13},{6,14},{7,15},{8,16},{9,17... | collective-permute-start | bytes 2408456 | tf_op jit(solution)/shard_map/ppermute | solution.py:242
  79.9 71.7 %collective-permute-start.24 = (bf16[448,896]{1,0:T(8,128)(2,1)S(1)}, bf16[448,896]{1,0:T(8,128)(2,1)}, u32[]{:S(2)}, u32[]{:S(2)}) collective-permute-start(bf16[448,896]{1,0:T(8,128)(2,1)S(1)} %copy-done.4), channel_id=1, source_target_pairs={{8,0},{9,1},{10,2},{11,3},{12,4},{13,5},{14,6},{15,7},{16,8},{17,9... | collective-permute-start | bytes 2408456 | tf_op jit(solution)/shard_map/ppermute | solution.py:242
  83.8 7.4 %collective-permute-start.7 = (bf16[448,1152]{1,0:T(8,128)(2,1)S(1)}, bf16[448,1152]{1,0:T(8,128)(2,1)S(1)}, u32[]{:S(2)}, u32[]{:S(2)}) collective-permute-start(bf16[448,1152]{1,0:T(8,128)(2,1)S(1)} %broadcast_select_fusion.5), channel_id=1, source_target_pairs={{0,1},{1,0},{2,3},{3,2},{4,5},{5,4},{6,7},{7,6},{8,9},{9,8},{10,11... | collective-permute-start | bytes 3096584 | tf_op jit(solution)/shard_map/ppermute | solution.py:242
  83.8 4.7 %collective-permute-start.12 = (bf16[448,1152]{1,0:T(8,128)(2,1)}, bf16[448,1152]{1,0:T(8,128)(2,1)S(1)}, u32[]{:S(2)}, u32[]{:S(2)}) collective-permute-start(bf16[448,1152]{1,0:T(8,128)(2,1)} %collective-permute-done.11), channel_id=1, source_target_pairs={{1,4},{3,6},{4,1},{6,3},{9,12},{11,14},{12,9},{14,11},{17,20},{19,... | collective-permute-start | bytes 3096584 | tf_op jit(solution)/shard_map/ppermute | solution.py:242
  85.9 18.2 %collective-permute-start.16 = (bf16[448,1152]{1,0:T(8,128)(2,1)S(1)}, bf16[448,1152]{1,0:T(8,128)(2,1)S(1)}, u32[]{:S(2)}, u32[]{:S(2)}) collective-permute-start(bf16[448,1152]{1,0:T(8,128)(2,1)S(1)} %broadcast_select_fusion), channel_id=1, source_target_pairs={{1,4},{3,6},{4,1},{6,3},{9,12},{11,14},{12,9},{14,11},{17,20},{19,... | collective-permute-start | bytes 3096584 | tf_op jit(solution)/shard_map/ppermute | solution.py:242
  88.5 31.2 %collective-permute-start.18 = (bf16[448,1152]{1,0:T(8,128)(2,1)S(1)}, bf16[448,1152]{1,0:T(8,128)(2,1)S(1)}, u32[]{:S(2)}, u32[]{:S(2)}) collective-permute-start(bf16[448,1152]{1,0:T(8,128)(2,1)S(1)} %broadcast_select_fusion), channel_id=1, source_target_pairs={{8,0},{9,1},{10,2},{11,3},{12,4},{13,5},{14,6},{15,7},{16,24},{17,... | collective-permute-start | bytes 3096584 | tf_op jit(solution)/shard_map/ppermute | solution.py:242
  91.3 20.7 %collective-permute-start.10 = (bf16[448,1152]{1,0:T(8,128)(2,1)S(1)}, bf16[448,1152]{1,0:T(8,128)(2,1)S(1)}, u32[]{:S(2)}, u32[]{:S(2)}) collective-permute-start(bf16[448,1152]{1,0:T(8,128)(2,1)S(1)} %broadcast_select_fusion.4), channel_id=1, source_target_pairs={{0,1},{1,0},{2,3},{3,2},{4,5},{5,4},{6,7},{7,6},{8,9},{9,8},{10,11... | collective-permute-start | bytes 3096584 | tf_op jit(solution)/shard_map/ppermute | solution.py:242
  104.2 35.3 %collective-permute-start.13 = (bf16[448,1152]{1,0:T(8,128)(2,1)S(1)}, bf16[448,1152]{1,0:T(8,128)(2,1)S(1)}, u32[]{:S(2)}, u32[]{:S(2)}) collective-permute-start(bf16[448,1152]{1,0:T(8,128)(2,1)S(1)} %broadcast_select_fusion.3), channel_id=1, source_target_pairs={{0,1},{1,0},{2,3},{3,2},{4,5},{5,4},{6,7},{7,6},{8,9},{9,8},{10,11... | collective-permute-start | bytes 3096584 | tf_op jit(solution)/shard_map/ppermute | solution.py:242
  112.0 28.4 %collective-permute-start.17 = (bf16[448,1152]{1,0:T(8,128)(2,1)S(1)}, bf16[448,1152]{1,0:T(8,128)(2,1)S(1)}, u32[]{:S(2)}, u32[]{:S(2)}) collective-permute-start(bf16[448,1152]{1,0:T(8,128)(2,1)S(1)} %broadcast_select_fusion.2), channel_id=1, source_target_pairs={{0,1},{1,0},{2,3},{3,2},{4,5},{5,4},{6,7},{7,6},{8,9},{9,8},{10,11... | collective-permute-start | bytes 3096584 | tf_op jit(solution)/shard_map/ppermute | solution.py:242
  119.7 3.5 %collective-permute-start.19 = (bf16[448,1152]{1,0:T(8,128)(2,1)S(1)}, bf16[448,1152]{1,0:T(8,128)(2,1)S(1)}, u32[]{:S(2)}, u32[]{:S(2)}) collective-permute-start(bf16[448,1152]{1,0:T(8,128)(2,1)S(1)} %collective-permute-done.18), channel_id=1, source_target_pairs={{1,4},{3,6},{4,1},{6,3},{9,12},{11,14},{12,9},{14,11},{17,20},{19,... | collective-permute-start | bytes 3096584 | tf_op jit(solution)/shard_map/ppermute | solution.py:242
  123.2 35.6 %collective-permute-start.22 = (bf16[448,896]{1,0:T(8,128)(2,1)S(1)}, bf16[448,896]{1,0:T(8,128)(2,1)S(1)}, u32[]{:S(2)}, u32[]{:S(2)}) collective-permute-start(bf16[448,896]{1,0:T(8,128)(2,1)S(1)} %copy-done.4), channel_id=1, source_target_pairs={{0,1},{1,0},{2,3},{3,2},{4,5},{5,4},{6,7},{7,6},{8,9},{9,8},{10,11... | collective-permute-start | bytes 2408456 | tf_op jit(solution)/shard_map/ppermute | solution.py:242
  139.5 3.3 %collective-permute-start.20 = (bf16[448,1152]{1,0:T(8,128)(2,1)S(1)}, bf16[448,1152]{1,0:T(8,128)(2,1)S(1)}, u32[]{:S(2)}, u32[]{:S(2)}) collective-permute-start(bf16[448,1152]{1,0:T(8,128)(2,1)S(1)} %broadcast_select_fusion.1), channel_id=1, source_target_pairs={{0,1},{1,0},{2,3},{3,2},{4,5},{5,4},{6,7},{7,6},{8,9},{9,8},{10,11... | collective-permute-start | bytes 3096584 | tf_op jit(solution)/shard_map/ppermute | solution.py:242
  151.6 9.7 %collective-permute-start.27 = (bf16[448,896]{1,0:T(8,128)(2,1)}, bf16[448,896]{1,0:T(8,128)(2,1)S(1)}, u32[]{:S(2)}, u32[]{:S(2)}) collective-permute-start(bf16[448,896]{1,0:T(8,128)(2,1)} %collective-permute-done.23), channel_id=1, source_target_pairs={{8,16},{9,17},{10,18},{11,19},{12,20},{13,21},{14,22},{15,23},{16,... | collective-permute-start | bytes 2408456 | tf_op jit(solution)/shard_map/ppermute | solution.py:242
  152.3 22.3 %collective-permute-start.28 = (bf16[448,896]{1,0:T(8,128)(2,1)}, bf16[448,896]{1,0:T(8,128)(2,1)S(1)}, u32[]{:S(2)}, u32[]{:S(2)}) collective-permute-start(bf16[448,896]{1,0:T(8,128)(2,1)} %collective-permute-done.24), channel_id=1, source_target_pairs={{8,0},{9,1},{10,2},{11,3},{12,4},{13,5},{14,6},{15,7},{16,8},{17,9... | collective-permute-start | bytes 2408456 | tf_op jit(solution)/shard_map/ppermute | solution.py:242
  158.2 18.1 %collective-permute-start.26 = (bf16[448,896]{1,0:T(8,128)(2,1)}, bf16[448,896]{1,0:T(8,128)(2,1)S(1)}, u32[]{:S(2)}, u32[]{:S(2)}) collective-permute-start(bf16[448,896]{1,0:T(8,128)(2,1)} %collective-permute-done.24), channel_id=1, source_target_pairs={{0,1},{1,0},{2,3},{3,2},{4,5},{5,4},{6,7},{7,6},{8,9},{9,8},{10,11... | collective-permute-start | bytes 2408456 | tf_op jit(solution)/shard_map/ppermute | solution.py:242
  158.6 20.3 %collective-permute-start.25 = (bf16[448,896]{1,0:T(8,128)(2,1)}, bf16[448,896]{1,0:T(8,128)(2,1)S(1)}, u32[]{:S(2)}, u32[]{:S(2)}) collective-permute-start(bf16[448,896]{1,0:T(8,128)(2,1)} %collective-permute-done.23), channel_id=1, source_target_pairs={{0,1},{1,0},{2,3},{3,2},{4,5},{5,4},{6,7},{7,6},{8,9},{9,8},{10,11... | collective-permute-start | bytes 2408456 | tf_op jit(solution)/shard_map/ppermute | solution.py:242
  174.7 21.2 %collective-permute-start.30 = (bf16[448,896]{1,0:T(8,128)(2,1)S(1)}, bf16[448,896]{1,0:T(8,128)(2,1)S(1)}, u32[]{:S(2)}, u32[]{:S(2)}) collective-permute-start(bf16[448,896]{1,0:T(8,128)(2,1)S(1)} %broadcast_select_fusion.6), channel_id=1, source_target_pairs={{8,0},{9,1},{10,2},{11,3},{12,4},{13,5},{14,6},{15,7},{16,24},{17,... | collective-permute-start | bytes 2408456 | tf_op jit(solution)/shard_map/ppermute | solution.py:242
  176.2 21.9 %collective-permute-start.29 = (bf16[448,896]{1,0:T(8,128)(2,1)S(1)}, bf16[448,896]{1,0:T(8,128)(2,1)S(1)}, u32[]{:S(2)}, u32[]{:S(2)}) collective-permute-start(bf16[448,896]{1,0:T(8,128)(2,1)S(1)} %broadcast_select_fusion.6), channel_id=1, source_target_pairs={{0,1},{1,0},{2,3},{3,2},{4,5},{5,4},{6,7},{7,6},{8,9},{9,8},{10,11... | collective-permute-start | bytes 2408456 | tf_op jit(solution)/shard_map/ppermute | solution.py:242
  182.8 46.0 %collective-permute-start.38 = (bf16[3,128,896]{2,1,0:T(8,128)(2,1)}, bf16[3,128,896]{2,1,0:T(8,128)(2,1)S(1)}, u32[]{:S(2)}, u32[]{:S(2)}) collective-permute-start(bf16[3,128,896]{2,1,0:T(8,128)(2,1)} %pad_maximum_fusion.4), channel_id=1, source_target_pairs={{0,6},{1,7},{2,4},{3,5},{4,2},{5,3},{6,0},{7,1},{8,14},{9,15},{10,... | collective-permute-start | bytes 2064392 | tf_op jit(solution)/shard_map/ppermute | solution.py:242
  185.2 46.2 %collective-permute-start.35 = (bf16[3,128,896]{2,1,0:T(8,128)(2,1)}, bf16[3,128,896]{2,1,0:T(8,128)(2,1)}, u32[]{:S(2)}, u32[]{:S(2)}) collective-permute-start(bf16[3,128,896]{2,1,0:T(8,128)(2,1)} %pad_maximum_fusion.3), channel_id=1, source_target_pairs={{0,2},{1,3},{2,0},{3,1},{4,6},{5,7},{6,4},{7,5},{8,10},{9,11},{10,... | collective-permute-start | bytes 2064392 | tf_op jit(solution)/shard_map/ppermute | solution.py:242
  195.9 3.6 %collective-permute-start.31 = (bf16[448,896]{1,0:T(8,128)(2,1)S(1)}, bf16[448,896]{1,0:T(8,128)(2,1)S(1)}, u32[]{:S(2)}, u32[]{:S(2)}) collective-permute-start(bf16[448,896]{1,0:T(8,128)(2,1)S(1)} %collective-permute-done.30), channel_id=1, source_target_pairs={{0,1},{1,0},{2,3},{3,2},{4,5},{5,4},{6,7},{7,6},{8,9},{9,8},{10,11... | collective-permute-start | bytes 2408456 | tf_op jit(solution)/shard_map/ppermute | solution.py:242
  196.9 35.1 %collective-permute-start.32 = (bf16[3,128,896]{2,1,0:T(8,128)(2,1)}, bf16[3,128,896]{2,1,0:T(8,128)(2,1)}, u32[]{:S(2)}, u32[]{:S(2)}) collective-permute-start(bf16[3,128,896]{2,1,0:T(8,128)(2,1)} %pad_maximum_fusion.2), channel_id=1, source_target_pairs={{0,4},{1,5},{2,6},{3,7},{4,0},{5,1},{6,2},{7,3},{8,12},{9,13},{10,... | collective-permute-start | bytes 2064392 | tf_op jit(solution)/shard_map/ppermute | solution.py:242
  200.8 16.1 %collective-permute-start.43 = (bf16[5,896]{1,0:T(8,128)(2,1)S(1)}, bf16[5,896]{1,0:T(8,128)(2,1)S(1)}, u32[]{:S(2)}, u32[]{:S(2)}) collective-permute-start(bf16[5,896]{1,0:T(8,128)(2,1)S(1)} %concatenate.71), channel_id=1, source_target_pairs={{0,6},{1,7},{2,4},{3,5},{4,2},{5,3},{6,0},{7,1},{8,14},{9,15},{10,... | collective-permute-start | bytes 26888 | tf_op jit(solution)/shard_map/ppermute | solution.py:242
  201.7 33.7 %copy-start.18 = (s32[32]{0:T(128)S(1)}, s32[32]{0:T(128)}, u32[]{:S(2)}) copy-start(s32[32]{0:T(128)} %param.12) | copy-start | bytes 388
  202.7 17.1 %collective-permute-start.42 = (bf16[5,896]{1,0:T(8,128)(2,1)S(1)}, bf16[5,896]{1,0:T(8,128)(2,1)S(1)}, u32[]{:S(2)}, u32[]{:S(2)}) collective-permute-start(bf16[5,896]{1,0:T(8,128)(2,1)S(1)} %concatenate.70), channel_id=1, source_target_pairs={{0,2},{1,3},{2,0},{3,1},{4,6},{5,7},{6,4},{7,5},{8,10},{9,11},{10,... | collective-permute-start | bytes 26888 | tf_op jit(solution)/shard_map/ppermute | solution.py:242
  216.9 3.7 %collective-permute-start.41 = (bf16[5,896]{1,0:T(8,128)(2,1)S(1)}, bf16[5,896]{1,0:T(8,128)(2,1)S(1)}, u32[]{:S(2)}, u32[]{:S(2)}) collective-permute-start(bf16[5,896]{1,0:T(8,128)(2,1)S(1)} %concatenate.69), channel_id=1, source_target_pairs={{0,4},{1,5},{2,6},{3,7},{4,0},{5,1},{6,2},{7,3},{8,12},{9,13},{10,... | collective-permute-start | bytes 26888 | tf_op jit(solution)/shard_map/ppermute | solution.py:242
  219.8 12.4 %collective-permute-start.33 = (bf16[1,128,896]{2,1,0:T(8,128)(2,1)S(1)}, bf16[1,128,896]{2,1,0:T(8,128)(2,1)S(1)}, u32[]{:S(2)}, u32[]{:S(2)}) collective-permute-start(bf16[1,128,896]{2,1,0:T(8,128)(2,1)S(1)} %get-tuple-element.47), channel_id=1, source_target_pairs={{0,4},{1,5},{2,6},{3,7},{4,0},{5,1},{6,2},{7,3},{8,12},{9,13},{10,... | collective-permute-start | bytes 688136 | tf_op jit(solution)/shard_map/ppermute | solution.py:242
  220.6 16.2 %collective-permute-start.36 = (bf16[1,128,896]{2,1,0:T(8,128)(2,1)S(1)}, bf16[1,128,896]{2,1,0:T(8,128)(2,1)S(1)}, u32[]{:S(2)}, u32[]{:S(2)}) collective-permute-start(bf16[1,128,896]{2,1,0:T(8,128)(2,1)S(1)} %get-tuple-element.46), channel_id=1, source_target_pairs={{0,2},{1,3},{2,0},{3,1},{4,6},{5,7},{6,4},{7,5},{8,10},{9,11},{10,... | collective-permute-start | bytes 688136 | tf_op jit(solution)/shard_map/ppermute | solution.py:242
  222.9 12.3 %all-to-all-start = ((f32[32,1,128]{2,1,0:T(1,128)}), f32[32,1,128]{2,1,0:T(1,128)S(1)}, u32[]{:S(2)}, u32[]{:S(2)}) async-start(f32[32,1,128]{2,1,0:T(1,128)} %bitcast.122), calls=%async_computation | async-start | bytes 32768 | tf_op jit(solution)/shard_map/all_to_all | solution.py:420
  228.7 9.5 %collective-permute-start.39 = (bf16[1,128,896]{2,1,0:T(8,128)(2,1)S(1)}, bf16[1,128,896]{2,1,0:T(8,128)(2,1)S(1)}, u32[]{:S(2)}, u32[]{:S(2)}) collective-permute-start(bf16[1,128,896]{2,1,0:T(8,128)(2,1)S(1)} %get-tuple-element.45), channel_id=1, source_target_pairs={{0,6},{1,7},{2,4},{3,5},{4,2},{5,3},{6,0},{7,1},{8,14},{9,15},{10,... | collective-permute-start | bytes 688136 | tf_op jit(solution)/shard_map/ppermute | solution.py:242
  231.4 11.7 %collective-permute-start.34 = (bf16[1,128,896]{2,1,0:T(8,128)(2,1)S(1)}, bf16[1,128,896]{2,1,0:T(8,128)(2,1)S(1)}, u32[]{:S(2)}, u32[]{:S(2)}) collective-permute-start(bf16[1,128,896]{2,1,0:T(8,128)(2,1)S(1)} %get-tuple-element.43), channel_id=1, source_target_pairs={{0,4},{1,5},{2,6},{3,7},{4,0},{5,1},{6,2},{7,3},{8,12},{9,13},{10,... | collective-permute-start | bytes 688136 | tf_op jit(solution)/shard_map/ppermute | solution.py:242
  232.0 11.4 %collective-permute-start.37 = (bf16[1,128,896]{2,1,0:T(8,128)(2,1)S(1)}, bf16[1,128,896]{2,1,0:T(8,128)(2,1)S(1)}, u32[]{:S(2)}, u32[]{:S(2)}) collective-permute-start(bf16[1,128,896]{2,1,0:T(8,128)(2,1)S(1)} %get-tuple-element.42), channel_id=1, source_target_pairs={{0,2},{1,3},{2,0},{3,1},{4,6},{5,7},{6,4},{7,5},{8,10},{9,11},{10,... | collective-permute-start | bytes 688136 | tf_op jit(solution)/shard_map/ppermute | solution.py:242
  232.2 15.2 %collective-permute-start.40 = (bf16[1,128,896]{2,1,0:T(8,128)(2,1)S(1)}, bf16[1,128,896]{2,1,0:T(8,128)(2,1)S(1)}, u32[]{:S(2)}, u32[]{:S(2)}) collective-permute-start(bf16[1,128,896]{2,1,0:T(8,128)(2,1)S(1)} %get-tuple-element.41), channel_id=1, source_target_pairs={{0,6},{1,7},{2,4},{3,5},{4,2},{5,3},{6,0},{7,1},{8,14},{9,15},{10,... | collective-permute-start | bytes 688136 | tf_op jit(solution)/shard_map/ppermute | solution.py:242
  (17 other events, 148.3 us)

commit v6 on v5

--- a/solution.py
+++ b/solution.py
@@ -38,9 +38,11 @@
 
 
 def attention_kernel(
-    query_heads, lengths_ref, acc_ref, bias_ref, cos_ref, sin_ref, out_ref
+    query_heads, lengths_refs, acc_ref, bias_ref, cos_ref, sin_ref, out_ref
 ):
-    length = lengths_ref[pl.program_id(0)]
+    length = lengths_refs[0][0]
+    for index in range(1, len(lengths_refs)):
+        length = jnp.where(pl.program_id(0) == index, lengths_refs[index][0], length)
     rows = acc_ref.shape[0]
     cosine = cos_ref[...]
     sine = sin_ref[...]
@@ -85,29 +87,29 @@
     query_cols = query_heads * HEAD_SIZE
 
     def kernel(*refs):
-        attention_kernel(query_heads, *refs)
+        attention_kernel(query_heads, refs[:seq_count], *refs[seq_count:])
 
     return pl.pallas_call(
         kernel,
         name="attention",
         out_shape=jax.ShapeDtypeStruct((total_rows, query_cols), jnp.bfloat16),
         grid_spec=pltpu.PrefetchScalarGridSpec(
-            num_scalar_prefetch=1,
+            num_scalar_prefetch=seq_count,
             grid=(seq_count,),
             in_specs=[
-                pl.BlockSpec((length_rows, width), lambda i, lengths: (i, 0)),
-                pl.BlockSpec((1, width), lambda i, lengths: (0, 0)),
-                pl.BlockSpec((length_rows, HEAD_SIZE), lambda i, lengths: (0, 0)),
-                pl.BlockSpec((length_rows, HEAD_SIZE), lambda i, lengths: (0, 0)),
+                pl.BlockSpec((length_rows, width), lambda i, *lengths: (i, 0)),
+                pl.BlockSpec((1, width), lambda i, *lengths: (0, 0)),
+                pl.BlockSpec((length_rows, HEAD_SIZE), lambda i, *lengths: (0, 0)),
+                pl.BlockSpec((length_rows, HEAD_SIZE), lambda i, *lengths: (0, 0)),
             ],
-            out_specs=pl.BlockSpec((length_rows, query_cols), lambda i, lengths: (i, 0)),
+            out_specs=pl.BlockSpec((length_rows, query_cols), lambda i, *lengths: (i, 0)),
         ),
         cost_estimate=pl.CostEstimate(
             flops=32 * seq_count * query_heads * length_rows * length_rows * HEAD_SIZE,
             bytes_accessed=acc.size * 4 + total_rows * query_cols * 2,
             transcendentals=seq_count * query_heads * length_rows * length_rows,
         ),
-    )(group_lengths, acc, bias_cols.reshape(1, width), *tables)
+    )(*group_lengths, acc, bias_cols.reshape(1, width), *tables)
 
 
 def norm_kernel(own_ref, by_y_ref, by_x_ref, far_ref, gain_ref, out_ref):
@@ -345,7 +347,7 @@
         normed = normalise([sequence, by_y, by_x, far], norm_gain, fsdp_size)
         near_lengths = [send(lengths, to_y), send(lengths, to_x), send(lengths, to_xy)]
         normed, *near_lengths = lax.optimization_barrier((normed, *near_lengths))
-        group_lengths = jnp.stack([lengths, *near_lengths])[:, 0]
+        group_lengths = [lengths, *near_lengths]
         acc = None
         for (plane, own), other in zip(qkv_blocks, others):
             for core, weights in ((c, own), (1 - c, other)):
@@ -388,7 +390,7 @@
         parts = [part for group in groups for part in group]
         ahead = []
         for j, move in enumerate((None, to_y, to_x, to_xy)):
-            at = j * length_rows + group_lengths[j] - 1
+            at = j * length_rows + group_lengths[j][0] - 1
             rows = [lax.dynamic_slice_in_dim(part, at, 1, 0) for part in parts]
             chosen = jnp.concatenate(rows, axis=0)
             ahead.append(chosen if move is None else send(chosen, move))

time: 255 us -> 273 us (1.071)
  waiting for transfers between devices: 65.8 us -> 104 us
  starting transfers between devices: 109 us -> 91 us
    ppermute x44, waiting for transfers between devices: 65.5 us -> 104 us  [send(): return lax.ppermute(array, AXES, route(move))]
    ppermute x44, starting transfers between devices: 104 us -> 86.6 us  [send(): return lax.ppermute(array, AXES, route(move))]
  transfers between devices with their start and end apart: 45 -> 45, of which waited for: 13 -> 15; matrix products, arithmetic and copies ran while one was open for 18% -> 16% of each run, Pallas kernels for 5% -> 6%
where the time goes in v6:
time: 273 us; the launch traced here: 272 us
  waiting for transfers between devices  104 us (38%)
  starting transfers between devices  91 us (33%)
  matrix products  20.2 us (7%)
  Pallas kernels  19.5 us (7%)
  other arithmetic  14.7 us (5%)
  local copies, waits for them, and re-layouts  14 us (5%)
  between operations  8.65 us (3%)
    ppermute x44, waiting for transfers between devices, send(): return lax.ppermute(array, AXES, route(move))  104 us
    ppermute x44, starting transfers between devices, send(): return lax.ppermute(array, AXES, route(move))  86.6 us
    dot_general x5, matrix products, whole(): lax.dot_general(attn, weights, (((1,), (1,)), ((), ())), preferred_elemen...  10.2 us
    dot_general x10, matrix products, whole(): jnp.dot(lax.dynamic_index_in_dim(normed, jnp.maximum(plane, 0) * 2 + core...  10 us
    pallas_call x1, Pallas kernels, attend(): pl.pallas_call(kernel, name='attention', out_shape=jax.ShapeDtypeStruct((...  7 us
    pallas_call x1, Pallas kernels, normalise(): pl.pallas_call(norm_kernel, name='normalise', out_shape=jax.ShapeDtypeStr...  6.5 us
  transfers between devices with their start and end apart: 45, of which 15 were waited for; matrix products, arithmetic and copies ran while one was open for 16% of the time, Pallas kernels for 6%

profile of v6, /device:TPU:0, one launch (start us, length us, event | category | flops | bytes accessed | tf_op | source)
XLA Modules:
  0.0 271.9 jit_solution(15775372109381878213)
XLA Ops:
  4.1 5.9 %collective-permute-start.8 = (bf16[448,1152]{1,0:T(8,128)(2,1)}, bf16[448,1152]{1,0:T(8,128)(2,1)}, u32[]{:S(2)}, u32[]{:S(2)}) collective-permute-start(bf16[448,1152]{1,0:T(8,128)(2,1)} %pad_maximum_fusion), channel_id=1, source_target_pairs={{0,8},{1,9},{2,10},{3,11},{4,12},{5,13},{6,14},{7,15},{8,16},{9,17... | collective-permute-start | bytes 3096584 | tf_op jit(solution)/shard_map/ppermute | solution.py:244
  11.4 1.6 collective-permute-start
  12.9 2.1 dynamic-slice_bitcast_fusion
  15.0 1.6 collective-permute-start.21
  19.9 11.5 %collective-permute-done.8 = bf16[448,1152]{1,0:T(8,128)(2,1)} collective-permute-done((bf16[448,1152]{1,0:T(8,128)(2,1)}, bf16[448,1152]{1,0:T(8,128)(2,1)}, u32[]{:S(2)}, u32[]{:S(2)}) %collective-permute-start.8) | collective-permute-done | bytes 1032224 | tf_op jit(solution)/shard_map/ppermute | solution.py:244
  31.4 1.6 collective-permute-start.14
  33.1 3.5 %collective-permute-done.11 = bf16[448,1152]{1,0:T(8,128)(2,1)} collective-permute-done((bf16[448,1152]{1,0:T(8,128)(2,1)}, bf16[448,1152]{1,0:T(8,128)(2,1)}, u32[]{:S(2)}, u32[]{:S(2)}) %collective-permute-start.11) | collective-permute-done | bytes 1032224 | tf_op jit(solution)/shard_map/ppermute | solution.py:244
  41.2 1.6 collective-permute-start.1
  44.1 2.2 broadcast_select_fusion.7
  47.4 1.6 collective-permute-start.9
  49.2 15.3 %collective-permute-done.1.by_x_ref = bf16[128,3584]{1,0:T(8,128)(2,1)S(1)} collective-permute-done((bf16[128,3584]{1,0:T(8,128)(2,1)S(1)}, bf16[128,3584]{1,0:T(8,128)(2,1)S(1)}, u32[]{:S(2)}, u32[]{:S(2)}) %collective-permute-start.1) | collective-permute-done | bytes 917536 | tf_op jit(solution)/shard_map/ppermute | solution.py:244
  65.4 2.2 collective-permute-start.3
  67.6 16.2 %collective-permute-done.2.far_ref = bf16[128,3584]{1,0:T(8,128)(2,1)} collective-permute-done((bf16[128,3584]{1,0:T(8,128)(2,1)}, bf16[128,3584]{1,0:T(8,128)(2,1)}, u32[]{:S(2)}, u32[]{:S(2)}) %collective-permute-start.2) | collective-permute-done | bytes 917536 | tf_op jit(solution)/shard_map/ppermute | solution.py:244
  83.8 1.5 collective-permute-start.4
  85.3 6.5 %normalise.1 = bf16[8,512,448]{2,1,0:T(8,128)(2,1)} custom-call(bf16[128,3584]{1,0:T(8,128)(2,1)} %bitcast.109, bf16[128,3584]{1,0:T(8,128)(2,1)} %collective-permute-done.by_y_ref, bf16[128,3584]{1,0:T(8,128)(2,1)} %copy-done.3, bf16[128,3584]{1,0:T(8,128)(2,1)} %collective-permute-done.2.far_ref, f32[1,3584]{1,0:T(1,128)} %reshape.52.gain_ref), custom_call_target="tpu_custom_call" | custom-call | flops 14680064 | bytes 7340032 | tf_op jit(solution)/shard_map/normalise/pallas_call | solution.py:137
  91.8 5.5 %collective-permute-start.23 = (bf16[448,896]{1,0:T(8,128)(2,1)S(1)}, bf16[448,896]{1,0:T(8,128)(2,1)}, u32[]{:S(2)}, u32[]{:S(2)}) collective-permute-start(bf16[448,896]{1,0:T(8,128)(2,1)S(1)} %copy-done.4), channel_id=1, source_target_pairs={{0,8},{1,9},{2,10},{3,11},{4,12},{5,13},{6,14},{7,15},{8,16},{9,17... | collective-permute-start | bytes 2408456 | tf_op jit(solution)/shard_map/ppermute | solution.py:244
  97.3 1.3 collective-permute-start.24
  99.4 1.4 broadcast_select_fusion
  101.6 1.7 broadcast_select_fusion.4
  103.4 1.3 collective-permute-start.18
  104.7 1.4 broadcast_select_fusion.3
  106.1 11.2 %collective-permute-start.10 = (bf16[448,1152]{1,0:T(8,128)(2,1)S(1)}, bf16[448,1152]{1,0:T(8,128)(2,1)S(1)}, u32[]{:S(2)}, u32[]{:S(2)}) collective-permute-start(bf16[448,1152]{1,0:T(8,128)(2,1)S(1)} %broadcast_select_fusion.4), channel_id=1, source_target_pairs={{0,1},{1,0},{2,3},{3,2},{4,5},{5,4},{6,7},{7,6},{8,9},{9,8},{10,11... | collective-permute-start | bytes 3096584 | tf_op jit(solution)/shard_map/ppermute | solution.py:244
  119.0 7.7 %collective-permute-start.13 = (bf16[448,1152]{1,0:T(8,128)(2,1)S(1)}, bf16[448,1152]{1,0:T(8,128)(2,1)S(1)}, u32[]{:S(2)}, u32[]{:S(2)}) collective-permute-start(bf16[448,1152]{1,0:T(8,128)(2,1)S(1)} %broadcast_select_fusion.3), channel_id=1, source_target_pairs={{0,1},{1,0},{2,3},{3,2},{4,5},{5,4},{6,7},{7,6},{8,9},{9,8},{10,11... | collective-permute-start | bytes 3096584 | tf_op jit(solution)/shard_map/ppermute | solution.py:244
  126.9 10.8 %collective-permute-done.18 = bf16[448,1152]{1,0:T(8,128)(2,1)S(1)} collective-permute-done((bf16[448,1152]{1,0:T(8,128)(2,1)S(1)}, bf16[448,1152]{1,0:T(8,128)(2,1)S(1)}, u32[]{:S(2)}, u32[]{:S(2)}) %collective-permute-start.18) | collective-permute-done | bytes 1032224 | tf_op jit(solution)/shard_map/ppermute | solution.py:244
  141.2 15.0 %collective-permute-start.22 = (bf16[448,896]{1,0:T(8,128)(2,1)S(1)}, bf16[448,896]{1,0:T(8,128)(2,1)S(1)}, u32[]{:S(2)}, u32[]{:S(2)}) collective-permute-start(bf16[448,896]{1,0:T(8,128)(2,1)S(1)} %copy-done.4), channel_id=1, source_target_pairs={{0,1},{1,0},{2,3},{3,2},{4,5},{5,4},{6,7},{7,6},{8,9},{9,8},{10,11... | collective-permute-start | bytes 2408456 | tf_op jit(solution)/shard_map/ppermute | solution.py:244
  160.4 2.3 fusion.3.refs_4_
  162.7 7.0 %attention.1 = bf16[512,896]{1,0:T(8,128)(2,1)} custom-call(s32[1]{0:T(128)S(6)} %copy.15.refs_0_, s32[1]{0:T(128)} %collective-permute-done.3.refs_1_, s32[1]{0:T(128)} %collective-permute-done.4.refs_2_, s32[1]{0:T(128)} %collective-permute-done.5.refs_3_, f32[512,1152]{1,0:T(8,128)} %fusion.3.refs_4_, f32[1,1152]{1,0:T(1,128)} %reshape.53.refs_5_, ...), custom_call_target="tpu_custom_call" | custom-call | flops 1879048192 | bytes 3276800 | tf_op jit(solution)/shard_map/attention/pallas_call | solution.py:92
  170.4 1.3 collective-permute-start.28
  176.8 2.4 fusion.44
  179.4 13.3 %collective-permute-done.28 = bf16[448,896]{1,0:T(8,128)(2,1)S(1)} collective-permute-done((bf16[448,896]{1,0:T(8,128)(2,1)}, bf16[448,896]{1,0:T(8,128)(2,1)S(1)}, u32[]{:S(2)}, u32[]{:S(2)}) %collective-permute-start.28) | collective-permute-done | bytes 802848 | tf_op jit(solution)/shard_map/ppermute | solution.py:244
  192.8 1.5 collective-permute-start.30
  194.4 2.6 fusion.42
  197.0 2.7 fusion.43
  200.8 2.7 collective-permute-start.38
  205.0 9.0 %collective-permute-done.30 = bf16[448,896]{1,0:T(8,128)(2,1)S(1)} collective-permute-done((bf16[448,896]{1,0:T(8,128)(2,1)S(1)}, bf16[448,896]{1,0:T(8,128)(2,1)S(1)}, u32[]{:S(2)}, u32[]{:S(2)}) %collective-permute-start.30) | collective-permute-done | bytes 802848 | tf_op jit(solution)/shard_map/ppermute | solution.py:244
  214.9 1.5 collective-permute-start.32
  219.2 1.5 collective-permute-start.43
  222.3 12.7 %collective-permute-done.43.refs_3_ = bf16[5,896]{1,0:T(8,128)(2,1)S(1)} collective-permute-done((bf16[5,896]{1,0:T(8,128)(2,1)S(1)}, bf16[5,896]{1,0:T(8,128)(2,1)S(1)}, u32[]{:S(2)}, u32[]{:S(2)}) %collective-permute-start.43) | collective-permute-done | bytes 8992 | tf_op jit(solution)/shard_map/ppermute | solution.py:244
  235.0 1.7 collective-permute-start.41
  238.7 1.5 collective-permute-start.36
  240.2 1.7 score.1
  241.9 4.5 %all-to-all-start = ((f32[32,1,128]{2,1,0:T(1,128)}), f32[32,1,128]{2,1,0:T(1,128)S(1)}, u32[]{:S(2)}, u32[]{:S(2)}) async-start(f32[32,1,128]{2,1,0:T(1,128)} %bitcast.115), calls=%async_computation | async-start | bytes 32768 | tf_op jit(solution)/shard_map/all_to_all | solution.py:422
  247.1 2.7 collective-permute-start.39
  250.6 2.7 collective-permute-start.40
  255.3 1.4 collective-permute-done.39.refs_12_
  256.6 4.8 %collective-permute-done.34.refs_7_ = bf16[1,128,896]{2,1,0:T(8,128)(2,1)S(1)} collective-permute-done((bf16[1,128,896]{2,1,0:T(8,128)(2,1)S(1)}, bf16[1,128,896]{2,1,0:T(8,128)(2,1)S(1)}, u32[]{:S(2)}, u32[]{:S(2)}) %collective-permute-start.34) | collective-permute-done | bytes 229408 | tf_op jit(solution)/shard_map/ppermute | solution.py:244
  261.8 4.0 %collective-permute-done.40.refs_13_ = bf16[1,128,896]{2,1,0:T(8,128)(2,1)S(1)} collective-permute-done((bf16[1,128,896]{2,1,0:T(8,128)(2,1)S(1)}, bf16[1,128,896]{2,1,0:T(8,128)(2,1)S(1)}, u32[]{:S(2)}, u32[]{:S(2)}) %collective-permute-start.40) | collective-permute-done | bytes 229408 | tf_op jit(solution)/shard_map/ppermute | solution.py:244
  266.5 4.3 %finish.1 = bf16[128,3584]{1,0:T(8,128)(2,1)} custom-call(s32[4]{0:T(128)} %pad_add_fusion.refs_0_.slots_ref, bf16[128,3584]{1,0:T(8,128)(2,1)} %bitcast.110, bf16[3,128,896]{2,1,0:T(8,128)(2,1)} %pad_maximum_fusion.1.refs_2_, bf16[1,128,896]{2,1,0:T(8,128)(2,1)} %get-tuple-element.48.refs_3_, bf16[1,128,896]{2,1,0:T(8,128)(2,1)} %get-tuple-element.44.refs_4_, ...), custom_call_target="tpu_custom_call" | custom-call | flops 3670016 | bytes 2752512 | tf_op jit(solution)/shard_map/finish/pallas_call | solution.py:174
  (147 shorter events, 41.8 us)
Async XLA Ops:
  2.0 37.8 %copy-start.12 = (f32[3584]{0:T(1024)S(1)}, f32[3584]{0:T(1024)}, u32[]{:S(2)}) copy-start(f32[3584]{0:T(1024)} %param.18) | copy-start | bytes 43012
  2.0 37.8 %copy-start.13 = (f32[3584]{0:T(1024)S(1)}, f32[3584]{0:T(1024)}, u32[]{:S(2)}) copy-start(f32[3584]{0:T(1024)} %param.19) | copy-start | bytes 43012
  4.1 27.3 %collective-permute-start.8 = (bf16[448,1152]{1,0:T(8,128)(2,1)}, bf16[448,1152]{1,0:T(8,128)(2,1)}, u32[]{:S(2)}, u32[]{:S(2)}) collective-permute-start(bf16[448,1152]{1,0:T(8,128)(2,1)} %pad_maximum_fusion), channel_id=1, source_target_pairs={{0,8},{1,9},{2,10},{3,11},{4,12},{5,13},{6,14},{7,15},{8,16},{9,17... | collective-permute-start | bytes 3096584 | tf_op jit(solution)/shard_map/ppermute | solution.py:244
  10.1 26.5 %collective-permute-start.11 = (bf16[448,1152]{1,0:T(8,128)(2,1)}, bf16[448,1152]{1,0:T(8,128)(2,1)}, u32[]{:S(2)}, u32[]{:S(2)}) collective-permute-start(bf16[448,1152]{1,0:T(8,128)(2,1)} %pad_maximum_fusion), channel_id=1, source_target_pairs={{8,0},{9,1},{10,2},{11,3},{12,4},{13,5},{14,6},{15,7},{16,8},{17,9... | collective-permute-start | bytes 3096584 | tf_op jit(solution)/shard_map/ppermute | solution.py:244
  11.4 31.4 %collective-permute-start = (bf16[128,3584]{1,0:T(8,128)(2,1)S(1)}, bf16[128,3584]{1,0:T(8,128)(2,1)}, u32[]{:S(2)}, u32[]{:S(2)}) collective-permute-start(bf16[128,3584]{1,0:T(8,128)(2,1)S(1)} %bitcast.111), channel_id=1, source_target_pairs={{0,4},{1,5},{2,6},{3,7},{4,0},{5,1},{6,2},{7,3},{8,12},{9,13},{10,... | collective-permute-start | bytes 2752520 | tf_op jit(solution)/shard_map/ppermute | solution.py:244
  15.0 26.2 %collective-permute-start.21 = (bf16[448,896]{1,0:T(8,128)(2,1)}, bf16[448,896]{1,0:T(8,128)(2,1)}, u32[]{:S(2)}, u32[]{:S(2)}) collective-permute-start(bf16[448,896]{1,0:T(8,128)(2,1)} %dynamic-slice_bitcast_fusion), channel_id=1, source_target_pairs={{1,4},{3,6},{4,1},{6,3},{9,12},{11,14},{12,9},{14,11},{17,20},{19,... | collective-permute-start | bytes 2408456 | tf_op jit(solution)/shard_map/ppermute | solution.py:244
  16.6 29.7 %collective-permute-start.6 = (bf16[448,1152]{1,0:T(8,128)(2,1)}, bf16[448,1152]{1,0:T(8,128)(2,1)S(1)}, u32[]{:S(2)}, u32[]{:S(2)}) collective-permute-start(bf16[448,1152]{1,0:T(8,128)(2,1)} %pad_maximum_fusion), channel_id=1, source_target_pairs={{1,4},{3,6},{4,1},{6,3},{9,12},{11,14},{12,9},{14,11},{17,20},{19,... | collective-permute-start | bytes 3096584 | tf_op jit(solution)/shard_map/ppermute | solution.py:244
  31.4 67.1 %collective-permute-start.14 = (bf16[448,1152]{1,0:T(8,128)(2,1)}, bf16[448,1152]{1,0:T(8,128)(2,1)}, u32[]{:S(2)}, u32[]{:S(2)}) collective-permute-start(bf16[448,1152]{1,0:T(8,128)(2,1)} %collective-permute-done.8), channel_id=1, source_target_pairs={{8,16},{9,17},{10,18},{11,19},{12,20},{13,21},{14,22},{15,23},{16,... | collective-permute-start | bytes 3096584 | tf_op jit(solution)/shard_map/ppermute | solution.py:244
  36.5 62.1 %collective-permute-start.15 = (bf16[448,1152]{1,0:T(8,128)(2,1)}, bf16[448,1152]{1,0:T(8,128)(2,1)}, u32[]{:S(2)}, u32[]{:S(2)}) collective-permute-start(bf16[448,1152]{1,0:T(8,128)(2,1)} %collective-permute-done.11), channel_id=1, source_target_pairs={{8,0},{9,1},{10,2},{11,3},{12,4},{13,5},{14,6},{15,7},{16,8},{17,9... | collective-permute-start | bytes 3096584 | tf_op jit(solution)/shard_map/ppermute | solution.py:244
  41.2 23.3 %collective-permute-start.1 = (bf16[128,3584]{1,0:T(8,128)(2,1)S(1)}, bf16[128,3584]{1,0:T(8,128)(2,1)S(1)}, u32[]{:S(2)}, u32[]{:S(2)}) collective-permute-start(bf16[128,3584]{1,0:T(8,128)(2,1)S(1)} %bitcast.112), channel_id=1, source_target_pairs={{0,2},{1,3},{2,0},{3,1},{4,6},{5,7},{6,4},{7,5},{8,10},{9,11},{10,... | collective-permute-start | bytes 2752520 | tf_op jit(solution)/shard_map/ppermute | solution.py:244
  42.8 41.0 %collective-permute-start.2 = (bf16[128,3584]{1,0:T(8,128)(2,1)}, bf16[128,3584]{1,0:T(8,128)(2,1)}, u32[]{:S(2)}, u32[]{:S(2)}) collective-permute-start(bf16[128,3584]{1,0:T(8,128)(2,1)} %collective-permute-done.by_y_ref), channel_id=1, source_target_pairs={{0,2},{1,3},{2,0},{3,1},{4,6},{5,7},{6,4},{7,5},{8,10},{9,11},{10,... | collective-permute-start | bytes 2752520 | tf_op jit(solution)/shard_map/ppermute | solution.py:244
  47.4 53.4 %collective-permute-start.9 = (bf16[448,1152]{1,0:T(8,128)(2,1)}, bf16[448,1152]{1,0:T(8,128)(2,1)}, u32[]{:S(2)}, u32[]{:S(2)}) collective-permute-start(bf16[448,1152]{1,0:T(8,128)(2,1)} %collective-permute-done.8), channel_id=1, source_target_pairs={{1,4},{3,6},{4,1},{6,3},{9,12},{11,14},{12,9},{14,11},{17,20},{19,... | collective-permute-start | bytes 3096584 | tf_op jit(solution)/shard_map/ppermute | solution.py:244
  49.2 42.6 %copy-start.4 = (bf16[448,896]{1,0:T(8,128)(2,1)S(1)}, bf16[448,896]{1,0:T(8,128)(2,1)}, u32[]{:S(2)}) copy-start(bf16[448,896]{1,0:T(8,128)(2,1)} %broadcast_select_fusion.7) | copy-start | bytes 2408452
  65.4 26.3 %collective-permute-start.3 = (s32[1]{0:T(128)}, s32[1]{0:T(128)}, u32[]{:S(2)}, u32[]{:S(2)}) collective-permute-start(s32[1]{0:T(128)} %param.11), channel_id=1, source_target_pairs={{0,4},{1,5},{2,6},{3,7},{4,0},{5,1},{6,2},{7,3},{8,12},{9,13},{10,... | collective-permute-start | bytes 20 | tf_op jit(solution)/shard_map/ppermute | solution.py:244
  83.8 8.0 %collective-permute-start.4 = (s32[1]{0:T(128)}, s32[1]{0:T(128)}, u32[]{:S(2)}, u32[]{:S(2)}) collective-permute-start(s32[1]{0:T(128)} %param.11), channel_id=1, source_target_pairs={{0,2},{1,3},{2,0},{3,1},{4,6},{5,7},{6,4},{7,5},{8,10},{9,11},{10,... | collective-permute-start | bytes 20 | tf_op jit(solution)/shard_map/ppermute | solution.py:244
  91.8 5.5 %collective-permute-start.5 = (s32[1]{0:T(128)}, s32[1]{0:T(128)}, u32[]{:S(2)}, u32[]{:S(2)}) collective-permute-start(s32[1]{0:T(128)} %param.11), channel_id=1, source_target_pairs={{0,6},{1,7},{2,4},{3,5},{4,2},{5,3},{6,0},{7,1},{8,14},{9,15},{10,... | collective-permute-start | bytes 20 | tf_op jit(solution)/shard_map/ppermute | solution.py:244
  91.8 77.9 %collective-permute-start.23 = (bf16[448,896]{1,0:T(8,128)(2,1)S(1)}, bf16[448,896]{1,0:T(8,128)(2,1)}, u32[]{:S(2)}, u32[]{:S(2)}) collective-permute-start(bf16[448,896]{1,0:T(8,128)(2,1)S(1)} %copy-done.4), channel_id=1, source_target_pairs={{0,8},{1,9},{2,10},{3,11},{4,12},{5,13},{6,14},{7,15},{8,16},{9,17... | collective-permute-start | bytes 2408456 | tf_op jit(solution)/shard_map/ppermute | solution.py:244
  97.3 72.4 %collective-permute-start.24 = (bf16[448,896]{1,0:T(8,128)(2,1)S(1)}, bf16[448,896]{1,0:T(8,128)(2,1)}, u32[]{:S(2)}, u32[]{:S(2)}) collective-permute-start(bf16[448,896]{1,0:T(8,128)(2,1)S(1)} %copy-done.4), channel_id=1, source_target_pairs={{8,0},{9,1},{10,2},{11,3},{12,4},{13,5},{14,6},{15,7},{16,8},{17,9... | collective-permute-start | bytes 2408456 | tf_op jit(solution)/shard_map/ppermute | solution.py:244
  98.6 7.5 %collective-permute-start.7 = (bf16[448,1152]{1,0:T(8,128)(2,1)S(1)}, bf16[448,1152]{1,0:T(8,128)(2,1)S(1)}, u32[]{:S(2)}, u32[]{:S(2)}) collective-permute-start(bf16[448,1152]{1,0:T(8,128)(2,1)S(1)} %broadcast_select_fusion.5), channel_id=1, source_target_pairs={{0,1},{1,0},{2,3},{3,2},{4,5},{5,4},{6,7},{7,6},{8,9},{9,8},{10,11... | collective-permute-start | bytes 3096584 | tf_op jit(solution)/shard_map/ppermute | solution.py:244
  98.7 4.7 %collective-permute-start.12 = (bf16[448,1152]{1,0:T(8,128)(2,1)}, bf16[448,1152]{1,0:T(8,128)(2,1)S(1)}, u32[]{:S(2)}, u32[]{:S(2)}) collective-permute-start(bf16[448,1152]{1,0:T(8,128)(2,1)} %collective-permute-done.11), channel_id=1, source_target_pairs={{1,4},{3,6},{4,1},{6,3},{9,12},{11,14},{12,9},{14,11},{17,20},{19,... | collective-permute-start | bytes 3096584 | tf_op jit(solution)/shard_map/ppermute | solution.py:244
  100.8 18.2 %collective-permute-start.16 = (bf16[448,1152]{1,0:T(8,128)(2,1)S(1)}, bf16[448,1152]{1,0:T(8,128)(2,1)S(1)}, u32[]{:S(2)}, u32[]{:S(2)}) collective-permute-start(bf16[448,1152]{1,0:T(8,128)(2,1)S(1)} %broadcast_select_fusion), channel_id=1, source_target_pairs={{1,4},{3,6},{4,1},{6,3},{9,12},{11,14},{12,9},{14,11},{17,20},{19,... | collective-permute-start | bytes 3096584 | tf_op jit(solution)/shard_map/ppermute | solution.py:244
  103.4 34.3 %collective-permute-start.18 = (bf16[448,1152]{1,0:T(8,128)(2,1)S(1)}, bf16[448,1152]{1,0:T(8,128)(2,1)S(1)}, u32[]{:S(2)}, u32[]{:S(2)}) collective-permute-start(bf16[448,1152]{1,0:T(8,128)(2,1)S(1)} %broadcast_select_fusion), channel_id=1, source_target_pairs={{8,0},{9,1},{10,2},{11,3},{12,4},{13,5},{14,6},{15,7},{16,24},{17,... | collective-permute-start | bytes 3096584 | tf_op jit(solution)/shard_map/ppermute | solution.py:244
  106.1 20.7 %collective-permute-start.10 = (bf16[448,1152]{1,0:T(8,128)(2,1)S(1)}, bf16[448,1152]{1,0:T(8,128)(2,1)S(1)}, u32[]{:S(2)}, u32[]{:S(2)}) collective-permute-start(bf16[448,1152]{1,0:T(8,128)(2,1)S(1)} %broadcast_select_fusion.4), channel_id=1, source_target_pairs={{0,1},{1,0},{2,3},{3,2},{4,5},{5,4},{6,7},{7,6},{8,9},{9,8},{10,11... | collective-permute-start | bytes 3096584 | tf_op jit(solution)/shard_map/ppermute | solution.py:244
  119.0 37.3 %collective-permute-start.13 = (bf16[448,1152]{1,0:T(8,128)(2,1)S(1)}, bf16[448,1152]{1,0:T(8,128)(2,1)S(1)}, u32[]{:S(2)}, u32[]{:S(2)}) collective-permute-start(bf16[448,1152]{1,0:T(8,128)(2,1)S(1)} %broadcast_select_fusion.3), channel_id=1, source_target_pairs={{0,1},{1,0},{2,3},{3,2},{4,5},{5,4},{6,7},{7,6},{8,9},{9,8},{10,11... | collective-permute-start | bytes 3096584 | tf_op jit(solution)/shard_map/ppermute | solution.py:244
  126.8 30.4 %collective-permute-start.17 = (bf16[448,1152]{1,0:T(8,128)(2,1)S(1)}, bf16[448,1152]{1,0:T(8,128)(2,1)S(1)}, u32[]{:S(2)}, u32[]{:S(2)}) collective-permute-start(bf16[448,1152]{1,0:T(8,128)(2,1)S(1)} %broadcast_select_fusion.2), channel_id=1, source_target_pairs={{0,1},{1,0},{2,3},{3,2},{4,5},{5,4},{6,7},{7,6},{8,9},{9,8},{10,11... | collective-permute-start | bytes 3096584 | tf_op jit(solution)/shard_map/ppermute | solution.py:244
  137.7 3.5 %collective-permute-start.19 = (bf16[448,1152]{1,0:T(8,128)(2,1)S(1)}, bf16[448,1152]{1,0:T(8,128)(2,1)S(1)}, u32[]{:S(2)}, u32[]{:S(2)}) collective-permute-start(bf16[448,1152]{1,0:T(8,128)(2,1)S(1)} %collective-permute-done.18), channel_id=1, source_target_pairs={{1,4},{3,6},{4,1},{6,3},{9,12},{11,14},{12,9},{14,11},{17,20},{19,... | collective-permute-start | bytes 3096584 | tf_op jit(solution)/shard_map/ppermute | solution.py:244
  141.2 35.7 %collective-permute-start.22 = (bf16[448,896]{1,0:T(8,128)(2,1)S(1)}, bf16[448,896]{1,0:T(8,128)(2,1)S(1)}, u32[]{:S(2)}, u32[]{:S(2)}) collective-permute-start(bf16[448,896]{1,0:T(8,128)(2,1)S(1)} %copy-done.4), channel_id=1, source_target_pairs={{0,1},{1,0},{2,3},{3,2},{4,5},{5,4},{6,7},{7,6},{8,9},{9,8},{10,11... | collective-permute-start | bytes 2408456 | tf_op jit(solution)/shard_map/ppermute | solution.py:244
  156.3 3.3 %collective-permute-start.20 = (bf16[448,1152]{1,0:T(8,128)(2,1)S(1)}, bf16[448,1152]{1,0:T(8,128)(2,1)S(1)}, u32[]{:S(2)}, u32[]{:S(2)}) collective-permute-start(bf16[448,1152]{1,0:T(8,128)(2,1)S(1)} %broadcast_select_fusion.1), channel_id=1, source_target_pairs={{0,1},{1,0},{2,3},{3,2},{4,5},{5,4},{6,7},{7,6},{8,9},{9,8},{10,11... | collective-permute-start | bytes 3096584 | tf_op jit(solution)/shard_map/ppermute | solution.py:244
  169.7 9.7 %collective-permute-start.27 = (bf16[448,896]{1,0:T(8,128)(2,1)}, bf16[448,896]{1,0:T(8,128)(2,1)S(1)}, u32[]{:S(2)}, u32[]{:S(2)}) collective-permute-start(bf16[448,896]{1,0:T(8,128)(2,1)} %collective-permute-done.23), channel_id=1, source_target_pairs={{8,16},{9,17},{10,18},{11,19},{12,20},{13,21},{14,22},{15,23},{16,... | collective-permute-start | bytes 2408456 | tf_op jit(solution)/shard_map/ppermute | solution.py:244
  170.4 22.3 %collective-permute-start.28 = (bf16[448,896]{1,0:T(8,128)(2,1)}, bf16[448,896]{1,0:T(8,128)(2,1)S(1)}, u32[]{:S(2)}, u32[]{:S(2)}) collective-permute-start(bf16[448,896]{1,0:T(8,128)(2,1)} %collective-permute-done.24), channel_id=1, source_target_pairs={{8,0},{9,1},{10,2},{11,3},{12,4},{13,5},{14,6},{15,7},{16,8},{17,9... | collective-permute-start | bytes 2408456 | tf_op jit(solution)/shard_map/ppermute | solution.py:244
  176.3 18.1 %collective-permute-start.26 = (bf16[448,896]{1,0:T(8,128)(2,1)}, bf16[448,896]{1,0:T(8,128)(2,1)S(1)}, u32[]{:S(2)}, u32[]{:S(2)}) collective-permute-start(bf16[448,896]{1,0:T(8,128)(2,1)} %collective-permute-done.24), channel_id=1, source_target_pairs={{0,1},{1,0},{2,3},{3,2},{4,5},{5,4},{6,7},{7,6},{8,9},{9,8},{10,11... | collective-permute-start | bytes 2408456 | tf_op jit(solution)/shard_map/ppermute | solution.py:244
  176.7 20.3 %collective-permute-start.25 = (bf16[448,896]{1,0:T(8,128)(2,1)}, bf16[448,896]{1,0:T(8,128)(2,1)S(1)}, u32[]{:S(2)}, u32[]{:S(2)}) collective-permute-start(bf16[448,896]{1,0:T(8,128)(2,1)} %collective-permute-done.23), channel_id=1, source_target_pairs={{0,1},{1,0},{2,3},{3,2},{4,5},{5,4},{6,7},{7,6},{8,9},{9,8},{10,11... | collective-permute-start | bytes 2408456 | tf_op jit(solution)/shard_map/ppermute | solution.py:244
  192.8 21.2 %collective-permute-start.30 = (bf16[448,896]{1,0:T(8,128)(2,1)S(1)}, bf16[448,896]{1,0:T(8,128)(2,1)S(1)}, u32[]{:S(2)}, u32[]{:S(2)}) collective-permute-start(bf16[448,896]{1,0:T(8,128)(2,1)S(1)} %broadcast_select_fusion.6), channel_id=1, source_target_pairs={{8,0},{9,1},{10,2},{11,3},{12,4},{13,5},{14,6},{15,7},{16,24},{17,... | collective-permute-start | bytes 2408456 | tf_op jit(solution)/shard_map/ppermute | solution.py:244
  194.3 22.2 %collective-permute-start.29 = (bf16[448,896]{1,0:T(8,128)(2,1)S(1)}, bf16[448,896]{1,0:T(8,128)(2,1)S(1)}, u32[]{:S(2)}, u32[]{:S(2)}) collective-permute-start(bf16[448,896]{1,0:T(8,128)(2,1)S(1)} %broadcast_select_fusion.6), channel_id=1, source_target_pairs={{0,1},{1,0},{2,3},{3,2},{4,5},{5,4},{6,7},{7,6},{8,9},{9,8},{10,11... | collective-permute-start | bytes 2408456 | tf_op jit(solution)/shard_map/ppermute | solution.py:244
  200.8 46.3 %collective-permute-start.38 = (bf16[3,128,896]{2,1,0:T(8,128)(2,1)}, bf16[3,128,896]{2,1,0:T(8,128)(2,1)S(1)}, u32[]{:S(2)}, u32[]{:S(2)}) collective-permute-start(bf16[3,128,896]{2,1,0:T(8,128)(2,1)} %pad_maximum_fusion.4), channel_id=1, source_target_pairs={{0,6},{1,7},{2,4},{3,5},{4,2},{5,3},{6,0},{7,1},{8,14},{9,15},{10,... | collective-permute-start | bytes 2064392 | tf_op jit(solution)/shard_map/ppermute | solution.py:244
  204.5 45.3 %collective-permute-start.35 = (bf16[3,128,896]{2,1,0:T(8,128)(2,1)}, bf16[3,128,896]{2,1,0:T(8,128)(2,1)}, u32[]{:S(2)}, u32[]{:S(2)}) collective-permute-start(bf16[3,128,896]{2,1,0:T(8,128)(2,1)} %pad_maximum_fusion.3), channel_id=1, source_target_pairs={{0,2},{1,3},{2,0},{3,1},{4,6},{5,7},{6,4},{7,5},{8,10},{9,11},{10,... | collective-permute-start | bytes 2064392 | tf_op jit(solution)/shard_map/ppermute | solution.py:244
  214.0 3.8 %collective-permute-start.31 = (bf16[448,896]{1,0:T(8,128)(2,1)S(1)}, bf16[448,896]{1,0:T(8,128)(2,1)S(1)}, u32[]{:S(2)}, u32[]{:S(2)}) collective-permute-start(bf16[448,896]{1,0:T(8,128)(2,1)S(1)} %collective-permute-done.30), channel_id=1, source_target_pairs={{0,1},{1,0},{2,3},{3,2},{4,5},{5,4},{6,7},{7,6},{8,9},{9,8},{10,11... | collective-permute-start | bytes 2408456 | tf_op jit(solution)/shard_map/ppermute | solution.py:244
  214.9 35.4 %collective-permute-start.32 = (bf16[3,128,896]{2,1,0:T(8,128)(2,1)}, bf16[3,128,896]{2,1,0:T(8,128)(2,1)}, u32[]{:S(2)}, u32[]{:S(2)}) collective-permute-start(bf16[3,128,896]{2,1,0:T(8,128)(2,1)} %pad_maximum_fusion.2), channel_id=1, source_target_pairs={{0,4},{1,5},{2,6},{3,7},{4,0},{5,1},{6,2},{7,3},{8,12},{9,13},{10,... | collective-permute-start | bytes 2064392 | tf_op jit(solution)/shard_map/ppermute | solution.py:244
  219.2 15.8 %collective-permute-start.43 = (bf16[5,896]{1,0:T(8,128)(2,1)S(1)}, bf16[5,896]{1,0:T(8,128)(2,1)S(1)}, u32[]{:S(2)}, u32[]{:S(2)}) collective-permute-start(bf16[5,896]{1,0:T(8,128)(2,1)S(1)} %concatenate.71), channel_id=1, source_target_pairs={{0,6},{1,7},{2,4},{3,5},{4,2},{5,3},{6,0},{7,1},{8,14},{9,15},{10,... | collective-permute-start | bytes 26888 | tf_op jit(solution)/shard_map/ppermute | solution.py:244
  221.7 16.4 %collective-permute-start.42 = (bf16[5,896]{1,0:T(8,128)(2,1)S(1)}, bf16[5,896]{1,0:T(8,128)(2,1)S(1)}, u32[]{:S(2)}, u32[]{:S(2)}) collective-permute-start(bf16[5,896]{1,0:T(8,128)(2,1)S(1)} %concatenate.70), channel_id=1, source_target_pairs={{0,2},{1,3},{2,0},{3,1},{4,6},{5,7},{6,4},{7,5},{8,10},{9,11},{10,... | collective-permute-start | bytes 26888 | tf_op jit(solution)/shard_map/ppermute | solution.py:244
  235.0 3.7 %collective-permute-start.41 = (bf16[5,896]{1,0:T(8,128)(2,1)S(1)}, bf16[5,896]{1,0:T(8,128)(2,1)S(1)}, u32[]{:S(2)}, u32[]{:S(2)}) collective-permute-start(bf16[5,896]{1,0:T(8,128)(2,1)S(1)} %concatenate.69), channel_id=1, source_target_pairs={{0,4},{1,5},{2,6},{3,7},{4,0},{5,1},{6,2},{7,3},{8,12},{9,13},{10,... | collective-permute-start | bytes 26888 | tf_op jit(solution)/shard_map/ppermute | solution.py:244
  238.1 12.5 %collective-permute-start.33 = (bf16[1,128,896]{2,1,0:T(8,128)(2,1)S(1)}, bf16[1,128,896]{2,1,0:T(8,128)(2,1)S(1)}, u32[]{:S(2)}, u32[]{:S(2)}) collective-permute-start(bf16[1,128,896]{2,1,0:T(8,128)(2,1)S(1)} %get-tuple-element.47), channel_id=1, source_target_pairs={{0,4},{1,5},{2,6},{3,7},{4,0},{5,1},{6,2},{7,3},{8,12},{9,13},{10,... | collective-permute-start | bytes 688136 | tf_op jit(solution)/shard_map/ppermute | solution.py:244
  238.7 16.5 %collective-permute-start.36 = (bf16[1,128,896]{2,1,0:T(8,128)(2,1)S(1)}, bf16[1,128,896]{2,1,0:T(8,128)(2,1)S(1)}, u32[]{:S(2)}, u32[]{:S(2)}) collective-permute-start(bf16[1,128,896]{2,1,0:T(8,128)(2,1)S(1)} %get-tuple-element.46), channel_id=1, source_target_pairs={{0,2},{1,3},{2,0},{3,1},{4,6},{5,7},{6,4},{7,5},{8,10},{9,11},{10,... | collective-permute-start | bytes 688136 | tf_op jit(solution)/shard_map/ppermute | solution.py:244
  241.9 11.7 %all-to-all-start = ((f32[32,1,128]{2,1,0:T(1,128)}), f32[32,1,128]{2,1,0:T(1,128)S(1)}, u32[]{:S(2)}, u32[]{:S(2)}) async-start(f32[32,1,128]{2,1,0:T(1,128)} %bitcast.115), calls=%async_computation | async-start | bytes 32768 | tf_op jit(solution)/shard_map/all_to_all | solution.py:422
  247.1 9.5 %collective-permute-start.39 = (bf16[1,128,896]{2,1,0:T(8,128)(2,1)S(1)}, bf16[1,128,896]{2,1,0:T(8,128)(2,1)S(1)}, u32[]{:S(2)}, u32[]{:S(2)}) collective-permute-start(bf16[1,128,896]{2,1,0:T(8,128)(2,1)S(1)} %get-tuple-element.45), channel_id=1, source_target_pairs={{0,6},{1,7},{2,4},{3,5},{4,2},{5,3},{6,0},{7,1},{8,14},{9,15},{10,... | collective-permute-start | bytes 688136 | tf_op jit(solution)/shard_map/ppermute | solution.py:244
  249.8 11.7 %collective-permute-start.34 = (bf16[1,128,896]{2,1,0:T(8,128)(2,1)S(1)}, bf16[1,128,896]{2,1,0:T(8,128)(2,1)S(1)}, u32[]{:S(2)}, u32[]{:S(2)}) collective-permute-start(bf16[1,128,896]{2,1,0:T(8,128)(2,1)S(1)} %get-tuple-element.43), channel_id=1, source_target_pairs={{0,4},{1,5},{2,6},{3,7},{4,0},{5,1},{6,2},{7,3},{8,12},{9,13},{10,... | collective-permute-start | bytes 688136 | tf_op jit(solution)/shard_map/ppermute | solution.py:244
  250.3 11.4 %collective-permute-start.37 = (bf16[1,128,896]{2,1,0:T(8,128)(2,1)S(1)}, bf16[1,128,896]{2,1,0:T(8,128)(2,1)S(1)}, u32[]{:S(2)}, u32[]{:S(2)}) collective-permute-start(bf16[1,128,896]{2,1,0:T(8,128)(2,1)S(1)} %get-tuple-element.42), channel_id=1, source_target_pairs={{0,2},{1,3},{2,0},{3,1},{4,6},{5,7},{6,4},{7,5},{8,10},{9,11},{10,... | collective-permute-start | bytes 688136 | tf_op jit(solution)/shard_map/ppermute | solution.py:244
  250.6 15.2 %collective-permute-start.40 = (bf16[1,128,896]{2,1,0:T(8,128)(2,1)S(1)}, bf16[1,128,896]{2,1,0:T(8,128)(2,1)S(1)}, u32[]{:S(2)}, u32[]{:S(2)}) collective-permute-start(bf16[1,128,896]{2,1,0:T(8,128)(2,1)S(1)} %get-tuple-element.41), channel_id=1, source_target_pairs={{0,6},{1,7},{2,4},{3,5},{4,2},{5,3},{6,0},{7,1},{8,14},{9,15},{10,... | collective-permute-start | bytes 688136 | tf_op jit(solution)/shard_map/ppermute | solution.py:244
  (17 other events, 164.2 us)

commit v7 on v6

--- a/solution.py
+++ b/solution.py
@@ -346,7 +346,13 @@
         far = send(by_y, to_x)
         normed = normalise([sequence, by_y, by_x, far], norm_gain, fsdp_size)
         near_lengths = [send(lengths, to_y), send(lengths, to_x), send(lengths, to_xy)]
-        normed, *near_lengths = lax.optimization_barrier((normed, *near_lengths))
+        group_lengths = [lengths, *near_lengths]
+        row_places = [
+            j * length_rows + group_length - 1 for j, group_length in enumerate(group_lengths)
+        ]
+        normed, near_lengths, row_places = lax.optimization_barrier(
+            (normed, near_lengths, row_places)
+        )
         group_lengths = [lengths, *near_lengths]
         acc = None
         for (plane, own), other in zip(qkv_blocks, others):
@@ -390,7 +396,7 @@
         parts = [part for group in groups for part in group]
         ahead = []
         for j, move in enumerate((None, to_y, to_x, to_xy)):
-            at = j * length_rows + group_lengths[j][0] - 1
+            at = row_places[j][0]
             rows = [lax.dynamic_slice_in_dim(part, at, 1, 0) for part in parts]
             chosen = jnp.concatenate(rows, axis=0)
             ahead.append(chosen if move is None else send(chosen, move))

time: 273 us -> 283 us (1.037)
  waiting for transfers between devices: 104 us -> 112 us
  starting transfers between devices: 91 us -> 94.7 us
    ppermute x44, waiting for transfers between devices: 104 us -> 111 us  [send(): return lax.ppermute(array, AXES, route(move))]
    ppermute x44, starting transfers between devices: 86.6 us -> 91.1 us  [send(): return lax.ppermute(array, AXES, route(move))]
  transfers between devices with their start and end apart: 45 -> 45, of which waited for: 15 -> 16; matrix products, arithmetic and copies ran while one was open for 16% -> 15% of each run, Pallas kernels for 6% -> 5%
where the time goes in v7:
time: 283 us; the launch traced here: 282 us
  waiting for transfers between devices  112 us (40%)
  starting transfers between devices  94.7 us (33%)
  matrix products  20.8 us (7%)
  Pallas kernels  19.4 us (7%)
  other arithmetic  14.7 us (5%)
  local copies, waits for them, and re-layouts  13.9 us (5%)
  between operations  6.53 us (2%)
    ppermute x44, waiting for transfers between devices, send(): return lax.ppermute(array, AXES, route(move))  111 us
    ppermute x44, starting transfers between devices, send(): return lax.ppermute(array, AXES, route(move))  91.1 us
    dot_general x5, matrix products, whole(): lax.dot_general(attn, weights, (((1,), (1,)), ((), ())), preferred_elemen...  10.8 us
    dot_general x10, matrix products, whole(): jnp.dot(lax.dynamic_index_in_dim(normed, jnp.maximum(plane, 0) * 2 + core...  10 us
    pallas_call x1, Pallas kernels, attend(): pl.pallas_call(kernel, name='attention', out_shape=jax.ShapeDtypeStruct((...  6.94 us
    pallas_call x1, Pallas kernels, normalise(): pl.pallas_call(norm_kernel, name='normalise', out_shape=jax.ShapeDtypeStr...  6.51 us
  transfers between devices with their start and end apart: 45, of which 16 were waited for; matrix products, arithmetic and copies ran while one was open for 15% of the time, Pallas kernels for 5%

profile of v7, /device:TPU:0, one launch (start us, length us, event | category | flops | bytes accessed | tf_op | source)
XLA Modules:
  0.0 281.9 jit_solution(2541366198996287919)
XLA Ops:
  4.1 5.9 %collective-permute-start.8 = (bf16[448,1152]{1,0:T(8,128)(2,1)}, bf16[448,1152]{1,0:T(8,128)(2,1)}, u32[]{:S(2)}, u32[]{:S(2)}) collective-permute-start(bf16[448,1152]{1,0:T(8,128)(2,1)} %pad_maximum_fusion), channel_id=1, source_target_pairs={{0,8},{1,9},{2,10},{3,11},{4,12},{5,13},{6,14},{7,15},{8,16},{9,17... | collective-permute-start | bytes 3096584 | tf_op jit(solution)/shard_map/ppermute | solution.py:244
  10.1 1.3 collective-permute-start.11
  11.4 1.6 collective-permute-start
  13.0 2.1 dynamic-slice_bitcast_fusion
  15.0 1.6 collective-permute-start.21
  16.6 1.3 collective-permute-start.3
  17.9 24.0 %collective-permute-done.3.refs_1_ = s32[1]{0:T(128)} collective-permute-done((s32[1]{0:T(128)}, s32[1]{0:T(128)}, u32[]{:S(2)}, u32[]{:S(2)}) %collective-permute-start.3) | collective-permute-done | bytes 36 | tf_op jit(solution)/shard_map/ppermute | solution.py:244
  42.0 1.5 collective-permute-start.4
  43.5 2.2 collective-permute-done.4.refs_2_
  46.1 4.1 %collective-permute-done.5.refs_3_ = s32[1]{0:T(128)} collective-permute-done((s32[1]{0:T(128)}, s32[1]{0:T(128)}, u32[]{:S(2)}, u32[]{:S(2)}) %collective-permute-start.5) | collective-permute-done | bytes 36 | tf_op jit(solution)/shard_map/ppermute | solution.py:244
  54.1 1.6 collective-permute-start.14
  55.8 1.3 collective-permute-start.15
  59.8 1.6 collective-permute-start.1
  64.5 2.2 broadcast_select_fusion.7
  67.8 1.6 collective-permute-start.9
  69.7 13.0 %collective-permute-done.1.by_x_ref = bf16[128,3584]{1,0:T(8,128)(2,1)S(1)} collective-permute-done((bf16[128,3584]{1,0:T(8,128)(2,1)S(1)}, bf16[128,3584]{1,0:T(8,128)(2,1)S(1)}, u32[]{:S(2)}, u32[]{:S(2)}) %collective-permute-start.1) | collective-permute-done | bytes 917536 | tf_op jit(solution)/shard_map/ppermute | solution.py:244
  83.6 8.0 %collective-permute-start.23 = (bf16[448,896]{1,0:T(8,128)(2,1)}, bf16[448,896]{1,0:T(8,128)(2,1)}, u32[]{:S(2)}, u32[]{:S(2)}) collective-permute-start(bf16[448,896]{1,0:T(8,128)(2,1)} %broadcast_select_fusion.7), channel_id=1, source_target_pairs={{0,8},{1,9},{2,10},{3,11},{4,12},{5,13},{6,14},{7,15},{8,16},{9,17... | collective-permute-start | bytes 2408456 | tf_op jit(solution)/shard_map/ppermute | solution.py:244
  91.6 10.9 %collective-permute-done.2.far_ref = bf16[128,3584]{1,0:T(8,128)(2,1)} collective-permute-done((bf16[128,3584]{1,0:T(8,128)(2,1)}, bf16[128,3584]{1,0:T(8,128)(2,1)}, u32[]{:S(2)}, u32[]{:S(2)}) %collective-permute-start.2) | collective-permute-done | bytes 917536 | tf_op jit(solution)/shard_map/ppermute | solution.py:244
  102.5 1.3 collective-permute-start.24
  103.8 6.5 %normalise.1 = bf16[8,512,448]{2,1,0:T(8,128)(2,1)} custom-call(bf16[128,3584]{1,0:T(8,128)(2,1)} %bitcast.106, bf16[128,3584]{1,0:T(8,128)(2,1)} %collective-permute-done.by_y_ref, bf16[128,3584]{1,0:T(8,128)(2,1)} %copy-done.3, bf16[128,3584]{1,0:T(8,128)(2,1)} %collective-permute-done.2.far_ref, f32[1,3584]{1,0:T(1,128)} %reshape.38.gain_ref), custom_call_target="tpu_custom_call" | custom-call | flops 14680064 | bytes 7340032 | tf_op jit(solution)/shard_map/normalise/pallas_call | solution.py:137
  111.2 1.4 broadcast_select_fusion
  113.4 1.7 broadcast_select_fusion.4
  115.2 1.3 collective-permute-start.18
  116.5 1.4 broadcast_select_fusion.3
  117.9 11.0 %collective-permute-start.10 = (bf16[448,1152]{1,0:T(8,128)(2,1)S(1)}, bf16[448,1152]{1,0:T(8,128)(2,1)S(1)}, u32[]{:S(2)}, u32[]{:S(2)}) collective-permute-start(bf16[448,1152]{1,0:T(8,128)(2,1)S(1)} %broadcast_select_fusion.4), channel_id=1, source_target_pairs={{0,1},{1,0},{2,3},{3,2},{4,5},{5,4},{6,7},{7,6},{8,9},{9,8},{10,11... | collective-permute-start | bytes 3096584 | tf_op jit(solution)/shard_map/ppermute | solution.py:244
  130.6 7.7 %collective-permute-start.13 = (bf16[448,1152]{1,0:T(8,128)(2,1)S(1)}, bf16[448,1152]{1,0:T(8,128)(2,1)S(1)}, u32[]{:S(2)}, u32[]{:S(2)}) collective-permute-start(bf16[448,1152]{1,0:T(8,128)(2,1)S(1)} %broadcast_select_fusion.3), channel_id=1, source_target_pairs={{0,1},{1,0},{2,3},{3,2},{4,5},{5,4},{6,7},{7,6},{8,9},{9,8},{10,11... | collective-permute-start | bytes 3096584 | tf_op jit(solution)/shard_map/ppermute | solution.py:244
  138.5 4.7 %collective-permute-done.18 = bf16[448,1152]{1,0:T(8,128)(2,1)S(1)} collective-permute-done((bf16[448,1152]{1,0:T(8,128)(2,1)S(1)}, bf16[448,1152]{1,0:T(8,128)(2,1)S(1)}, u32[]{:S(2)}, u32[]{:S(2)}) %collective-permute-start.18) | collective-permute-done | bytes 1032224 | tf_op jit(solution)/shard_map/ppermute | solution.py:244
  146.7 19.1 %collective-permute-start.22 = (bf16[448,896]{1,0:T(8,128)(2,1)}, bf16[448,896]{1,0:T(8,128)(2,1)S(1)}, u32[]{:S(2)}, u32[]{:S(2)}) collective-permute-start(bf16[448,896]{1,0:T(8,128)(2,1)} %broadcast_select_fusion.7), channel_id=1, source_target_pairs={{0,1},{1,0},{2,3},{3,2},{4,5},{5,4},{6,7},{7,6},{8,9},{9,8},{10,11... | collective-permute-start | bytes 2408456 | tf_op jit(solution)/shard_map/ppermute | solution.py:244
  170.3 2.3 fusion.3.refs_4_
  172.5 6.9 %attention.1 = bf16[512,896]{1,0:T(8,128)(2,1)} custom-call(s32[1]{0:T(128)S(6)} %copy.15.refs_0_, s32[1]{0:T(128)} %collective-permute-done.3.refs_1_, s32[1]{0:T(128)} %collective-permute-done.4.refs_2_, s32[1]{0:T(128)} %collective-permute-done.5.refs_3_, f32[512,1152]{1,0:T(8,128)} %fusion.3.refs_4_, f32[1,1152]{1,0:T(1,128)} %reshape.39.refs_5_, ...), custom_call_target="tpu_custom_call" | custom-call | flops 1879048192 | bytes 3276800 | tf_op jit(solution)/shard_map/attention/pallas_call | solution.py:92
  180.2 1.3 collective-permute-start.28
  182.7 2.9 %fusion.44 = bf16[512,896]{1,0:T(8,128)(2,1)S(1)} fusion(bf16[512,896]{1,0:T(8,128)(2,1)} %attention.1, bf16[448,896]{1,0:T(8,128)(2,1)S(1)} %collective-permute-done.22, bf16[448,896]{1,0:T(8,128)(2,1)} %broadcast_select_fusion.7, pred[]{:T(512)S(6)} %eq.97), kind=kOutput, calls=%fused_computation.53 | convolution fusion | flops 829767680 | bytes 3440641 | tf_op jit(solution)/shard_map/dot_general | solution.py:390
  185.7 18.1 %collective-permute-done.28 = bf16[448,896]{1,0:T(8,128)(2,1)S(1)} collective-permute-done((bf16[448,896]{1,0:T(8,128)(2,1)}, bf16[448,896]{1,0:T(8,128)(2,1)S(1)}, u32[]{:S(2)}, u32[]{:S(2)}) %collective-permute-start.28) | collective-permute-done | bytes 802848 | tf_op jit(solution)/shard_map/ppermute | solution.py:244
  203.9 1.5 collective-permute-start.30
  205.5 2.7 fusion.42
  208.3 2.7 fusion.43
  215.1 10.0 %collective-permute-done.30 = bf16[448,896]{1,0:T(8,128)(2,1)S(1)} collective-permute-done((bf16[448,896]{1,0:T(8,128)(2,1)S(1)}, bf16[448,896]{1,0:T(8,128)(2,1)S(1)}, u32[]{:S(2)}, u32[]{:S(2)}) %collective-permute-start.30) | collective-permute-done | bytes 802848 | tf_op jit(solution)/shard_map/ppermute | solution.py:244
  229.1 2.2 collective-permute-start.43
  233.4 12.8 %collective-permute-done.43.refs_3_ = bf16[5,896]{1,0:T(8,128)(2,1)S(1)} collective-permute-done((bf16[5,896]{1,0:T(8,128)(2,1)S(1)}, bf16[5,896]{1,0:T(8,128)(2,1)S(1)}, u32[]{:S(2)}, u32[]{:S(2)}) %collective-permute-start.43) | collective-permute-done | bytes 8992 | tf_op jit(solution)/shard_map/ppermute | solution.py:244
  248.2 1.4 collective-permute-start.33
  251.1 1.7 score.1
  252.8 3.6 %all-to-all-start = ((f32[32,1,128]{2,1,0:T(1,128)}), f32[32,1,128]{2,1,0:T(1,128)S(1)}, u32[]{:S(2)}, u32[]{:S(2)}) async-start(f32[32,1,128]{2,1,0:T(1,128)} %bitcast.112), calls=%async_computation | async-start | bytes 32768 | tf_op jit(solution)/shard_map/all_to_all | solution.py:428
  257.1 2.7 collective-permute-start.39
  260.6 2.7 collective-permute-start.40
  265.3 1.3 collective-permute-done.39.refs_12_
  266.7 4.8 %collective-permute-done.34.refs_7_ = bf16[1,128,896]{2,1,0:T(8,128)(2,1)S(1)} collective-permute-done((bf16[1,128,896]{2,1,0:T(8,128)(2,1)S(1)}, bf16[1,128,896]{2,1,0:T(8,128)(2,1)S(1)}, u32[]{:S(2)}, u32[]{:S(2)}) %collective-permute-start.34) | collective-permute-done | bytes 229408 | tf_op jit(solution)/shard_map/ppermute | solution.py:244
  271.8 4.0 %collective-permute-done.40.refs_13_ = bf16[1,128,896]{2,1,0:T(8,128)(2,1)S(1)} collective-permute-done((bf16[1,128,896]{2,1,0:T(8,128)(2,1)S(1)}, bf16[1,128,896]{2,1,0:T(8,128)(2,1)S(1)}, u32[]{:S(2)}, u32[]{:S(2)}) %collective-permute-start.40) | collective-permute-done | bytes 229408 | tf_op jit(solution)/shard_map/ppermute | solution.py:244
  276.5 4.3 %finish.1 = bf16[128,3584]{1,0:T(8,128)(2,1)} custom-call(s32[4]{0:T(128)} %pad_add_fusion.refs_0_.slots_ref, bf16[128,3584]{1,0:T(8,128)(2,1)} %bitcast.107, bf16[3,128,896]{2,1,0:T(8,128)(2,1)} %pad_maximum_fusion.1.refs_2_, bf16[1,128,896]{2,1,0:T(8,128)(2,1)} %get-tuple-element.56.refs_3_, bf16[1,128,896]{2,1,0:T(8,128)(2,1)} %get-tuple-element.52.refs_4_, ...), custom_call_target="tpu_custom_call" | custom-call | flops 3670016 | bytes 2752512 | tf_op jit(solution)/shard_map/finish/pallas_call | solution.py:174
  (145 shorter events, 43.7 us)
Async XLA Ops:
  2.0 49.7 %copy-start.13 = (f32[3584]{0:T(1024)S(1)}, f32[3584]{0:T(1024)}, u32[]{:S(2)}) copy-start(f32[3584]{0:T(1024)} %param.14) | copy-start | bytes 43012
  2.0 56.4 %copy-start.11 = (f32[3584]{0:T(1024)S(1)}, f32[3584]{0:T(1024)}, u32[]{:S(2)}) copy-start(f32[3584]{0:T(1024)} %param.18) | copy-start | bytes 43012
  2.0 56.4 %copy-start.12 = (f32[3584]{0:T(1024)S(1)}, f32[3584]{0:T(1024)}, u32[]{:S(2)}) copy-start(f32[3584]{0:T(1024)} %param.19) | copy-start | bytes 43012
  4.1 50.0 %collective-permute-start.8 = (bf16[448,1152]{1,0:T(8,128)(2,1)}, bf16[448,1152]{1,0:T(8,128)(2,1)}, u32[]{:S(2)}, u32[]{:S(2)}) collective-permute-start(bf16[448,1152]{1,0:T(8,128)(2,1)} %pad_maximum_fusion), channel_id=1, source_target_pairs={{0,8},{1,9},{2,10},{3,11},{4,12},{5,13},{6,14},{7,15},{8,16},{9,17... | collective-permute-start | bytes 3096584 | tf_op jit(solution)/shard_map/ppermute | solution.py:244
  10.1 45.7 %collective-permute-start.11 = (bf16[448,1152]{1,0:T(8,128)(2,1)}, bf16[448,1152]{1,0:T(8,128)(2,1)}, u32[]{:S(2)}, u32[]{:S(2)}) collective-permute-start(bf16[448,1152]{1,0:T(8,128)(2,1)} %pad_maximum_fusion), channel_id=1, source_target_pairs={{8,0},{9,1},{10,2},{11,3},{12,4},{13,5},{14,6},{15,7},{16,8},{17,9... | collective-permute-start | bytes 3096584 | tf_op jit(solution)/shard_map/ppermute | solution.py:244
  11.4 50.0 %collective-permute-start = (bf16[128,3584]{1,0:T(8,128)(2,1)S(1)}, bf16[128,3584]{1,0:T(8,128)(2,1)}, u32[]{:S(2)}, u32[]{:S(2)}) collective-permute-start(bf16[128,3584]{1,0:T(8,128)(2,1)S(1)} %bitcast.108), channel_id=1, source_target_pairs={{0,4},{1,5},{2,6},{3,7},{4,0},{5,1},{6,2},{7,3},{8,12},{9,13},{10,... | collective-permute-start | bytes 2752520 | tf_op jit(solution)/shard_map/ppermute | solution.py:244
  15.0 44.7 %collective-permute-start.21 = (bf16[448,896]{1,0:T(8,128)(2,1)}, bf16[448,896]{1,0:T(8,128)(2,1)}, u32[]{:S(2)}, u32[]{:S(2)}) collective-permute-start(bf16[448,896]{1,0:T(8,128)(2,1)} %dynamic-slice_bitcast_fusion), channel_id=1, source_target_pairs={{1,4},{3,6},{4,1},{6,3},{9,12},{11,14},{12,9},{14,11},{17,20},{19,... | collective-permute-start | bytes 2408456 | tf_op jit(solution)/shard_map/ppermute | solution.py:244
  16.6 25.4 %collective-permute-start.3 = (s32[1]{0:T(128)}, s32[1]{0:T(128)}, u32[]{:S(2)}, u32[]{:S(2)}) collective-permute-start(s32[1]{0:T(128)} %param.11), channel_id=1, source_target_pairs={{0,4},{1,5},{2,6},{3,7},{4,0},{5,1},{6,2},{7,3},{8,12},{9,13},{10,... | collective-permute-start | bytes 20 | tf_op jit(solution)/shard_map/ppermute | solution.py:244
  42.0 3.7 %collective-permute-start.4 = (s32[1]{0:T(128)}, s32[1]{0:T(128)}, u32[]{:S(2)}, u32[]{:S(2)}) collective-permute-start(s32[1]{0:T(128)} %param.11), channel_id=1, source_target_pairs={{0,2},{1,3},{2,0},{3,1},{4,6},{5,7},{6,4},{7,5},{8,10},{9,11},{10,... | collective-permute-start | bytes 20 | tf_op jit(solution)/shard_map/ppermute | solution.py:244
  45.6 4.6 %collective-permute-start.5 = (s32[1]{0:T(128)}, s32[1]{0:T(128)}, u32[]{:S(2)}, u32[]{:S(2)}) collective-permute-start(s32[1]{0:T(128)} %param.11), channel_id=1, source_target_pairs={{0,6},{1,7},{2,4},{3,5},{4,2},{5,3},{6,0},{7,1},{8,14},{9,15},{10,... | collective-permute-start | bytes 20 | tf_op jit(solution)/shard_map/ppermute | solution.py:244
  50.2 16.6 %collective-permute-start.6 = (bf16[448,1152]{1,0:T(8,128)(2,1)}, bf16[448,1152]{1,0:T(8,128)(2,1)S(1)}, u32[]{:S(2)}, u32[]{:S(2)}) collective-permute-start(bf16[448,1152]{1,0:T(8,128)(2,1)} %pad_maximum_fusion), channel_id=1, source_target_pairs={{1,4},{3,6},{4,1},{6,3},{9,12},{11,14},{12,9},{14,11},{17,20},{19,... | collective-permute-start | bytes 3096584 | tf_op jit(solution)/shard_map/ppermute | solution.py:244
  54.1 56.1 %collective-permute-start.14 = (bf16[448,1152]{1,0:T(8,128)(2,1)}, bf16[448,1152]{1,0:T(8,128)(2,1)}, u32[]{:S(2)}, u32[]{:S(2)}) collective-permute-start(bf16[448,1152]{1,0:T(8,128)(2,1)} %collective-permute-done.8), channel_id=1, source_target_pairs={{8,16},{9,17},{10,18},{11,19},{12,20},{13,21},{14,22},{15,23},{16,... | collective-permute-start | bytes 3096584 | tf_op jit(solution)/shard_map/ppermute | solution.py:244
  55.8 54.7 %collective-permute-start.15 = (bf16[448,1152]{1,0:T(8,128)(2,1)}, bf16[448,1152]{1,0:T(8,128)(2,1)}, u32[]{:S(2)}, u32[]{:S(2)}) collective-permute-start(bf16[448,1152]{1,0:T(8,128)(2,1)} %collective-permute-done.11), channel_id=1, source_target_pairs={{8,0},{9,1},{10,2},{11,3},{12,4},{13,5},{14,6},{15,7},{16,8},{17,9... | collective-permute-start | bytes 3096584 | tf_op jit(solution)/shard_map/ppermute | solution.py:244
  59.8 22.9 %collective-permute-start.1 = (bf16[128,3584]{1,0:T(8,128)(2,1)S(1)}, bf16[128,3584]{1,0:T(8,128)(2,1)S(1)}, u32[]{:S(2)}, u32[]{:S(2)}) collective-permute-start(bf16[128,3584]{1,0:T(8,128)(2,1)S(1)} %bitcast.109), channel_id=1, source_target_pairs={{0,2},{1,3},{2,0},{3,1},{4,6},{5,7},{6,4},{7,5},{8,10},{9,11},{10,... | collective-permute-start | bytes 2752520 | tf_op jit(solution)/shard_map/ppermute | solution.py:244
  61.3 41.1 %collective-permute-start.2 = (bf16[128,3584]{1,0:T(8,128)(2,1)}, bf16[128,3584]{1,0:T(8,128)(2,1)}, u32[]{:S(2)}, u32[]{:S(2)}) collective-permute-start(bf16[128,3584]{1,0:T(8,128)(2,1)} %collective-permute-done.by_y_ref), channel_id=1, source_target_pairs={{0,2},{1,3},{2,0},{3,1},{4,6},{5,7},{6,4},{7,5},{8,10},{9,11},{10,... | collective-permute-start | bytes 2752520 | tf_op jit(solution)/shard_map/ppermute | solution.py:244
  67.8 44.8 %collective-permute-start.9 = (bf16[448,1152]{1,0:T(8,128)(2,1)}, bf16[448,1152]{1,0:T(8,128)(2,1)}, u32[]{:S(2)}, u32[]{:S(2)}) collective-permute-start(bf16[448,1152]{1,0:T(8,128)(2,1)} %collective-permute-done.8), channel_id=1, source_target_pairs={{1,4},{3,6},{4,1},{6,3},{9,12},{11,14},{12,9},{14,11},{17,20},{19,... | collective-permute-start | bytes 3096584 | tf_op jit(solution)/shard_map/ppermute | solution.py:244
  83.6 95.9 %collective-permute-start.23 = (bf16[448,896]{1,0:T(8,128)(2,1)}, bf16[448,896]{1,0:T(8,128)(2,1)}, u32[]{:S(2)}, u32[]{:S(2)}) collective-permute-start(bf16[448,896]{1,0:T(8,128)(2,1)} %broadcast_select_fusion.7), channel_id=1, source_target_pairs={{0,8},{1,9},{2,10},{3,11},{4,12},{5,13},{6,14},{7,15},{8,16},{9,17... | collective-permute-start | bytes 2408456 | tf_op jit(solution)/shard_map/ppermute | solution.py:244
  102.5 77.0 %collective-permute-start.24 = (bf16[448,896]{1,0:T(8,128)(2,1)}, bf16[448,896]{1,0:T(8,128)(2,1)}, u32[]{:S(2)}, u32[]{:S(2)}) collective-permute-start(bf16[448,896]{1,0:T(8,128)(2,1)} %broadcast_select_fusion.7), channel_id=1, source_target_pairs={{8,0},{9,1},{10,2},{11,3},{12,4},{13,5},{14,6},{15,7},{16,8},{17,9... | collective-permute-start | bytes 2408456 | tf_op jit(solution)/shard_map/ppermute | solution.py:244
  110.3 7.6 %collective-permute-start.7 = (bf16[448,1152]{1,0:T(8,128)(2,1)S(1)}, bf16[448,1152]{1,0:T(8,128)(2,1)S(1)}, u32[]{:S(2)}, u32[]{:S(2)}) collective-permute-start(bf16[448,1152]{1,0:T(8,128)(2,1)S(1)} %broadcast_select_fusion.5), channel_id=1, source_target_pairs={{0,1},{1,0},{2,3},{3,2},{4,5},{5,4},{6,7},{7,6},{8,9},{9,8},{10,11... | collective-permute-start | bytes 3096584 | tf_op jit(solution)/shard_map/ppermute | solution.py:244
  110.5 4.7 %collective-permute-start.12 = (bf16[448,1152]{1,0:T(8,128)(2,1)}, bf16[448,1152]{1,0:T(8,128)(2,1)S(1)}, u32[]{:S(2)}, u32[]{:S(2)}) collective-permute-start(bf16[448,1152]{1,0:T(8,128)(2,1)} %collective-permute-done.11), channel_id=1, source_target_pairs={{1,4},{3,6},{4,1},{6,3},{9,12},{11,14},{12,9},{14,11},{17,20},{19,... | collective-permute-start | bytes 3096584 | tf_op jit(solution)/shard_map/ppermute | solution.py:244
  112.6 18.0 %collective-permute-start.16 = (bf16[448,1152]{1,0:T(8,128)(2,1)S(1)}, bf16[448,1152]{1,0:T(8,128)(2,1)S(1)}, u32[]{:S(2)}, u32[]{:S(2)}) collective-permute-start(bf16[448,1152]{1,0:T(8,128)(2,1)S(1)} %broadcast_select_fusion), channel_id=1, source_target_pairs={{1,4},{3,6},{4,1},{6,3},{9,12},{11,14},{12,9},{14,11},{17,20},{19,... | collective-permute-start | bytes 3096584 | tf_op jit(solution)/shard_map/ppermute | solution.py:244
  115.2 28.1 %collective-permute-start.18 = (bf16[448,1152]{1,0:T(8,128)(2,1)S(1)}, bf16[448,1152]{1,0:T(8,128)(2,1)S(1)}, u32[]{:S(2)}, u32[]{:S(2)}) collective-permute-start(bf16[448,1152]{1,0:T(8,128)(2,1)S(1)} %broadcast_select_fusion), channel_id=1, source_target_pairs={{8,0},{9,1},{10,2},{11,3},{12,4},{13,5},{14,6},{15,7},{16,24},{17,... | collective-permute-start | bytes 3096584 | tf_op jit(solution)/shard_map/ppermute | solution.py:244
  117.9 20.6 %collective-permute-start.10 = (bf16[448,1152]{1,0:T(8,128)(2,1)S(1)}, bf16[448,1152]{1,0:T(8,128)(2,1)S(1)}, u32[]{:S(2)}, u32[]{:S(2)}) collective-permute-start(bf16[448,1152]{1,0:T(8,128)(2,1)S(1)} %broadcast_select_fusion.4), channel_id=1, source_target_pairs={{0,1},{1,0},{2,3},{3,2},{4,5},{5,4},{6,7},{7,6},{8,9},{9,8},{10,11... | collective-permute-start | bytes 3096584 | tf_op jit(solution)/shard_map/ppermute | solution.py:244
  130.6 35.3 %collective-permute-start.13 = (bf16[448,1152]{1,0:T(8,128)(2,1)S(1)}, bf16[448,1152]{1,0:T(8,128)(2,1)S(1)}, u32[]{:S(2)}, u32[]{:S(2)}) collective-permute-start(bf16[448,1152]{1,0:T(8,128)(2,1)S(1)} %broadcast_select_fusion.3), channel_id=1, source_target_pairs={{0,1},{1,0},{2,3},{3,2},{4,5},{5,4},{6,7},{7,6},{8,9},{9,8},{10,11... | collective-permute-start | bytes 3096584 | tf_op jit(solution)/shard_map/ppermute | solution.py:244
  138.4 28.4 %collective-permute-start.17 = (bf16[448,1152]{1,0:T(8,128)(2,1)S(1)}, bf16[448,1152]{1,0:T(8,128)(2,1)S(1)}, u32[]{:S(2)}, u32[]{:S(2)}) collective-permute-start(bf16[448,1152]{1,0:T(8,128)(2,1)S(1)} %broadcast_select_fusion.2), channel_id=1, source_target_pairs={{0,1},{1,0},{2,3},{3,2},{4,5},{5,4},{6,7},{7,6},{8,9},{9,8},{10,11... | collective-permute-start | bytes 3096584 | tf_op jit(solution)/shard_map/ppermute | solution.py:244
  143.2 3.5 %collective-permute-start.19 = (bf16[448,1152]{1,0:T(8,128)(2,1)S(1)}, bf16[448,1152]{1,0:T(8,128)(2,1)S(1)}, u32[]{:S(2)}, u32[]{:S(2)}) collective-permute-start(bf16[448,1152]{1,0:T(8,128)(2,1)S(1)} %collective-permute-done.18), channel_id=1, source_target_pairs={{1,4},{3,6},{4,1},{6,3},{9,12},{11,14},{12,9},{14,11},{17,20},{19,... | collective-permute-start | bytes 3096584 | tf_op jit(solution)/shard_map/ppermute | solution.py:244
  146.7 36.0 %collective-permute-start.22 = (bf16[448,896]{1,0:T(8,128)(2,1)}, bf16[448,896]{1,0:T(8,128)(2,1)S(1)}, u32[]{:S(2)}, u32[]{:S(2)}) collective-permute-start(bf16[448,896]{1,0:T(8,128)(2,1)} %broadcast_select_fusion.7), channel_id=1, source_target_pairs={{0,1},{1,0},{2,3},{3,2},{4,5},{5,4},{6,7},{7,6},{8,9},{9,8},{10,11... | collective-permute-start | bytes 2408456 | tf_op jit(solution)/shard_map/ppermute | solution.py:244
  165.9 3.5 %collective-permute-start.20 = (bf16[448,1152]{1,0:T(8,128)(2,1)S(1)}, bf16[448,1152]{1,0:T(8,128)(2,1)S(1)}, u32[]{:S(2)}, u32[]{:S(2)}) collective-permute-start(bf16[448,1152]{1,0:T(8,128)(2,1)S(1)} %broadcast_select_fusion.1), channel_id=1, source_target_pairs={{0,1},{1,0},{2,3},{3,2},{4,5},{5,4},{6,7},{7,6},{8,9},{9,8},{10,11... | collective-permute-start | bytes 3096584 | tf_op jit(solution)/shard_map/ppermute | solution.py:244
  179.5 6.2 %collective-permute-start.27 = (bf16[448,896]{1,0:T(8,128)(2,1)}, bf16[448,896]{1,0:T(8,128)(2,1)S(1)}, u32[]{:S(2)}, u32[]{:S(2)}) collective-permute-start(bf16[448,896]{1,0:T(8,128)(2,1)} %collective-permute-done.23), channel_id=1, source_target_pairs={{8,16},{9,17},{10,18},{11,19},{12,20},{13,21},{14,22},{15,23},{16,... | collective-permute-start | bytes 2408456 | tf_op jit(solution)/shard_map/ppermute | solution.py:244
  180.2 23.6 %collective-permute-start.28 = (bf16[448,896]{1,0:T(8,128)(2,1)}, bf16[448,896]{1,0:T(8,128)(2,1)S(1)}, u32[]{:S(2)}, u32[]{:S(2)}) collective-permute-start(bf16[448,896]{1,0:T(8,128)(2,1)} %collective-permute-done.24), channel_id=1, source_target_pairs={{8,0},{9,1},{10,2},{11,3},{12,4},{13,5},{14,6},{15,7},{16,8},{17,9... | collective-permute-start | bytes 2408456 | tf_op jit(solution)/shard_map/ppermute | solution.py:244
  182.2 23.4 %collective-permute-start.26 = (bf16[448,896]{1,0:T(8,128)(2,1)}, bf16[448,896]{1,0:T(8,128)(2,1)S(1)}, u32[]{:S(2)}, u32[]{:S(2)}) collective-permute-start(bf16[448,896]{1,0:T(8,128)(2,1)} %collective-permute-done.24), channel_id=1, source_target_pairs={{0,1},{1,0},{2,3},{3,2},{4,5},{5,4},{6,7},{7,6},{8,9},{9,8},{10,11... | collective-permute-start | bytes 2408456 | tf_op jit(solution)/shard_map/ppermute | solution.py:244
  182.5 25.7 %collective-permute-start.25 = (bf16[448,896]{1,0:T(8,128)(2,1)}, bf16[448,896]{1,0:T(8,128)(2,1)S(1)}, u32[]{:S(2)}, u32[]{:S(2)}) collective-permute-start(bf16[448,896]{1,0:T(8,128)(2,1)} %collective-permute-done.23), channel_id=1, source_target_pairs={{0,1},{1,0},{2,3},{3,2},{4,5},{5,4},{6,7},{7,6},{8,9},{9,8},{10,11... | collective-permute-start | bytes 2408456 | tf_op jit(solution)/shard_map/ppermute | solution.py:244
  203.9 21.2 %collective-permute-start.30 = (bf16[448,896]{1,0:T(8,128)(2,1)S(1)}, bf16[448,896]{1,0:T(8,128)(2,1)S(1)}, u32[]{:S(2)}, u32[]{:S(2)}) collective-permute-start(bf16[448,896]{1,0:T(8,128)(2,1)S(1)} %broadcast_select_fusion.6), channel_id=1, source_target_pairs={{8,0},{9,1},{10,2},{11,3},{12,4},{13,5},{14,6},{15,7},{16,24},{17,... | collective-permute-start | bytes 2408456 | tf_op jit(solution)/shard_map/ppermute | solution.py:244
  205.4 21.1 %collective-permute-start.29 = (bf16[448,896]{1,0:T(8,128)(2,1)S(1)}, bf16[448,896]{1,0:T(8,128)(2,1)S(1)}, u32[]{:S(2)}, u32[]{:S(2)}) collective-permute-start(bf16[448,896]{1,0:T(8,128)(2,1)S(1)} %broadcast_select_fusion.6), channel_id=1, source_target_pairs={{0,1},{1,0},{2,3},{3,2},{4,5},{5,4},{6,7},{7,6},{8,9},{9,8},{10,11... | collective-permute-start | bytes 2408456 | tf_op jit(solution)/shard_map/ppermute | solution.py:244
  212.1 45.0 %collective-permute-start.38 = (bf16[3,128,896]{2,1,0:T(8,128)(2,1)}, bf16[3,128,896]{2,1,0:T(8,128)(2,1)S(1)}, u32[]{:S(2)}, u32[]{:S(2)}) collective-permute-start(bf16[3,128,896]{2,1,0:T(8,128)(2,1)} %pad_maximum_fusion.4), channel_id=1, source_target_pairs={{0,6},{1,7},{2,4},{3,5},{4,2},{5,3},{6,0},{7,1},{8,14},{9,15},{10,... | collective-permute-start | bytes 2064392 | tf_op jit(solution)/shard_map/ppermute | solution.py:244
  214.1 45.7 %collective-permute-start.35 = (bf16[3,128,896]{2,1,0:T(8,128)(2,1)}, bf16[3,128,896]{2,1,0:T(8,128)(2,1)}, u32[]{:S(2)}, u32[]{:S(2)}) collective-permute-start(bf16[3,128,896]{2,1,0:T(8,128)(2,1)} %pad_maximum_fusion.3), channel_id=1, source_target_pairs={{0,2},{1,3},{2,0},{3,1},{4,6},{5,7},{6,4},{7,5},{8,10},{9,11},{10,... | collective-permute-start | bytes 2064392 | tf_op jit(solution)/shard_map/ppermute | solution.py:244
  225.1 2.7 collective-permute-start.31
  226.1 34.3 %collective-permute-start.32 = (bf16[3,128,896]{2,1,0:T(8,128)(2,1)}, bf16[3,128,896]{2,1,0:T(8,128)(2,1)}, u32[]{:S(2)}, u32[]{:S(2)}) collective-permute-start(bf16[3,128,896]{2,1,0:T(8,128)(2,1)} %pad_maximum_fusion.2), channel_id=1, source_target_pairs={{0,4},{1,5},{2,6},{3,7},{4,0},{5,1},{6,2},{7,3},{8,12},{9,13},{10,... | collective-permute-start | bytes 2064392 | tf_op jit(solution)/shard_map/ppermute | solution.py:244
  229.1 17.1 %collective-permute-start.43 = (bf16[5,896]{1,0:T(8,128)(2,1)S(1)}, bf16[5,896]{1,0:T(8,128)(2,1)S(1)}, u32[]{:S(2)}, u32[]{:S(2)}) collective-permute-start(bf16[5,896]{1,0:T(8,128)(2,1)S(1)} %concatenate.71), channel_id=1, source_target_pairs={{0,6},{1,7},{2,4},{3,5},{4,2},{5,3},{6,0},{7,1},{8,14},{9,15},{10,... | collective-permute-start | bytes 26888 | tf_op jit(solution)/shard_map/ppermute | solution.py:244
  232.3 15.9 %collective-permute-start.42 = (bf16[5,896]{1,0:T(8,128)(2,1)S(1)}, bf16[5,896]{1,0:T(8,128)(2,1)S(1)}, u32[]{:S(2)}, u32[]{:S(2)}) collective-permute-start(bf16[5,896]{1,0:T(8,128)(2,1)S(1)} %concatenate.70), channel_id=1, source_target_pairs={{0,2},{1,3},{2,0},{3,1},{4,6},{5,7},{6,4},{7,5},{8,10},{9,11},{10,... | collective-permute-start | bytes 26888 | tf_op jit(solution)/shard_map/ppermute | solution.py:244
  246.2 3.9 %collective-permute-start.41 = (bf16[5,896]{1,0:T(8,128)(2,1)S(1)}, bf16[5,896]{1,0:T(8,128)(2,1)S(1)}, u32[]{:S(2)}, u32[]{:S(2)}) collective-permute-start(bf16[5,896]{1,0:T(8,128)(2,1)S(1)} %concatenate.69), channel_id=1, source_target_pairs={{0,4},{1,5},{2,6},{3,7},{4,0},{5,1},{6,2},{7,3},{8,12},{9,13},{10,... | collective-permute-start | bytes 26888 | tf_op jit(solution)/shard_map/ppermute | solution.py:244
  248.2 12.4 %collective-permute-start.33 = (bf16[1,128,896]{2,1,0:T(8,128)(2,1)S(1)}, bf16[1,128,896]{2,1,0:T(8,128)(2,1)S(1)}, u32[]{:S(2)}, u32[]{:S(2)}) collective-permute-start(bf16[1,128,896]{2,1,0:T(8,128)(2,1)S(1)} %get-tuple-element.55), channel_id=1, source_target_pairs={{0,4},{1,5},{2,6},{3,7},{4,0},{5,1},{6,2},{7,3},{8,12},{9,13},{10,... | collective-permute-start | bytes 688136 | tf_op jit(solution)/shard_map/ppermute | solution.py:244
  250.1 15.2 %collective-permute-start.36 = (bf16[1,128,896]{2,1,0:T(8,128)(2,1)S(1)}, bf16[1,128,896]{2,1,0:T(8,128)(2,1)S(1)}, u32[]{:S(2)}, u32[]{:S(2)}) collective-permute-start(bf16[1,128,896]{2,1,0:T(8,128)(2,1)S(1)} %get-tuple-element.54), channel_id=1, source_target_pairs={{0,2},{1,3},{2,0},{3,1},{4,6},{5,7},{6,4},{7,5},{8,10},{9,11},{10,... | collective-permute-start | bytes 688136 | tf_op jit(solution)/shard_map/ppermute | solution.py:244
  252.8 10.8 %all-to-all-start = ((f32[32,1,128]{2,1,0:T(1,128)}), f32[32,1,128]{2,1,0:T(1,128)S(1)}, u32[]{:S(2)}, u32[]{:S(2)}) async-start(f32[32,1,128]{2,1,0:T(1,128)} %bitcast.112), calls=%async_computation | async-start | bytes 32768 | tf_op jit(solution)/shard_map/all_to_all | solution.py:428
  257.1 9.5 %collective-permute-start.39 = (bf16[1,128,896]{2,1,0:T(8,128)(2,1)S(1)}, bf16[1,128,896]{2,1,0:T(8,128)(2,1)S(1)}, u32[]{:S(2)}, u32[]{:S(2)}) collective-permute-start(bf16[1,128,896]{2,1,0:T(8,128)(2,1)S(1)} %get-tuple-element.53), channel_id=1, source_target_pairs={{0,6},{1,7},{2,4},{3,5},{4,2},{5,3},{6,0},{7,1},{8,14},{9,15},{10,... | collective-permute-start | bytes 688136 | tf_op jit(solution)/shard_map/ppermute | solution.py:244
  259.8 11.7 %collective-permute-start.34 = (bf16[1,128,896]{2,1,0:T(8,128)(2,1)S(1)}, bf16[1,128,896]{2,1,0:T(8,128)(2,1)S(1)}, u32[]{:S(2)}, u32[]{:S(2)}) collective-permute-start(bf16[1,128,896]{2,1,0:T(8,128)(2,1)S(1)} %get-tuple-element.51), channel_id=1, source_target_pairs={{0,4},{1,5},{2,6},{3,7},{4,0},{5,1},{6,2},{7,3},{8,12},{9,13},{10,... | collective-permute-start | bytes 688136 | tf_op jit(solution)/shard_map/ppermute | solution.py:244
  260.4 11.4 %collective-permute-start.37 = (bf16[1,128,896]{2,1,0:T(8,128)(2,1)S(1)}, bf16[1,128,896]{2,1,0:T(8,128)(2,1)S(1)}, u32[]{:S(2)}, u32[]{:S(2)}) collective-permute-start(bf16[1,128,896]{2,1,0:T(8,128)(2,1)S(1)} %get-tuple-element.50), channel_id=1, source_target_pairs={{0,2},{1,3},{2,0},{3,1},{4,6},{5,7},{6,4},{7,5},{8,10},{9,11},{10,... | collective-permute-start | bytes 688136 | tf_op jit(solution)/shard_map/ppermute | solution.py:244
  260.6 15.2 %collective-permute-start.40 = (bf16[1,128,896]{2,1,0:T(8,128)(2,1)S(1)}, bf16[1,128,896]{2,1,0:T(8,128)(2,1)S(1)}, u32[]{:S(2)}, u32[]{:S(2)}) collective-permute-start(bf16[1,128,896]{2,1,0:T(8,128)(2,1)S(1)} %get-tuple-element.49), channel_id=1, source_target_pairs={{0,6},{1,7},{2,4},{3,5},{4,2},{5,3},{6,0},{7,1},{8,14},{9,15},{10,... | collective-permute-start | bytes 688136 | tf_op jit(solution)/shard_map/ppermute | solution.py:244
  (16 other events, 152.8 us)

commit v8 on v7

--- a/solution.py
+++ b/solution.py
@@ -38,11 +38,9 @@
 
 
 def attention_kernel(
-    query_heads, lengths_refs, acc_ref, bias_ref, cos_ref, sin_ref, out_ref
+    query_heads, lengths_ref, acc_ref, bias_ref, cos_ref, sin_ref, out_ref
 ):
-    length = lengths_refs[0][0]
-    for index in range(1, len(lengths_refs)):
-        length = jnp.where(pl.program_id(0) == index, lengths_refs[index][0], length)
+    length = lengths_ref[pl.program_id(0)]
     rows = acc_ref.shape[0]
     cosine = cos_ref[...]
     sine = sin_ref[...]
@@ -87,14 +85,14 @@
     query_cols = query_heads * HEAD_SIZE
 
     def kernel(*refs):
-        attention_kernel(query_heads, refs[:seq_count], *refs[seq_count:])
+        attention_kernel(query_heads, *refs)
 
     return pl.pallas_call(
         kernel,
         name="attention",
         out_shape=jax.ShapeDtypeStruct((total_rows, query_cols), jnp.bfloat16),
         grid_spec=pltpu.PrefetchScalarGridSpec(
-            num_scalar_prefetch=seq_count,
+            num_scalar_prefetch=1,
             grid=(seq_count,),
             in_specs=[
                 pl.BlockSpec((length_rows, width), lambda i, *lengths: (i, 0)),
@@ -109,7 +107,7 @@
             bytes_accessed=acc.size * 4 + total_rows * query_cols * 2,
             transcendentals=seq_count * query_heads * length_rows * length_rows,
         ),
-    )(*group_lengths, acc, bias_cols.reshape(1, width), *tables)
+    )(group_lengths, acc, bias_cols.reshape(1, width), *tables)
 
 
 def norm_kernel(own_ref, by_y_ref, by_x_ref, far_ref, gain_ref, out_ref):
@@ -350,10 +348,9 @@
         row_places = [
             j * length_rows + group_length - 1 for j, group_length in enumerate(group_lengths)
         ]
-        normed, near_lengths, row_places = lax.optimization_barrier(
-            (normed, near_lengths, row_places)
+        normed, group_lengths, row_places = lax.optimization_barrier(
+            (normed, jnp.stack(group_lengths)[:, 0], row_places)
         )
-        group_lengths = [lengths, *near_lengths]
         acc = None
         for (plane, own), other in zip(qkv_blocks, others):
             for core, weights in ((c, own), (1 - c, other)):

time: 283 us -> 282 us (level)
  waiting for transfers between devices: 112 us -> 109 us
  transfers between devices with their start and end apart: 45 -> 45, of which waited for: 16 -> 16; matrix products, arithmetic and copies ran while one was open for 15% -> 16% of each run, Pallas kernels for 5% -> 5%
where the time goes in v8:
time: 282 us; the launch traced here: 281 us
  waiting for transfers between devices  109 us (39%)
  starting transfers between devices  94.8 us (34%)
  matrix products  20.8 us (7%)
  Pallas kernels  18.2 us (6%)
  other arithmetic  17.4 us (6%)
  local copies, waits for them, and re-layouts  13.9 us (5%)
  between operations  6.67 us (2%)
    ppermute x44, waiting for transfers between devices, send(): return lax.ppermute(array, AXES, route(move))  109 us
    ppermute x44, starting transfers between devices, send(): return lax.ppermute(array, AXES, route(move))  91.4 us
    dot_general x5, matrix products, whole(): lax.dot_general(attn, weights, (((1,), (1,)), ((), ())), preferred_elemen...  10.8 us
    dot_general x10, matrix products, whole(): jnp.dot(lax.dynamic_index_in_dim(normed, jnp.maximum(plane, 0) * 2 + core...  10 us
    pallas_call x1, Pallas kernels, normalise(): pl.pallas_call(norm_kernel, name='normalise', out_shape=jax.ShapeDtypeStr...  6.51 us
    pallas_call x1, Pallas kernels, attend(): pl.pallas_call(kernel, name='attention', out_shape=jax.ShapeDtypeStruct((...  5.72 us
  transfers between devices with their start and end apart: 45, of which 16 were waited for; matrix products, arithmetic and copies ran while one was open for 16% of the time, Pallas kernels for 5%

profile of v8, /device:TPU:0, one launch (start us, length us, event | category | flops | bytes accessed | tf_op | source)
XLA Modules:
  0.0 281.1 jit_solution(7418298880713866165)
XLA Ops:
  4.1 5.9 %collective-permute-start.8 = (bf16[448,1152]{1,0:T(8,128)(2,1)}, bf16[448,1152]{1,0:T(8,128)(2,1)}, u32[]{:S(2)}, u32[]{:S(2)}) collective-permute-start(bf16[448,1152]{1,0:T(8,128)(2,1)} %pad_maximum_fusion), channel_id=1, source_target_pairs={{0,8},{1,9},{2,10},{3,11},{4,12},{5,13},{6,14},{7,15},{8,16},{9,17... | collective-permute-start | bytes 3096584 | tf_op jit(solution)/shard_map/ppermute | solution.py:242
  11.4 1.6 collective-permute-start
  13.0 2.1 dynamic-slice_bitcast_fusion
  15.0 1.6 collective-permute-start.21
  16.6 1.3 collective-permute-start.3
  20.1 21.7 %collective-permute-done.3 = s32[1]{0:T(128)} collective-permute-done((s32[1]{0:T(128)}, s32[1]{0:T(128)}, u32[]{:S(2)}, u32[]{:S(2)}) %collective-permute-start.3) | collective-permute-done | bytes 36 | tf_op jit(solution)/shard_map/ppermute | solution.py:242
  41.8 1.5 collective-permute-start.4
  43.3 2.2 collective-permute-done.4
  46.1 3.9 %collective-permute-done.5 = s32[1]{0:T(128)} collective-permute-done((s32[1]{0:T(128)}, s32[1]{0:T(128)}, u32[]{:S(2)}, u32[]{:S(2)}) %collective-permute-start.5) | collective-permute-done | bytes 36 | tf_op jit(solution)/shard_map/ppermute | solution.py:242
  54.5 1.6 collective-permute-start.14
  56.2 1.3 collective-permute-start.15
  60.2 1.6 collective-permute-start.1
  62.3 2.7 add_bitcast_fusion.refs_0_
  65.0 2.2 broadcast_select_fusion.7
  68.2 1.6 collective-permute-start.9
  70.1 13.0 %collective-permute-done.1.by_x_ref = bf16[128,3584]{1,0:T(8,128)(2,1)S(1)} collective-permute-done((bf16[128,3584]{1,0:T(8,128)(2,1)S(1)}, bf16[128,3584]{1,0:T(8,128)(2,1)S(1)}, u32[]{:S(2)}, u32[]{:S(2)}) %collective-permute-start.1) | collective-permute-done | bytes 917536 | tf_op jit(solution)/shard_map/ppermute | solution.py:242
  84.1 8.0 %collective-permute-start.23 = (bf16[448,896]{1,0:T(8,128)(2,1)}, bf16[448,896]{1,0:T(8,128)(2,1)}, u32[]{:S(2)}, u32[]{:S(2)}) collective-permute-start(bf16[448,896]{1,0:T(8,128)(2,1)} %broadcast_select_fusion.7), channel_id=1, source_target_pairs={{0,8},{1,9},{2,10},{3,11},{4,12},{5,13},{6,14},{7,15},{8,16},{9,17... | collective-permute-start | bytes 2408456 | tf_op jit(solution)/shard_map/ppermute | solution.py:242
  92.1 10.9 %collective-permute-done.2.far_ref = bf16[128,3584]{1,0:T(8,128)(2,1)} collective-permute-done((bf16[128,3584]{1,0:T(8,128)(2,1)}, bf16[128,3584]{1,0:T(8,128)(2,1)}, u32[]{:S(2)}, u32[]{:S(2)}) %collective-permute-start.2) | collective-permute-done | bytes 917536 | tf_op jit(solution)/shard_map/ppermute | solution.py:242
  102.9 1.3 collective-permute-start.24
  104.2 6.5 %normalise.1 = bf16[8,512,448]{2,1,0:T(8,128)(2,1)} custom-call(bf16[128,3584]{1,0:T(8,128)(2,1)} %bitcast.113, bf16[128,3584]{1,0:T(8,128)(2,1)} %collective-permute-done.by_y_ref, bf16[128,3584]{1,0:T(8,128)(2,1)} %copy-done.3, bf16[128,3584]{1,0:T(8,128)(2,1)} %collective-permute-done.2.far_ref, f32[1,3584]{1,0:T(1,128)} %reshape.38.gain_ref), custom_call_target="tpu_custom_call" | custom-call | flops 14680064 | bytes 7340032 | tf_op jit(solution)/shard_map/normalise/pallas_call | solution.py:135
  111.6 1.4 broadcast_select_fusion
  113.9 1.7 broadcast_select_fusion.4
  115.6 1.3 collective-permute-start.18
  116.9 1.4 broadcast_select_fusion.3
  118.3 11.0 %collective-permute-start.10 = (bf16[448,1152]{1,0:T(8,128)(2,1)S(1)}, bf16[448,1152]{1,0:T(8,128)(2,1)S(1)}, u32[]{:S(2)}, u32[]{:S(2)}) collective-permute-start(bf16[448,1152]{1,0:T(8,128)(2,1)S(1)} %broadcast_select_fusion.4), channel_id=1, source_target_pairs={{0,1},{1,0},{2,3},{3,2},{4,5},{5,4},{6,7},{7,6},{8,9},{9,8},{10,11... | collective-permute-start | bytes 3096584 | tf_op jit(solution)/shard_map/ppermute | solution.py:242
  131.1 7.7 %collective-permute-start.13 = (bf16[448,1152]{1,0:T(8,128)(2,1)S(1)}, bf16[448,1152]{1,0:T(8,128)(2,1)S(1)}, u32[]{:S(2)}, u32[]{:S(2)}) collective-permute-start(bf16[448,1152]{1,0:T(8,128)(2,1)S(1)} %broadcast_select_fusion.3), channel_id=1, source_target_pairs={{0,1},{1,0},{2,3},{3,2},{4,5},{5,4},{6,7},{7,6},{8,9},{9,8},{10,11... | collective-permute-start | bytes 3096584 | tf_op jit(solution)/shard_map/ppermute | solution.py:242
  139.0 4.7 %collective-permute-done.18 = bf16[448,1152]{1,0:T(8,128)(2,1)S(1)} collective-permute-done((bf16[448,1152]{1,0:T(8,128)(2,1)S(1)}, bf16[448,1152]{1,0:T(8,128)(2,1)S(1)}, u32[]{:S(2)}, u32[]{:S(2)}) %collective-permute-start.18) | collective-permute-done | bytes 1032224 | tf_op jit(solution)/shard_map/ppermute | solution.py:242
  147.1 19.1 %collective-permute-start.22 = (bf16[448,896]{1,0:T(8,128)(2,1)}, bf16[448,896]{1,0:T(8,128)(2,1)S(1)}, u32[]{:S(2)}, u32[]{:S(2)}) collective-permute-start(bf16[448,896]{1,0:T(8,128)(2,1)} %broadcast_select_fusion.7), channel_id=1, source_target_pairs={{0,1},{1,0},{2,3},{3,2},{4,5},{5,4},{6,7},{7,6},{8,9},{9,8},{10,11... | collective-permute-start | bytes 2408456 | tf_op jit(solution)/shard_map/ppermute | solution.py:242
  170.7 2.3 fusion.3.refs_1_
  173.0 5.7 %attention.1 = bf16[512,896]{1,0:T(8,128)(2,1)} custom-call(s32[4]{0:T(128)} %add_bitcast_fusion.refs_0_, f32[512,1152]{1,0:T(8,128)} %fusion.3.refs_1_, f32[1,1152]{1,0:T(1,128)} %reshape.39.refs_2_, f32[128,128]{1,0:T(8,128)} %get-tuple-element.70.refs_3_, f32[128,128]{1,0:T(8,128)} %get-tuple-element.71.refs_4_), custom_call_target="tpu_custom_call" | custom-call | flops 1879048192 | bytes 3276800 | tf_op jit(solution)/shard_map/attention/pallas_call | solution.py:90
  179.4 1.3 collective-permute-start.28
  181.9 2.9 %fusion.44 = bf16[512,896]{1,0:T(8,128)(2,1)S(1)} fusion(bf16[512,896]{1,0:T(8,128)(2,1)} %attention.1, bf16[448,896]{1,0:T(8,128)(2,1)S(1)} %collective-permute-done.22, bf16[448,896]{1,0:T(8,128)(2,1)} %broadcast_select_fusion.7, pred[]{:T(512)S(6)} %eq.97), kind=kOutput, calls=%fused_computation.53 | convolution fusion | flops 829767680 | bytes 3440641 | tf_op jit(solution)/shard_map/dot_general | solution.py:387
  184.9 18.1 %collective-permute-done.28 = bf16[448,896]{1,0:T(8,128)(2,1)S(1)} collective-permute-done((bf16[448,896]{1,0:T(8,128)(2,1)}, bf16[448,896]{1,0:T(8,128)(2,1)S(1)}, u32[]{:S(2)}, u32[]{:S(2)}) %collective-permute-start.28) | collective-permute-done | bytes 802848 | tf_op jit(solution)/shard_map/ppermute | solution.py:242
  203.1 1.5 collective-permute-start.30
  204.7 2.7 fusion.42
  207.5 2.7 fusion.43
  214.3 10.0 %collective-permute-done.30 = bf16[448,896]{1,0:T(8,128)(2,1)S(1)} collective-permute-done((bf16[448,896]{1,0:T(8,128)(2,1)S(1)}, bf16[448,896]{1,0:T(8,128)(2,1)S(1)}, u32[]{:S(2)}, u32[]{:S(2)}) %collective-permute-start.30) | collective-permute-done | bytes 802848 | tf_op jit(solution)/shard_map/ppermute | solution.py:242
  228.3 2.3 collective-permute-start.43
  232.7 12.8 %collective-permute-done.43.refs_3_ = bf16[5,896]{1,0:T(8,128)(2,1)S(1)} collective-permute-done((bf16[5,896]{1,0:T(8,128)(2,1)S(1)}, bf16[5,896]{1,0:T(8,128)(2,1)S(1)}, u32[]{:S(2)}, u32[]{:S(2)}) %collective-permute-start.43) | collective-permute-done | bytes 8992 | tf_op jit(solution)/shard_map/ppermute | solution.py:242
  247.5 1.4 collective-permute-start.33
  250.5 1.7 score.1
  252.2 3.4 %all-to-all-start = ((f32[32,1,128]{2,1,0:T(1,128)}), f32[32,1,128]{2,1,0:T(1,128)S(1)}, u32[]{:S(2)}, u32[]{:S(2)}) async-start(f32[32,1,128]{2,1,0:T(1,128)} %bitcast.119), calls=%async_computation | async-start | bytes 32768 | tf_op jit(solution)/shard_map/all_to_all | solution.py:425
  256.4 2.7 collective-permute-start.39
  259.9 2.7 collective-permute-start.40
  264.5 1.3 collective-permute-done.39.refs_12_
  265.9 4.8 %collective-permute-done.34.refs_7_ = bf16[1,128,896]{2,1,0:T(8,128)(2,1)S(1)} collective-permute-done((bf16[1,128,896]{2,1,0:T(8,128)(2,1)S(1)}, bf16[1,128,896]{2,1,0:T(8,128)(2,1)S(1)}, u32[]{:S(2)}, u32[]{:S(2)}) %collective-permute-start.34) | collective-permute-done | bytes 229408 | tf_op jit(solution)/shard_map/ppermute | solution.py:242
  271.0 4.0 %collective-permute-done.40.refs_13_ = bf16[1,128,896]{2,1,0:T(8,128)(2,1)S(1)} collective-permute-done((bf16[1,128,896]{2,1,0:T(8,128)(2,1)S(1)}, bf16[1,128,896]{2,1,0:T(8,128)(2,1)S(1)}, u32[]{:S(2)}, u32[]{:S(2)}) %collective-permute-start.40) | collective-permute-done | bytes 229408 | tf_op jit(solution)/shard_map/ppermute | solution.py:242
  275.7 4.3 %finish.1 = bf16[128,3584]{1,0:T(8,128)(2,1)} custom-call(s32[4]{0:T(128)} %pad_add_fusion.refs_0_.slots_ref, bf16[128,3584]{1,0:T(8,128)(2,1)} %bitcast.114, bf16[3,128,896]{2,1,0:T(8,128)(2,1)} %pad_maximum_fusion.1.refs_2_, bf16[1,128,896]{2,1,0:T(8,128)(2,1)} %get-tuple-element.52.refs_3_, bf16[1,128,896]{2,1,0:T(8,128)(2,1)} %get-tuple-element.48.refs_4_, ...), custom_call_target="tpu_custom_call" | custom-call | flops 3670016 | bytes 2752512 | tf_op jit(solution)/shard_map/finish/pallas_call | solution.py:172
  (146 shorter events, 45.1 us)
Async XLA Ops:
  2.0 50.8 %copy-start.11 = (f32[3584]{0:T(1024)S(1)}, f32[3584]{0:T(1024)}, u32[]{:S(2)}) copy-start(f32[3584]{0:T(1024)} %param.18) | copy-start | bytes 43012
  2.0 50.8 %copy-start.12 = (f32[3584]{0:T(1024)S(1)}, f32[3584]{0:T(1024)}, u32[]{:S(2)}) copy-start(f32[3584]{0:T(1024)} %param.19) | copy-start | bytes 43012
  4.1 50.4 %collective-permute-start.8 = (bf16[448,1152]{1,0:T(8,128)(2,1)}, bf16[448,1152]{1,0:T(8,128)(2,1)}, u32[]{:S(2)}, u32[]{:S(2)}) collective-permute-start(bf16[448,1152]{1,0:T(8,128)(2,1)} %pad_maximum_fusion), channel_id=1, source_target_pairs={{0,8},{1,9},{2,10},{3,11},{4,12},{5,13},{6,14},{7,15},{8,16},{9,17... | collective-permute-start | bytes 3096584 | tf_op jit(solution)/shard_map/ppermute | solution.py:242
  10.1 46.1 %collective-permute-start.11 = (bf16[448,1152]{1,0:T(8,128)(2,1)}, bf16[448,1152]{1,0:T(8,128)(2,1)}, u32[]{:S(2)}, u32[]{:S(2)}) collective-permute-start(bf16[448,1152]{1,0:T(8,128)(2,1)} %pad_maximum_fusion), channel_id=1, source_target_pairs={{8,0},{9,1},{10,2},{11,3},{12,4},{13,5},{14,6},{15,7},{16,8},{17,9... | collective-permute-start | bytes 3096584 | tf_op jit(solution)/shard_map/ppermute | solution.py:242
  11.4 50.4 %collective-permute-start = (bf16[128,3584]{1,0:T(8,128)(2,1)S(1)}, bf16[128,3584]{1,0:T(8,128)(2,1)}, u32[]{:S(2)}, u32[]{:S(2)}) collective-permute-start(bf16[128,3584]{1,0:T(8,128)(2,1)S(1)} %bitcast.115), channel_id=1, source_target_pairs={{0,4},{1,5},{2,6},{3,7},{4,0},{5,1},{6,2},{7,3},{8,12},{9,13},{10,... | collective-permute-start | bytes 2752520 | tf_op jit(solution)/shard_map/ppermute | solution.py:242
  15.0 45.2 %collective-permute-start.21 = (bf16[448,896]{1,0:T(8,128)(2,1)}, bf16[448,896]{1,0:T(8,128)(2,1)}, u32[]{:S(2)}, u32[]{:S(2)}) collective-permute-start(bf16[448,896]{1,0:T(8,128)(2,1)} %dynamic-slice_bitcast_fusion), channel_id=1, source_target_pairs={{1,4},{3,6},{4,1},{6,3},{9,12},{11,14},{12,9},{14,11},{17,20},{19,... | collective-permute-start | bytes 2408456 | tf_op jit(solution)/shard_map/ppermute | solution.py:242
  16.6 25.2 %collective-permute-start.3 = (s32[1]{0:T(128)}, s32[1]{0:T(128)}, u32[]{:S(2)}, u32[]{:S(2)}) collective-permute-start(s32[1]{0:T(128)} %param.11), channel_id=1, source_target_pairs={{0,4},{1,5},{2,6},{3,7},{4,0},{5,1},{6,2},{7,3},{8,12},{9,13},{10,... | collective-permute-start | bytes 20 | tf_op jit(solution)/shard_map/ppermute | solution.py:242
  41.8 3.7 %collective-permute-start.4 = (s32[1]{0:T(128)}, s32[1]{0:T(128)}, u32[]{:S(2)}, u32[]{:S(2)}) collective-permute-start(s32[1]{0:T(128)} %param.11), channel_id=1, source_target_pairs={{0,2},{1,3},{2,0},{3,1},{4,6},{5,7},{6,4},{7,5},{8,10},{9,11},{10,... | collective-permute-start | bytes 20 | tf_op jit(solution)/shard_map/ppermute | solution.py:242
  45.5 4.6 %collective-permute-start.5 = (s32[1]{0:T(128)}, s32[1]{0:T(128)}, u32[]{:S(2)}, u32[]{:S(2)}) collective-permute-start(s32[1]{0:T(128)} %param.11), channel_id=1, source_target_pairs={{0,6},{1,7},{2,4},{3,5},{4,2},{5,3},{6,0},{7,1},{8,14},{9,15},{10,... | collective-permute-start | bytes 20 | tf_op jit(solution)/shard_map/ppermute | solution.py:242
  50.0 17.2 %collective-permute-start.6 = (bf16[448,1152]{1,0:T(8,128)(2,1)}, bf16[448,1152]{1,0:T(8,128)(2,1)S(1)}, u32[]{:S(2)}, u32[]{:S(2)}) collective-permute-start(bf16[448,1152]{1,0:T(8,128)(2,1)} %pad_maximum_fusion), channel_id=1, source_target_pairs={{1,4},{3,6},{4,1},{6,3},{9,12},{11,14},{12,9},{14,11},{17,20},{19,... | collective-permute-start | bytes 3096584 | tf_op jit(solution)/shard_map/ppermute | solution.py:242
  54.5 56.2 %collective-permute-start.14 = (bf16[448,1152]{1,0:T(8,128)(2,1)}, bf16[448,1152]{1,0:T(8,128)(2,1)}, u32[]{:S(2)}, u32[]{:S(2)}) collective-permute-start(bf16[448,1152]{1,0:T(8,128)(2,1)} %collective-permute-done.8), channel_id=1, source_target_pairs={{8,16},{9,17},{10,18},{11,19},{12,20},{13,21},{14,22},{15,23},{16,... | collective-permute-start | bytes 3096584 | tf_op jit(solution)/shard_map/ppermute | solution.py:242
  56.2 54.7 %collective-permute-start.15 = (bf16[448,1152]{1,0:T(8,128)(2,1)}, bf16[448,1152]{1,0:T(8,128)(2,1)}, u32[]{:S(2)}, u32[]{:S(2)}) collective-permute-start(bf16[448,1152]{1,0:T(8,128)(2,1)} %collective-permute-done.11), channel_id=1, source_target_pairs={{8,0},{9,1},{10,2},{11,3},{12,4},{13,5},{14,6},{15,7},{16,8},{17,9... | collective-permute-start | bytes 3096584 | tf_op jit(solution)/shard_map/ppermute | solution.py:242
  60.2 22.9 %collective-permute-start.1 = (bf16[128,3584]{1,0:T(8,128)(2,1)S(1)}, bf16[128,3584]{1,0:T(8,128)(2,1)S(1)}, u32[]{:S(2)}, u32[]{:S(2)}) collective-permute-start(bf16[128,3584]{1,0:T(8,128)(2,1)S(1)} %bitcast.116), channel_id=1, source_target_pairs={{0,2},{1,3},{2,0},{3,1},{4,6},{5,7},{6,4},{7,5},{8,10},{9,11},{10,... | collective-permute-start | bytes 2752520 | tf_op jit(solution)/shard_map/ppermute | solution.py:242
  61.8 41.1 %collective-permute-start.2 = (bf16[128,3584]{1,0:T(8,128)(2,1)}, bf16[128,3584]{1,0:T(8,128)(2,1)}, u32[]{:S(2)}, u32[]{:S(2)}) collective-permute-start(bf16[128,3584]{1,0:T(8,128)(2,1)} %collective-permute-done.by_y_ref), channel_id=1, source_target_pairs={{0,2},{1,3},{2,0},{3,1},{4,6},{5,7},{6,4},{7,5},{8,10},{9,11},{10,... | collective-permute-start | bytes 2752520 | tf_op jit(solution)/shard_map/ppermute | solution.py:242
  68.2 44.8 %collective-permute-start.9 = (bf16[448,1152]{1,0:T(8,128)(2,1)}, bf16[448,1152]{1,0:T(8,128)(2,1)}, u32[]{:S(2)}, u32[]{:S(2)}) collective-permute-start(bf16[448,1152]{1,0:T(8,128)(2,1)} %collective-permute-done.8), channel_id=1, source_target_pairs={{1,4},{3,6},{4,1},{6,3},{9,12},{11,14},{12,9},{14,11},{17,20},{19,... | collective-permute-start | bytes 3096584 | tf_op jit(solution)/shard_map/ppermute | solution.py:242
  84.1 94.6 %collective-permute-start.23 = (bf16[448,896]{1,0:T(8,128)(2,1)}, bf16[448,896]{1,0:T(8,128)(2,1)}, u32[]{:S(2)}, u32[]{:S(2)}) collective-permute-start(bf16[448,896]{1,0:T(8,128)(2,1)} %broadcast_select_fusion.7), channel_id=1, source_target_pairs={{0,8},{1,9},{2,10},{3,11},{4,12},{5,13},{6,14},{7,15},{8,16},{9,17... | collective-permute-start | bytes 2408456 | tf_op jit(solution)/shard_map/ppermute | solution.py:242
  102.9 75.8 %collective-permute-start.24 = (bf16[448,896]{1,0:T(8,128)(2,1)}, bf16[448,896]{1,0:T(8,128)(2,1)}, u32[]{:S(2)}, u32[]{:S(2)}) collective-permute-start(bf16[448,896]{1,0:T(8,128)(2,1)} %broadcast_select_fusion.7), channel_id=1, source_target_pairs={{8,0},{9,1},{10,2},{11,3},{12,4},{13,5},{14,6},{15,7},{16,8},{17,9... | collective-permute-start | bytes 2408456 | tf_op jit(solution)/shard_map/ppermute | solution.py:242
  110.7 7.6 %collective-permute-start.7 = (bf16[448,1152]{1,0:T(8,128)(2,1)S(1)}, bf16[448,1152]{1,0:T(8,128)(2,1)S(1)}, u32[]{:S(2)}, u32[]{:S(2)}) collective-permute-start(bf16[448,1152]{1,0:T(8,128)(2,1)S(1)} %broadcast_select_fusion.5), channel_id=1, source_target_pairs={{0,1},{1,0},{2,3},{3,2},{4,5},{5,4},{6,7},{7,6},{8,9},{9,8},{10,11... | collective-permute-start | bytes 3096584 | tf_op jit(solution)/shard_map/ppermute | solution.py:242
  110.9 4.7 %collective-permute-start.12 = (bf16[448,1152]{1,0:T(8,128)(2,1)}, bf16[448,1152]{1,0:T(8,128)(2,1)S(1)}, u32[]{:S(2)}, u32[]{:S(2)}) collective-permute-start(bf16[448,1152]{1,0:T(8,128)(2,1)} %collective-permute-done.11), channel_id=1, source_target_pairs={{1,4},{3,6},{4,1},{6,3},{9,12},{11,14},{12,9},{14,11},{17,20},{19,... | collective-permute-start | bytes 3096584 | tf_op jit(solution)/shard_map/ppermute | solution.py:242
  113.0 18.0 %collective-permute-start.16 = (bf16[448,1152]{1,0:T(8,128)(2,1)S(1)}, bf16[448,1152]{1,0:T(8,128)(2,1)S(1)}, u32[]{:S(2)}, u32[]{:S(2)}) collective-permute-start(bf16[448,1152]{1,0:T(8,128)(2,1)S(1)} %broadcast_select_fusion), channel_id=1, source_target_pairs={{1,4},{3,6},{4,1},{6,3},{9,12},{11,14},{12,9},{14,11},{17,20},{19,... | collective-permute-start | bytes 3096584 | tf_op jit(solution)/shard_map/ppermute | solution.py:242
  115.6 28.1 %collective-permute-start.18 = (bf16[448,1152]{1,0:T(8,128)(2,1)S(1)}, bf16[448,1152]{1,0:T(8,128)(2,1)S(1)}, u32[]{:S(2)}, u32[]{:S(2)}) collective-permute-start(bf16[448,1152]{1,0:T(8,128)(2,1)S(1)} %broadcast_select_fusion), channel_id=1, source_target_pairs={{8,0},{9,1},{10,2},{11,3},{12,4},{13,5},{14,6},{15,7},{16,24},{17,... | collective-permute-start | bytes 3096584 | tf_op jit(solution)/shard_map/ppermute | solution.py:242
  118.3 20.6 %collective-permute-start.10 = (bf16[448,1152]{1,0:T(8,128)(2,1)S(1)}, bf16[448,1152]{1,0:T(8,128)(2,1)S(1)}, u32[]{:S(2)}, u32[]{:S(2)}) collective-permute-start(bf16[448,1152]{1,0:T(8,128)(2,1)S(1)} %broadcast_select_fusion.4), channel_id=1, source_target_pairs={{0,1},{1,0},{2,3},{3,2},{4,5},{5,4},{6,7},{7,6},{8,9},{9,8},{10,11... | collective-permute-start | bytes 3096584 | tf_op jit(solution)/shard_map/ppermute | solution.py:242
  131.1 35.3 %collective-permute-start.13 = (bf16[448,1152]{1,0:T(8,128)(2,1)S(1)}, bf16[448,1152]{1,0:T(8,128)(2,1)S(1)}, u32[]{:S(2)}, u32[]{:S(2)}) collective-permute-start(bf16[448,1152]{1,0:T(8,128)(2,1)S(1)} %broadcast_select_fusion.3), channel_id=1, source_target_pairs={{0,1},{1,0},{2,3},{3,2},{4,5},{5,4},{6,7},{7,6},{8,9},{9,8},{10,11... | collective-permute-start | bytes 3096584 | tf_op jit(solution)/shard_map/ppermute | solution.py:242
  138.9 28.4 %collective-permute-start.17 = (bf16[448,1152]{1,0:T(8,128)(2,1)S(1)}, bf16[448,1152]{1,0:T(8,128)(2,1)S(1)}, u32[]{:S(2)}, u32[]{:S(2)}) collective-permute-start(bf16[448,1152]{1,0:T(8,128)(2,1)S(1)} %broadcast_select_fusion.2), channel_id=1, source_target_pairs={{0,1},{1,0},{2,3},{3,2},{4,5},{5,4},{6,7},{7,6},{8,9},{9,8},{10,11... | collective-permute-start | bytes 3096584 | tf_op jit(solution)/shard_map/ppermute | solution.py:242
  143.7 3.5 %collective-permute-start.19 = (bf16[448,1152]{1,0:T(8,128)(2,1)S(1)}, bf16[448,1152]{1,0:T(8,128)(2,1)S(1)}, u32[]{:S(2)}, u32[]{:S(2)}) collective-permute-start(bf16[448,1152]{1,0:T(8,128)(2,1)S(1)} %collective-permute-done.18), channel_id=1, source_target_pairs={{1,4},{3,6},{4,1},{6,3},{9,12},{11,14},{12,9},{14,11},{17,20},{19,... | collective-permute-start | bytes 3096584 | tf_op jit(solution)/shard_map/ppermute | solution.py:242
  147.1 34.8 %collective-permute-start.22 = (bf16[448,896]{1,0:T(8,128)(2,1)}, bf16[448,896]{1,0:T(8,128)(2,1)S(1)}, u32[]{:S(2)}, u32[]{:S(2)}) collective-permute-start(bf16[448,896]{1,0:T(8,128)(2,1)} %broadcast_select_fusion.7), channel_id=1, source_target_pairs={{0,1},{1,0},{2,3},{3,2},{4,5},{5,4},{6,7},{7,6},{8,9},{9,8},{10,11... | collective-permute-start | bytes 2408456 | tf_op jit(solution)/shard_map/ppermute | solution.py:242
  166.4 3.5 %collective-permute-start.20 = (bf16[448,1152]{1,0:T(8,128)(2,1)S(1)}, bf16[448,1152]{1,0:T(8,128)(2,1)S(1)}, u32[]{:S(2)}, u32[]{:S(2)}) collective-permute-start(bf16[448,1152]{1,0:T(8,128)(2,1)S(1)} %broadcast_select_fusion.1), channel_id=1, source_target_pairs={{0,1},{1,0},{2,3},{3,2},{4,5},{5,4},{6,7},{7,6},{8,9},{9,8},{10,11... | collective-permute-start | bytes 3096584 | tf_op jit(solution)/shard_map/ppermute | solution.py:242
  178.7 6.2 %collective-permute-start.27 = (bf16[448,896]{1,0:T(8,128)(2,1)}, bf16[448,896]{1,0:T(8,128)(2,1)S(1)}, u32[]{:S(2)}, u32[]{:S(2)}) collective-permute-start(bf16[448,896]{1,0:T(8,128)(2,1)} %collective-permute-done.23), channel_id=1, source_target_pairs={{8,16},{9,17},{10,18},{11,19},{12,20},{13,21},{14,22},{15,23},{16,... | collective-permute-start | bytes 2408456 | tf_op jit(solution)/shard_map/ppermute | solution.py:242
  179.4 23.6 %collective-permute-start.28 = (bf16[448,896]{1,0:T(8,128)(2,1)}, bf16[448,896]{1,0:T(8,128)(2,1)S(1)}, u32[]{:S(2)}, u32[]{:S(2)}) collective-permute-start(bf16[448,896]{1,0:T(8,128)(2,1)} %collective-permute-done.24), channel_id=1, source_target_pairs={{8,0},{9,1},{10,2},{11,3},{12,4},{13,5},{14,6},{15,7},{16,8},{17,9... | collective-permute-start | bytes 2408456 | tf_op jit(solution)/shard_map/ppermute | solution.py:242
  181.4 23.4 %collective-permute-start.26 = (bf16[448,896]{1,0:T(8,128)(2,1)}, bf16[448,896]{1,0:T(8,128)(2,1)S(1)}, u32[]{:S(2)}, u32[]{:S(2)}) collective-permute-start(bf16[448,896]{1,0:T(8,128)(2,1)} %collective-permute-done.24), channel_id=1, source_target_pairs={{0,1},{1,0},{2,3},{3,2},{4,5},{5,4},{6,7},{7,6},{8,9},{9,8},{10,11... | collective-permute-start | bytes 2408456 | tf_op jit(solution)/shard_map/ppermute | solution.py:242
  181.8 25.7 %collective-permute-start.25 = (bf16[448,896]{1,0:T(8,128)(2,1)}, bf16[448,896]{1,0:T(8,128)(2,1)S(1)}, u32[]{:S(2)}, u32[]{:S(2)}) collective-permute-start(bf16[448,896]{1,0:T(8,128)(2,1)} %collective-permute-done.23), channel_id=1, source_target_pairs={{0,1},{1,0},{2,3},{3,2},{4,5},{5,4},{6,7},{7,6},{8,9},{9,8},{10,11... | collective-permute-start | bytes 2408456 | tf_op jit(solution)/shard_map/ppermute | solution.py:242
  203.1 21.2 %collective-permute-start.30 = (bf16[448,896]{1,0:T(8,128)(2,1)S(1)}, bf16[448,896]{1,0:T(8,128)(2,1)S(1)}, u32[]{:S(2)}, u32[]{:S(2)}) collective-permute-start(bf16[448,896]{1,0:T(8,128)(2,1)S(1)} %broadcast_select_fusion.6), channel_id=1, source_target_pairs={{8,0},{9,1},{10,2},{11,3},{12,4},{13,5},{14,6},{15,7},{16,24},{17,... | collective-permute-start | bytes 2408456 | tf_op jit(solution)/shard_map/ppermute | solution.py:242
  204.6 21.1 %collective-permute-start.29 = (bf16[448,896]{1,0:T(8,128)(2,1)S(1)}, bf16[448,896]{1,0:T(8,128)(2,1)S(1)}, u32[]{:S(2)}, u32[]{:S(2)}) collective-permute-start(bf16[448,896]{1,0:T(8,128)(2,1)S(1)} %broadcast_select_fusion.6), channel_id=1, source_target_pairs={{0,1},{1,0},{2,3},{3,2},{4,5},{5,4},{6,7},{7,6},{8,9},{9,8},{10,11... | collective-permute-start | bytes 2408456 | tf_op jit(solution)/shard_map/ppermute | solution.py:242
  211.3 45.0 %collective-permute-start.38 = (bf16[3,128,896]{2,1,0:T(8,128)(2,1)}, bf16[3,128,896]{2,1,0:T(8,128)(2,1)S(1)}, u32[]{:S(2)}, u32[]{:S(2)}) collective-permute-start(bf16[3,128,896]{2,1,0:T(8,128)(2,1)} %pad_maximum_fusion.4), channel_id=1, source_target_pairs={{0,6},{1,7},{2,4},{3,5},{4,2},{5,3},{6,0},{7,1},{8,14},{9,15},{10,... | collective-permute-start | bytes 2064392 | tf_op jit(solution)/shard_map/ppermute | solution.py:242
  213.4 45.6 %collective-permute-start.35 = (bf16[3,128,896]{2,1,0:T(8,128)(2,1)}, bf16[3,128,896]{2,1,0:T(8,128)(2,1)}, u32[]{:S(2)}, u32[]{:S(2)}) collective-permute-start(bf16[3,128,896]{2,1,0:T(8,128)(2,1)} %pad_maximum_fusion.3), channel_id=1, source_target_pairs={{0,2},{1,3},{2,0},{3,1},{4,6},{5,7},{6,4},{7,5},{8,10},{9,11},{10,... | collective-permute-start | bytes 2064392 | tf_op jit(solution)/shard_map/ppermute | solution.py:242
  224.3 2.7 collective-permute-start.31
  225.3 34.3 %collective-permute-start.32 = (bf16[3,128,896]{2,1,0:T(8,128)(2,1)}, bf16[3,128,896]{2,1,0:T(8,128)(2,1)}, u32[]{:S(2)}, u32[]{:S(2)}) collective-permute-start(bf16[3,128,896]{2,1,0:T(8,128)(2,1)} %pad_maximum_fusion.2), channel_id=1, source_target_pairs={{0,4},{1,5},{2,6},{3,7},{4,0},{5,1},{6,2},{7,3},{8,12},{9,13},{10,... | collective-permute-start | bytes 2064392 | tf_op jit(solution)/shard_map/ppermute | solution.py:242
  228.3 17.1 %collective-permute-start.43 = (bf16[5,896]{1,0:T(8,128)(2,1)S(1)}, bf16[5,896]{1,0:T(8,128)(2,1)S(1)}, u32[]{:S(2)}, u32[]{:S(2)}) collective-permute-start(bf16[5,896]{1,0:T(8,128)(2,1)S(1)} %concatenate.71), channel_id=1, source_target_pairs={{0,6},{1,7},{2,4},{3,5},{4,2},{5,3},{6,0},{7,1},{8,14},{9,15},{10,... | collective-permute-start | bytes 26888 | tf_op jit(solution)/shard_map/ppermute | solution.py:242
  230.7 32.4 %copy-start.17 = (s32[32]{0:T(128)S(1)}, s32[32]{0:T(128)}, u32[]{:S(2)}) copy-start(s32[32]{0:T(128)} %param.12) | copy-start | bytes 388
  231.7 15.8 %collective-permute-start.42 = (bf16[5,896]{1,0:T(8,128)(2,1)S(1)}, bf16[5,896]{1,0:T(8,128)(2,1)S(1)}, u32[]{:S(2)}, u32[]{:S(2)}) collective-permute-start(bf16[5,896]{1,0:T(8,128)(2,1)S(1)} %concatenate.70), channel_id=1, source_target_pairs={{0,2},{1,3},{2,0},{3,1},{4,6},{5,7},{6,4},{7,5},{8,10},{9,11},{10,... | collective-permute-start | bytes 26888 | tf_op jit(solution)/shard_map/ppermute | solution.py:242
  245.5 3.9 %collective-permute-start.41 = (bf16[5,896]{1,0:T(8,128)(2,1)S(1)}, bf16[5,896]{1,0:T(8,128)(2,1)S(1)}, u32[]{:S(2)}, u32[]{:S(2)}) collective-permute-start(bf16[5,896]{1,0:T(8,128)(2,1)S(1)} %concatenate.69), channel_id=1, source_target_pairs={{0,4},{1,5},{2,6},{3,7},{4,0},{5,1},{6,2},{7,3},{8,12},{9,13},{10,... | collective-permute-start | bytes 26888 | tf_op jit(solution)/shard_map/ppermute | solution.py:242
  247.5 12.4 %collective-permute-start.33 = (bf16[1,128,896]{2,1,0:T(8,128)(2,1)S(1)}, bf16[1,128,896]{2,1,0:T(8,128)(2,1)S(1)}, u32[]{:S(2)}, u32[]{:S(2)}) collective-permute-start(bf16[1,128,896]{2,1,0:T(8,128)(2,1)S(1)} %get-tuple-element.51), channel_id=1, source_target_pairs={{0,4},{1,5},{2,6},{3,7},{4,0},{5,1},{6,2},{7,3},{8,12},{9,13},{10,... | collective-permute-start | bytes 688136 | tf_op jit(solution)/shard_map/ppermute | solution.py:242
  249.3 15.2 %collective-permute-start.36 = (bf16[1,128,896]{2,1,0:T(8,128)(2,1)S(1)}, bf16[1,128,896]{2,1,0:T(8,128)(2,1)S(1)}, u32[]{:S(2)}, u32[]{:S(2)}) collective-permute-start(bf16[1,128,896]{2,1,0:T(8,128)(2,1)S(1)} %get-tuple-element.50), channel_id=1, source_target_pairs={{0,2},{1,3},{2,0},{3,1},{4,6},{5,7},{6,4},{7,5},{8,10},{9,11},{10,... | collective-permute-start | bytes 688136 | tf_op jit(solution)/shard_map/ppermute | solution.py:242
  252.2 10.7 %all-to-all-start = ((f32[32,1,128]{2,1,0:T(1,128)}), f32[32,1,128]{2,1,0:T(1,128)S(1)}, u32[]{:S(2)}, u32[]{:S(2)}) async-start(f32[32,1,128]{2,1,0:T(1,128)} %bitcast.119), calls=%async_computation | async-start | bytes 32768 | tf_op jit(solution)/shard_map/all_to_all | solution.py:425
  256.4 9.5 %collective-permute-start.39 = (bf16[1,128,896]{2,1,0:T(8,128)(2,1)S(1)}, bf16[1,128,896]{2,1,0:T(8,128)(2,1)S(1)}, u32[]{:S(2)}, u32[]{:S(2)}) collective-permute-start(bf16[1,128,896]{2,1,0:T(8,128)(2,1)S(1)} %get-tuple-element.49), channel_id=1, source_target_pairs={{0,6},{1,7},{2,4},{3,5},{4,2},{5,3},{6,0},{7,1},{8,14},{9,15},{10,... | collective-permute-start | bytes 688136 | tf_op jit(solution)/shard_map/ppermute | solution.py:242
  259.0 11.7 %collective-permute-start.34 = (bf16[1,128,896]{2,1,0:T(8,128)(2,1)S(1)}, bf16[1,128,896]{2,1,0:T(8,128)(2,1)S(1)}, u32[]{:S(2)}, u32[]{:S(2)}) collective-permute-start(bf16[1,128,896]{2,1,0:T(8,128)(2,1)S(1)} %get-tuple-element.47), channel_id=1, source_target_pairs={{0,4},{1,5},{2,6},{3,7},{4,0},{5,1},{6,2},{7,3},{8,12},{9,13},{10,... | collective-permute-start | bytes 688136 | tf_op jit(solution)/shard_map/ppermute | solution.py:242
  259.6 11.4 %collective-permute-start.37 = (bf16[1,128,896]{2,1,0:T(8,128)(2,1)S(1)}, bf16[1,128,896]{2,1,0:T(8,128)(2,1)S(1)}, u32[]{:S(2)}, u32[]{:S(2)}) collective-permute-start(bf16[1,128,896]{2,1,0:T(8,128)(2,1)S(1)} %get-tuple-element.46), channel_id=1, source_target_pairs={{0,2},{1,3},{2,0},{3,1},{4,6},{5,7},{6,4},{7,5},{8,10},{9,11},{10,... | collective-permute-start | bytes 688136 | tf_op jit(solution)/shard_map/ppermute | solution.py:242
  259.9 15.2 %collective-permute-start.40 = (bf16[1,128,896]{2,1,0:T(8,128)(2,1)S(1)}, bf16[1,128,896]{2,1,0:T(8,128)(2,1)S(1)}, u32[]{:S(2)}, u32[]{:S(2)}) collective-permute-start(bf16[1,128,896]{2,1,0:T(8,128)(2,1)S(1)} %get-tuple-element.45), channel_id=1, source_target_pairs={{0,6},{1,7},{2,4},{3,5},{4,2},{5,3},{6,0},{7,1},{8,14},{9,15},{10,... | collective-permute-start | bytes 688136 | tf_op jit(solution)/shard_map/ppermute | solution.py:242
  (16 other events, 137.5 us)
